TPU v7x, 32 devices: a whole 2x2x4 slice. The times are simulated.
32 devices in a mesh: dp: 8 (over z, y), group: 4 (over x, core).
Axes of the slice: x: 2, y: 2, z: 4, core: 2. Of those that a mesh axis runs over, the one named last changes fastest.
Arguments:
- tokens: bfloat16 [16384, 1024], P(('dp', 'group')), may hold values from -16 to 16
- segment_ids: int32 [16384], P(('dp', 'group')), may hold values from 0 to 3, as said below
- positions: int32 [16384], P(('dp', 'group')), may hold values from 0 to 1999, as said below
- cotangent: bfloat16 [16384, 1024], P(('dp', 'group')), may hold values from -6 to 6
- qkv_weight: float32 [1024, 4096], P('group'), may hold values from -1 to 1
- out_weight: float32 [2048, 1024], P('group'), may hold values from -1 to 1
- gate_up_weight: float32 [1024, 6144], P('group'), may hold values from -0.1875 to 0.1875
- down_weight: float32 [3072, 1024], P('group'), may hold values from -0.109375 to 0.109375
- norm_gains: float32 [2, 1024], P(None, 'group'), may hold values from 0.5 to 1.5
- head_gains: float32 [2, 128], P(None, 'group'), may hold values from 0.6 to 1.4
- qkv_moments: float32 [2, 1024, 4096], P(None, 'group'), as said below
- out_moments: float32 [2, 2048, 1024], P(None, 'group'), as said below
- gate_up_moments: float32 [2, 1024, 6144], P(None, 'group'), as said below
- down_moments: float32 [2, 3072, 1024], P(None, 'group'), as said below
- norm_moments: float32 [2, 2, 1024], P(None, None, 'group'), as said below
- head_moments: float32 [2, 2, 128], P(None, None, 'group'), as said below
Outputs:
- output: bfloat16 [16384, 1024], P(('dp', 'group'))
- tokens_grad: bfloat16 [16384, 1024], P(('dp', 'group'))
- qkv_grad: float32 [1024, 4096], P('group', 'dp')
- out_grad: float32 [2048, 1024], P('group', 'dp')
- gate_up_grad: float32 [1024, 6144], P('group', 'dp')
- down_grad: float32 [3072, 1024], P('group', 'dp')
- norm_grad: float32 [2, 1024], P(None, 'group')
- head_grad: float32 [2, 128], P(None, 'group')
- new_qkv_weight: float32 [1024, 4096], P('group')
- new_out_weight: float32 [2048, 1024], P('group')
- new_gate_up_weight: float32 [1024, 6144], P('group')
- new_down_weight: float32 [3072, 1024], P('group')
- new_norm_gains: float32 [2, 1024], P(None, 'group')
- new_head_gains: float32 [2, 128], P(None, 'group')
- new_qkv_moments: float32 [2, 1024, 4096], P(None, 'group')
- new_out_moments: float32 [2, 2048, 1024], P(None, 'group')
- new_gate_up_moments: float32 [2, 1024, 6144], P(None, 'group')
- new_down_moments: float32 [2, 3072, 1024], P(None, 'group')
- new_norm_moments: float32 [2, 2, 1024], P(None, None, 'group')
- new_head_moments: float32 [2, 2, 128], P(None, None, 'group')
Inputs may be any that keep to these rules, and one draw needn't show every extreme that they name: `segment_ids`: along each sequence of 512 consecutive tokens the ids never fall; equal ids within a sequence mark one document. A token's position counts from its document's first token, which may lie in an earlier sequence; within a document positions rise by one. `qkv_moments`: the second moments are positive. `out_moments`: the second moments are positive. `gate_up_moments`: the second moments are positive. `down_moments`: the second moments are positive. `norm_moments`: the second moments are positive. `head_moments`: the second moments are positive.
All inputs are finite; a program needn't handle non-finite values.
Results may differ from a plain program's by a relative error of at most 0.013.
The roundings to bfloat16 on the way count: a program that leaves them out, or rounds other values in their place, can miss the bound.
Values may be sent and summed in bfloat16 or wider, within the bound.
A program may use at most 320 MiB of HBM per device.

v0:
```python
import math

import jax
import jax.numpy as jnp
from jax import lax
from jax.sharding import PartitionSpec as P

HQ = 16
HK = 8
HD = 128
FF = 3072
SEQ_LEN = 512
PARAMS = 15730944


EPS_NORM = 1e-06
ROPE_BASE = 1000000.0
MASKED = -1e30
LEARN_RATE = 0.03
GAIN_RATE = 0.3
WEIGHT_DECAY = 0.1
BETA_ONE = 0.9
BETA_TWO = 0.95
ADAM_EPS = 1e-08
STEP_COUNT = 3.0


def rotary_tables(places, width):
    half_width = width // 2
    frequency = ROPE_BASE ** (-(jnp.arange(half_width, dtype=jnp.float32) * 2.0) / width)
    angles = places.astype(jnp.float32)[:, None] * frequency[None, :]
    return (jnp.cos(angles), jnp.sin(angles))


def rotate(values, cosine, sine_table):
    half_width = values.shape[-1] // 2
    front_half = values[..., :half_width]
    back_half = values[..., half_width:]
    cosine = cosine[:, None, :]
    sine_table = sine_table[:, None, :]
    return jnp.concatenate(
        [
            front_half * cosine - back_half * sine_table,
            back_half * cosine + front_half * sine_table,
        ],
        axis=-1,
    )


def contract_rows(left_side, right_side):
    return lax.dot_general(
        left_side, right_side, (((0,), (0,)), ((), ())), preferred_element_type=jnp.float32
    )


def contract_cols(left_side, right_side):
    return lax.dot_general(
        left_side, right_side, (((1,), (1,)), ((), ())), preferred_element_type=jnp.float32
    )


def norm_back(grad_out, normed, inv_root, gain):
    scaled = grad_out * gain
    return inv_root * (scaled - normed * jnp.mean(normed * scaled, axis=-1, keepdims=True))


def joined_order(gradient, along, owners, copies):
    layout = gradient.shape
    pieces_shape = (
        layout[:along] + (owners, copies, layout[along] // (owners * copies)) + layout[along + 1 :]
    )
    return jnp.swapaxes(gradient.reshape(pieces_shape), along, along + 1).reshape(layout)


def own_columns(gradient, index, count):
    width = gradient.shape[1] // count
    return lax.dynamic_slice_in_dim(gradient, index * width, width, 1)


def adam_update(master, moment, gradient, factor, step_rate, decay_rate):
    clipped = gradient * factor
    first_moment = BETA_ONE * moment[0] + (1.0 - BETA_ONE) * clipped
    second = BETA_TWO * moment[1] + (1.0 - BETA_TWO) * clipped * clipped
    first_hat = first_moment / (1.0 - BETA_ONE**STEP_COUNT)
    second_hat = second / (1.0 - BETA_TWO**STEP_COUNT)
    renewed = master - step_rate * (
        first_hat / (jnp.sqrt(second_hat) + ADAM_EPS) + decay_rate * master
    )
    return (renewed, jnp.stack([first_moment, second]))


def on_device(
    tokens,
    segment_ids,
    positions,
    cotangent,
    qkv_weight,
    out_weight,
    gate_up_weight,
    down_weight,
    norm_gains,
    head_gains,
    qkv_moments,
    out_moments,
    gate_up_moments,
    down_moments,
    norm_moments,
    head_moments,
):
    full_qkv, full_out, full_gate_up, full_down, full_norm, full_head = (
        lax.all_gather(qkv_weight.astype(jnp.bfloat16), "group", axis=0, tiled=True),
        lax.all_gather(out_weight.astype(jnp.bfloat16), "group", axis=0, tiled=True),
        lax.all_gather(gate_up_weight.astype(jnp.bfloat16), "group", axis=0, tiled=True),
        lax.all_gather(down_weight.astype(jnp.bfloat16), "group", axis=0, tiled=True),
        lax.all_gather(norm_gains.astype(jnp.bfloat16), "group", axis=1, tiled=True),
        lax.all_gather(head_gains.astype(jnp.bfloat16), "group", axis=1, tiled=True),
    )
    token_rows = tokens.shape[0]
    seq_count = token_rows // SEQ_LEN
    groups = HQ // HK
    inv_head = 1.0 / math.sqrt(HD)
    gain_one = full_norm[0].astype(jnp.float32)
    gain_two = full_norm[1].astype(jnp.float32)
    gain_query = full_head[0].astype(jnp.float32)
    gain_key = full_head[1].astype(jnp.float32)
    inputs = tokens.astype(jnp.float32)
    root_one = lax.rsqrt(jnp.mean(inputs * inputs, axis=-1, keepdims=True) + EPS_NORM)
    normed_one = inputs * root_one
    hidden_one = (normed_one * gain_one).astype(jnp.bfloat16)
    projected = jnp.dot(hidden_one, full_qkv, preferred_element_type=jnp.float32)
    query_raw = projected[:, : HQ * HD].reshape(token_rows, HQ, HD)
    key_raw = projected[:, HQ * HD : (HQ + HK) * HD].reshape(token_rows, HK, HD)
    value_low = projected[:, (HQ + HK) * HD :].reshape(token_rows, HK, HD).astype(jnp.bfloat16)
    cosine, sine_table = rotary_tables(positions, HD)
    query_root = lax.rsqrt(jnp.mean(query_raw * query_raw, axis=-1, keepdims=True) + EPS_NORM)
    query_normed = query_raw * query_root
    query_low = rotate(query_normed * gain_query, cosine, sine_table).astype(jnp.bfloat16)
    key_root = lax.rsqrt(jnp.mean(key_raw * key_raw, axis=-1, keepdims=True) + EPS_NORM)
    key_normed = key_raw * key_root
    key_low = rotate(key_normed * gain_key, cosine, sine_table).astype(jnp.bfloat16)
    query_blocks = query_low.reshape(seq_count, SEQ_LEN, HK, groups, HD)
    key_blocks = key_low.reshape(seq_count, SEQ_LEN, HK, HD)
    value_blocks = value_low.reshape(seq_count, SEQ_LEN, HK, HD)
    seg_blocks = segment_ids.reshape(seq_count, SEQ_LEN)
    places_idx = jnp.arange(SEQ_LEN)
    allowed = (seg_blocks[:, :, None] == seg_blocks[:, None, :]) & (
        places_idx[:, None] >= places_idx[None, :]
    )[None]
    allowed = allowed[:, None, None, :, :]

    def scores_of():
        raw_scores = (
            jnp.einsum(
                "sqkgd,spkd->skgqp", query_blocks, key_blocks, preferred_element_type=jnp.float32
            )
            * inv_head
        )
        return jnp.where(allowed, raw_scores, MASKED)

    scores = scores_of()
    row_peak = jnp.max(scores, axis=-1, keepdims=True)
    exp_total = jnp.sum(jnp.exp(scores - row_peak), axis=-1, keepdims=True)
    log_total = row_peak + jnp.log(exp_total)
    probs_low = jnp.exp(scores - log_total).astype(jnp.bfloat16)
    mixed_heads = jnp.einsum(
        "skgqp,spkd->sqkgd", probs_low, value_blocks, preferred_element_type=jnp.float32
    )
    mixed_low = mixed_heads.reshape(token_rows, HQ * HD).astype(jnp.bfloat16)
    attended = jnp.dot(mixed_low, full_out, preferred_element_type=jnp.float32)
    residual = inputs + attended
    root_two = lax.rsqrt(jnp.mean(residual * residual, axis=-1, keepdims=True) + EPS_NORM)
    normed_two = residual * root_two
    hidden_two = (normed_two * gain_two).astype(jnp.bfloat16)
    gate_up = jnp.dot(hidden_two, full_gate_up, preferred_element_type=jnp.float32)
    gate_part = gate_up[:, :FF]
    upward = gate_up[:, FF:]
    sigmoid_gate = jax.nn.sigmoid(gate_part)
    activated = (gate_part * sigmoid_gate * upward).astype(jnp.bfloat16)
    branch = jnp.dot(activated, full_down, preferred_element_type=jnp.float32)
    output = (residual + branch).astype(jnp.bfloat16)
    upstream = cotangent.astype(jnp.float32)
    down_local = contract_rows(activated, cotangent)
    grad_act = contract_cols(cotangent, full_down)
    grad_gate = grad_act * upward * sigmoid_gate * (1.0 + gate_part * (1.0 - sigmoid_gate))
    grad_up = grad_act * gate_part * sigmoid_gate
    grad_gate_up = jnp.concatenate([grad_gate, grad_up], axis=-1).astype(jnp.bfloat16)
    gate_up_local = contract_rows(hidden_two, grad_gate_up)
    grad_hidden_two = contract_cols(grad_gate_up, full_gate_up)
    grad_gain_two = jnp.sum(grad_hidden_two * normed_two, axis=0)
    grad_residual = upstream + norm_back(grad_hidden_two, normed_two, root_two, gain_two)
    residual_low = grad_residual.astype(jnp.bfloat16)
    out_local = contract_rows(mixed_low, residual_low)
    grad_mixed = (
        contract_cols(residual_low, full_out)
        .astype(jnp.bfloat16)
        .reshape(seq_count, SEQ_LEN, HK, groups, HD)
    )
    attn_probs = jnp.exp(scores_of() - log_total)
    grad_probs = jnp.einsum(
        "sqkgd,spkd->skgqp", grad_mixed, value_blocks, preferred_element_type=jnp.float32
    )
    grad_value = jnp.einsum(
        "skgqp,sqkgd->spkd",
        attn_probs.astype(jnp.bfloat16),
        grad_mixed,
        preferred_element_type=jnp.float32,
    )
    grad_scores = (
        attn_probs * (grad_probs - jnp.sum(attn_probs * grad_probs, axis=-1, keepdims=True))
    ).astype(jnp.bfloat16)
    grad_query = (
        jnp.einsum("skgqp,spkd->sqkgd", grad_scores, key_blocks, preferred_element_type=jnp.float32)
        * inv_head
    )
    grad_key = (
        jnp.einsum(
            "skgqp,sqkgd->spkd", grad_scores, query_blocks, preferred_element_type=jnp.float32
        )
        * inv_head
    )
    grad_query = rotate(grad_query.reshape(token_rows, HQ, HD), cosine, -sine_table)
    grad_key = rotate(grad_key.reshape(token_rows, HK, HD), cosine, -sine_table)
    grad_gain_query = jnp.sum(grad_query * query_normed, axis=(0, 1))
    grad_gain_key = jnp.sum(grad_key * key_normed, axis=(0, 1))
    grad_query_raw = norm_back(grad_query, query_normed, query_root, gain_query)
    grad_key_raw = norm_back(grad_key, key_normed, key_root, gain_key)
    grad_projected = jnp.concatenate(
        [
            grad_query_raw.reshape(token_rows, HQ * HD),
            grad_key_raw.reshape(token_rows, HK * HD),
            grad_value.reshape(token_rows, HK * HD),
        ],
        axis=-1,
    ).astype(jnp.bfloat16)
    qkv_local = contract_rows(hidden_one, grad_projected)
    grad_hidden_one = contract_cols(grad_projected, full_qkv)
    grad_gain_one = jnp.sum(grad_hidden_one * normed_one, axis=0)
    grad_inputs = grad_residual + norm_back(grad_hidden_one, normed_one, root_one, gain_one)
    tokens_grad = grad_inputs.astype(jnp.bfloat16)
    norm_local = jnp.stack([grad_gain_one, grad_gain_two])
    head_local = jnp.stack([grad_gain_query, grad_gain_key])
    owners = lax.axis_size("group")
    copies = lax.axis_size("dp")
    pieces = (
        lax.psum_scatter(
            joined_order(qkv_local, 0, owners, copies),
            ("dp", "group"),
            scatter_dimension=0,
            tiled=True,
        ),
        lax.psum_scatter(
            joined_order(out_local, 0, owners, copies),
            ("dp", "group"),
            scatter_dimension=0,
            tiled=True,
        ),
        lax.psum_scatter(
            joined_order(gate_up_local, 0, owners, copies),
            ("dp", "group"),
            scatter_dimension=0,
            tiled=True,
        ),
        lax.psum_scatter(
            joined_order(down_local, 0, owners, copies),
            ("dp", "group"),
            scatter_dimension=0,
            tiled=True,
        ),
        lax.psum_scatter(
            joined_order(norm_local, 1, owners, copies),
            ("dp", "group"),
            scatter_dimension=1,
            tiled=True,
        ),
        lax.psum_scatter(
            joined_order(head_local, 1, owners, copies),
            ("dp", "group"),
            scatter_dimension=1,
            tiled=True,
        ),
    )
    summed = (
        lax.all_gather(pieces[0], "dp", axis=0, tiled=True),
        lax.all_gather(pieces[1], "dp", axis=0, tiled=True),
        lax.all_gather(pieces[2], "dp", axis=0, tiled=True),
        lax.all_gather(pieces[3], "dp", axis=0, tiled=True),
        lax.all_gather(pieces[4], "dp", axis=1, tiled=True),
        lax.all_gather(pieces[5], "dp", axis=1, tiled=True),
    )
    squares = sum((jnp.sum(gradient * gradient) for gradient in summed))
    grad_total = lax.psum(squares, "group")
    clip_limit = math.sqrt(PARAMS)
    factor = clip_limit / jnp.maximum(jnp.sqrt(grad_total), clip_limit)
    masters = (qkv_weight, out_weight, gate_up_weight, down_weight, norm_gains, head_gains)
    moments = (qkv_moments, out_moments, gate_up_moments, down_moments, norm_moments, head_moments)
    rates = (LEARN_RATE, LEARN_RATE, LEARN_RATE, LEARN_RATE, GAIN_RATE, GAIN_RATE)
    decays = (WEIGHT_DECAY, WEIGHT_DECAY, WEIGHT_DECAY, WEIGHT_DECAY, 0.0, 0.0)
    renewed_all = []
    moments_all = []
    for master, moment, gradient, step_rate, decay_rate in zip(
        masters, moments, summed, rates, decays
    ):
        renewed, stacked = adam_update(master, moment, gradient, factor, step_rate, decay_rate)
        renewed_all.append(renewed)
        moments_all.append(stacked)
    column_index = lax.axis_index("dp")
    column_count = lax.axis_size("dp")
    return (
        output,
        tokens_grad,
        own_columns(summed[0], column_index, column_count),
        own_columns(summed[1], column_index, column_count),
        own_columns(summed[2], column_index, column_count),
        own_columns(summed[3], column_index, column_count),
        summed[4],
        summed[5],
        renewed_all[0],
        renewed_all[1],
        renewed_all[2],
        renewed_all[3],
        renewed_all[4],
        renewed_all[5],
        moments_all[0],
        moments_all[1],
        moments_all[2],
        moments_all[3],
        moments_all[4],
        moments_all[5],
    )


def solution(mesh):
    placed = (
        P(("dp", "group"), None),
        P(("dp", "group")),
        P(("dp", "group")),
        P(("dp", "group"), None),
        P("group", None),
        P("group", None),
        P("group", None),
        P("group", None),
        P(None, "group"),
        P(None, "group"),
        P(None, "group", None),
        P(None, "group", None),
        P(None, "group", None),
        P(None, "group", None),
        P(None, None, "group"),
        P(None, None, "group"),
    )
    return jax.shard_map(
        on_device,
        mesh=mesh,
        in_specs=placed,
        out_specs=(
            P(("dp", "group"), None),
            P(("dp", "group"), None),
            P("group", "dp"),
            P("group", "dp"),
            P("group", "dp"),
            P("group", "dp"),
            P(None, "group"),
            P(None, "group"),
            P("group", None),
            P("group", None),
            P("group", None),
            P("group", None),
            P(None, "group"),
            P(None, "group"),
            P(None, "group", None),
            P(None, "group", None),
            P(None, "group", None),
            P(None, "group", None),
            P(None, None, "group"),
            P(None, None, "group"),
        ),
        check_vma=False,
    )
```

profile of v0, /device:TPU:0, one launch (start us, length us, event | category | flops | bytes accessed | tf_op | source)
XLA Modules:
  0.0 1525.3 jit_solution(2794801300747954)
XLA Ops:
  35.1 37.2 %all-gather.12.cloned.1.call-done = bf16[1024,4096]{1,0:T(8,128)(2,1)} async-done(((bf16[256,4096]{1,0:T(8,128)(2,1)}), bf16[1024,4096]{1,0:T(8,128)(2,1)}) %all-gather.12.cloned.1.call-update) | async-done | bytes 8388624 | tf_op jit(solution)/shard_map/all_gather | solution.py:111
  72.4 7.4 fusion.63
  98.5 8.5 fusion.81
  107.0 8.2 exponential_reduce_fusion
  115.3 12.1 fusion.37
  133.9 59.3 %all-gather.16.cloned.1.call-done = bf16[1024,6144]{1,0:T(8,128)(2,1)} async-done(((bf16[256,6144]{1,0:T(8,128)(2,1)}), bf16[1024,6144]{1,0:T(8,128)(2,1)}) %all-gather.16.cloned.1.call-update) | async-done | bytes 12582928 | tf_op jit(solution)/shard_map/all_gather | solution.py:113
  193.2 14.6 fusion.79
  207.9 33.8 %all-gather.18.cloned.1.call-done = bf16[3072,1024]{1,0:T(8,128)(2,1)} async-done(((bf16[768,1024]{1,0:T(8,128)(2,1)}), bf16[3072,1024]{1,0:T(8,128)(2,1)}) %all-gather.18.cloned.1.call-update) | async-done | bytes 6291472 | tf_op jit(solution)/shard_map/all_gather | solution.py:114
  241.6 13.2 multiply_convert_fusion.1
  254.9 14.3 multiply_reduce_fusion.6
  279.2 10.4 fusion.82
  289.6 11.9 copy.233
  311.5 11.0 fusion
  322.6 12.8 fusion.5
  363.6 8.9 bitcast_convert_fusion
  387.4 7.8 fusion.11
  408.0 15.1 fusion.12
  423.0 17.7 %copy.232 = f32[8,4,32,6144]{3,2,1,0:T(8,128)} copy(f32[8,4,32,6144]{3,2,0,1:T(8,128)} %bitcast.333) | data formatting | bytes 50331648 | tf_op jit(solution)/shard_map/transpose | solution.py:72
  442.4 10.6 fusion.29
  455.0 130.7 %reduce-scatter.15.cloned.1.call-done = f32[96,1024]{1,0:T(8,128)} async-done(((f32[3072,1024]{1,0:T(8,128)}), f32[96,1024]{1,0:T(8,128)}) %reduce-scatter.15.cloned.1.call-update) | async-done | bytes 393232 | tf_op jit(solution)/shard_map/reduce_scatter | solution.py:263
  585.7 184.1 %reduce-scatter.9.cloned.1.call-done = f32[32,4096]{1,0:T(8,128)} async-done(((f32[1024,4096]{1,0:T(8,128)}), f32[32,4096]{1,0:T(8,128)}) %reduce-scatter.9.cloned.1.call-update) | async-done | bytes 524304 | tf_op jit(solution)/shard_map/reduce_scatter | solution.py:245
  769.9 251.2 %reduce-scatter.13.cloned.1.call-done = f32[32,6144]{1,0:T(8,128)} async-done(((f32[1024,6144]{1,0:T(8,128)}), f32[32,6144]{1,0:T(8,128)}) %reduce-scatter.13.cloned.1.call-update) | async-done | bytes 786448 | tf_op jit(solution)/shard_map/reduce_scatter | solution.py:257
  1021.5 40.2 %all-reduce = f32[2,128]{1,0:T(2,128)S(1)} all-reduce(f32[2,128]{1,0:T(2,128)S(1)} %reshape.437), channel_id=7, replica_groups=mesh['dp'=8,'group'=4] {'dp','group'}, use_global_device_ids=true, to_apply=%region_22.23.clone | all-reduce | flops 256 | bytes 2048
  1061.8 20.0 %all-gather.2 = f32[8,4,2]{1,2,0:T(2,128)S(1)} all-gather(f32[1,4,2]{1,2,0:T(2,128)S(1)} %dynamic-slice_bitcast_fusion), channel_id=1, replica_groups=mesh['dp'=8,'group'=4] {'dp'}, dimensions={0}, use_global_device_ids=true | all-gather | bytes 288 | tf_op jit(solution)/shard_map/all_gather | solution.py:288
  1093.1 66.1 %reduce-scatter.17.cloned.1.call-done = f32[32,2]{1,0:T(8,128)} async-done(((f32[1024,2]{1,0:T(8,128)}), f32[32,2]{1,0:T(8,128)}) %reduce-scatter.17.cloned.1.call-update) | async-done | bytes 272
  1160.0 16.3 %all-gather.1 = f32[8,32,2]{1,2,0:T(2,128)S(1)} all-gather(f32[1,32,2]{1,2,0:T(2,128)S(1)} %bitcast.382), channel_id=1, replica_groups=mesh['dp'=8,'group'=4] {'dp'}, dimensions={0}, use_global_device_ids=true | all-gather | bytes 2304 | tf_op jit(solution)/shard_map/all_gather | solution.py:287
  1177.0 29.3 %all-gather.22.cloned.1.call-done = f32[512,1024]{1,0:T(8,128)} async-done(((f32[64,1024]{1,0:T(8,128)}), f32[512,1024]{1,0:T(8,128)}) %all-gather.22.cloned.1.call-update) | async-done | bytes 2097168 | tf_op jit(solution)/shard_map/all_gather | solution.py:284
  1210.7 56.4 %all-gather.26.cloned.1.call-done = f32[768,1024]{1,0:T(8,128)} async-done(((f32[96,1024]{1,0:T(8,128)}), f32[768,1024]{1,0:T(8,128)}) %all-gather.26.cloned.1.call-update) | async-done | bytes 3145744 | tf_op jit(solution)/shard_map/all_gather | solution.py:286
  1272.2 68.4 %all-gather.20.cloned.1.call-done = f32[256,4096]{1,0:T(8,128)} async-done(((f32[32,4096]{1,0:T(8,128)}), f32[256,4096]{1,0:T(8,128)}) %all-gather.20.cloned.1.call-update) | async-done | bytes 4194320 | tf_op jit(solution)/shard_map/all_gather | solution.py:283
  1346.1 93.9 %all-gather.24.cloned.1.call-done = f32[256,6144]{1,0:T(8,128)} async-done(((f32[32,6144]{1,0:T(8,128)}), f32[256,6144]{1,0:T(8,128)}) %all-gather.24.cloned.1.call-update) | async-done | bytes 6291472 | tf_op jit(solution)/shard_map/all_gather | solution.py:285
  1470.3 13.3 fusion.45
  1483.6 10.9 pad_maximum_fusion
  (258 shorter events, 209.2 us)
Async XLA Ops:
  7.2 65.2 %all-gather.12.cloned.1.call-start = ((), (), s32[]{:S(2)}) async-start(), calls=%async_computation.5 | async-start | bytes 10485760 | tf_op jit(solution)/shard_map/all_gather | solution.py:111
  11.2 116.2 %all-gather.14.cloned.1.call-start = ((), (), s32[]{:S(2)}) async-start(), calls=%async_computation.6 | async-start | bytes 5242880 | tf_op jit(solution)/shard_map/all_gather | solution.py:112
  12.4 180.8 %all-gather.16.cloned.1.call-start = ((), (), s32[]{:S(2)}) async-start(), calls=%async_computation.7 | async-start | bytes 15728640 | tf_op jit(solution)/shard_map/all_gather | solution.py:113
  17.6 14.9 copy-start.51
  17.6 14.9 copy-start.45
  17.6 224.1 %all-gather.18.cloned.1.call-start = ((), (), s32[]{:S(2)}) async-start(), calls=%async_computation.8 | async-start | bytes 7864320 | tf_op jit(solution)/shard_map/all_gather | solution.py:114
  19.1 435.3 %reduce-scatter.11.cloned.1.call-start = ((), (), s32[]{:S(2)}) async-start(), calls=%async_computation.11 | async-start | bytes 8650752 | tf_op jit(solution)/shard_map/reduce_scatter | solution.py:251
  25.2 54.6 %copy-start.39 = (f32[1,1024]{1,0:T(1,128)}, f32[1,1024]{1,0:T(1,128)S(1)}, u32[]{:S(2)}) copy-start(f32[1,1024]{1,0:T(1,128)S(1)} %get-tuple-element.63) | copy-start | bytes 12292
  26.8 53.0 %copy-start.42 = (f32[512]{0:T(512)}, f32[512]{0:T(512)S(1)}, u32[]{:S(2)}) copy-start(f32[512]{0:T(512)S(1)} %add_rsqrt_fusion.3) | copy-start | bytes 6148
  35.1 56.0 %copy-start.33 = (f32[512,64]{1,0:T(8,128)}, f32[512,64]{1,0:T(8,128)S(1)}, u32[]{:S(2)}) copy-start(f32[512,64]{1,0:T(8,128)S(1)} %get-tuple-element.68) | copy-start | bytes 393220
  35.1 62.4 %copy-start.22 = (f32[512,64]{1,0:T(8,128)}, f32[512,64]{1,0:T(8,128)S(1)}, u32[]{:S(2)}) copy-start(f32[512,64]{1,0:T(8,128)S(1)} %get-tuple-element.69) | copy-start | bytes 393220
  80.1 16.8 %copy-start.5 = (f32[64,8,8,128]{3,2,1,0:T(8,128)}, f32[64,8,8,128]{3,2,1,0:T(8,128)S(1)}, u32[]{:S(2)}) copy-start(f32[64,8,8,128]{3,2,1,0:T(8,128)S(1)} %get-tuple-element.45) | copy-start | bytes 6291460
  207.9 47.0 %copy-start.14 = (f32[512,1024]{1,0:T(8,128)S(1)}, f32[512,1024]{1,0:T(8,128)}, u32[]{:S(2)}) copy-start(f32[512,1024]{1,0:T(8,128)} %get-tuple-element.75) | copy-start | bytes 6291460
  272.4 30.1 %copy-start.7 = (f32[512,1024]{1,0:T(8,128)}, f32[512,1024]{1,0:T(8,128)S(1)}, u32[]{:S(2)}) copy-start(f32[512,1024]{1,0:T(8,128)S(1)} %multiply_add_fusion.2) | copy-start | bytes 6291460
  279.0 306.7 %reduce-scatter.15.cloned.1.call-start = ((), (), s32[]{:S(2)}) async-start(), calls=%async_computation.15 | async-start | bytes 12976128 | tf_op jit(solution)/shard_map/reduce_scatter | solution.py:263
  301.6 468.3 %reduce-scatter.9.cloned.1.call-start = ((), (), s32[]{:S(2)}) async-start(), calls=%async_computation.9 | async-start | bytes 17301504 | tf_op jit(solution)/shard_map/reduce_scatter | solution.py:245
  322.5 12.9 copy-start.27
  373.1 22.2 %copy-start.30 = (bf16[512,1024]{1,0:T(8,128)(2,1)}, bf16[512,1024]{1,0:T(8,128)(2,1)S(1)}, u32[]{:S(2)}) copy-start(bf16[512,1024]{1,0:T(8,128)(2,1)S(1)} %copy.257) | copy-start | bytes 3145732
  406.4 614.7 %reduce-scatter.13.cloned.1.call-start = ((), (), s32[]{:S(2)}) async-start(), calls=%async_computation.13 | async-start | bytes 25952256 | tf_op jit(solution)/shard_map/reduce_scatter | solution.py:257
  440.8 718.5 %reduce-scatter.17.cloned.1.call-start = ((), (), s32[]{:S(2)}) async-start(), calls=%async_computation.17 | async-start | bytes 540672
  453.1 629.4 %copy-start.8 = (f32[512,1024]{1,0:T(8,128)S(1)}, f32[512,1024]{1,0:T(8,128)}, u32[]{:S(2)}) copy-start(f32[512,1024]{1,0:T(8,128)} %copy-done.7) | copy-start | bytes 6291460
  454.3 752.0 %all-gather.22.cloned.1.call-start = ((), (), s32[]{:S(2)}) async-start(), calls=%async_computation.12 | async-start | bytes 2359296 | tf_op jit(solution)/shard_map/all_gather | solution.py:284
  454.9 812.2 %all-gather.26.cloned.1.call-start = ((), (), s32[]{:S(2)}) async-start(), calls=%async_computation.16 | async-start | bytes 3538944 | tf_op jit(solution)/shard_map/all_gather | solution.py:286
  585.7 754.9 %all-gather.20.cloned.1.call-start = ((), (), s32[]{:S(2)}) async-start(), calls=%async_computation.10 | async-start | bytes 4718592 | tf_op jit(solution)/shard_map/all_gather | solution.py:283
  769.9 670.1 %all-gather.24.cloned.1.call-start = ((), (), s32[]{:S(2)}) async-start(), calls=%async_computation.14 | async-start | bytes 7077888 | tf_op jit(solution)/shard_map/all_gather | solution.py:285
  1081.9 374.7 %copy-start.49 = (f32[32,2]{0,1:T(2,128)}, f32[32,2]{0,1:T(2,128)S(1)}, u32[]{:S(2)}) copy-start(f32[32,2]{0,1:T(2,128)S(1)} %reshape.447) | copy-start | bytes 772
  1176.4 280.8 %copy-start.44 = (f32[256,2]{0,1:T(2,128)}, f32[256,2]{0,1:T(2,128)S(1)}, u32[]{:S(2)}) copy-start(f32[256,2]{0,1:T(2,128)S(1)} %reshape.445) | copy-start | bytes 6148
  1344.4 112.2 %copy-start.52 = (f32[2,2,32]{2,1,0:T(2,128)S(1)}, f32[2,2,32]{2,1,0:T(2,128)}, u32[]{:S(2)}) copy-start(f32[2,2,32]{2,1,0:T(2,128)} %param.31) | copy-start | bytes 1540
  1344.4 112.2 %copy-start.54 = (f32[2,32]{1,0:T(2,128)S(1)}, f32[2,32]{1,0:T(2,128)}, u32[]{:S(2)}) copy-start(f32[2,32]{1,0:T(2,128)} %param.25) | copy-start | bytes 772
  1344.4 112.8 %copy-start.47 = (f32[2,256]{1,0:T(2,128)S(1)}, f32[2,256]{1,0:T(2,128)}, u32[]{:S(2)}) copy-start(f32[2,256]{1,0:T(2,128)} %param.24) | copy-start | bytes 6148
  1344.4 112.8 %copy-start.50 = (f32[2,2,256]{2,1,0:T(2,128)S(1)}, f32[2,2,256]{2,1,0:T(2,128)}, u32[]{:S(2)}) copy-start(f32[2,2,256]{2,1,0:T(2,128)} %param.30) | copy-start | bytes 12292
  1344.4 114.6 %copy-start.10 = (f32[768,1024]{1,0:T(8,128)S(1)}, f32[768,1024]{1,0:T(8,128)}, u32[]{:S(2)}) copy-start(f32[768,1024]{1,0:T(8,128)} %all-gather.26.cloned.1.call-done) | copy-start | bytes 9437188
  (41 other events, 218.9 us)
Sparse Core Ops, SparseCore 0:
  11.3 60.9 all-gather.11
  74.5 34.4 all-gather.13
  111.1 82.0 all-gather.15
  195.2 46.3 all-gather.17
  279.1 149.9 reduce-scatter.10
  434.9 150.6 reduce-scatter.14
  588.0 181.8 reduce-scatter.8
  776.3 244.7 reduce-scatter.12
  1023.9 135.3 reduce-scatter.16
  1161.2 45.0 all-gather.21
  1208.5 58.5 all-gather.25
  1269.1 71.4 all-gather.19
  1342.7 97.2 all-gather.23
where the time goes:
time: 1540 us; the launch traced here: 1530 us
  waiting for transfers between devices  1010 us (66%)
  matrix products  162 us (11%)
  other arithmetic  145 us (9%)
  blocking collectives  94.4 us (6%)
  local copies, waits for them, and re-layouts  91.4 us (6%)
  between operations  20.3 us (1%)
    reduce_scatter x1, waiting for transfers between devices, on_device(): lax.psum_scatter(joined_order(gate_up_local, 0, owners, copies), ('dp', '...  251 us
    reduce_scatter x1, waiting for transfers between devices, on_device(): lax.psum_scatter(joined_order(qkv_local, 0, owners, copies), ('dp', 'grou...  184 us
    reduce_scatter x1, waiting for transfers between devices, on_device(): lax.psum_scatter(joined_order(down_local, 0, owners, copies), ('dp', 'gro...  131 us
    all_gather x1, waiting for transfers between devices, on_device(): lax.all_gather(pieces[2], 'dp', axis=0, tiled=True)  93.9 us
    all_gather x1, waiting for transfers between devices, on_device(): lax.all_gather(pieces[0], 'dp', axis=0, tiled=True)  68.4 us
    unnamed x14, waiting for transfers between devices  66.8 us
    all_gather x1, waiting for transfers between devices, on_device(): lax.all_gather(gate_up_weight.astype(jnp.bfloat16), 'group', axis=0, tile...  59.3 us
    another operation x12, other arithmetic, adam_update(): return (renewed, jnp.stack([first_moment, second]))  57.1 us
  transfers between devices with their start and end apart: 13, of which 11 were waited for; matrix products, arithmetic and copies ran while one was open for 18% of the time, Pallas kernels for 0%

commit v1 on v0

--- a/solution.py
+++ b/solution.py
@@ -3,6 +3,8 @@
 import jax
 import jax.numpy as jnp
 from jax import lax
+from jax.experimental import pallas as pl
+from jax.experimental.pallas import tpu as pltpu
 from jax.sharding import PartitionSpec as P
 
 HQ = 16
@@ -64,17 +66,242 @@
     return inv_root * (scaled - normed * jnp.mean(normed * scaled, axis=-1, keepdims=True))
 
 
-def joined_order(gradient, along, owners, copies):
-    layout = gradient.shape
-    pieces_shape = (
-        layout[:along] + (owners, copies, layout[along] // (owners * copies)) + layout[along + 1 :]
-    )
-    return jnp.swapaxes(gradient.reshape(pieces_shape), along, along + 1).reshape(layout)
-
-
-def own_columns(gradient, index, count):
-    width = gradient.shape[1] // count
-    return lax.dynamic_slice_in_dim(gradient, index * width, width, 1)
+def swap(value, axis, mask):
+    count = lax.axis_size(axis)
+    return lax.ppermute(value, axis, [(i, i ^ mask) for i in range(count)])
+
+
+def bit_masks(count):
+    return [1 << i for i in range(count.bit_length() - 1)]
+
+
+def gather_rows(shard):
+    owners = lax.axis_size("group")
+    copies = lax.axis_size("dp")
+    mine = lax.axis_index("group")
+    rows, columns = shard.shape
+    half = rows // 2
+    side = lax.axis_index("dp") & 1
+    split = copies > 1
+    pieces = [(shard, 0, 0)]
+    for mask in bit_masks(owners)[1:]:
+        if mask == 2 and split:
+            near = lax.dynamic_slice_in_dim(shard, side * half, half, 0)
+            first = swap(near, "group", mask)
+            second = swap(first, "dp", 1)
+            pieces += [(first, mask, side * half), (second, mask, (1 - side) * half)]
+        else:
+            pieces += [(swap(v, "group", mask), dg ^ mask, off) for v, dg, off in pieces]
+    pieces += [(swap(v, "group", 1), dg ^ 1, off) for v, dg, off in pieces]
+    full = jnp.zeros((rows * owners, columns), shard.dtype)
+    for value, delta, offset in pieces:
+        start = (mine ^ delta) * rows + offset
+        full = lax.dynamic_update_slice(full, value, (start, 0))
+    return full
+
+
+def spread_bits(position, masks):
+    total = 0
+    count = len(masks)
+    for i, mask in enumerate(masks):
+        total = total + ((position >> (count - 1 - i)) & 1) * mask
+    return total
+
+
+def grad_blocks(left, right, row_sets, column_masks):
+    tokens, rows = left.shape
+    columns = right.shape[1]
+    owners = lax.axis_size("group")
+    copies = lax.axis_size("dp")
+    row_block = rows // owners
+    column_block = columns // copies
+    mine = lax.axis_index("group")
+    here = lax.axis_index("dp")
+    if column_block % 128 or row_block % 16:
+        ordered = jnp.concatenate(
+            [
+                lax.dynamic_slice_in_dim(
+                    right, (here ^ spread_bits(p, column_masks)) * column_block, column_block, 1
+                )
+                for p in range(copies)
+            ],
+            axis=1,
+        )
+        return [
+            jnp.stack(
+                [
+                    contract_rows(
+                        lax.dynamic_slice_in_dim(left, (mine ^ dg) * row_block, row_block, 1),
+                        ordered,
+                    ).astype(jnp.bfloat16)
+                    for dg in row_set
+                ]
+            )
+            for row_set in row_sets
+        ]
+
+    def body(where, left_ref, right_ref, *rest):
+        outs, turned = rest[:-1], rest[-1]
+
+        @pl.when(pl.program_id(0) == 0)
+        def _():
+            turned[...] = left_ref[...].T
+
+        for out, row_set in zip(outs, row_sets):
+            for k, dg in enumerate(row_set):
+                start = pl.multiple_of((where[0] ^ dg) * row_block, row_block)
+                out[k] = jnp.dot(
+                    turned[pl.ds(start, row_block), :],
+                    right_ref[...],
+                    preferred_element_type=jnp.float32,
+                ).astype(jnp.bfloat16)
+
+    count = sum(len(row_set) for row_set in row_sets)
+    return pl.pallas_call(
+        body,
+        out_shape=[
+            jax.ShapeDtypeStruct((len(row_set), row_block, columns), jnp.bfloat16)
+            for row_set in row_sets
+        ],
+        grid_spec=pltpu.PrefetchScalarGridSpec(
+            num_scalar_prefetch=1,
+            grid=(copies,),
+            in_specs=[
+                pl.BlockSpec((tokens, rows), lambda p, where: (0, 0)),
+                pl.BlockSpec(
+                    (tokens, column_block),
+                    lambda p, where: (0, where[1] ^ spread_bits(p, column_masks)),
+                ),
+            ],
+            out_specs=[
+                pl.BlockSpec((len(row_set), row_block, column_block), lambda p, where: (0, 0, p))
+                for row_set in row_sets
+            ],
+            scratch_shapes=[pltpu.VMEM((rows, tokens), jnp.bfloat16)],
+        ),
+        compiler_params=pltpu.CompilerParams(vmem_limit_bytes=48 * 1024 * 1024),
+        cost_estimate=pl.CostEstimate(
+            flops=2 * tokens * count * row_block * columns,
+            bytes_accessed=2 * (tokens * rows + tokens * columns + count * row_block * columns),
+            transcendentals=0,
+        ),
+    )(jnp.stack([mine, here]).astype(jnp.int32), left, right)
+
+
+def reduce_grad(left, right):
+    owners = lax.axis_size("group")
+    copies = lax.axis_size("dp")
+    group_masks = bit_masks(owners)
+    column_masks = bit_masks(copies)
+    row_sets = []
+    for i, mask in enumerate(group_masks):
+        later = group_masks[i + 1 :]
+        row_sets.append([mask + spread_bits(p, later) for p in range(1 << len(later))])
+    row_sets.append([0])
+    first = grad_blocks(left, right, row_sets[:1], column_masks)
+    others = grad_blocks(left, right, row_sets[1:], column_masks)
+    kept = list(first) + list(others)
+    got = []
+    for i, mask in enumerate(group_masks):
+        size = 1 << (len(group_masks) - 1 - i)
+        outgoing = kept[i]
+        if got:
+            outgoing = sum(
+                (v[size : 2 * size].astype(jnp.float32) for v in got),
+                outgoing.astype(jnp.float32),
+            ).astype(jnp.bfloat16)
+        got.append(swap(outgoing, "group", mask))
+    parts = [kept[-1][0]] + [v[0] for v in got]
+    width = right.shape[1]
+    for mask in column_masks:
+        width //= 2
+        outgoing = sum(v[:, width : 2 * width].astype(jnp.float32) for v in parts)
+        parts.append(swap(outgoing.astype(jnp.bfloat16), "dp", mask))
+    return sum(v[:, :width].astype(jnp.float32) for v in parts)
+
+
+def gather_grad(own):
+    blocks = [(own.astype(jnp.bfloat16), 0)]
+    for mask in reversed(bit_masks(lax.axis_size("dp"))):
+        blocks += [(swap(v, "dp", mask), dd ^ mask) for v, dd in blocks]
+    return blocks
+
+
+def adam_core(master, first_moment, second_moment, clipped, step_rate, decay_rate):
+    first_new = BETA_ONE * first_moment + (1.0 - BETA_ONE) * clipped
+    second_new = BETA_TWO * second_moment + (1.0 - BETA_TWO) * clipped * clipped
+    first_hat = first_new / (1.0 - BETA_ONE**STEP_COUNT)
+    second_hat = second_new / (1.0 - BETA_TWO**STEP_COUNT)
+    renewed = master - step_rate * (
+        first_hat / (jnp.sqrt(second_hat) + ADAM_EPS) + decay_rate * master
+    )
+    return renewed, first_new, second_new
+
+
+def adam_blocks(master, moment, blocks, factor, step_rate, decay_rate):
+    rows, columns = master.shape
+    copies = lax.axis_size("dp")
+    here = lax.axis_index("dp")
+    width = columns // copies
+    if width % 128:
+        full = jnp.zeros(master.shape, jnp.float32)
+        for value, dd in blocks:
+            full = lax.dynamic_update_slice(
+                full, value.astype(jnp.float32), (0, (here ^ dd) * width)
+            )
+        return adam_update(master, moment, full, factor, step_rate, decay_rate)
+    tile = 32
+
+    def body(where, factor_ref, master_ref, moment_ref, *rest):
+        grads, (new_ref, state_ref) = rest[:-2], rest[-2:]
+        scale = factor_ref[0, 0]
+        for grad, (_, dd) in zip(grads, blocks):
+            at = pl.ds(pl.multiple_of((where[0] ^ dd) * width, 128), width)
+            renewed, first_new, second_new = adam_core(
+                master_ref[:, at],
+                moment_ref[0, :, at],
+                moment_ref[1, :, at],
+                grad[...].astype(jnp.float32) * scale,
+                step_rate,
+                decay_rate,
+            )
+            new_ref[:, at] = renewed
+            state_ref[0, :, at] = first_new
+            state_ref[1, :, at] = second_new
+
+    return pl.pallas_call(
+        body,
+        out_shape=[
+            jax.ShapeDtypeStruct(master.shape, jnp.float32),
+            jax.ShapeDtypeStruct(moment.shape, jnp.float32),
+        ],
+        grid_spec=pltpu.PrefetchScalarGridSpec(
+            num_scalar_prefetch=1,
+            grid=(rows // tile,),
+            in_specs=[
+                pl.BlockSpec(memory_space=pltpu.SMEM),
+                pl.BlockSpec((tile, columns), lambda i, where: (i, 0)),
+                pl.BlockSpec((2, tile, columns), lambda i, where: (0, i, 0)),
+            ]
+            + [pl.BlockSpec((tile, width), lambda i, where: (i, 0))] * len(blocks),
+            out_specs=[
+                pl.BlockSpec((tile, columns), lambda i, where: (i, 0)),
+                pl.BlockSpec((2, tile, columns), lambda i, where: (0, i, 0)),
+            ],
+        ),
+        compiler_params=pltpu.CompilerParams(vmem_limit_bytes=48 * 1024 * 1024),
+        cost_estimate=pl.CostEstimate(
+            flops=20 * rows * columns,
+            bytes_accessed=26 * rows * columns,
+            transcendentals=rows * columns,
+        ),
+    )(
+        here.reshape(1).astype(jnp.int32),
+        factor.reshape(1, 1),
+        master,
+        moment,
+        *[value for value, _ in blocks],
+    )
 
 
 def adam_update(master, moment, gradient, factor, step_rate, decay_rate):
@@ -107,14 +334,12 @@
     norm_moments,
     head_moments,
 ):
-    full_qkv, full_out, full_gate_up, full_down, full_norm, full_head = (
-        lax.all_gather(qkv_weight.astype(jnp.bfloat16), "group", axis=0, tiled=True),
-        lax.all_gather(out_weight.astype(jnp.bfloat16), "group", axis=0, tiled=True),
-        lax.all_gather(gate_up_weight.astype(jnp.bfloat16), "group", axis=0, tiled=True),
-        lax.all_gather(down_weight.astype(jnp.bfloat16), "group", axis=0, tiled=True),
-        lax.all_gather(norm_gains.astype(jnp.bfloat16), "group", axis=1, tiled=True),
-        lax.all_gather(head_gains.astype(jnp.bfloat16), "group", axis=1, tiled=True),
-    )
+    full_norm = lax.all_gather(norm_gains.astype(jnp.bfloat16), "group", axis=1, tiled=True)
+    full_head = lax.all_gather(head_gains.astype(jnp.bfloat16), "group", axis=1, tiled=True)
+    full_qkv = gather_rows(qkv_weight.astype(jnp.bfloat16))
+    full_out = gather_rows(out_weight.astype(jnp.bfloat16))
+    full_gate_up = gather_rows(gate_up_weight.astype(jnp.bfloat16))
+    full_down = gather_rows(down_weight.astype(jnp.bfloat16))
     token_rows = tokens.shape[0]
     seq_count = token_rows // SEQ_LEN
     groups = HQ // HK
@@ -179,17 +404,17 @@
     branch = jnp.dot(activated, full_down, preferred_element_type=jnp.float32)
     output = (residual + branch).astype(jnp.bfloat16)
     upstream = cotangent.astype(jnp.float32)
-    down_local = contract_rows(activated, cotangent)
+    down_own = reduce_grad(activated, cotangent)
     grad_act = contract_cols(cotangent, full_down)
     grad_gate = grad_act * upward * sigmoid_gate * (1.0 + gate_part * (1.0 - sigmoid_gate))
     grad_up = grad_act * gate_part * sigmoid_gate
     grad_gate_up = jnp.concatenate([grad_gate, grad_up], axis=-1).astype(jnp.bfloat16)
-    gate_up_local = contract_rows(hidden_two, grad_gate_up)
+    gate_up_own = reduce_grad(hidden_two, grad_gate_up)
     grad_hidden_two = contract_cols(grad_gate_up, full_gate_up)
     grad_gain_two = jnp.sum(grad_hidden_two * normed_two, axis=0)
     grad_residual = upstream + norm_back(grad_hidden_two, normed_two, root_two, gain_two)
     residual_low = grad_residual.astype(jnp.bfloat16)
-    out_local = contract_rows(mixed_low, residual_low)
+    out_own = reduce_grad(mixed_low, residual_low)
     grad_mixed = (
         contract_cols(residual_low, full_out)
         .astype(jnp.bfloat16)
@@ -232,100 +457,51 @@
         ],
         axis=-1,
     ).astype(jnp.bfloat16)
-    qkv_local = contract_rows(hidden_one, grad_projected)
+    qkv_own = reduce_grad(hidden_one, grad_projected)
     grad_hidden_one = contract_cols(grad_projected, full_qkv)
     grad_gain_one = jnp.sum(grad_hidden_one * normed_one, axis=0)
     grad_inputs = grad_residual + norm_back(grad_hidden_one, normed_one, root_one, gain_one)
     tokens_grad = grad_inputs.astype(jnp.bfloat16)
-    norm_local = jnp.stack([grad_gain_one, grad_gain_two])
-    head_local = jnp.stack([grad_gain_query, grad_gain_key])
-    owners = lax.axis_size("group")
-    copies = lax.axis_size("dp")
-    pieces = (
-        lax.psum_scatter(
-            joined_order(qkv_local, 0, owners, copies),
-            ("dp", "group"),
-            scatter_dimension=0,
-            tiled=True,
-        ),
-        lax.psum_scatter(
-            joined_order(out_local, 0, owners, copies),
-            ("dp", "group"),
-            scatter_dimension=0,
-            tiled=True,
-        ),
-        lax.psum_scatter(
-            joined_order(gate_up_local, 0, owners, copies),
-            ("dp", "group"),
-            scatter_dimension=0,
-            tiled=True,
-        ),
-        lax.psum_scatter(
-            joined_order(down_local, 0, owners, copies),
-            ("dp", "group"),
-            scatter_dimension=0,
-            tiled=True,
-        ),
-        lax.psum_scatter(
-            joined_order(norm_local, 1, owners, copies),
-            ("dp", "group"),
-            scatter_dimension=1,
-            tiled=True,
-        ),
-        lax.psum_scatter(
-            joined_order(head_local, 1, owners, copies),
-            ("dp", "group"),
-            scatter_dimension=1,
-            tiled=True,
-        ),
-    )
-    summed = (
-        lax.all_gather(pieces[0], "dp", axis=0, tiled=True),
-        lax.all_gather(pieces[1], "dp", axis=0, tiled=True),
-        lax.all_gather(pieces[2], "dp", axis=0, tiled=True),
-        lax.all_gather(pieces[3], "dp", axis=0, tiled=True),
-        lax.all_gather(pieces[4], "dp", axis=1, tiled=True),
-        lax.all_gather(pieces[5], "dp", axis=1, tiled=True),
-    )
-    squares = sum((jnp.sum(gradient * gradient) for gradient in summed))
-    grad_total = lax.psum(squares, "group")
+    small = jnp.concatenate(
+        [
+            jnp.stack([grad_gain_one, grad_gain_two]),
+            jnp.stack([grad_gain_query, grad_gain_key]),
+        ],
+        axis=1,
+    )
+    small = lax.psum(small, ("dp", "group"))
+    width = small.shape[1] - HD
+    norm_total = small[:, :width]
+    head_total = small[:, width:]
+    owned = (qkv_own, out_own, gate_up_own, down_own)
+    squares = lax.psum(sum(jnp.sum(v * v) for v in owned), ("dp", "group"))
+    squares = squares + jnp.sum(small * small)
     clip_limit = math.sqrt(PARAMS)
-    factor = clip_limit / jnp.maximum(jnp.sqrt(grad_total), clip_limit)
-    masters = (qkv_weight, out_weight, gate_up_weight, down_weight, norm_gains, head_gains)
-    moments = (qkv_moments, out_moments, gate_up_moments, down_moments, norm_moments, head_moments)
-    rates = (LEARN_RATE, LEARN_RATE, LEARN_RATE, LEARN_RATE, GAIN_RATE, GAIN_RATE)
-    decays = (WEIGHT_DECAY, WEIGHT_DECAY, WEIGHT_DECAY, WEIGHT_DECAY, 0.0, 0.0)
-    renewed_all = []
-    moments_all = []
-    for master, moment, gradient, step_rate, decay_rate in zip(
-        masters, moments, summed, rates, decays
-    ):
-        renewed, stacked = adam_update(master, moment, gradient, factor, step_rate, decay_rate)
-        renewed_all.append(renewed)
-        moments_all.append(stacked)
-    column_index = lax.axis_index("dp")
-    column_count = lax.axis_size("dp")
+    factor = clip_limit / jnp.maximum(jnp.sqrt(squares), clip_limit)
+    gathered = [gather_grad(v) for v in owned]
+    masters = (qkv_weight, out_weight, gate_up_weight, down_weight)
+    moments = (qkv_moments, out_moments, gate_up_moments, down_moments)
+    renewed = [
+        adam_blocks(master, moment, blocks, factor, LEARN_RATE, WEIGHT_DECAY)
+        for master, moment, blocks in zip(masters, moments, gathered)
+    ]
+    mine = lax.axis_index("group")
+    norm_grad = lax.dynamic_slice_in_dim(
+        norm_total, mine * norm_gains.shape[1], norm_gains.shape[1], 1
+    )
+    head_grad = lax.dynamic_slice_in_dim(
+        head_total, mine * head_gains.shape[1], head_gains.shape[1], 1
+    )
+    renewed.append(adam_update(norm_gains, norm_moments, norm_grad, factor, GAIN_RATE, 0.0))
+    renewed.append(adam_update(head_gains, head_moments, head_grad, factor, GAIN_RATE, 0.0))
     return (
         output,
         tokens_grad,
-        own_columns(summed[0], column_index, column_count),
-        own_columns(summed[1], column_index, column_count),
-        own_columns(summed[2], column_index, column_count),
-        own_columns(summed[3], column_index, column_count),
-        summed[4],
-        summed[5],
-        renewed_all[0],
-        renewed_all[1],
-        renewed_all[2],
-        renewed_all[3],
-        renewed_all[4],
-        renewed_all[5],
-        moments_all[0],
-        moments_all[1],
-        moments_all[2],
-        moments_all[3],
-        moments_all[4],
-        moments_all[5],
+        *owned,
+        norm_grad,
+        head_grad,
+        *[new for new, _ in renewed],
+        *[state for _, state in renewed],
     )
 
 

time: 1540 us -> 890 us (0.58)
  waiting for transfers between devices: 1010 us -> 255 us
  Pallas kernels: 0 us -> 126 us
  starting transfers between devices: 0.7 us -> 73.5 us
  matrix products: 162 us -> 107 us
  local copies, waits for them, and re-layouts: 91.4 us -> 123 us
  other arithmetic: 145 us -> 120 us
  blocking collectives: 94.4 us -> 71.2 us
    reduce_scatter x4 -> x0, waiting for transfers between devices: 566 us -> none  [the longest x1 251 us: on_device(): lax.psum_scatter(joined_order(gate_up_local, 0, owners, copies), ('dp', '...]
    all_gather x8 -> x0, waiting for transfers between devices: 378 us -> none  [the longest x1 93.9 us: on_device(): lax.all_gather(pieces[2], 'dp', axis=0, tiled=True)]
    ppermute x0 -> x68, waiting for transfers between devices: none -> 255 us  [swap(): return lax.ppermute(value, axis, [(i, i ^ mask) for i in range(count)])]
    pallas_call x0 -> x12, Pallas kernels: none -> 126 us  [the longest x8 66.9 us: grad_blocks(): pl.pallas_call(body, out_shape=[jax.ShapeDtypeStruct((len(row_set), row_b...]
    ppermute x0 -> x68, starting transfers between devices: none -> 73.5 us  [swap(): return lax.ppermute(value, axis, [(i, i ^ mask) for i in range(count)])]
    unnamed x14 -> x0, waiting for transfers between devices: 66.8 us -> none
    another operation x12 -> x6, other arithmetic: 57.1 us -> 2.45 us  [adam_update(): return (renewed, jnp.stack([first_moment, second]))]
    unnamed x1 -> x0, blocking collectives: 40.2 us -> none
  transfers between devices with their start and end apart: 13 -> 68, of which waited for: 11 -> 24; matrix products, arithmetic and copies ran while one was open for 18% -> 25% of each run, Pallas kernels for 0% -> 9%
where the time goes in v1:
time: 890 us; the launch traced here: 883 us
  waiting for transfers between devices  255 us (29%)
  Pallas kernels  126 us (14%)
  local copies, waits for them, and re-layouts  123 us (14%)
  other arithmetic  120 us (13%)
  matrix products  107 us (12%)
  starting transfers between devices  73.5 us (8%)
  blocking collectives  71.2 us (8%)
    ppermute x68, waiting for transfers between devices, swap(): return lax.ppermute(value, axis, [(i, i ^ mask) for i in range(count)])  255 us
    ppermute x68, starting transfers between devices, swap(): return lax.ppermute(value, axis, [(i, i ^ mask) for i in range(count)])  73.5 us
    pallas_call x8, Pallas kernels, grad_blocks(): pl.pallas_call(body, out_shape=[jax.ShapeDtypeStruct((len(row_set), row_b...  66.9 us
    pallas_call x4, Pallas kernels, adam_blocks(): pl.pallas_call(body, out_shape=[jax.ShapeDtypeStruct(master.shape, jnp.fl...  59.6 us
    unnamed x240, local copies, waits for them, and re-layouts  49.7 us
    psum x1, blocking collectives, on_device(): small = lax.psum(small, ('dp', 'group'))  42.4 us
    dot_general x4, matrix products, contract_cols(): lax.dot_general(left_side, right_side, (((1,), (1,)), ((), ())), preferre...  34.1 us
    dynamic_update_slice x20, local copies, waits for them, and re-layouts, gather_rows(): full = lax.dynamic_update_slice(full, value, (start, 0))  31.1 us
  transfers between devices with their start and end apart: 68, of which 24 were waited for; matrix products, arithmetic and copies ran while one was open for 25% of the time, Pallas kernels for 9%

profile of v1, /device:TPU:0, one launch (start us, length us, event | category | flops | bytes accessed | tf_op | source)
XLA Modules:
  0.0 882.9 jit_solution(8201705037355217467)
XLA Ops:
  41.1 23.4 %all_gather.6 = bf16[2,1024]{1,0:T(2,128)(2,1)S(1)} all-gather(bf16[2,256]{1,0:T(2,128)(2,1)S(1)} %convert_element_type.406), channel_id=1, replica_groups=mesh['dp'=8,'group'=4] {'group'}, dimensions={1}, use_global_device_ids=true | all-gather | bytes 5120 | tf_op jit(solution)/shard_map/all_gather | solution.py:337
  78.4 9.9 %collective-permute-done.6 = bf16[256,1024]{1,0:T(8,128)(2,1)S(1)} collective-permute-done((bf16[256,1024]{1,0:T(8,128)(2,1)}, bf16[256,1024]{1,0:T(8,128)(2,1)S(1)}, u32[]{:S(2)}, u32[]{:S(2)}) %collective-permute-start.6) | collective-permute-done | bytes 524320 | tf_op jit(solution)/shard_map/ppermute | solution.py:71
  101.9 11.5 %collective-permute-done.16 = bf16[384,1024]{1,0:T(8,128)(2,1)S(1)} collective-permute-done((bf16[384,1024]{1,0:T(8,128)(2,1)}, bf16[384,1024]{1,0:T(8,128)(2,1)S(1)}, u32[]{:S(2)}, u32[]{:S(2)}) %collective-permute-start.16) | collective-permute-done | bytes 786464 | tf_op jit(solution)/shard_map/ppermute | solution.py:71
  123.9 15.8 %collective-permute-done.1 = bf16[128,4096]{1,0:T(8,128)(2,1)S(1)} collective-permute-done((bf16[128,4096]{1,0:T(8,128)(2,1)}, bf16[128,4096]{1,0:T(8,128)(2,1)S(1)}, u32[]{:S(2)}, u32[]{:S(2)}) %collective-permute-start.1) | collective-permute-done | bytes 1048608 | tf_op jit(solution)/shard_map/ppermute | solution.py:71
  167.0 8.7 fusion.66
  175.8 8.3 exponential_reduce_fusion
  186.2 8.9 %fusion.36 = bf16[8,128,2,512]{3,1,2,0:T(8,128)(2,1)S(1)} fusion(f32[1,8,2,512,512]{3,4,2,1,0:T(8,128)} %get-tuple-element.113, f32[8,2,512]{2,1,0:T(2,128)S(1)} %bitcast.307, bf16[512,8,128,1]{2,1,0,3:T(8,128)(2,1)S(1)} %bitcast.275), kind=kOutput, calls=%fused_computation.93 | convolution fusion | flops 1083179008 | bytes 19955712 | tf_op jit(solution)/shard_map/skgqp,spkd->sqkgd/dot_general | solution.py:390
  214.7 9.9 %fusion.68 = f32[512,6144]{1,0:T(8,128)S(1)} fusion(bf16[512,1024]{1,0:T(8,128)(2,1)S(1)} %copy-done.10, bf16[1024,6144]{1,0:T(8,128)(2,1)} %constant_dynamic-update-slice_fusion.6), kind=kOutput, calls=%fused_computation.207 | convolution fusion | flops 6442450944 | bytes 26214400 | tf_op jit(solution)/shard_map/dot_general | solution.py:399
  224.6 8.4 fusion.8
  233.1 14.0 %multiply_reduce_fusion.2 = (f32[1024]{0:T(1024)S(1)}, f32[512]{0:T(512)S(1)}, f32[512,1024]{1,0:T(8,128)}) fusion(f32[512,1024]{1,0:T(8,128)} %copy-done.41, f32[512]{0:T(512)S(1)} %add_rsqrt_fusion.2, f32[1024]{0:T(1024)S(1)} %bitcast.318, bf16[1024,6144]{1,0:T(8,128)(2,1)} %constant_dynamic-update-slice_fusion.6, ...), kind=kOutput, calls=%fused_computation.79 | convolution fusion | flops 6458178048 | bytes 23080960 | tf_op jit(solution)/shard_map/dot_general | solution.py:59
  259.3 15.7 %fusion = (f32[8,2,512]{2,1,0:T(2,128)S(1)}, f32[8,512,512,2]{2,1,3,0:T(8,128)}) fusion(f32[1,8,2,512,512]{3,4,2,1,0:T(8,128)} %get-tuple-element.113, f32[8,2,512]{2,1,0:T(2,128)S(1)} %bitcast.308, bf16[512,8,2,128]{0,3,2,1:T(8,128)(2,1)} %bitcast.267, bf16[512,8,128,1]{2,1,0,3:T(8,128)(2,1)} %bitcast.276), kind=kOutput, calls=%fused_computation.3 | convolution fusion | flops 1086316544 | bytes 36765696 | tf_op jit(solution)/shard_map/sqkgd,spkd->skgqp/dot_general | solution.py:424
  275.0 12.6 %fusion.5 = bf16[8,2,512,512]{2,3,1,0:T(8,128)(2,1)S(1)} fusion(f32[8,512,512,2]{2,1,3,0:T(8,128)} %get-tuple-element.118, f32[1,8,2,512,512]{3,4,2,1,0:T(8,128)} %get-tuple-element.113, f32[8,2,512]{2,1,0:T(2,128)S(1)} %get-tuple-element.117, f32[8,2,512]{2,1,0:T(2,128)S(1)} %bitcast.309), kind=kLoop, calls=%fused_computation.10 | loop fusion | flops 16777216 | bytes 42008576 | tf_op jit(solution)/shard_map/reshape.16
  293.8 9.8 %bitcast_convert_fusion = bf16[8,128,512]{2,1,0:T(8,128)(2,1)} fusion(bf16[512,8,2,128]{0,3,2,1:T(8,128)(2,1)S(1)} %bitcast.268, f32[1,8,2,512,512]{3,4,2,1,0:T(8,128)} %get-tuple-element.113, f32[8,2,512]{2,1,0:T(2,128)S(1)} %bitcast.310), kind=kOutput, calls=%fused_computation.76 | convolution fusion | flops 1082654720 | bytes 19955712 | tf_op jit(solution)/shard_map/skgqp,sqkgd->spkd/dot_general | solution.py:427
  308.9 10.1 %shard_map.318 = bf16[2,768,1024]{2,1,0:T(8,128)(2,1)} custom-call(s32[2]{0:T(128)S(1)} %pad_add_fusion.where, bf16[512,3072]{1,0:T(8,128)(2,1)} %get-tuple-element.86.left_ref, bf16[512,1024]{1,0:T(8,128)(2,1)S(1)} %copy-done.2), custom_call_target="tpu_custom_call" | custom-call | flops 1610612736 | bytes 7340032 | tf_op jit(solution)/shard_map/pallas_call | solution.py:160
  319.0 9.0 %shard_map.317 = (bf16[1,768,1024]{2,1,0:T(8,128)(2,1)S(1)}, bf16[1,768,1024]{2,1,0:T(8,128)(2,1)S(1)}) custom-call(s32[2]{0:T(128)S(1)} %pad_add_fusion.where, bf16[512,3072]{1,0:T(8,128)(2,1)} %get-tuple-element.86.left_ref, bf16[512,1024]{1,0:T(8,128)(2,1)S(1)} %copy-done.2), custom_call_target="tpu_custom_call" | custom-call | flops 1610612736 | bytes 7340032 | tf_op jit(solution)/shard_map/pallas_call | solution.py:160
  354.4 16.6 %multiply_reduce_fusion = (f32[512,16]{1,0:T(8,128)S(1)}, f32[512,16,128]{2,1,0:T(8,128)}) fusion(f32[512,16,128]{2,1,0:T(8,128)S(1)} %bitcast.266, f32[128]{0:T(128)S(1)} %copy-done.97, f32[512,16]{1,0:T(8,128)S(1)} %copy-done.60, f32[512,16,64]{2,1,0:T(8,128)S(1)} %get-tuple-element.88, f32[512,16,64]{2,1,0:T(8,128)S(1)} %get-tuple-element.87), kind=kLoop, calls=%fused_computation.33 | loop fusion | flops 5234688 | bytes 12648960 | tf_op jit(solution)/shard_map/reduce_sum | solution.py:66
  379.8 10.7 %shard_map.316 = bf16[2,256,6144]{2,1,0:T(8,128)(2,1)} custom-call(s32[2]{0:T(128)S(1)} %pad_add_fusion.where, bf16[512,1024]{1,0:T(8,128)(2,1)S(1)} %copy-done.11, bf16[512,6144]{1,0:T(8,128)(2,1)} %pad_maximum_fusion.right_ref), custom_call_target="tpu_custom_call" | custom-call | flops 3221225472 | bytes 13631488 | tf_op jit(solution)/shard_map/pallas_call | solution.py:160
  394.4 10.0 %fusion.14 = (f32[2048]{0:T(1024)S(1)}, bf16[512,2048]{1,0:T(8,128)(2,1)}) fusion(f32[64,8,16,128]{3,2,1,0:T(8,128)S(1)} %bitcast.272, f32[64,8,16,128]{3,2,1,0:T(8,128)S(1)} %bitcast.274, f32[512,4096]{1,0:T(8,128)} %copy-done.38, f32[64,8,16,128]{3,2,1,0:T(8,128)S(1)} %bitcast.273, f32[2048]{0:T(1024)S(1)} %copy-done.91), kind=kLoop, calls=%fused_computation.28 | loop fusion | flops 8386560 | bytes 18890752 | tf_op jit(solution)/shard_map/reduce_sum | solution.py:448
  410.2 8.0 fusion.29
  443.7 10.0 %shard_map.315 = (bf16[1,256,6144]{2,1,0:T(8,128)(2,1)S(1)}, bf16[1,256,6144]{2,1,0:T(8,128)(2,1)}) custom-call(s32[2]{0:T(128)S(1)} %pad_add_fusion.where, bf16[512,1024]{1,0:T(8,128)(2,1)S(1)} %copy-done.12, bf16[512,6144]{1,0:T(8,128)(2,1)} %pad_maximum_fusion.right_ref), custom_call_target="tpu_custom_call" | custom-call | flops 3221225472 | bytes 13631488 | tf_op jit(solution)/shard_map/pallas_call | solution.py:160
  470.8 15.1 %collective-permute-done.26 = bf16[1,512,1024]{2,1,0:T(8,128)(2,1)S(1)} collective-permute-done((bf16[1,512,1024]{2,1,0:T(8,128)(2,1)S(1)}, bf16[1,512,1024]{2,1,0:T(8,128)(2,1)S(1)}, u32[]{:S(2)}, u32[]{:S(2)}) %collective-permute-start.26) | collective-permute-done | bytes 1048608 | tf_op jit(solution)/shard_map/ppermute | solution.py:71
  511.1 16.3 %collective-permute-done.36 = bf16[1,768,1024]{2,1,0:T(8,128)(2,1)S(1)} collective-permute-done((bf16[1,768,1024]{2,1,0:T(8,128)(2,1)S(1)}, bf16[1,768,1024]{2,1,0:T(8,128)(2,1)S(1)}, u32[]{:S(2)}, u32[]{:S(2)}) %collective-permute-start.36) | collective-permute-done | bytes 1572896 | tf_op jit(solution)/shard_map/ppermute | solution.py:71
  530.8 64.1 %collective-permute-done.31 = bf16[1,256,6144]{2,1,0:T(8,128)(2,1)S(1)} collective-permute-done((bf16[1,256,6144]{2,1,0:T(8,128)(2,1)S(1)}, bf16[1,256,6144]{2,1,0:T(8,128)(2,1)S(1)}, u32[]{:S(2)}, u32[]{:S(2)}) %collective-permute-start.31) | collective-permute-done | bytes 3145760 | tf_op jit(solution)/shard_map/ppermute | solution.py:71
  596.0 42.0 %collective-permute-done.21 = bf16[1,256,4096]{2,1,0:T(8,128)(2,1)S(1)} collective-permute-done((bf16[1,256,4096]{2,1,0:T(8,128)(2,1)S(1)}, bf16[1,256,4096]{2,1,0:T(8,128)(2,1)S(1)}, u32[]{:S(2)}, u32[]{:S(2)}) %collective-permute-start.21) | collective-permute-done | bytes 2097184 | tf_op jit(solution)/shard_map/ppermute | solution.py:71
  669.4 8.1 collective-permute-done.23
  681.6 17.0 %collective-permute-done.33 = bf16[256,1536]{1,0:T(8,128)(2,1)S(1)} collective-permute-done((bf16[256,1536]{1,0:T(8,128)(2,1)S(1)}, bf16[256,1536]{1,0:T(8,128)(2,1)S(1)}, u32[]{:S(2)}, u32[]{:S(2)}) %collective-permute-start.33) | collective-permute-done | bytes 786464 | tf_op jit(solution)/shard_map/ppermute | solution.py:71
  702.9 10.2 %collective-permute-done.24 = bf16[256,512]{1,0:T(8,128)(2,1)S(1)} collective-permute-done((bf16[256,512]{1,0:T(8,128)(2,1)S(1)}, bf16[256,512]{1,0:T(8,128)(2,1)S(1)}, u32[]{:S(2)}, u32[]{:S(2)}) %collective-permute-start.24) | collective-permute-done | bytes 262176 | tf_op jit(solution)/shard_map/ppermute | solution.py:71
  741.7 42.4 %all-reduce = (f32[2,1152]{1,0:T(2,128)S(1)}, f32[]{:T(128)}) all-reduce(f32[2,1152]{1,0:T(2,128)S(1)} %maximum_maximum_fusion, f32[]{:T(128)S(6)} %add.529), channel_id=1, replica_groups=mesh['dp'=8,'group'=4] {'dp','group'}, use_global_device_ids=true, to_apply=%region_17.18 | all-reduce | flops 2305 | bytes 18440 | tf_op jit(solution)/shard_map/psum | solution.py:472
  821.6 11.5 %shard_map.320 = (f32[512,1024]{1,0:T(8,128)}, f32[2,512,1024]{2,1,0:T(8,128)}) custom-call(s32[1]{0:T(128)} %bitcast.46.where, f32[1,1]{1,0:T(1,128)} %bitcast.67.factor_ref, f32[512,1024]{1,0:T(8,128)S(1)} %copy-done.4, f32[2,512,1024]{2,1,0:T(8,128)} %moment_ref.5, bf16[512,128]{1,0:T(8,128)(2,1)S(1)} %get-tuple-element.66.rest_0_, ...), custom_call_target="tpu_custom_call" | custom-call | flops 10485760 | bytes 13631488 | tf_op jit(solution)/shard_map/pallas_call | solution.py:272
  833.2 16.5 %shard_map.322 = (f32[768,1024]{1,0:T(8,128)}, f32[2,768,1024]{2,1,0:T(8,128)}) custom-call(s32[1]{0:T(128)} %bitcast.46.where, f32[1,1]{1,0:T(1,128)} %bitcast.67.factor_ref, f32[768,1024]{1,0:T(8,128)S(1)} %copy-done.1, f32[2,768,1024]{2,1,0:T(8,128)} %moment_ref.7, bf16[768,128]{1,0:T(8,128)(2,1)S(1)} %get-tuple-element.62.rest_0_, ...), custom_call_target="tpu_custom_call" | custom-call | flops 15728640 | bytes 20447232 | tf_op jit(solution)/shard_map/pallas_call | solution.py:272
  849.8 13.2 %shard_map.319 = (f32[256,4096]{1,0:T(8,128)}, f32[2,256,4096]{2,1,0:T(8,128)}) custom-call(s32[1]{0:T(128)} %bitcast.46.where, f32[1,1]{1,0:T(1,128)} %bitcast.67.factor_ref, f32[256,4096]{1,0:T(8,128)} %master_ref.4, f32[2,256,4096]{2,1,0:T(8,128)} %moment_ref.4, bf16[256,512]{1,0:T(8,128)(2,1)S(1)} %get-tuple-element.68.rest_0_, ...), custom_call_target="tpu_custom_call" | custom-call | flops 20971520 | bytes 27262976 | tf_op jit(solution)/shard_map/pallas_call | solution.py:272
  864.2 18.3 %shard_map.321 = (f32[256,6144]{1,0:T(8,128)}, f32[2,256,6144]{2,1,0:T(8,128)}) custom-call(s32[1]{0:T(128)} %bitcast.46.where, f32[1,1]{1,0:T(1,128)} %bitcast.67.factor_ref, f32[256,6144]{1,0:T(8,128)} %master_ref.6, f32[2,256,6144]{2,1,0:T(8,128)} %moment_ref.6, bf16[256,768]{1,0:T(8,128)(2,1)S(1)} %get-tuple-element.64.rest_0_, ...), custom_call_target="tpu_custom_call" | custom-call | flops 31457280 | bytes 40894464 | tf_op jit(solution)/shard_map/pallas_call | solution.py:272
  (502 shorter events, 370.2 us)
Async XLA Ops:
  9.1 89.2 %collective-permute-start = (bf16[128,4096]{1,0:T(8,128)(2,1)}, bf16[128,4096]{1,0:T(8,128)(2,1)}, u32[]{:S(2)}, u32[]{:S(2)}) collective-permute-start(bf16[128,4096]{1,0:T(8,128)(2,1)} %constant_dynamic-slice_fusion.5), channel_id=1, source_target_pairs={{0,2},{1,3},{2,0},{3,1},{4,6},{5,7},{6,4},{7,5},{8,10},{9,11},{10,... | collective-permute-start | bytes 3145736 | tf_op jit(solution)/shard_map/ppermute | solution.py:71
  15.9 77.3 %collective-permute-start.7 = (bf16[512,1024]{1,0:T(8,128)(2,1)}, bf16[512,1024]{1,0:T(8,128)(2,1)}, u32[]{:S(2)}, u32[]{:S(2)}) collective-permute-start(bf16[512,1024]{1,0:T(8,128)(2,1)} %get-tuple-element.77), channel_id=1, source_target_pairs={{0,1},{1,0},{2,3},{3,2},{4,5},{5,4},{6,7},{7,6},{8,9},{9,8},{10,11... | collective-permute-start | bytes 3145736 | tf_op jit(solution)/shard_map/ppermute | solution.py:71
  17.8 56.1 %collective-permute-start.5 = (bf16[256,1024]{1,0:T(8,128)(2,1)}, bf16[256,1024]{1,0:T(8,128)(2,1)}, u32[]{:S(2)}, u32[]{:S(2)}) collective-permute-start(bf16[256,1024]{1,0:T(8,128)(2,1)} %constant_dynamic-slice_fusion.4), channel_id=1, source_target_pairs={{0,2},{1,3},{2,0},{3,1},{4,6},{5,7},{6,4},{7,5},{8,10},{9,11},{10,... | collective-permute-start | bytes 1572872 | tf_op jit(solution)/shard_map/ppermute | solution.py:71
  24.2 91.8 %collective-permute-start.17 = (bf16[768,1024]{1,0:T(8,128)(2,1)}, bf16[768,1024]{1,0:T(8,128)(2,1)}, u32[]{:S(2)}, u32[]{:S(2)}) collective-permute-start(bf16[768,1024]{1,0:T(8,128)(2,1)} %get-tuple-element.73), channel_id=1, source_target_pairs={{0,1},{1,0},{2,3},{3,2},{4,5},{5,4},{6,7},{7,6},{8,9},{9,8},{10,11... | collective-permute-start | bytes 4718600 | tf_op jit(solution)/shard_map/ppermute | solution.py:71
  26.7 50.2 %collective-permute-start.15 = (bf16[384,1024]{1,0:T(8,128)(2,1)}, bf16[384,1024]{1,0:T(8,128)(2,1)}, u32[]{:S(2)}, u32[]{:S(2)}) collective-permute-start(bf16[384,1024]{1,0:T(8,128)(2,1)} %constant_dynamic-slice_fusion.2), channel_id=1, source_target_pairs={{0,2},{1,3},{2,0},{3,1},{4,6},{5,7},{6,4},{7,5},{8,10},{9,11},{10,... | collective-permute-start | bytes 2359304 | tf_op jit(solution)/shard_map/ppermute | solution.py:71
  76.9 42.6 %collective-permute-start.10 = (bf16[128,6144]{1,0:T(8,128)(2,1)}, bf16[128,6144]{1,0:T(8,128)(2,1)}, u32[]{:S(2)}, u32[]{:S(2)}) collective-permute-start(bf16[128,6144]{1,0:T(8,128)(2,1)} %constant_dynamic-slice_fusion.3), channel_id=1, source_target_pairs={{0,2},{1,3},{2,0},{3,1},{4,6},{5,7},{6,4},{7,5},{8,10},{9,11},{10,... | collective-permute-start | bytes 4718600 | tf_op jit(solution)/shard_map/ppermute | solution.py:71
  100.9 105.9 %collective-permute-start.12 = (bf16[256,6144]{1,0:T(8,128)(2,1)}, bf16[256,6144]{1,0:T(8,128)(2,1)}, u32[]{:S(2)}, u32[]{:S(2)}) collective-permute-start(bf16[256,6144]{1,0:T(8,128)(2,1)} %get-tuple-element.75), channel_id=1, source_target_pairs={{0,1},{1,0},{2,3},{3,2},{4,5},{5,4},{6,7},{7,6},{8,9},{9,8},{10,11... | collective-permute-start | bytes 9437192 | tf_op jit(solution)/shard_map/ppermute | solution.py:71
  122.5 81.4 %collective-permute-start.11 = (bf16[128,6144]{1,0:T(8,128)(2,1)}, bf16[128,6144]{1,0:T(8,128)(2,1)}, u32[]{:S(2)}, u32[]{:S(2)}) collective-permute-start(bf16[128,6144]{1,0:T(8,128)(2,1)} %collective-permute-done.10), channel_id=1, source_target_pairs={{0,4},{4,0},{8,12},{12,8},{16,20},{20,16},{24,28},{28,24},{1,5},{5... | collective-permute-start | bytes 4718600 | tf_op jit(solution)/shard_map/ppermute | solution.py:71
  140.6 70.0 %collective-permute-start.13 = (bf16[128,6144]{1,0:T(8,128)(2,1)}, bf16[128,6144]{1,0:T(8,128)(2,1)}, u32[]{:S(2)}, u32[]{:S(2)}) collective-permute-start(bf16[128,6144]{1,0:T(8,128)(2,1)} %collective-permute-done.10), channel_id=1, source_target_pairs={{0,1},{1,0},{2,3},{3,2},{4,5},{5,4},{6,7},{7,6},{8,9},{9,8},{10,11... | collective-permute-start | bytes 4718600 | tf_op jit(solution)/shard_map/ppermute | solution.py:71
  336.9 121.7 %collective-permute-start.25 = (bf16[2,512,1024]{2,1,0:T(8,128)(2,1)}, bf16[2,512,1024]{2,1,0:T(8,128)(2,1)}, u32[]{:S(2)}, u32[]{:S(2)}) collective-permute-start(bf16[2,512,1024]{2,1,0:T(8,128)(2,1)} %shard_map.314), channel_id=1, source_target_pairs={{0,1},{1,0},{2,3},{3,2},{4,5},{5,4},{6,7},{7,6},{8,9},{9,8},{10,11... | collective-permute-start | bytes 6291464 | tf_op jit(solution)/shard_map/ppermute | solution.py:71
  390.5 111.2 %collective-permute-start.30 = (bf16[2,256,6144]{2,1,0:T(8,128)(2,1)}, bf16[2,256,6144]{2,1,0:T(8,128)(2,1)}, u32[]{:S(2)}, u32[]{:S(2)}) collective-permute-start(bf16[2,256,6144]{2,1,0:T(8,128)(2,1)} %shard_map.316), channel_id=1, source_target_pairs={{0,1},{1,0},{2,3},{3,2},{4,5},{5,4},{6,7},{7,6},{8,9},{9,8},{10,11... | collective-permute-start | bytes 18874376 | tf_op jit(solution)/shard_map/ppermute | solution.py:71
  390.7 97.3 %collective-permute-start.35 = (bf16[2,768,1024]{2,1,0:T(8,128)(2,1)}, bf16[2,768,1024]{2,1,0:T(8,128)(2,1)}, u32[]{:S(2)}, u32[]{:S(2)}) collective-permute-start(bf16[2,768,1024]{2,1,0:T(8,128)(2,1)} %shard_map.318), channel_id=1, source_target_pairs={{0,1},{1,0},{2,3},{3,2},{4,5},{5,4},{6,7},{7,6},{8,9},{9,8},{10,11... | collective-permute-start | bytes 9437192 | tf_op jit(solution)/shard_map/ppermute | solution.py:71
  436.0 70.3 %collective-permute-start.20 = (bf16[2,256,4096]{2,1,0:T(8,128)(2,1)S(1)}, bf16[2,256,4096]{2,1,0:T(8,128)(2,1)}, u32[]{:S(2)}, u32[]{:S(2)}) collective-permute-start(bf16[2,256,4096]{2,1,0:T(8,128)(2,1)S(1)} %shard_map.312), channel_id=1, source_target_pairs={{0,1},{1,0},{2,3},{3,2},{4,5},{5,4},{6,7},{7,6},{8,9},{9,8},{10,11... | collective-permute-start | bytes 12582920 | tf_op jit(solution)/shard_map/ppermute | solution.py:71
  499.8 139.1 %collective-permute-start.28 = (bf16[512,256]{1,0:T(8,128)(2,1)S(1)}, bf16[512,256]{1,0:T(8,128)(2,1)S(1)}, u32[]{:S(2)}, u32[]{:S(2)}) collective-permute-start(bf16[512,256]{1,0:T(8,128)(2,1)S(1)} %add_convert_fusion.15), channel_id=1, source_target_pairs={{0,8},{4,12},{8,0},{12,4},{16,24},{20,28},{24,16},{28,20},{1,9},{5... | collective-permute-start | bytes 786440 | tf_op jit(solution)/shard_map/ppermute | solution.py:71
  504.7 90.1 %collective-permute-start.31 = (bf16[1,256,6144]{2,1,0:T(8,128)(2,1)S(1)}, bf16[1,256,6144]{2,1,0:T(8,128)(2,1)S(1)}, u32[]{:S(2)}, u32[]{:S(2)}) collective-permute-start(bf16[1,256,6144]{2,1,0:T(8,128)(2,1)S(1)} %add_convert_fusion), channel_id=1, source_target_pairs={{0,2},{1,3},{2,0},{3,1},{4,6},{5,7},{6,4},{7,5},{8,10},{9,11},{10,... | collective-permute-start | bytes 9437192 | tf_op jit(solution)/shard_map/ppermute | solution.py:71
  508.6 129.4 %collective-permute-start.21 = (bf16[1,256,4096]{2,1,0:T(8,128)(2,1)S(1)}, bf16[1,256,4096]{2,1,0:T(8,128)(2,1)S(1)}, u32[]{:S(2)}, u32[]{:S(2)}) collective-permute-start(bf16[1,256,4096]{2,1,0:T(8,128)(2,1)S(1)} %add_convert_fusion.1), channel_id=1, source_target_pairs={{0,2},{1,3},{2,0},{3,1},{4,6},{5,7},{6,4},{7,5},{8,10},{9,11},{10,... | collective-permute-start | bytes 6291464 | tf_op jit(solution)/shard_map/ppermute | solution.py:71
  528.0 113.9 %collective-permute-start.37 = (bf16[768,512]{1,0:T(8,128)(2,1)S(1)}, bf16[768,512]{1,0:T(8,128)(2,1)S(1)}, u32[]{:S(2)}, u32[]{:S(2)}) collective-permute-start(bf16[768,512]{1,0:T(8,128)(2,1)S(1)} %add_convert_fusion.9), channel_id=1, source_target_pairs={{0,4},{4,0},{8,12},{12,8},{16,20},{20,16},{24,28},{28,24},{1,5},{5... | collective-permute-start | bytes 2359304 | tf_op jit(solution)/shard_map/ppermute | solution.py:71
  595.6 68.7 %collective-permute-start.32 = (bf16[256,3072]{1,0:T(8,128)(2,1)S(1)}, bf16[256,3072]{1,0:T(8,128)(2,1)S(1)}, u32[]{:S(2)}, u32[]{:S(2)}) collective-permute-start(bf16[256,3072]{1,0:T(8,128)(2,1)S(1)} %add_convert_fusion.4), channel_id=1, source_target_pairs={{0,4},{4,0},{8,12},{12,8},{16,20},{20,16},{24,28},{28,24},{1,5},{5... | collective-permute-start | bytes 4718600 | tf_op jit(solution)/shard_map/ppermute | solution.py:71
  665.4 48.1 %collective-permute-start.48 = (bf16[512,128]{1,0:T(8,128)(2,1)S(1)}, bf16[512,128]{1,0:T(8,128)(2,1)S(1)}, u32[]{:S(2)}, u32[]{:S(2)}) collective-permute-start(bf16[512,128]{1,0:T(8,128)(2,1)S(1)} %get-tuple-element.66.rest_0_), channel_id=1, source_target_pairs={{0,8},{4,12},{8,0},{12,4},{16,24},{20,28},{24,16},{28,20},{1,9},{5... | collective-permute-start | bytes 393224 | tf_op jit(solution)/shard_map/ppermute | solution.py:71
  667.7 47.3 %collective-permute-start.50 = (bf16[512,128]{1,0:T(8,128)(2,1)S(1)}, bf16[512,128]{1,0:T(8,128)(2,1)S(1)}, u32[]{:S(2)}, u32[]{:S(2)}) collective-permute-start(bf16[512,128]{1,0:T(8,128)(2,1)S(1)} %get-tuple-element.66.rest_0_), channel_id=1, source_target_pairs={{0,4},{4,0},{8,12},{12,8},{16,20},{20,16},{24,28},{28,24},{1,5},{5... | collective-permute-start | bytes 393224 | tf_op jit(solution)/shard_map/ppermute | solution.py:71
  668.2 47.4 %collective-permute-start.49 = (bf16[512,128]{1,0:T(8,128)(2,1)S(1)}, bf16[512,128]{1,0:T(8,128)(2,1)S(1)}, u32[]{:S(2)}, u32[]{:S(2)}) collective-permute-start(bf16[512,128]{1,0:T(8,128)(2,1)S(1)} %collective-permute-done.47.rest_1_), channel_id=1, source_target_pairs={{0,8},{4,12},{8,0},{12,4},{16,24},{20,28},{24,16},{28,20},{1,9},{5... | collective-permute-start | bytes 393224 | tf_op jit(solution)/shard_map/ppermute | solution.py:71
  677.5 46.6 %collective-permute-start.61 = (bf16[768,128]{1,0:T(8,128)(2,1)S(1)}, bf16[768,128]{1,0:T(8,128)(2,1)}, u32[]{:S(2)}, u32[]{:S(2)}) collective-permute-start(bf16[768,128]{1,0:T(8,128)(2,1)S(1)} %get-tuple-element.62.rest_0_), channel_id=1, source_target_pairs={{0,16},{4,20},{8,24},{12,28},{16,0},{20,4},{24,8},{28,12},{1,17},{... | collective-permute-start | bytes 589832 | tf_op jit(solution)/shard_map/ppermute | solution.py:71
  724.1 60.0 %collective-permute-start.63 = (bf16[768,128]{1,0:T(8,128)(2,1)}, bf16[768,128]{1,0:T(8,128)(2,1)}, u32[]{:S(2)}, u32[]{:S(2)}) collective-permute-start(bf16[768,128]{1,0:T(8,128)(2,1)} %collective-permute-done.61.rest_1_), channel_id=1, source_target_pairs={{0,8},{4,12},{8,0},{12,4},{16,24},{20,28},{24,16},{28,20},{1,9},{5... | collective-permute-start | bytes 589832 | tf_op jit(solution)/shard_map/ppermute | solution.py:71
  726.0 58.1 %collective-permute-start.65 = (bf16[768,128]{1,0:T(8,128)(2,1)}, bf16[768,128]{1,0:T(8,128)(2,1)}, u32[]{:S(2)}, u32[]{:S(2)}) collective-permute-start(bf16[768,128]{1,0:T(8,128)(2,1)} %collective-permute-done.61.rest_1_), channel_id=1, source_target_pairs={{0,4},{4,0},{8,12},{12,8},{16,20},{20,16},{24,28},{28,24},{1,5},{5... | collective-permute-start | bytes 589832 | tf_op jit(solution)/shard_map/ppermute | solution.py:71
  730.5 58.4 %collective-permute-start.40 = (bf16[256,512]{1,0:T(8,128)(2,1)S(1)}, bf16[256,512]{1,0:T(8,128)(2,1)}, u32[]{:S(2)}, u32[]{:S(2)}) collective-permute-start(bf16[256,512]{1,0:T(8,128)(2,1)S(1)} %get-tuple-element.68.rest_0_), channel_id=1, source_target_pairs={{0,16},{4,20},{8,24},{12,28},{16,0},{20,4},{24,8},{28,12},{1,17},{... | collective-permute-start | bytes 786440 | tf_op jit(solution)/shard_map/ppermute | solution.py:71
  734.8 54.1 %collective-permute-start.66 = (bf16[768,128]{1,0:T(8,128)(2,1)}, bf16[768,128]{1,0:T(8,128)(2,1)}, u32[]{:S(2)}, u32[]{:S(2)}) collective-permute-start(bf16[768,128]{1,0:T(8,128)(2,1)} %collective-permute-done.62.rest_2_), channel_id=1, source_target_pairs={{0,4},{4,0},{8,12},{12,8},{16,20},{20,16},{24,28},{28,24},{1,5},{5... | collective-permute-start | bytes 589832 | tf_op jit(solution)/shard_map/ppermute | solution.py:71
  738.0 61.7 %collective-permute-start.54 = (bf16[256,768]{1,0:T(8,128)(2,1)S(1)}, bf16[256,768]{1,0:T(8,128)(2,1)S(1)}, u32[]{:S(2)}, u32[]{:S(2)}) collective-permute-start(bf16[256,768]{1,0:T(8,128)(2,1)S(1)} %get-tuple-element.64.rest_0_), channel_id=1, source_target_pairs={{0,16},{4,20},{8,24},{12,28},{16,0},{20,4},{24,8},{28,12},{1,17},{... | collective-permute-start | bytes 1179656 | tf_op jit(solution)/shard_map/ppermute | solution.py:71
  800.7 49.1 %collective-permute-start.46 = (bf16[256,512]{1,0:T(8,128)(2,1)S(1)}, bf16[256,512]{1,0:T(8,128)(2,1)S(1)}, u32[]{:S(2)}, u32[]{:S(2)}) collective-permute-start(bf16[256,512]{1,0:T(8,128)(2,1)S(1)} %collective-permute-done.42.rest_3_), channel_id=1, source_target_pairs={{0,4},{4,0},{8,12},{12,8},{16,20},{20,16},{24,28},{28,24},{1,5},{5... | collective-permute-start | bytes 786440 | tf_op jit(solution)/shard_map/ppermute | solution.py:71
  805.4 58.8 %collective-permute-start.57 = (bf16[256,768]{1,0:T(8,128)(2,1)S(1)}, bf16[256,768]{1,0:T(8,128)(2,1)S(1)}, u32[]{:S(2)}, u32[]{:S(2)}) collective-permute-start(bf16[256,768]{1,0:T(8,128)(2,1)S(1)} %get-tuple-element.64.rest_0_), channel_id=1, source_target_pairs={{0,4},{4,0},{8,12},{12,8},{16,20},{20,16},{24,28},{28,24},{1,5},{5... | collective-permute-start | bytes 1179656 | tf_op jit(solution)/shard_map/ppermute | solution.py:71
  811.0 53.1 %collective-permute-start.58 = (bf16[256,768]{1,0:T(8,128)(2,1)S(1)}, bf16[256,768]{1,0:T(8,128)(2,1)S(1)}, u32[]{:S(2)}, u32[]{:S(2)}) collective-permute-start(bf16[256,768]{1,0:T(8,128)(2,1)S(1)} %collective-permute-done.54.rest_1_), channel_id=1, source_target_pairs={{0,4},{4,0},{8,12},{12,8},{16,20},{20,16},{24,28},{28,24},{1,5},{5... | collective-permute-start | bytes 1179656 | tf_op jit(solution)/shard_map/ppermute | solution.py:71
  812.4 51.8 %collective-permute-start.59 = (bf16[256,768]{1,0:T(8,128)(2,1)S(1)}, bf16[256,768]{1,0:T(8,128)(2,1)S(1)}, u32[]{:S(2)}, u32[]{:S(2)}) collective-permute-start(bf16[256,768]{1,0:T(8,128)(2,1)S(1)} %collective-permute-done.55.rest_2_), channel_id=1, source_target_pairs={{0,4},{4,0},{8,12},{12,8},{16,20},{20,16},{24,28},{28,24},{1,5},{5... | collective-permute-start | bytes 1179656 | tf_op jit(solution)/shard_map/ppermute | solution.py:71
  815.0 49.2 %collective-permute-start.60 = (bf16[256,768]{1,0:T(8,128)(2,1)S(1)}, bf16[256,768]{1,0:T(8,128)(2,1)S(1)}, u32[]{:S(2)}, u32[]{:S(2)}) collective-permute-start(bf16[256,768]{1,0:T(8,128)(2,1)S(1)} %collective-permute-done.56.rest_3_), channel_id=1, source_target_pairs={{0,4},{4,0},{8,12},{12,8},{16,20},{20,16},{24,28},{28,24},{1,5},{5... | collective-permute-start | bytes 1179656 | tf_op jit(solution)/shard_map/ppermute | solution.py:71
  (151 other events, 2556.1 us)

commit v2 on v1

v2 whole, which is shorter than its diff:
```python
import math

import jax
import jax.numpy as jnp
from jax import lax
from jax.experimental import pallas as pl
from jax.experimental.pallas import tpu as pltpu
from jax.sharding import PartitionSpec as P

HQ = 16
HK = 8
HD = 128
FF = 3072
SEQ_LEN = 512
PARAMS = 15730944


EPS_NORM = 1e-06
ROPE_BASE = 1000000.0
MASKED = -1e30
LEARN_RATE = 0.03
GAIN_RATE = 0.3
WEIGHT_DECAY = 0.1
BETA_ONE = 0.9
BETA_TWO = 0.95
ADAM_EPS = 1e-08
STEP_COUNT = 3.0


def rotary_tables(places, width):
    half_width = width // 2
    frequency = ROPE_BASE ** (-(jnp.arange(half_width, dtype=jnp.float32) * 2.0) / width)
    angles = places.astype(jnp.float32)[:, None] * frequency[None, :]
    cosine, sine = jnp.cos(angles), jnp.sin(angles)
    return (
        jnp.concatenate([cosine, cosine], axis=1),
        jnp.concatenate([-sine, sine], axis=1),
    )


def contract_rows(left_side, right_side):
    return lax.dot_general(
        left_side, right_side, (((0,), (0,)), ((), ())), preferred_element_type=jnp.float32
    )


def contract_cols(left_side, right_side):
    return lax.dot_general(
        left_side, right_side, (((1,), (1,)), ((), ())), preferred_element_type=jnp.float32
    )


def norm_back(grad_out, normed, inv_root, gain):
    scaled = grad_out * gain
    return inv_root * (scaled - normed * jnp.mean(normed * scaled, axis=-1, keepdims=True))


def swap(value, axis, mask):
    count = lax.axis_size(axis)
    return lax.ppermute(value, axis, [(i, i ^ mask) for i in range(count)])


def bit_masks(count):
    return [1 << i for i in range(count.bit_length() - 1)]


def after(value, *others):
    return lax.optimization_barrier((value, others))[0]


def gather_rows(shard, chunks, previous):
    owners = lax.axis_size("group")
    copies = lax.axis_size("dp")
    mine = lax.axis_index("group")
    rows, columns = shard.shape
    half = rows // 2
    side = lax.axis_index("dp") & 1
    split = copies > 1
    pieces = [(shard, 0, 0)]
    order = previous
    for mask in bit_masks(owners)[1:]:
        if mask == 2 and split:
            size = half // chunks
            for c in range(chunks):
                near_at = side * half + c * size
                far_at = (1 - side) * half + c * size
                near = lax.dynamic_slice_in_dim(shard, near_at, size, 0)
                if order is not None:
                    near = after(near, order)
                order = swap(near, "group", mask)
                pieces += [
                    (order, mask, near_at),
                    (swap(order, "dp", 1), mask, far_at),
                ]
        else:
            pieces += [(swap(v, "group", mask), dg ^ mask, off) for v, dg, off in pieces]
    pieces += [(swap(v, "group", 1), dg ^ 1, off) for v, dg, off in pieces]
    full = jnp.zeros((rows * owners, columns), shard.dtype)
    for value, delta, offset in pieces:
        start = (mine ^ delta) * rows + offset
        full = lax.dynamic_update_slice(full, value, (start, 0))
    return full, order


def gather_small(shard):
    owners = lax.axis_size("group")
    mine = lax.axis_index("group")
    width = shard.shape[1]
    held = shard[None]
    deltas = [0]
    for mask in reversed(bit_masks(owners)):
        held = jnp.concatenate([held, swap(held, "group", mask)], axis=0)
        deltas += [d ^ mask for d in deltas]
    full = jnp.zeros((shard.shape[0], width * owners), shard.dtype)
    for k, delta in enumerate(deltas):
        full = lax.dynamic_update_slice(full, held[k], (0, (mine ^ delta) * width))
    return full


def sum_all(value):
    for axis in ("group", "dp"):
        for mask in bit_masks(lax.axis_size(axis)):
            value = value + swap(value, axis, mask)
    return value


def spread_bits(position, masks):
    total = 0
    count = len(masks)
    for i, mask in enumerate(masks):
        total = total + ((position >> (count - 1 - i)) & 1) * mask
    return total


def grad_blocks(left, right):
    tokens, rows = left.shape
    columns = right.shape[1]
    owners = lax.axis_size("group")
    copies = lax.axis_size("dp")
    column_masks = bit_masks(copies)
    later = bit_masks(owners)[1:]
    staying = [spread_bits(p, later) for p in range(1 << len(later))]
    row_sets = [[dg + 1 for dg in staying], staying] if owners > 1 else [[0]]
    row_block = rows // owners
    column_block = columns // copies
    mine = lax.axis_index("group")
    here = lax.axis_index("dp")
    if column_block % 128 or row_block % 16:
        ordered = jnp.concatenate(
            [
                lax.dynamic_slice_in_dim(
                    right, (here ^ spread_bits(p, column_masks)) * column_block, column_block, 1
                )
                for p in range(copies)
            ],
            axis=1,
        )
        return [
            jnp.stack(
                [
                    contract_rows(
                        lax.dynamic_slice_in_dim(left, (mine ^ dg) * row_block, row_block, 1),
                        ordered,
                    ).astype(jnp.bfloat16)
                    for dg in row_set
                ]
            )
            for row_set in row_sets
        ]
    wide = 2 if column_block % 256 and copies % 2 == 0 else 1

    def body(where, left_ref, *rest):
        rights, outs, turned = rest[:wide], rest[wide:-1], rest[-1]

        @pl.when(pl.program_id(0) == 0)
        def _():
            turned[...] = left_ref[...].T

        block = jnp.concatenate([ref[...] for ref in rights], axis=1)
        for out, row_set in zip(outs, row_sets):
            for k, dg in enumerate(row_set):
                start = pl.multiple_of((where[0] ^ dg) * row_block, row_block)
                out[k] = jnp.dot(
                    turned[pl.ds(start, row_block), :],
                    block,
                    preferred_element_type=jnp.float32,
                ).astype(jnp.bfloat16)

    def right_spec(j):
        return pl.BlockSpec(
            (tokens, column_block),
            lambda p, where: (0, where[1] ^ spread_bits(p * wide + j, column_masks)),
        )

    return pl.pallas_call(
        body,
        out_shape=[
            jax.ShapeDtypeStruct((len(row_set), row_block, columns), jnp.bfloat16)
            for row_set in row_sets
        ],
        grid_spec=pltpu.PrefetchScalarGridSpec(
            num_scalar_prefetch=1,
            grid=(copies // wide,),
            in_specs=[pl.BlockSpec((tokens, rows), lambda p, where: (0, 0))]
            + [right_spec(j) for j in range(wide)],
            out_specs=[
                pl.BlockSpec(
                    (len(row_set), row_block, column_block * wide), lambda p, where: (0, 0, p)
                )
                for row_set in row_sets
            ],
            scratch_shapes=[pltpu.VMEM((rows, tokens), jnp.bfloat16)],
        ),
        compiler_params=pltpu.CompilerParams(vmem_limit_bytes=48 * 1024 * 1024),
        cost_estimate=pl.CostEstimate(
            flops=2 * tokens * rows * columns,
            bytes_accessed=2 * (tokens * rows + tokens * columns + rows * columns),
            transcendentals=0,
        ),
    )(jnp.stack([mine, here]).astype(jnp.int32), left, *[right] * wide)


class GradSum:
    def __init__(self, left, right):
        blocks = grad_blocks(left, right)
        self.blocks = blocks
        group = [("group", m) for m in bit_masks(lax.axis_size("group"))]
        other = [("dp", m) for m in bit_masks(lax.axis_size("dp"))]
        held = [blocks[-1]]
        if group:
            held.append(swap(blocks[0], "group", 1))
        rest = group[1:]
        self.orders = [rest + other, other[:1] + rest + other[1:]]
        half = blocks[-1].shape[1] // 2
        self.parts = [
            [v[:, i * half : (i + 1) * half] for v in held] for i in range(2)
        ]
        self.length = len(rest) + len(other)
        self.step = 0

    def advance(self):
        sent = []
        if self.step == self.length:
            return sent
        for i, order in enumerate(self.orders):
            axis, mask = order[self.step]
            dim = 0 if axis == "group" else 2
            size = self.parts[i][0].shape[dim] // 2
            away = sum(
                lax.slice_in_dim(v, size, 2 * size, axis=dim).astype(jnp.float32)
                for v in self.parts[i]
            ).astype(jnp.bfloat16)
            stay = [lax.slice_in_dim(v, 0, size, axis=dim) for v in self.parts[i]]
            self.parts[i] = stay + [swap(away, axis, mask)]
            sent.append(away)
        self.step += 1
        return sent

    def finish(self):
        while self.step < self.length:
            self.advance()
        return jnp.concatenate(
            [sum(v[0].astype(jnp.float32) for v in part) for part in self.parts], axis=0
        )


def gather_grad(own):
    held = own.astype(jnp.bfloat16)[None]
    deltas = [0]
    groups = [(held, deltas)]
    masks = list(reversed(bit_masks(lax.axis_size("dp"))))
    for i, mask in enumerate(masks):
        got = swap(held, "dp", mask)
        got_deltas = [d ^ mask for d in deltas]
        if i + 1 < len(masks):
            held = jnp.concatenate([held, got], axis=0)
            deltas = deltas + got_deltas
            groups = [(held, deltas)]
        else:
            groups.append((got, got_deltas))
    return groups


def adam_core(master, first_moment, second_moment, clipped, step_rate, decay_rate):
    first_new = BETA_ONE * first_moment + (1.0 - BETA_ONE) * clipped
    second_new = BETA_TWO * second_moment + (1.0 - BETA_TWO) * clipped * clipped
    first_hat = first_new / (1.0 - BETA_ONE**STEP_COUNT)
    second_hat = second_new / (1.0 - BETA_TWO**STEP_COUNT)
    renewed = master - step_rate * (
        first_hat / (jnp.sqrt(second_hat) + ADAM_EPS) + decay_rate * master
    )
    return renewed, first_new, second_new


def adam_blocks(master, moment, blocks, factor, step_rate, decay_rate):
    rows, columns = master.shape
    copies = lax.axis_size("dp")
    here = lax.axis_index("dp")
    width = columns // copies
    if width % 128:
        full = jnp.zeros(master.shape, jnp.float32)
        for value, deltas in blocks:
            for k, dd in enumerate(deltas):
                full = lax.dynamic_update_slice(
                    full, value[k].astype(jnp.float32), (0, (here ^ dd) * width)
                )
        return adam_update(master, moment, full, factor, step_rate, decay_rate)
    tile = 32

    def body(where, factor_ref, master_ref, moment_ref, *rest):
        grads, (new_ref, state_ref) = rest[:-2], rest[-2:]
        scale = factor_ref[0, 0]
        for grad, (_, deltas) in zip(grads, blocks):
            for k, dd in enumerate(deltas):
                at = pl.ds(pl.multiple_of((where[0] ^ dd) * width, 128), width)
                renewed, first_new, second_new = adam_core(
                    master_ref[:, at],
                    moment_ref[0, :, at],
                    moment_ref[1, :, at],
                    grad[k].astype(jnp.float32) * scale,
                    step_rate,
                    decay_rate,
                )
                new_ref[:, at] = renewed
                state_ref[0, :, at] = first_new
                state_ref[1, :, at] = second_new

    return pl.pallas_call(
        body,
        out_shape=[
            jax.ShapeDtypeStruct(master.shape, jnp.float32),
            jax.ShapeDtypeStruct(moment.shape, jnp.float32),
        ],
        grid_spec=pltpu.PrefetchScalarGridSpec(
            num_scalar_prefetch=1,
            grid=(rows // tile,),
            in_specs=[
                pl.BlockSpec(memory_space=pltpu.SMEM),
                pl.BlockSpec((tile, columns), lambda i, where: (i, 0)),
                pl.BlockSpec((2, tile, columns), lambda i, where: (0, i, 0)),
            ]
            + [
                pl.BlockSpec((len(deltas), tile, width), lambda i, where: (0, i, 0))
                for _, deltas in blocks
            ],
            out_specs=[
                pl.BlockSpec((tile, columns), lambda i, where: (i, 0)),
                pl.BlockSpec((2, tile, columns), lambda i, where: (0, i, 0)),
            ],
        ),
        compiler_params=pltpu.CompilerParams(vmem_limit_bytes=48 * 1024 * 1024),
        cost_estimate=pl.CostEstimate(
            flops=20 * rows * columns,
            bytes_accessed=26 * rows * columns,
            transcendentals=rows * columns,
        ),
    )(
        here.reshape(1).astype(jnp.int32),
        factor.reshape(1, 1),
        master,
        moment,
        *[value for value, _ in blocks],
    )


def adam_update(master, moment, gradient, factor, step_rate, decay_rate):
    clipped = gradient * factor
    first_moment = BETA_ONE * moment[0] + (1.0 - BETA_ONE) * clipped
    second = BETA_TWO * moment[1] + (1.0 - BETA_TWO) * clipped * clipped
    first_hat = first_moment / (1.0 - BETA_ONE**STEP_COUNT)
    second_hat = second / (1.0 - BETA_TWO**STEP_COUNT)
    renewed = master - step_rate * (
        first_hat / (jnp.sqrt(second_hat) + ADAM_EPS) + decay_rate * master
    )
    return (renewed, jnp.stack([first_moment, second]))


def head_forward(raw, gain, cosine, sine):
    root = lax.rsqrt(jnp.mean(raw * raw, axis=-1, keepdims=True) + EPS_NORM)
    normed = raw * root
    scaled = normed * gain
    turned = scaled * cosine + pltpu.roll(scaled, HD // 2, 1) * sine
    return turned.astype(jnp.bfloat16), normed, root


def head_backward(grad, normed, root, gain, cosine, sine):
    turned = grad * cosine - pltpu.roll(grad, HD // 2, 1) * sine
    grad_gain = jnp.sum(turned * normed, axis=0, keepdims=True)
    scaled = turned * gain
    raw = root * (scaled - normed * jnp.mean(normed * scaled, axis=-1, keepdims=True))
    return raw, grad_gain


SPAN = 256


def span_weights(query_low, key_low, seg_row_ref, seg_col_ref, start):
    stop = start + SPAN
    scores = lax.dot_general(
        key_low[:stop],
        query_low[start:stop],
        (((1,), (1,)), ((), ())),
        preferred_element_type=jnp.float32,
    ) * (1.0 / math.sqrt(HD))
    key_at = lax.broadcasted_iota(jnp.int32, (stop, SPAN), 0)
    query_at = lax.broadcasted_iota(jnp.int32, (stop, SPAN), 1) + start
    allowed = (key_at <= query_at) & (seg_col_ref[:stop, :] == seg_row_ref[:, start:stop])
    scores = jnp.where(allowed, scores, MASKED)
    raised = jnp.exp(scores - jnp.max(scores, axis=0, keepdims=True))
    return raised * (1.0 / jnp.sum(raised, axis=0, keepdims=True))


def attend_body(
    query_ref, key_ref, value_ref, cos_ref, sin_ref, row_ref, col_ref, gain_ref, out_ref
):
    cosine, sine = cos_ref[...], sin_ref[...]
    key_low, _, _ = head_forward(key_ref[...], gain_ref[1:2, :], cosine, sine)
    value_turned = value_ref[...].astype(jnp.bfloat16).T
    for g in range(HQ // HK):
        at = slice(g * HD, (g + 1) * HD)
        query_low, _, _ = head_forward(query_ref[:, at], gain_ref[0:1, :], cosine, sine)
        for start in range(0, SEQ_LEN, SPAN):
            stop = start + SPAN
            weights = span_weights(query_low, key_low, row_ref, col_ref, start)
            mixed = jnp.dot(
                value_turned[:, :stop],
                weights.astype(jnp.bfloat16),
                preferred_element_type=jnp.float32,
            )
            out_ref[start:stop, at] = mixed.T.astype(jnp.bfloat16)


def attend_back_body(
    query_ref, key_ref, value_ref, cos_ref, sin_ref, row_ref, col_ref, gain_ref, grad_ref,
    out_ref, gain_out_ref,
):
    head = pl.program_id(1)
    cosine, sine = cos_ref[...], sin_ref[...]
    inv_head = 1.0 / math.sqrt(HD)

    @pl.when((pl.program_id(0) == 0) & (head == 0))
    def _():
        gain_out_ref[...] = jnp.zeros_like(gain_out_ref)

    key_low, key_normed, key_root = head_forward(key_ref[...], gain_ref[1:2, :], cosine, sine)
    value_low = value_ref[...].astype(jnp.bfloat16)
    key_turned = key_low.T
    grad_key = [jnp.zeros((SPAN, HD), jnp.float32)] * (SEQ_LEN // SPAN)
    grad_value = list(grad_key)
    gain_query = jnp.zeros((1, HD), jnp.float32)
    for g in range(HQ // HK):
        at = slice(g * HD, (g + 1) * HD)
        query_low, normed, root = head_forward(query_ref[:, at], gain_ref[0:1, :], cosine, sine)
        grad_query = []
        for start in range(0, SEQ_LEN, SPAN):
            stop = start + SPAN
            weights = span_weights(query_low, key_low, row_ref, col_ref, start)
            grad_out = grad_ref[start:stop, at]
            grad_weights = lax.dot_general(
                value_low[:stop],
                grad_out,
                (((1,), (1,)), ((), ())),
                preferred_element_type=jnp.float32,
            )
            more_value = jnp.dot(
                weights.astype(jnp.bfloat16), grad_out, preferred_element_type=jnp.float32
            )
            product = weights * grad_weights
            grad_scores = (
                weights * (grad_weights - jnp.sum(product, axis=0, keepdims=True))
            ).astype(jnp.bfloat16)
            more_key = jnp.dot(
                grad_scores, query_low[start:stop], preferred_element_type=jnp.float32
            )
            grad_query.append(
                jnp.dot(
                    key_turned[:, :stop], grad_scores, preferred_element_type=jnp.float32
                ).T
            )
            for j in range(stop // SPAN):
                part = slice(j * SPAN, (j + 1) * SPAN)
                grad_key[j] = grad_key[j] + more_key[part]
                grad_value[j] = grad_value[j] + more_value[part]
        raw, more_gain = head_backward(
            jnp.concatenate(grad_query, axis=0) * inv_head,
            normed,
            root,
            gain_ref[0:1, :],
            cosine,
            sine,
        )
        gain_query = gain_query + more_gain
        place = pl.multiple_of((head * (HQ // HK) + g) * HD, HD)
        out_ref[:, pl.ds(place, HD)] = raw.astype(jnp.bfloat16)
    raw, gain_key = head_backward(
        jnp.concatenate(grad_key, axis=0) * inv_head,
        key_normed,
        key_root,
        gain_ref[1:2, :],
        cosine,
        sine,
    )
    out_ref[:, pl.ds(pl.multiple_of((HQ + head) * HD, HD), HD)] = raw.astype(jnp.bfloat16)
    out_ref[:, pl.ds(pl.multiple_of((HQ + HK + head) * HD, HD), HD)] = jnp.concatenate(
        grad_value, axis=0
    ).astype(jnp.bfloat16)
    gain_out_ref[0:1, :] += gain_query
    gain_out_ref[1:2, :] += gain_key


def attention_call(body, projected, tables, segments, gains, grad_out):
    token_rows = projected.shape[0]
    seq_count = token_rows // SEQ_LEN
    groups = HQ // HK
    wide = groups * HD
    full = lambda s, h: (s, 0)
    in_specs = [
        pl.BlockSpec((SEQ_LEN, wide), lambda s, h: (s, h)),
        pl.BlockSpec((SEQ_LEN, HD), lambda s, h: (s, HQ + h)),
        pl.BlockSpec((SEQ_LEN, HD), lambda s, h: (s, HQ + HK + h)),
        pl.BlockSpec((SEQ_LEN, HD), full),
        pl.BlockSpec((SEQ_LEN, HD), full),
        pl.BlockSpec((1, SEQ_LEN), lambda s, h: (0, s)),
        pl.BlockSpec((SEQ_LEN, 1), full),
        pl.BlockSpec((2, HD), lambda s, h: (0, 0)),
    ]
    operands = [
        projected,
        projected,
        projected,
        *tables,
        segments[None, :],
        segments[:, None],
        gains,
    ]
    pairs = token_rows * SEQ_LEN * HQ
    if grad_out is None:
        out_specs = pl.BlockSpec((SEQ_LEN, wide), lambda s, h: (s, h))
        out_shape = jax.ShapeDtypeStruct((token_rows, HQ * HD), jnp.bfloat16)
    else:
        columns = projected.shape[1]
        in_specs.append(pl.BlockSpec((SEQ_LEN, wide), lambda s, h: (s, h)))
        operands.append(grad_out)
        out_specs = [
            pl.BlockSpec((SEQ_LEN, columns), full),
            pl.BlockSpec((2, HD), lambda s, h: (0, 0)),
        ]
        out_shape = [
            jax.ShapeDtypeStruct((token_rows, columns), jnp.bfloat16),
            jax.ShapeDtypeStruct((2, HD), jnp.float32),
        ]
    return pl.pallas_call(
        body,
        grid=(seq_count, HK),
        in_specs=in_specs,
        out_specs=out_specs,
        out_shape=out_shape,
        compiler_params=pltpu.CompilerParams(vmem_limit_bytes=48 * 1024 * 1024),
        cost_estimate=pl.CostEstimate(
            flops=(4 if grad_out is None else 10) * pairs * HD * 2,
            bytes_accessed=projected.size * 6,
            transcendentals=pairs,
        ),
    )(*operands)


def on_device(
    tokens,
    segment_ids,
    positions,
    cotangent,
    qkv_weight,
    out_weight,
    gate_up_weight,
    down_weight,
    norm_gains,
    head_gains,
    qkv_moments,
    out_moments,
    gate_up_moments,
    down_moments,
    norm_moments,
    head_moments,
):
    width = norm_gains.shape[1]
    gains_low = jnp.concatenate([norm_gains, head_gains], axis=1).astype(jnp.bfloat16)
    owners = lax.axis_size("group")
    gains_all = gather_small(gains_low).reshape(2, owners, -1)
    full_norm = gains_all[:, :, :width].reshape(2, -1)
    full_head = gains_all[:, :, width:].reshape(2, -1)
    full_qkv, order = gather_rows(qkv_weight.astype(jnp.bfloat16), 2, None)
    full_out, order = gather_rows(out_weight.astype(jnp.bfloat16), 1, order)
    full_gate_up, order = gather_rows(gate_up_weight.astype(jnp.bfloat16), 2, order)
    full_down, order = gather_rows(down_weight.astype(jnp.bfloat16), 1, order)
    gain_one = full_norm[0].astype(jnp.float32)
    gain_two = full_norm[1].astype(jnp.float32)
    head_gain = full_head.astype(jnp.float32)
    inputs = tokens.astype(jnp.float32)
    root_one = lax.rsqrt(jnp.mean(inputs * inputs, axis=-1, keepdims=True) + EPS_NORM)
    normed_one = inputs * root_one
    hidden_one = (normed_one * gain_one).astype(jnp.bfloat16)
    projected = jnp.dot(hidden_one, full_qkv, preferred_element_type=jnp.float32)
    tables = rotary_tables(positions, HD)
    mixed_low = attention_call(attend_body, projected, tables, segment_ids, head_gain, None)
    attended = jnp.dot(mixed_low, full_out, preferred_element_type=jnp.float32)
    residual = inputs + attended
    root_two = lax.rsqrt(jnp.mean(residual * residual, axis=-1, keepdims=True) + EPS_NORM)
    normed_two = residual * root_two
    hidden_two = (normed_two * gain_two).astype(jnp.bfloat16)
    gate_up = jnp.dot(hidden_two, full_gate_up, preferred_element_type=jnp.float32)
    gate_part = gate_up[:, :FF]
    upward = gate_up[:, FF:]
    sigmoid_gate = jax.nn.sigmoid(gate_part)
    activated = (gate_part * sigmoid_gate * upward).astype(jnp.bfloat16)
    branch = jnp.dot(activated, full_down, preferred_element_type=jnp.float32)
    output = (residual + branch).astype(jnp.bfloat16)
    upstream = cotangent.astype(jnp.float32)
    down_sum = GradSum(activated, cotangent)
    grad_act = contract_cols(after(cotangent, *down_sum.blocks), full_down)
    grad_gate = grad_act * upward * sigmoid_gate * (1.0 + gate_part * (1.0 - sigmoid_gate))
    grad_up = grad_act * gate_part * sigmoid_gate
    grad_gate_up = jnp.concatenate([grad_gate, grad_up], axis=-1).astype(jnp.bfloat16)
    gate_up_sum = GradSum(hidden_two, after(grad_gate_up, *down_sum.advance()))
    grad_hidden_two = contract_cols(after(grad_gate_up, *gate_up_sum.blocks), full_gate_up)
    grad_gain_two = jnp.sum(grad_hidden_two * normed_two, axis=0)
    grad_residual = upstream + norm_back(grad_hidden_two, normed_two, root_two, gain_two)
    residual_low = grad_residual.astype(jnp.bfloat16)
    out_sum = GradSum(mixed_low, after(residual_low, *gate_up_sum.advance()))
    grad_mixed = contract_cols(after(residual_low, *out_sum.blocks), full_out).astype(
        jnp.bfloat16
    )
    grad_mixed = after(grad_mixed, *down_sum.advance(), *out_sum.advance())
    grad_projected, grad_gain_head = attention_call(
        attend_back_body, projected, tables, segment_ids, head_gain, grad_mixed
    )
    qkv_sum = GradSum(hidden_one, grad_projected)
    grad_hidden_one = contract_cols(after(grad_projected, *qkv_sum.blocks), full_qkv)
    grad_gain_one = jnp.sum(grad_hidden_one * normed_one, axis=0)
    grad_inputs = grad_residual + norm_back(grad_hidden_one, normed_one, root_one, gain_one)
    tokens_grad = grad_inputs.astype(jnp.bfloat16)
    small = jnp.concatenate(
        [jnp.stack([grad_gain_one, grad_gain_two]), grad_gain_head],
        axis=1,
    )
    small = sum_all(small)
    norm_total = small[:, :-HD]
    head_total = small[:, -HD:]
    owned = tuple(v.finish() for v in (qkv_sum, out_sum, gate_up_sum, down_sum))
    squares = sum_all(sum(jnp.sum(v * v) for v in owned).reshape(1, 1))[0, 0]
    squares = squares + jnp.sum(small * small)
    clip_limit = math.sqrt(PARAMS)
    factor = clip_limit / jnp.maximum(jnp.sqrt(squares), clip_limit)
    gathered = [gather_grad(v) for v in owned]
    masters = (qkv_weight, out_weight, gate_up_weight, down_weight)
    moments = (qkv_moments, out_moments, gate_up_moments, down_moments)
    renewed = [
        adam_blocks(master, moment, blocks, factor, LEARN_RATE, WEIGHT_DECAY)
        for master, moment, blocks in zip(masters, moments, gathered)
    ]
    mine = lax.axis_index("group")
    norm_grad = lax.dynamic_slice_in_dim(
        norm_total, mine * norm_gains.shape[1], norm_gains.shape[1], 1
    )
    head_grad = lax.dynamic_slice_in_dim(
        head_total, mine * head_gains.shape[1], head_gains.shape[1], 1
    )
    renewed.append(adam_update(norm_gains, norm_moments, norm_grad, factor, GAIN_RATE, 0.0))
    renewed.append(adam_update(head_gains, head_moments, head_grad, factor, GAIN_RATE, 0.0))
    return (
        output,
        tokens_grad,
        *owned,
        norm_grad,
        head_grad,
        *[new for new, _ in renewed],
        *[state for _, state in renewed],
    )


def solution(mesh):
    placed = (
        P(("dp", "group"), None),
        P(("dp", "group")),
        P(("dp", "group")),
        P(("dp", "group"), None),
        P("group", None),
        P("group", None),
        P("group", None),
        P("group", None),
        P(None, "group"),
        P(None, "group"),
        P(None, "group", None),
        P(None, "group", None),
        P(None, "group", None),
        P(None, "group", None),
        P(None, None, "group"),
        P(None, None, "group"),
    )
    return jax.shard_map(
        on_device,
        mesh=mesh,
        in_specs=placed,
        out_specs=(
            P(("dp", "group"), None),
            P(("dp", "group"), None),
            P("group", "dp"),
            P("group", "dp"),
            P("group", "dp"),
            P("group", "dp"),
            P(None, "group"),
            P(None, "group"),
            P("group", None),
            P("group", None),
            P("group", None),
            P("group", None),
            P(None, "group"),
            P(None, "group"),
            P(None, "group", None),
            P(None, "group", None),
            P(None, "group", None),
            P(None, "group", None),
            P(None, None, "group"),
            P(None, None, "group"),
        ),
        check_vma=False,
    )
```

time: 890 us -> 641 us (0.72)
  waiting for transfers between devices: 255 us -> 174 us
  blocking collectives: 71.2 us -> 0 us
  local copies, waits for them, and re-layouts: 123 us -> 64.8 us
  other arithmetic: 120 us -> 76.5 us
  matrix products: 107 us -> 71.7 us
  Pallas kernels: 126 us -> 148 us
  starting transfers between devices: 73.5 us -> 90.3 us
    ppermute x68 -> x88, waiting for transfers between devices: 255 us -> 174 us  [swap(): return lax.ppermute(value, axis, [(i, i ^ mask) for i in range(count)])]
    pallas_call x0 -> x2, Pallas kernels: none -> 49.5 us  [attention_call(): pl.pallas_call(body, grid=(seq_count, HK), in_specs=in_specs, out_specs=o...]
    dot_general x6 -> x0, matrix products: 48.9 us -> none  [the longest x1 15.7 us: on_device(): jnp.einsum('sqkgd,spkd->skgqp', grad_mixed, value_blocks, preferred_eleme...]
    psum x1 -> x0, blocking collectives: 42.4 us -> none  [on_device(): small = lax.psum(small, ('dp', 'group'))]
    unnamed x240 -> x112, local copies, waits for them, and re-layouts: 49.7 us -> 9.96 us
    reduce_sum x12 -> x4, other arithmetic: 44.4 us -> 5.76 us  [on_device(): squares = sum_all(sum((jnp.sum(v * v) for v in owned)).reshape(1, 1))[0, 0]]
    all_gather x2 -> x0, blocking collectives: 28.7 us -> none  [the longest x1 23.4 us: on_device(): lax.all_gather(norm_gains.astype(jnp.bfloat16), 'group', axis=1, tiled=True)]
    pallas_call x8 -> x4, Pallas kernels: 66.9 us -> 38.7 us  [grad_blocks(): pl.pallas_call(body, out_shape=[jax.ShapeDtypeStruct((len(row_set), row_b...]
  transfers between devices with their start and end apart: 68 -> 88, of which waited for: 24 -> 34; matrix products, arithmetic and copies ran while one was open for 25% -> 31% of each run, Pallas kernels for 9% -> 19%
where the time goes in v2:
time: 641 us; the launch traced here: 633 us
  waiting for transfers between devices  174 us (27%)
  Pallas kernels  148 us (23%)
  starting transfers between devices  90.3 us (14%)
  other arithmetic  76.5 us (12%)
  matrix products  71.7 us (11%)
  local copies, waits for them, and re-layouts  64.8 us (10%)
  between operations  8.44 us (1%)
    ppermute x88, waiting for transfers between devices, swap(): return lax.ppermute(value, axis, [(i, i ^ mask) for i in range(count)])  174 us
    ppermute x88, starting transfers between devices, swap(): return lax.ppermute(value, axis, [(i, i ^ mask) for i in range(count)])  90.3 us
    pallas_call x4, Pallas kernels, adam_blocks(): pl.pallas_call(body, out_shape=[jax.ShapeDtypeStruct(master.shape, jnp.fl...  59.7 us
    pallas_call x2, Pallas kernels, attention_call(): pl.pallas_call(body, grid=(seq_count, HK), in_specs=in_specs, out_specs=o...  49.5 us
    dot_general x4, matrix products, contract_cols(): lax.dot_general(left_side, right_side, (((1,), (1,)), ((), ())), preferre...  40 us
    pallas_call x4, Pallas kernels, grad_blocks(): pl.pallas_call(body, out_shape=[jax.ShapeDtypeStruct((len(row_set), row_b...  38.7 us
    dynamic_update_slice x28, local copies, waits for them, and re-layouts, gather_rows(): full = lax.dynamic_update_slice(full, value, (start, 0))  35.5 us
    convert_element_type x20, other arithmetic, advance(): away = sum((lax.slice_in_dim(v, size, 2 * size, axis=dim).astype(jnp.floa...  27.5 us
  transfers between devices with their start and end apart: 88, of which 34 were waited for; matrix products, arithmetic and copies ran while one was open for 31% of the time, Pallas kernels for 19%

profile of v2, /device:TPU:0, one launch (start us, length us, event | category | flops | bytes accessed | tf_op | source)
XLA Modules:
  0.0 633.3 jit_solution(16223534937295356458)
XLA Ops:
  29.2 6.3 %broadcast_in_dim.19 = bf16[1024,6144]{1,0:T(8,128)(2,1)} broadcast(bf16[]{:T(256)} %constant.40.clone.1), dimensions={} | broadcast | bytes 12582914 | tf_op jit(solution)/shard_map/broadcast_in_dim | solution.py:98
  35.5 5.2 constant_dynamic-update-slice_fusion.15
  53.9 9.1 %collective-permute-done.4 = bf16[64,4096]{1,0:T(8,128)(2,1)} collective-permute-done((bf16[64,4096]{1,0:T(8,128)(2,1)}, bf16[64,4096]{1,0:T(8,128)(2,1)}, u32[]{:S(2)}, u32[]{:S(2)}) %collective-permute-start.4) | collective-permute-done | bytes 524320 | tf_op jit(solution)/shard_map/ppermute | solution.py:60
  69.9 7.9 %collective-permute-done.5 = bf16[64,4096]{1,0:T(8,128)(2,1)S(1)} collective-permute-done((bf16[64,4096]{1,0:T(8,128)(2,1)}, bf16[64,4096]{1,0:T(8,128)(2,1)S(1)}, u32[]{:S(2)}, u32[]{:S(2)}) %collective-permute-start.5) | collective-permute-done | bytes 524320 | tf_op jit(solution)/shard_map/ppermute | solution.py:60
  89.7 10.2 %fusion.37.query_ref.key_ref.value_ref = f32[512,4096]{1,0:T(8,128)} fusion(bf16[512,1024]{1,0:T(8,128)(2,1)S(1)} %copy-done.9, bf16[1024,4096]{1,0:T(8,128)(2,1)} %constant_dynamic-update-slice_fusion.22), kind=kOutput, calls=%fused_computation.180 | convolution fusion | flops 4294967296 | bytes 17825792 | tf_op jit(solution)/shard_map/dot_general | solution.py:602
  105.8 18.5 %shard_map.311.left_ref = bf16[512,2048]{1,0:T(8,128)(2,1)S(1)} custom-call(f32[512,4096]{1,0:T(8,128)} %fusion.37.query_ref.key_ref.value_ref, f32[512,4096]{1,0:T(8,128)} %fusion.37.query_ref.key_ref.value_ref, f32[512,4096]{1,0:T(8,128)} %fusion.37.query_ref.key_ref.value_ref, f32[512,128]{1,0:T(8,128)S(1)} %get-tuple-element.163.cos_ref, ...), custom_call_target="tpu_custom_call" | custom-call | flops 4294967296 | bytes 12582912 | tf_op jit(solution)/shard_map/pallas_call | solution.py:552
  135.8 8.9 %collective-permute-done.18 = bf16[64,6144]{1,0:T(8,128)(2,1)S(1)} collective-permute-done((bf16[64,6144]{1,0:T(8,128)(2,1)}, bf16[64,6144]{1,0:T(8,128)(2,1)S(1)}, u32[]{:S(2)}, u32[]{:S(2)}) %collective-permute-start.18) | collective-permute-done | bytes 786464 | tf_op jit(solution)/shard_map/ppermute | solution.py:60
  151.8 15.5 %collective-permute-done.19 = bf16[64,6144]{1,0:T(8,128)(2,1)S(1)} collective-permute-done((bf16[64,6144]{1,0:T(8,128)(2,1)S(1)}, bf16[64,6144]{1,0:T(8,128)(2,1)S(1)}, u32[]{:S(2)}, u32[]{:S(2)}) %collective-permute-start.19) | collective-permute-done | bytes 786464 | tf_op jit(solution)/shard_map/ppermute | solution.py:60
  177.2 9.7 %fusion.38 = f32[512,6144]{1,0:T(8,128)S(1)} fusion(bf16[512,1024]{1,0:T(8,128)(2,1)S(1)} %multiply_convert_fusion.3.left_ref, bf16[1024,6144]{1,0:T(8,128)(2,1)} %constant_dynamic-update-slice_fusion.6), kind=kOutput, calls=%fused_computation.181 | convolution fusion | flops 6442450944 | bytes 26214400 | tf_op jit(solution)/shard_map/dot_general | solution.py:610
  194.5 8.9 %shard_map.312 = (bf16[2,768,1024]{2,1,0:T(8,128)(2,1)S(1)}, bf16[2,768,1024]{2,1,0:T(8,128)(2,1)}) custom-call(s32[2]{0:T(128)S(1)} %pad_add_fusion.where, bf16[512,3072]{1,0:T(8,128)(2,1)} %multiply_convert_fusion.2.left_ref, bf16[512,1024]{1,0:T(8,128)(2,1)S(1)} %copy-done.3, bf16[512,1024]{1,0:T(8,128)(2,1)S(1)} %copy-done.3), custom_call_target="tpu_custom_call" | custom-call | flops 3221225472 | bytes 10485760 | tf_op jit(solution)/shard_map/pallas_call | solution.py:195
  209.3 11.8 %multiply_convert_fusion.1 = (bf16[512,3072]{1,0:T(8,128)(2,1)}, bf16[512,3072]{1,0:T(8,128)(2,1)}) fusion(f32[512,6144]{1,0:T(8,128)} %copy-done.15, bf16[512,1024]{1,0:T(8,128)(2,1)S(1)} %copy-done.3, bf16[3072,1024]{1,0:T(8,128)(2,1)} %constant_dynamic-update-slice_fusion), kind=kOutput, calls=%fused_computation.2 | convolution fusion | flops 3241672704 | bytes 26214400 | tf_op jit(solution)/shard_map/dot_general | solution.py:48
  221.1 6.2 pad_maximum_fusion.rest_0_
  232.5 12.5 %shard_map.313 = (bf16[2,256,6144]{2,1,0:T(8,128)(2,1)}, bf16[2,256,6144]{2,1,0:T(8,128)(2,1)}) custom-call(s32[2]{0:T(128)S(1)} %pad_add_fusion.where, bf16[512,1024]{1,0:T(8,128)(2,1)S(1)} %multiply_convert_fusion.3.left_ref, bf16[512,6144]{1,0:T(8,128)(2,1)} %pad_maximum_fusion.rest_0_), custom_call_target="tpu_custom_call" | custom-call | flops 6442450944 | bytes 19922944 | tf_op jit(solution)/shard_map/pallas_call | solution.py:195
  246.8 18.5 %collective-permute-done.32 = bf16[1,384,1024]{2,1,0:T(8,128)(2,1)} collective-permute-done((bf16[1,384,1024]{2,1,0:T(8,128)(2,1)}, bf16[1,384,1024]{2,1,0:T(8,128)(2,1)}, u32[]{:S(2)}, u32[]{:S(2)}) %collective-permute-start.32) | collective-permute-done | bytes 786464 | tf_op jit(solution)/shard_map/ppermute | solution.py:60
  270.0 12.9 %multiply_reduce_fusion = (f32[1024]{0:T(1024)S(1)}, f32[512]{0:T(512)S(1)}, f32[512,1024]{1,0:T(8,128)}) fusion(f32[512,1024]{1,0:T(8,128)S(1)} %copy-done.13, f32[512]{0:T(512)S(1)} %add_rsqrt_fusion, f32[1024]{0:T(1024)S(1)} %bitcast.92, bf16[512,6144]{1,0:T(8,128)(2,1)} %pad_maximum_fusion.rest_0_, ...), kind=kOutput, calls=%fused_computation.23 | convolution fusion | flops 6445595136 | bytes 23080960 | tf_op jit(solution)/shard_map/dot_general | solution.py:48
  301.4 6.8 %shard_map.314 = (bf16[2,512,1024]{2,1,0:T(8,128)(2,1)S(1)}, bf16[2,512,1024]{2,1,0:T(8,128)(2,1)S(1)}) custom-call(s32[2]{0:T(128)S(1)} %pad_add_fusion.where, bf16[512,2048]{1,0:T(8,128)(2,1)} %copy-done.4, bf16[512,1024]{1,0:T(8,128)(2,1)S(1)} %fusion.36.rest_0_.rest_1_, bf16[512,1024]{1,0:T(8,128)(2,1)S(1)} %fusion.36.rest_0_.rest_1_), custom_call_target="tpu_custom_call" | custom-call | flops 2147483648 | bytes 7340032 | tf_op jit(solution)/shard_map/pallas_call | solution.py:195
  310.7 7.2 %add_convert_fusion.4 = bf16[512,1024]{1,0:T(8,128)(2,1)} fusion(f32[512,1024]{1,0:T(8,128)S(1)} %copy-done.13, bf16[512,3072]{1,0:T(8,128)(2,1)S(1)} %copy-done.27, bf16[3072,1024]{1,0:T(8,128)(2,1)} %constant_dynamic-update-slice_fusion), kind=kOutput, calls=%fused_computation.28 | convolution fusion | flops 3222274048 | bytes 12582912 | tf_op jit(solution)/shard_map/dot_general | solution.py:615
  328.3 30.9 %shard_map.315 = (bf16[512,4096]{1,0:T(8,128)(2,1)}, f32[2,128]{1,0:T(2,128)S(1)}) custom-call(f32[512,4096]{1,0:T(8,128)} %fusion.37.query_ref.key_ref.value_ref, f32[512,4096]{1,0:T(8,128)} %fusion.37.query_ref.key_ref.value_ref, f32[512,4096]{1,0:T(8,128)} %fusion.37.query_ref.key_ref.value_ref, f32[512,128]{1,0:T(8,128)S(1)} %get-tuple-element.163.cos_ref, ...), custom_call_target="tpu_custom_call" | custom-call | flops 10737418240 | bytes 12582912 | tf_op jit(solution)/shard_map/pallas_call | solution.py:552
  359.2 10.5 %shard_map.316 = (bf16[2,256,4096]{2,1,0:T(8,128)(2,1)S(1)}, bf16[2,256,4096]{2,1,0:T(8,128)(2,1)}) custom-call(s32[2]{0:T(128)S(1)} %pad_add_fusion.where, bf16[512,1024]{1,0:T(8,128)(2,1)S(1)} %copy-done.10, bf16[512,4096]{1,0:T(8,128)(2,1)} %get-tuple-element.70.rest_0_), custom_call_target="tpu_custom_call" | custom-call | flops 4294967296 | bytes 13631488 | tf_op jit(solution)/shard_map/pallas_call | solution.py:195
  378.6 10.7 %fusion.10 = (f32[1024]{0:T(1024)S(1)}, f32[512]{0:T(512)S(1)}, f32[512,1024]{1,0:T(8,128)}) fusion(bf16[512,1024]{1,0:T(8,128)(2,1)S(1)} %copy-done.18, f32[512]{0:T(512)S(1)} %add_rsqrt_fusion.1, f32[1024]{0:T(1024)S(1)} %bitcast.96, bf16[512,4096]{1,0:T(8,128)(2,1)} %get-tuple-element.70.rest_0_, bf16[1024,4096]{1,0:T(8,128)(2,1)} %constant_dynamic-update-slice_fusion.22), kind=kOutput, calls=%fused_computation.21 | convolution fusion | flops 4298635776 | bytes 15740928 | tf_op jit(solution)/shard_map/dot_general | solution.py:48
  401.2 6.8 %collective-permute-done.44 = bf16[1,256,1024]{2,1,0:T(8,128)(2,1)S(1)} collective-permute-done((bf16[1,256,1024]{2,1,0:T(8,128)(2,1)}, bf16[1,256,1024]{2,1,0:T(8,128)(2,1)S(1)}, u32[]{:S(2)}, u32[]{:S(2)}) %collective-permute-start.44) | collective-permute-done | bytes 524320 | tf_op jit(solution)/shard_map/ppermute | solution.py:60
  423.7 10.0 %collective-permute-done.58 = bf16[1,128,1536]{2,1,0:T(8,128)(2,1)S(1)} collective-permute-done((bf16[1,128,1536]{2,1,0:T(8,128)(2,1)S(1)}, bf16[1,128,1536]{2,1,0:T(8,128)(2,1)S(1)}, u32[]{:S(2)}, u32[]{:S(2)}) %collective-permute-start.58) | collective-permute-done | bytes 393248 | tf_op jit(solution)/shard_map/ppermute | solution.py:60
  444.8 11.6 %collective-permute-done.47 = bf16[1,256,128]{2,1,0:T(8,128)(2,1)S(1)} collective-permute-done((bf16[1,256,128]{2,1,0:T(8,128)(2,1)S(1)}, bf16[1,256,128]{2,1,0:T(8,128)(2,1)S(1)}, u32[]{:S(2)}, u32[]{:S(2)}) %collective-permute-start.47) | collective-permute-done | bytes 65568 | tf_op jit(solution)/shard_map/ppermute | solution.py:60
  462.6 10.5 %collective-permute-done.82 = bf16[1,256,768]{2,1,0:T(8,128)(2,1)S(1)} collective-permute-done((bf16[1,256,768]{2,1,0:T(8,128)(2,1)S(1)}, bf16[1,256,768]{2,1,0:T(8,128)(2,1)S(1)}, u32[]{:S(2)}, u32[]{:S(2)}) %collective-permute-start.82) | collective-permute-done | bytes 393248 | tf_op jit(solution)/shard_map/ppermute | solution.py:60
  480.5 19.1 %collective-permute-done.42 = bf16[1,128,1024]{2,1,0:T(8,128)(2,1)S(1)} collective-permute-done((bf16[1,128,1024]{2,1,0:T(8,128)(2,1)S(1)}, bf16[1,128,1024]{2,1,0:T(8,128)(2,1)S(1)}, u32[]{:S(2)}, u32[]{:S(2)}) %collective-permute-start.42) | collective-permute-done | bytes 262176 | tf_op jit(solution)/shard_map/ppermute | solution.py:60
  502.4 8.9 %collective-permute-done.43 = bf16[1,128,512]{2,1,0:T(8,128)(2,1)S(1)} collective-permute-done((bf16[1,128,512]{2,1,0:T(8,128)(2,1)S(1)}, bf16[1,128,512]{2,1,0:T(8,128)(2,1)S(1)}, u32[]{:S(2)}, u32[]{:S(2)}) %collective-permute-start.43) | collective-permute-done | bytes 131104 | tf_op jit(solution)/shard_map/ppermute | solution.py:60
  535.5 6.9 %collective-permute-start.73 = (f32[1,1]{1,0:T(1,128)}, f32[1,1]{1,0:T(1,128)}, u32[]{:S(2)}, u32[]{:S(2)}) collective-permute-start(f32[1,1]{1,0:T(1,128)} %add.944), channel_id=1, source_target_pairs={{0,4},{4,0},{8,12},{12,8},{16,20},{20,16},{24,28},{28,24},{1,5},{5... | collective-permute-start | bytes 20 | tf_op jit(solution)/shard_map/ppermute | solution.py:60
  555.1 11.6 %shard_map.318 = (f32[512,1024]{1,0:T(8,128)}, f32[2,512,1024]{2,1,0:T(8,128)}) custom-call(s32[1]{0:T(128)} %bitcast.8.where, f32[1,1]{1,0:T(1,128)} %bitcast.21.factor_ref, f32[512,1024]{1,0:T(8,128)S(1)} %copy-done.2, f32[2,512,1024]{2,1,0:T(8,128)} %moment_ref.5, bf16[4,512,128]{2,1,0:T(8,128)(2,1)S(1)} %pad_maximum_fusion.8.rest_0_, ...), custom_call_target="tpu_custom_call" | custom-call | flops 10485760 | bytes 13631488 | tf_op jit(solution)/shard_map/pallas_call | solution.py:328
  566.7 16.5 %shard_map.320 = (f32[768,1024]{1,0:T(8,128)}, f32[2,768,1024]{2,1,0:T(8,128)}) custom-call(s32[1]{0:T(128)} %bitcast.8.where, f32[1,1]{1,0:T(1,128)} %bitcast.21.factor_ref, f32[768,1024]{1,0:T(8,128)S(1)} %copy-done.1, f32[2,768,1024]{2,1,0:T(8,128)} %moment_ref.7, bf16[4,768,128]{2,1,0:T(8,128)(2,1)} %pad_maximum_fusion.5.rest_0_, ...), custom_call_target="tpu_custom_call" | custom-call | flops 15728640 | bytes 20447232 | tf_op jit(solution)/shard_map/pallas_call | solution.py:328
  583.2 18.5 %shard_map.319 = (f32[256,6144]{1,0:T(8,128)}, f32[2,256,6144]{2,1,0:T(8,128)}) custom-call(s32[1]{0:T(128)} %bitcast.8.where, f32[1,1]{1,0:T(1,128)} %bitcast.21.factor_ref, f32[256,6144]{1,0:T(8,128)} %master_ref.6, f32[2,256,6144]{2,1,0:T(8,128)} %moment_ref.6, bf16[4,256,768]{2,1,0:T(8,128)(2,1)} %pad_maximum_fusion.1.rest_0_, ...), custom_call_target="tpu_custom_call" | custom-call | flops 31457280 | bytes 40894464 | tf_op jit(solution)/shard_map/pallas_call | solution.py:328
  606.1 13.6 %collective-permute-done.78.rest_1_ = bf16[4,256,512]{2,1,0:T(8,128)(2,1)S(1)} collective-permute-done((bf16[4,256,512]{2,1,0:T(8,128)(2,1)S(1)}, bf16[4,256,512]{2,1,0:T(8,128)(2,1)S(1)}, u32[]{:S(2)}, u32[]{:S(2)}) %collective-permute-start.78) | collective-permute-done | bytes 1048608 | tf_op jit(solution)/shard_map/ppermute | solution.py:60
  619.7 13.2 %shard_map.317 = (f32[256,4096]{1,0:T(8,128)}, f32[2,256,4096]{2,1,0:T(8,128)}) custom-call(s32[1]{0:T(128)} %bitcast.8.where, f32[1,1]{1,0:T(1,128)} %bitcast.21.factor_ref, f32[256,4096]{1,0:T(8,128)} %master_ref.4, f32[2,256,4096]{2,1,0:T(8,128)} %moment_ref.4, bf16[4,256,512]{2,1,0:T(8,128)(2,1)S(1)} %pad_maximum_fusion.2.rest_0_, ...), custom_call_target="tpu_custom_call" | custom-call | flops 20971520 | bytes 27262976 | tf_op jit(solution)/shard_map/pallas_call | solution.py:328
  (406 shorter events, 249.6 us)
Async XLA Ops:
  2.2 41.4 %collective-permute-start = (bf16[1,2,288]{2,1,0:T(2,128)(2,1)S(1)}, bf16[1,2,288]{2,1,0:T(2,128)(2,1)S(1)}, u32[]{:S(2)}, u32[]{:S(2)}) collective-permute-start(bf16[1,2,288]{2,1,0:T(2,128)(2,1)S(1)} %pad_maximum_fusion.24), channel_id=1, source_target_pairs={{0,2},{1,3},{2,0},{3,1},{4,6},{5,7},{6,4},{7,5},{8,10},{9,11},{10,... | collective-permute-start | bytes 3464 | tf_op jit(solution)/shard_map/ppermute | solution.py:60
  9.4 93.4 %collective-permute-start.13 = (bf16[512,1024]{1,0:T(8,128)(2,1)}, bf16[512,1024]{1,0:T(8,128)(2,1)}, u32[]{:S(2)}, u32[]{:S(2)}) collective-permute-start(bf16[512,1024]{1,0:T(8,128)(2,1)} %get-tuple-element.103), channel_id=1, source_target_pairs={{0,1},{1,0},{2,3},{3,2},{4,5},{5,4},{6,7},{7,6},{8,9},{9,8},{10,11... | collective-permute-start | bytes 3145736 | tf_op jit(solution)/shard_map/ppermute | solution.py:60
  15.4 189.3 %collective-permute-start.27 = (bf16[768,1024]{1,0:T(8,128)(2,1)}, bf16[768,1024]{1,0:T(8,128)(2,1)}, u32[]{:S(2)}, u32[]{:S(2)}) collective-permute-start(bf16[768,1024]{1,0:T(8,128)(2,1)} %get-tuple-element.99), channel_id=1, source_target_pairs={{0,1},{1,0},{2,3},{3,2},{4,5},{5,4},{6,7},{7,6},{8,9},{9,8},{10,11... | collective-permute-start | bytes 4718600 | tf_op jit(solution)/shard_map/ppermute | solution.py:60
  23.3 56.7 %collective-permute-start.6 = (bf16[256,4096]{1,0:T(8,128)(2,1)}, bf16[256,4096]{1,0:T(8,128)(2,1)}, u32[]{:S(2)}, u32[]{:S(2)}) collective-permute-start(bf16[256,4096]{1,0:T(8,128)(2,1)} %get-tuple-element.105), channel_id=1, source_target_pairs={{0,1},{1,0},{2,3},{3,2},{4,5},{5,4},{6,7},{7,6},{8,9},{9,8},{10,11... | collective-permute-start | bytes 6291464 | tf_op jit(solution)/shard_map/ppermute | solution.py:60
  25.6 22.9 %collective-permute-start.2 = (bf16[64,4096]{1,0:T(8,128)(2,1)}, bf16[64,4096]{1,0:T(8,128)(2,1)}, u32[]{:S(2)}, u32[]{:S(2)}) collective-permute-start(bf16[64,4096]{1,0:T(8,128)(2,1)} %get-tuple-element.147), channel_id=1, source_target_pairs={{0,2},{1,3},{2,0},{3,1},{4,6},{5,7},{6,4},{7,5},{8,10},{9,11},{10,... | collective-permute-start | bytes 1572872 | tf_op jit(solution)/shard_map/ppermute | solution.py:60
  77.8 90.4 %collective-permute-start.20 = (bf16[256,6144]{1,0:T(8,128)(2,1)S(1)}, bf16[256,6144]{1,0:T(8,128)(2,1)S(1)}, u32[]{:S(2)}, u32[]{:S(2)}) collective-permute-start(bf16[256,6144]{1,0:T(8,128)(2,1)S(1)} %copy-done.22), channel_id=1, source_target_pairs={{0,1},{1,0},{2,3},{3,2},{4,5},{5,4},{6,7},{7,6},{8,9},{9,8},{10,11... | collective-permute-start | bytes 9437192 | tf_op jit(solution)/shard_map/ppermute | solution.py:60
  101.6 22.8 %collective-permute-start.16 = (bf16[64,6144]{1,0:T(8,128)(2,1)S(1)}, bf16[64,6144]{1,0:T(8,128)(2,1)}, u32[]{:S(2)}, u32[]{:S(2)}) collective-permute-start(bf16[64,6144]{1,0:T(8,128)(2,1)S(1)} %copy-done.34), channel_id=1, source_target_pairs={{0,2},{1,3},{2,0},{3,1},{4,6},{5,7},{6,4},{7,5},{8,10},{9,11},{10,... | collective-permute-start | bytes 2359304 | tf_op jit(solution)/shard_map/ppermute | solution.py:60
  102.7 25.7 %collective-permute-start.15 = (bf16[256,1024]{1,0:T(8,128)(2,1)S(1)}, bf16[256,1024]{1,0:T(8,128)(2,1)S(1)}, u32[]{:S(2)}, u32[]{:S(2)}) collective-permute-start(bf16[256,1024]{1,0:T(8,128)(2,1)S(1)} %collective-permute-done.12), channel_id=1, source_target_pairs={{0,1},{1,0},{2,3},{3,2},{4,5},{5,4},{6,7},{7,6},{8,9},{9,8},{10,11... | collective-permute-start | bytes 1572872 | tf_op jit(solution)/shard_map/ppermute | solution.py:60
  124.4 20.2 %collective-permute-start.18 = (bf16[64,6144]{1,0:T(8,128)(2,1)}, bf16[64,6144]{1,0:T(8,128)(2,1)S(1)}, u32[]{:S(2)}, u32[]{:S(2)}) collective-permute-start(bf16[64,6144]{1,0:T(8,128)(2,1)} %get-tuple-element.53), channel_id=1, source_target_pairs={{0,2},{1,3},{2,0},{3,1},{4,6},{5,7},{6,4},{7,5},{8,10},{9,11},{10,... | collective-permute-start | bytes 2359304 | tf_op jit(solution)/shard_map/ppermute | solution.py:60
  126.2 44.6 %collective-permute-start.21 = (bf16[64,6144]{1,0:T(8,128)(2,1)}, bf16[64,6144]{1,0:T(8,128)(2,1)S(1)}, u32[]{:S(2)}, u32[]{:S(2)}) collective-permute-start(bf16[64,6144]{1,0:T(8,128)(2,1)} %collective-permute-done.16), channel_id=1, source_target_pairs={{0,1},{1,0},{2,3},{3,2},{4,5},{5,4},{6,7},{7,6},{8,9},{9,8},{10,11... | collective-permute-start | bytes 2359304 | tf_op jit(solution)/shard_map/ppermute | solution.py:60
  128.5 19.9 %collective-permute-start.17 = (bf16[64,6144]{1,0:T(8,128)(2,1)}, bf16[64,6144]{1,0:T(8,128)(2,1)S(1)}, u32[]{:S(2)}, u32[]{:S(2)}) collective-permute-start(bf16[64,6144]{1,0:T(8,128)(2,1)} %collective-permute-done.16), channel_id=1, source_target_pairs={{0,4},{4,0},{8,12},{12,8},{16,20},{20,16},{24,28},{28,24},{1,5},{5... | collective-permute-start | bytes 2359304 | tf_op jit(solution)/shard_map/ppermute | solution.py:60
  144.6 24.1 %collective-permute-start.25 = (bf16[384,1024]{1,0:T(8,128)(2,1)S(1)}, bf16[384,1024]{1,0:T(8,128)(2,1)S(1)}, u32[]{:S(2)}, u32[]{:S(2)}) collective-permute-start(bf16[384,1024]{1,0:T(8,128)(2,1)S(1)} %copy-done.33), channel_id=1, source_target_pairs={{0,2},{1,3},{2,0},{3,1},{4,6},{5,7},{6,4},{7,5},{8,10},{9,11},{10,... | collective-permute-start | bytes 2359304 | tf_op jit(solution)/shard_map/ppermute | solution.py:60
  168.7 38.7 %collective-permute-start.28 = (bf16[384,1024]{1,0:T(8,128)(2,1)S(1)}, bf16[384,1024]{1,0:T(8,128)(2,1)S(1)}, u32[]{:S(2)}, u32[]{:S(2)}) collective-permute-start(bf16[384,1024]{1,0:T(8,128)(2,1)S(1)} %collective-permute-done.25), channel_id=1, source_target_pairs={{0,1},{1,0},{2,3},{3,2},{4,5},{5,4},{6,7},{7,6},{8,9},{9,8},{10,11... | collective-permute-start | bytes 2359304 | tf_op jit(solution)/shard_map/ppermute | solution.py:60
  203.4 23.8 %collective-permute-start.30 = (bf16[2,768,1024]{2,1,0:T(8,128)(2,1)S(1)}, bf16[2,768,1024]{2,1,0:T(8,128)(2,1)S(1)}, u32[]{:S(2)}, u32[]{:S(2)}) collective-permute-start(bf16[2,768,1024]{2,1,0:T(8,128)(2,1)S(1)} %get-tuple-element.55), channel_id=1, source_target_pairs={{0,1},{1,0},{2,3},{3,2},{4,5},{5,4},{6,7},{7,6},{8,9},{9,8},{10,11... | collective-permute-start | bytes 9437192 | tf_op jit(solution)/shard_map/ppermute | solution.py:60
  245.0 50.3 %collective-permute-start.31 = (bf16[2,256,6144]{2,1,0:T(8,128)(2,1)}, bf16[2,256,6144]{2,1,0:T(8,128)(2,1)}, u32[]{:S(2)}, u32[]{:S(2)}) collective-permute-start(bf16[2,256,6144]{2,1,0:T(8,128)(2,1)} %get-tuple-element.59), channel_id=1, source_target_pairs={{0,1},{1,0},{2,3},{3,2},{4,5},{5,4},{6,7},{7,6},{8,9},{9,8},{10,11... | collective-permute-start | bytes 18874376 | tf_op jit(solution)/shard_map/ppermute | solution.py:60
  245.2 20.1 %collective-permute-start.32 = (bf16[1,384,1024]{2,1,0:T(8,128)(2,1)}, bf16[1,384,1024]{2,1,0:T(8,128)(2,1)}, u32[]{:S(2)}, u32[]{:S(2)}) collective-permute-start(bf16[1,384,1024]{2,1,0:T(8,128)(2,1)} %add_convert_fusion.8), channel_id=1, source_target_pairs={{0,2},{1,3},{2,0},{3,1},{4,6},{5,7},{6,4},{7,5},{8,10},{9,11},{10,... | collective-permute-start | bytes 2359304 | tf_op jit(solution)/shard_map/ppermute | solution.py:60
  319.8 53.4 %collective-permute-start.52 = (bf16[1,128,6144]{2,1,0:T(8,128)(2,1)}, bf16[1,128,6144]{2,1,0:T(8,128)(2,1)}, u32[]{:S(2)}, u32[]{:S(2)}) collective-permute-start(bf16[1,128,6144]{2,1,0:T(8,128)(2,1)} %add_convert_fusion.1), channel_id=1, source_target_pairs={{0,2},{1,3},{2,0},{3,1},{4,6},{5,7},{6,4},{7,5},{8,10},{9,11},{10,... | collective-permute-start | bytes 4718600 | tf_op jit(solution)/shard_map/ppermute | solution.py:60
  320.5 52.6 %collective-permute-start.56 = (bf16[2,128,3072]{2,1,0:T(8,128)(2,1)}, bf16[2,128,3072]{2,1,0:T(8,128)(2,1)}, u32[]{:S(2)}, u32[]{:S(2)}) collective-permute-start(bf16[2,128,3072]{2,1,0:T(8,128)(2,1)} %add_convert_fusion), channel_id=1, source_target_pairs={{0,4},{4,0},{8,12},{12,8},{16,20},{20,16},{24,28},{28,24},{1,5},{5... | collective-permute-start | bytes 4718600 | tf_op jit(solution)/shard_map/ppermute | solution.py:60
  369.7 42.2 %collective-permute-start.35 = (bf16[2,256,4096]{2,1,0:T(8,128)(2,1)S(1)}, bf16[2,256,4096]{2,1,0:T(8,128)(2,1)S(1)}, u32[]{:S(2)}, u32[]{:S(2)}) collective-permute-start(bf16[2,256,4096]{2,1,0:T(8,128)(2,1)S(1)} %get-tuple-element.68), channel_id=1, source_target_pairs={{0,1},{1,0},{2,3},{3,2},{4,5},{5,4},{6,7},{7,6},{8,9},{9,8},{10,11... | collective-permute-start | bytes 12582920 | tf_op jit(solution)/shard_map/ppermute | solution.py:60
  377.3 20.4 %collective-permute-start.57 = (bf16[1,128,3072]{2,1,0:T(8,128)(2,1)S(1)}, bf16[1,128,3072]{2,1,0:T(8,128)(2,1)S(1)}, u32[]{:S(2)}, u32[]{:S(2)}) collective-permute-start(bf16[1,128,3072]{2,1,0:T(8,128)(2,1)S(1)} %get-tuple-element.116), channel_id=1, source_target_pairs={{0,2},{1,3},{2,0},{3,1},{4,6},{5,7},{6,4},{7,5},{8,10},{9,11},{10,... | collective-permute-start | bytes 2359304 | tf_op jit(solution)/shard_map/ppermute | solution.py:60
  389.5 24.5 %collective-permute-start.86 = (bf16[2,768,128]{2,1,0:T(8,128)(2,1)S(1)}, bf16[2,768,128]{2,1,0:T(8,128)(2,1)S(1)}, u32[]{:S(2)}, u32[]{:S(2)}) collective-permute-start(bf16[2,768,128]{2,1,0:T(8,128)(2,1)S(1)} %pad_maximum_fusion.11), channel_id=1, source_target_pairs={{0,8},{4,12},{8,0},{12,4},{16,24},{20,28},{24,16},{28,20},{1,9},{5... | collective-permute-start | bytes 1179656 | tf_op jit(solution)/shard_map/ppermute | solution.py:60
  414.0 27.0 %collective-permute-start.36 = (bf16[1,128,4096]{2,1,0:T(8,128)(2,1)S(1)}, bf16[1,128,4096]{2,1,0:T(8,128)(2,1)S(1)}, u32[]{:S(2)}, u32[]{:S(2)}) collective-permute-start(bf16[1,128,4096]{2,1,0:T(8,128)(2,1)S(1)} %add_convert_fusion.3), channel_id=1, source_target_pairs={{0,2},{1,3},{2,0},{3,1},{4,6},{5,7},{6,4},{7,5},{8,10},{9,11},{10,... | collective-permute-start | bytes 3145736 | tf_op jit(solution)/shard_map/ppermute | solution.py:60
  414.7 27.1 %collective-permute-start.40 = (bf16[2,128,2048]{2,1,0:T(8,128)(2,1)S(1)}, bf16[2,128,2048]{2,1,0:T(8,128)(2,1)S(1)}, u32[]{:S(2)}, u32[]{:S(2)}) collective-permute-start(bf16[2,128,2048]{2,1,0:T(8,128)(2,1)S(1)} %add_convert_fusion.2), channel_id=1, source_target_pairs={{0,4},{4,0},{8,12},{12,8},{16,20},{20,16},{24,28},{28,24},{1,5},{5... | collective-permute-start | bytes 3145736 | tf_op jit(solution)/shard_map/ppermute | solution.py:60
  421.8 55.9 %collective-permute-start.68 = (f32[2,1152]{1,0:T(2,128)S(1)}, f32[2,1152]{1,0:T(2,128)S(1)}, u32[]{:S(2)}, u32[]{:S(2)}) collective-permute-start(f32[2,1152]{1,0:T(2,128)S(1)} %add.935), channel_id=1, source_target_pairs={{0,4},{4,0},{8,12},{12,8},{16,20},{20,16},{24,28},{28,24},{1,5},{5... | collective-permute-start | bytes 27656 | tf_op jit(solution)/shard_map/ppermute | solution.py:60
  473.2 27.1 %collective-permute-start.83 = (bf16[2,256,768]{2,1,0:T(8,128)(2,1)S(1)}, bf16[2,256,768]{2,1,0:T(8,128)(2,1)S(1)}, u32[]{:S(2)}, u32[]{:S(2)}) collective-permute-start(bf16[2,256,768]{2,1,0:T(8,128)(2,1)S(1)} %pad_maximum_fusion.4), channel_id=1, source_target_pairs={{0,8},{4,12},{8,0},{12,4},{16,24},{20,28},{24,16},{28,20},{1,9},{5... | collective-permute-start | bytes 2359304 | tf_op jit(solution)/shard_map/ppermute | solution.py:60
  473.2 26.3 %collective-permute-start.42 = (bf16[1,128,1024]{2,1,0:T(8,128)(2,1)S(1)}, bf16[1,128,1024]{2,1,0:T(8,128)(2,1)S(1)}, u32[]{:S(2)}, u32[]{:S(2)}) collective-permute-start(bf16[1,128,1024]{2,1,0:T(8,128)(2,1)S(1)} %get-tuple-element.123), channel_id=1, source_target_pairs={{0,8},{4,12},{8,0},{12,4},{16,24},{20,28},{24,16},{28,20},{1,9},{5... | collective-permute-start | bytes 786440 | tf_op jit(solution)/shard_map/ppermute | solution.py:60
  476.8 22.7 %collective-permute-start.39 = (bf16[1,128,512]{2,1,0:T(8,128)(2,1)S(1)}, bf16[1,128,512]{2,1,0:T(8,128)(2,1)S(1)}, u32[]{:S(2)}, u32[]{:S(2)}) collective-permute-start(bf16[1,128,512]{2,1,0:T(8,128)(2,1)S(1)} %add_convert_fusion.28), channel_id=1, source_target_pairs={{0,16},{4,20},{8,24},{12,28},{16,0},{20,4},{24,8},{28,12},{1,17},{... | collective-permute-start | bytes 393224 | tf_op jit(solution)/shard_map/ppermute | solution.py:60
  477.8 88.9 %collective-permute-start.87 = (bf16[4,768,128]{2,1,0:T(8,128)(2,1)}, bf16[4,768,128]{2,1,0:T(8,128)(2,1)}, u32[]{:S(2)}, u32[]{:S(2)}) collective-permute-start(bf16[4,768,128]{2,1,0:T(8,128)(2,1)} %pad_maximum_fusion.5.rest_0_), channel_id=1, source_target_pairs={{0,4},{4,0},{8,12},{12,8},{16,20},{20,16},{24,28},{28,24},{1,5},{5... | collective-permute-start | bytes 2359304 | tf_op jit(solution)/shard_map/ppermute | solution.py:60
  478.8 35.3 %collective-permute-start.69 = (f32[2,1152]{1,0:T(2,128)S(1)}, f32[2,1152]{1,0:T(2,128)S(1)}, u32[]{:S(2)}, u32[]{:S(2)}) collective-permute-start(f32[2,1152]{1,0:T(2,128)S(1)} %add.936), channel_id=1, source_target_pairs={{0,8},{4,12},{8,0},{12,4},{16,24},{20,28},{24,16},{28,20},{1,9},{5... | collective-permute-start | bytes 27656 | tf_op jit(solution)/shard_map/ppermute | solution.py:60
  501.5 81.7 %collective-permute-start.84 = (bf16[4,256,768]{2,1,0:T(8,128)(2,1)}, bf16[4,256,768]{2,1,0:T(8,128)(2,1)}, u32[]{:S(2)}, u32[]{:S(2)}) collective-permute-start(bf16[4,256,768]{2,1,0:T(8,128)(2,1)} %pad_maximum_fusion.1.rest_0_), channel_id=1, source_target_pairs={{0,4},{4,0},{8,12},{12,8},{16,20},{20,16},{24,28},{28,24},{1,5},{5... | collective-permute-start | bytes 4718600 | tf_op jit(solution)/shard_map/ppermute | solution.py:60
  517.0 38.0 %collective-permute-start.81 = (bf16[4,512,128]{2,1,0:T(8,128)(2,1)S(1)}, bf16[4,512,128]{2,1,0:T(8,128)(2,1)S(1)}, u32[]{:S(2)}, u32[]{:S(2)}) collective-permute-start(bf16[4,512,128]{2,1,0:T(8,128)(2,1)S(1)} %pad_maximum_fusion.8.rest_0_), channel_id=1, source_target_pairs={{0,4},{4,0},{8,12},{12,8},{16,20},{20,16},{24,28},{28,24},{1,5},{5... | collective-permute-start | bytes 1572872 | tf_op jit(solution)/shard_map/ppermute | solution.py:60
  521.7 80.0 %collective-permute-start.77 = (bf16[2,256,512]{2,1,0:T(8,128)(2,1)}, bf16[2,256,512]{2,1,0:T(8,128)(2,1)}, u32[]{:S(2)}, u32[]{:S(2)}) collective-permute-start(bf16[2,256,512]{2,1,0:T(8,128)(2,1)} %pad_maximum_fusion.7), channel_id=1, source_target_pairs={{0,8},{4,12},{8,0},{12,4},{16,24},{20,28},{24,16},{28,20},{1,9},{5... | collective-permute-start | bytes 1572872 | tf_op jit(solution)/shard_map/ppermute | solution.py:60
  (111 other events, 2034.8 us)

commit v3 on v2

--- a/solution.py
+++ b/solution.py
@@ -6,6 +6,7 @@
 from jax.experimental import pallas as pl
 from jax.experimental.pallas import tpu as pltpu
 from jax.sharding import PartitionSpec as P
+
 
 HQ = 16
 HK = 8
@@ -68,31 +69,35 @@
     return lax.optimization_barrier((value, others))[0]
 
 
-def gather_rows(shard, chunks, previous):
+def gather_rows(shard, previous):
     owners = lax.axis_size("group")
     copies = lax.axis_size("dp")
     mine = lax.axis_index("group")
+    here = lax.axis_index("dp")
+    if previous is not None:
+        shard = after(shard, previous)
+    shard = shard.astype(jnp.bfloat16)
     rows, columns = shard.shape
-    half = rows // 2
-    side = lax.axis_index("dp") & 1
-    split = copies > 1
     pieces = [(shard, 0, 0)]
-    order = previous
-    for mask in bit_masks(owners)[1:]:
-        if mask == 2 and split:
-            size = half // chunks
-            for c in range(chunks):
-                near_at = side * half + c * size
-                far_at = (1 - side) * half + c * size
-                near = lax.dynamic_slice_in_dim(shard, near_at, size, 0)
-                if order is not None:
-                    near = after(near, order)
-                order = swap(near, "group", mask)
-                pieces += [
-                    (order, mask, near_at),
-                    (swap(order, "dp", 1), mask, far_at),
-                ]
-        else:
+    order = shard
+    if owners == 4 and copies % 4 == 0 and rows % 128 == 0:
+        quarter, half = rows // 4, rows // 8
+        place = (here & 1) * 2 + ((here >> 1) & 1)
+        order = swap(
+            lax.dynamic_slice_in_dim(shard, place * quarter, quarter, 0), "group", 2
+        )
+        by_one = swap(order, "dp", 1)
+        by_two = swap(order, "dp", 2)
+        last = (place ^ 3) * quarter
+        pieces += [
+            (order, 2, place * quarter),
+            (by_one, 2, (place ^ 2) * quarter),
+            (by_two, 2, (place ^ 1) * quarter),
+            (swap(by_two[:half], "dp", 1), 2, last),
+            (swap(by_one[half:], "dp", 2), 2, last + half),
+        ]
+    else:
+        for mask in bit_masks(owners)[1:]:
             pieces += [(swap(v, "group", mask), dg ^ mask, off) for v, dg, off in pieces]
     pieces += [(swap(v, "group", 1), dg ^ 1, off) for v, dg, off in pieces]
     full = jnp.zeros((rows * owners, columns), shard.dtype)
@@ -118,10 +123,62 @@
 
 
 def sum_all(value):
-    for axis in ("group", "dp"):
-        for mask in bit_masks(lax.axis_size(axis)):
-            value = value + swap(value, axis, mask)
-    return value
+    owners = lax.axis_size("group")
+    copies = lax.axis_size("dp")
+    mesh_type = pl.DeviceIdType.MESH
+
+    def body(in_ref, out_ref, near, near_sum, far, near_send, near_recv, far_send, far_recv):
+        mine = lax.axis_index("group")
+        here = lax.axis_index("dp")
+        near_peers = [(here, mine ^ k) for k in range(1, owners)]
+        far_peers = [(here ^ k, mine) for k in range(1, copies)]
+        barrier = pltpu.get_barrier_semaphore()
+        for peer in near_peers + far_peers:
+            pl.semaphore_signal(barrier, inc=1, device_id=peer, device_id_type=mesh_type)
+        pl.semaphore_wait(barrier, len(near_peers) + len(far_peers))
+
+        def exchange(source, slots, index, peers, sends, recvs):
+            slots[index] = source[...]
+            copies_out = [
+                pltpu.make_async_remote_copy(
+                    src_ref=source,
+                    dst_ref=slots.at[index],
+                    send_sem=sends.at[k],
+                    recv_sem=recvs.at[k],
+                    device_id=peer,
+                    device_id_type=mesh_type,
+                )
+                for k, peer in enumerate(peers)
+            ]
+            for copy in copies_out:
+                copy.start()
+            for copy in copies_out:
+                copy.wait()
+            total = slots[0]
+            for k in range(1, len(peers) + 1):
+                total = total + slots[k]
+            return total
+
+        near_sum[...] = exchange(in_ref, near, mine, near_peers, near_send, near_recv)
+        out_ref[...] = exchange(near_sum, far, here, far_peers, far_send, far_recv)
+
+    shape = value.shape
+    return pl.pallas_call(
+        body,
+        out_shape=jax.ShapeDtypeStruct(shape, jnp.float32),
+        in_specs=[pl.BlockSpec(memory_space=pltpu.VMEM)],
+        out_specs=pl.BlockSpec(memory_space=pltpu.VMEM),
+        scratch_shapes=[
+            pltpu.VMEM((owners,) + shape, jnp.float32),
+            pltpu.VMEM(shape, jnp.float32),
+            pltpu.VMEM((copies,) + shape, jnp.float32),
+            pltpu.SemaphoreType.DMA((owners - 1,)),
+            pltpu.SemaphoreType.DMA((owners - 1,)),
+            pltpu.SemaphoreType.DMA((copies - 1,)),
+            pltpu.SemaphoreType.DMA((copies - 1,)),
+        ],
+        compiler_params=pltpu.CompilerParams(collective_id=0, has_side_effects=True),
+    )(value)
 
 
 def spread_bits(position, masks):
@@ -221,7 +278,7 @@
 
 
 class GradSum:
-    def __init__(self, left, right):
+    def __init__(self, left, right, split):
         blocks = grad_blocks(left, right)
         self.blocks = blocks
         group = [("group", m) for m in bit_masks(lax.axis_size("group"))]
@@ -230,18 +287,24 @@
         if group:
             held.append(swap(blocks[0], "group", 1))
         rest = group[1:]
-        self.orders = [rest + other, other[:1] + rest + other[1:]]
-        half = blocks[-1].shape[1] // 2
-        self.parts = [
-            [v[:, i * half : (i + 1) * half] for v in held] for i in range(2)
-        ]
+        self.orders = [rest + other]
+        if split:
+            self.orders.append(other[:1] + rest + other[1:])
+        count = len(self.orders)
+        size = blocks[-1].shape[1] // count
+        self.parts = [[v[:, i * size : (i + 1) * size] for v in held] for i in range(count)]
+        self.common = len(rest) + 1
         self.length = len(rest) + len(other)
         self.step = 0
+
+    def hold(self, *others):
+        self.parts = [[after(v, *others) for v in part] for part in self.parts]
 
     def advance(self):
         sent = []
         if self.step == self.length:
             return sent
+        exchange = []
         for i, order in enumerate(self.orders):
             axis, mask = order[self.step]
             dim = 0 if axis == "group" else 2
@@ -250,9 +313,19 @@
                 lax.slice_in_dim(v, size, 2 * size, axis=dim).astype(jnp.float32)
                 for v in self.parts[i]
             ).astype(jnp.bfloat16)
-            stay = [lax.slice_in_dim(v, 0, size, axis=dim) for v in self.parts[i]]
-            self.parts[i] = stay + [swap(away, axis, mask)]
+            self.parts[i] = [lax.slice_in_dim(v, 0, size, axis=dim) for v in self.parts[i]]
+            exchange.append((away, axis, mask))
+        if self.step >= self.common:
+            rows = exchange[0][0].shape[1]
+            away = jnp.concatenate([v for v, _, _ in exchange], axis=1)
+            got = swap(away, *exchange[0][1:])
+            for i, part in enumerate(self.parts):
+                part.append(got[:, i * rows : (i + 1) * rows])
             sent.append(away)
+        else:
+            for i, (away, axis, mask) in enumerate(exchange):
+                self.parts[i].append(swap(away, axis, mask))
+                sent.append(away)
         self.step += 1
         return sent
 
@@ -284,8 +357,8 @@
 def adam_core(master, first_moment, second_moment, clipped, step_rate, decay_rate):
     first_new = BETA_ONE * first_moment + (1.0 - BETA_ONE) * clipped
     second_new = BETA_TWO * second_moment + (1.0 - BETA_TWO) * clipped * clipped
-    first_hat = first_new / (1.0 - BETA_ONE**STEP_COUNT)
-    second_hat = second_new / (1.0 - BETA_TWO**STEP_COUNT)
+    first_hat = first_new * (1.0 / (1.0 - BETA_ONE**STEP_COUNT))
+    second_hat = second_new * (1.0 / (1.0 - BETA_TWO**STEP_COUNT))
     renewed = master - step_rate * (
         first_hat / (jnp.sqrt(second_hat) + ADAM_EPS) + decay_rate * master
     )
@@ -305,7 +378,9 @@
                     full, value[k].astype(jnp.float32), (0, (here ^ dd) * width)
                 )
         return adam_update(master, moment, full, factor, step_rate, decay_rate)
-    tile = 32
+    tile = rows
+    while tile % 32 == 0 and tile * columns > 256 * 1024:
+        tile //= 2
 
     def body(where, factor_ref, master_ref, moment_ref, *rest):
         grads, (new_ref, state_ref) = rest[:-2], rest[-2:]
@@ -588,10 +663,9 @@
     gains_all = gather_small(gains_low).reshape(2, owners, -1)
     full_norm = gains_all[:, :, :width].reshape(2, -1)
     full_head = gains_all[:, :, width:].reshape(2, -1)
-    full_qkv, order = gather_rows(qkv_weight.astype(jnp.bfloat16), 2, None)
-    full_out, order = gather_rows(out_weight.astype(jnp.bfloat16), 1, order)
-    full_gate_up, order = gather_rows(gate_up_weight.astype(jnp.bfloat16), 2, order)
-    full_down, order = gather_rows(down_weight.astype(jnp.bfloat16), 1, order)
+    full_qkv, order = gather_rows(qkv_weight, None)
+    full_out, order = gather_rows(out_weight, order)
+    full_gate_up, order = gather_rows(gate_up_weight, order)
     gain_one = full_norm[0].astype(jnp.float32)
     gain_two = full_norm[1].astype(jnp.float32)
     head_gain = full_head.astype(jnp.float32)
@@ -600,6 +674,7 @@
     normed_one = inputs * root_one
     hidden_one = (normed_one * gain_one).astype(jnp.bfloat16)
     projected = jnp.dot(hidden_one, full_qkv, preferred_element_type=jnp.float32)
+    full_down, _ = gather_rows(down_weight, (order, projected))
     tables = rotary_tables(positions, HD)
     mixed_low = attention_call(attend_body, projected, tables, segment_ids, head_gain, None)
     attended = jnp.dot(mixed_low, full_out, preferred_element_type=jnp.float32)
@@ -615,47 +690,65 @@
     branch = jnp.dot(activated, full_down, preferred_element_type=jnp.float32)
     output = (residual + branch).astype(jnp.bfloat16)
     upstream = cotangent.astype(jnp.float32)
-    down_sum = GradSum(activated, cotangent)
+    down_sum = GradSum(activated, cotangent, False)
     grad_act = contract_cols(after(cotangent, *down_sum.blocks), full_down)
     grad_gate = grad_act * upward * sigmoid_gate * (1.0 + gate_part * (1.0 - sigmoid_gate))
     grad_up = grad_act * gate_part * sigmoid_gate
     grad_gate_up = jnp.concatenate([grad_gate, grad_up], axis=-1).astype(jnp.bfloat16)
-    gate_up_sum = GradSum(hidden_two, after(grad_gate_up, *down_sum.advance()))
+    gate_up_sum = GradSum(hidden_two, after(grad_gate_up, *down_sum.advance()), True)
     grad_hidden_two = contract_cols(after(grad_gate_up, *gate_up_sum.blocks), full_gate_up)
     grad_gain_two = jnp.sum(grad_hidden_two * normed_two, axis=0)
     grad_residual = upstream + norm_back(grad_hidden_two, normed_two, root_two, gain_two)
     residual_low = grad_residual.astype(jnp.bfloat16)
-    out_sum = GradSum(mixed_low, after(residual_low, *gate_up_sum.advance()))
+    out_sum = GradSum(mixed_low, after(residual_low, *gate_up_sum.advance()), False)
     grad_mixed = contract_cols(after(residual_low, *out_sum.blocks), full_out).astype(
         jnp.bfloat16
     )
+    down_sum.hold(out_sum.blocks)
     grad_mixed = after(grad_mixed, *down_sum.advance(), *out_sum.advance())
     grad_projected, grad_gain_head = attention_call(
         attend_back_body, projected, tables, segment_ids, head_gain, grad_mixed
     )
-    qkv_sum = GradSum(hidden_one, grad_projected)
-    grad_hidden_one = contract_cols(after(grad_projected, *qkv_sum.blocks), full_qkv)
+    gate_up_sum.hold(grad_projected)
+    down_sum.hold(grad_projected)
+    sent = gate_up_sum.advance() + down_sum.advance()
+    qkv_sum = GradSum(hidden_one, after(grad_projected, *sent), True)
+    sent = qkv_sum.advance()
+    out_sum.hold(sent)
+    gate_up_sum.hold(sent)
+    sent = sent + out_sum.advance()
+    grad_hidden_one = contract_cols(after(grad_projected, *qkv_sum.blocks, *sent), full_qkv)
     grad_gain_one = jnp.sum(grad_hidden_one * normed_one, axis=0)
     grad_inputs = grad_residual + norm_back(grad_hidden_one, normed_one, root_one, gain_one)
     tokens_grad = grad_inputs.astype(jnp.bfloat16)
+    down_sum.hold(sent)
     small = jnp.concatenate(
         [jnp.stack([grad_gain_one, grad_gain_two]), grad_gain_head],
         axis=1,
     )
-    small = sum_all(small)
+    sent = qkv_sum.advance()
+    owned = tuple(v.finish() for v in (qkv_sum, out_sum, gate_up_sum, down_sum))
+    local = sum(jnp.sum(v * v) for v in owned)
+    summed = sum_all(
+        jnp.concatenate(
+            [small, jnp.full((6, small.shape[1]), local, jnp.float32)], axis=0
+        )
+    )
+    small = summed[:2]
     norm_total = small[:, :-HD]
     head_total = small[:, -HD:]
-    owned = tuple(v.finish() for v in (qkv_sum, out_sum, gate_up_sum, down_sum))
-    squares = sum_all(sum(jnp.sum(v * v) for v in owned).reshape(1, 1))[0, 0]
-    squares = squares + jnp.sum(small * small)
+    squares = summed[2, 0] + jnp.sum(small * small)
     clip_limit = math.sqrt(PARAMS)
     factor = clip_limit / jnp.maximum(jnp.sqrt(squares), clip_limit)
-    gathered = [gather_grad(v) for v in owned]
+    gathered = [gather_grad(after(v, *sent)) for v in owned]
     masters = (qkv_weight, out_weight, gate_up_weight, down_weight)
     moments = (qkv_moments, out_moments, gate_up_moments, down_moments)
+    later = after(factor, gathered[0][0][0])
     renewed = [
-        adam_blocks(master, moment, blocks, factor, LEARN_RATE, WEIGHT_DECAY)
-        for master, moment, blocks in zip(masters, moments, gathered)
+        adam_blocks(master, moment, blocks, scale, LEARN_RATE, WEIGHT_DECAY)
+        for master, moment, blocks, scale in zip(
+            masters, moments, gathered, (later, factor, later, later)
+        )
     ]
     mine = lax.axis_index("group")
     norm_grad = lax.dynamic_slice_in_dim(

time: 641 us -> 693 us (1.081)
  Pallas kernels: 148 us -> 182 us
  local copies, waits for them, and re-layouts: 64.8 us -> 88.9 us
  other arithmetic: 76.5 us -> 85.6 us
  starting transfers between devices: 90.3 us -> 81.3 us
    pallas_call x0 -> x1, Pallas kernels: none -> 49.7 us  [sum_all(): pl.pallas_call(body, out_shape=jax.ShapeDtypeStruct(shape, jnp.float32),...]
    slice x0 -> x30, local copies, waits for them, and re-layouts: none -> 22 us  [the longest x21 18.4 us: advance(): lax.slice_in_dim(v, 0, size, axis=dim)]
    pallas_call x4, Pallas kernels: 59.7 us -> 43.3 us  [adam_blocks(): pl.pallas_call(body, out_shape=[jax.ShapeDtypeStruct(master.shape, jnp.fl...]
    ppermute x88 -> x82, starting transfers between devices: 90.3 us -> 81.3 us  [swap(): return lax.ppermute(value, axis, [(i, i ^ mask) for i in range(count)])]
    convert_element_type x20, other arithmetic: 27.5 us -> 36.2 us  [advance(): away = sum((lax.slice_in_dim(v, size, 2 * size, axis=dim).astype(jnp.floa...]
    dynamic_update_slice x28 -> x44, local copies, waits for them, and re-layouts: 35.5 us -> 41.8 us  [gather_rows(): full = lax.dynamic_update_slice(full, value, (start, 0))]
    ppermute x88 -> x82, waiting for transfers between devices: 174 us -> 170 us  [swap(): return lax.ppermute(value, axis, [(i, i ^ mask) for i in range(count)])]
  transfers between devices with their start and end apart: 88 -> 82, of which waited for: 34 -> 21; matrix products, arithmetic and copies ran while one was open for 31% -> 34% of each run, Pallas kernels for 19% -> 22%
where the time goes in v3:
time: 693 us; the launch traced here: 688 us
  Pallas kernels  182 us (26%)
  waiting for transfers between devices  170 us (25%)
  local copies, waits for them, and re-layouts  88.9 us (13%)
  other arithmetic  85.6 us (12%)
  starting transfers between devices  81.3 us (12%)
  matrix products  73.4 us (11%)
    ppermute x82, waiting for transfers between devices, swap(): return lax.ppermute(value, axis, [(i, i ^ mask) for i in range(count)])  170 us
    ppermute x82, starting transfers between devices, swap(): return lax.ppermute(value, axis, [(i, i ^ mask) for i in range(count)])  81.3 us
    pallas_call x2, Pallas kernels, attention_call(): pl.pallas_call(body, grid=(seq_count, HK), in_specs=in_specs, out_specs=o...  50 us
    pallas_call x1, Pallas kernels, sum_all(): pl.pallas_call(body, out_shape=jax.ShapeDtypeStruct(shape, jnp.float32),...  49.7 us
    pallas_call x4, Pallas kernels, adam_blocks(): pl.pallas_call(body, out_shape=[jax.ShapeDtypeStruct(master.shape, jnp.fl...  43.3 us
    dynamic_update_slice x44, local copies, waits for them, and re-layouts, gather_rows(): full = lax.dynamic_update_slice(full, value, (start, 0))  41.8 us
    dot_general x4, matrix products, contract_cols(): lax.dot_general(left_side, right_side, (((1,), (1,)), ((), ())), preferre...  39.7 us
    pallas_call x4, Pallas kernels, grad_blocks(): pl.pallas_call(body, out_shape=[jax.ShapeDtypeStruct((len(row_set), row_b...  38.7 us
  transfers between devices with their start and end apart: 82, of which 21 were waited for; matrix products, arithmetic and copies ran while one was open for 34% of the time, Pallas kernels for 22%

profile of v3, /device:TPU:0, one launch (start us, length us, event | category | flops | bytes accessed | tf_op | source)
XLA Modules:
  0.0 687.8 jit_solution(13533178539690489)
XLA Ops:
  19.8 8.8 %collective-permute-done.2 = bf16[64,4096]{1,0:T(8,128)(2,1)S(1)} collective-permute-done((bf16[64,4096]{1,0:T(8,128)(2,1)}, bf16[64,4096]{1,0:T(8,128)(2,1)S(1)}, u32[]{:S(2)}, u32[]{:S(2)}) %collective-permute-start.2) | collective-permute-done | bytes 524320 | tf_op jit(solution)/shard_map/ppermute | solution.py:61
  40.3 6.3 broadcast_in_dim.52
  46.6 6.3 constant_dynamic-update-slice_fusion.23
  73.6 7.3 %collective-permute-done.6 = bf16[32,4096]{1,0:T(8,128)(2,1)S(1)} collective-permute-done((bf16[32,4096]{1,0:T(8,128)(2,1)S(1)}, bf16[32,4096]{1,0:T(8,128)(2,1)S(1)}, u32[]{:S(2)}, u32[]{:S(2)}) %collective-permute-start.6) | collective-permute-done | bytes 262176 | tf_op jit(solution)/shard_map/ppermute | solution.py:61
  81.6 9.7 %collective-permute-done.24 = bf16[64,6144]{1,0:T(8,128)(2,1)} collective-permute-done((bf16[64,6144]{1,0:T(8,128)(2,1)S(1)}, bf16[64,6144]{1,0:T(8,128)(2,1)}, u32[]{:S(2)}, u32[]{:S(2)}) %collective-permute-start.24) | collective-permute-done | bytes 786464 | tf_op jit(solution)/shard_map/ppermute | solution.py:61
  112.1 10.1 %fusion.20.query_ref.key_ref.value_ref = f32[512,4096]{1,0:T(8,128)} fusion(bf16[512,1024]{1,0:T(8,128)(2,1)S(1)} %fusion.4.left_ref, bf16[1024,4096]{1,0:T(8,128)(2,1)} %constant_dynamic-update-slice_fusion.36), kind=kOutput, calls=%fused_computation.171 | convolution fusion | flops 4294967296 | bytes 17825792 | tf_op jit(solution)/shard_map/dot_general | solution.py:676
  128.2 18.9 %shard_map.311.left_ref = bf16[512,2048]{1,0:T(8,128)(2,1)S(1)} custom-call(f32[512,4096]{1,0:T(8,128)} %fusion.20.query_ref.key_ref.value_ref, f32[512,4096]{1,0:T(8,128)} %fusion.20.query_ref.key_ref.value_ref, f32[512,4096]{1,0:T(8,128)} %fusion.20.query_ref.key_ref.value_ref, f32[512,128]{1,0:T(8,128)S(1)} %get-tuple-element.199.cos_ref, ...), custom_call_target="tpu_custom_call" | custom-call | flops 4294967296 | bytes 12582912 | tf_op jit(solution)/shard_map/pallas_call | solution.py:627
  168.5 6.5 collective-permute-done.37
  192.1 9.4 %fusion.21 = f32[512,6144]{1,0:T(8,128)} fusion(bf16[512,1024]{1,0:T(8,128)(2,1)S(1)} %multiply_convert_fusion.3.left_ref, bf16[1024,6144]{1,0:T(8,128)(2,1)S(1)} %constant_dynamic-update-slice_fusion.12), kind=kOutput, calls=%fused_computation.172 | convolution fusion | flops 6442450944 | bytes 26214400 | tf_op jit(solution)/shard_map/dot_general | solution.py:685
  201.5 6.8 multiply_convert_fusion.2.left_ref
  208.3 8.9 %shard_map.312 = (bf16[2,768,1024]{2,1,0:T(8,128)(2,1)S(1)}, bf16[2,768,1024]{2,1,0:T(8,128)(2,1)}) custom-call(s32[2]{0:T(128)S(1)} %pad_add_fusion.where, bf16[512,3072]{1,0:T(8,128)(2,1)} %multiply_convert_fusion.2.left_ref, bf16[512,1024]{1,0:T(8,128)(2,1)S(1)} %copy-done.3, bf16[512,1024]{1,0:T(8,128)(2,1)S(1)} %copy-done.3), custom_call_target="tpu_custom_call" | custom-call | flops 3221225472 | bytes 10485760 | tf_op jit(solution)/shard_map/pallas_call | solution.py:252
  224.0 12.2 %multiply_convert_fusion.1 = (bf16[512,3072]{1,0:T(8,128)(2,1)}, bf16[512,3072]{1,0:T(8,128)(2,1)}) fusion(f32[512,6144]{1,0:T(8,128)} %fusion.21, bf16[512,1024]{1,0:T(8,128)(2,1)S(1)} %copy-done.3, bf16[3072,1024]{1,0:T(8,128)(2,1)} %constant_dynamic-update-slice_fusion), kind=kOutput, calls=%fused_computation.2 | convolution fusion | flops 3241672704 | bytes 26214400 | tf_op jit(solution)/shard_map/dot_general | solution.py:49
  236.2 6.2 pad_maximum_fusion.rest_0_
  246.8 12.5 %shard_map.313 = (bf16[2,256,6144]{2,1,0:T(8,128)(2,1)}, bf16[2,256,6144]{2,1,0:T(8,128)(2,1)}) custom-call(s32[2]{0:T(128)S(1)} %pad_add_fusion.where, bf16[512,1024]{1,0:T(8,128)(2,1)S(1)} %multiply_convert_fusion.3.left_ref, bf16[512,6144]{1,0:T(8,128)(2,1)} %pad_maximum_fusion.rest_0_), custom_call_target="tpu_custom_call" | custom-call | flops 6442450944 | bytes 19922944 | tf_op jit(solution)/shard_map/pallas_call | solution.py:252
  261.7 14.2 %multiply_reduce_fusion = (f32[1024]{0:T(1024)S(1)}, f32[512]{0:T(512)S(1)}, f32[512,1024]{1,0:T(8,128)}) fusion(f32[512,1024]{1,0:T(8,128)} %copy-done.12, f32[512]{0:T(512)S(1)} %add_rsqrt_fusion, f32[1024]{0:T(1024)S(1)} %bitcast.100, bf16[512,6144]{1,0:T(8,128)(2,1)} %pad_maximum_fusion.rest_0_, bf16[1024,6144]{1,0:T(8,128)(2,1)} %copy-done.16), kind=kOutput, calls=%fused_computation.24 | convolution fusion | flops 6445595136 | bytes 23080960 | tf_op jit(solution)/shard_map/dot_general | solution.py:49
  285.2 6.9 %shard_map.314 = (bf16[2,512,1024]{2,1,0:T(8,128)(2,1)S(1)}, bf16[2,512,1024]{2,1,0:T(8,128)(2,1)S(1)}) custom-call(s32[2]{0:T(128)S(1)} %pad_add_fusion.where, bf16[512,2048]{1,0:T(8,128)(2,1)} %copy-done.4, bf16[512,1024]{1,0:T(8,128)(2,1)S(1)} %fusion.19.rest_0_.rest_1_, bf16[512,1024]{1,0:T(8,128)(2,1)S(1)} %fusion.19.rest_0_.rest_1_), custom_call_target="tpu_custom_call" | custom-call | flops 2147483648 | bytes 7340032 | tf_op jit(solution)/shard_map/pallas_call | solution.py:252
  317.8 31.1 %shard_map.315 = (bf16[512,4096]{1,0:T(8,128)(2,1)}, f32[2,128]{1,0:T(2,128)S(1)}) custom-call(f32[512,4096]{1,0:T(8,128)} %fusion.20.query_ref.key_ref.value_ref, f32[512,4096]{1,0:T(8,128)} %fusion.20.query_ref.key_ref.value_ref, f32[512,4096]{1,0:T(8,128)} %fusion.20.query_ref.key_ref.value_ref, f32[512,128]{1,0:T(8,128)S(1)} %get-tuple-element.199.cos_ref, ...), custom_call_target="tpu_custom_call" | custom-call | flops 10737418240 | bytes 12582912 | tf_op jit(solution)/shard_map/pallas_call | solution.py:627
  357.9 10.4 %shard_map.316 = (bf16[2,256,4096]{2,1,0:T(8,128)(2,1)}, bf16[2,256,4096]{2,1,0:T(8,128)(2,1)}) custom-call(s32[2]{0:T(128)S(1)} %pad_add_fusion.where, bf16[512,1024]{1,0:T(8,128)(2,1)S(1)} %fusion.4.left_ref, bf16[512,4096]{1,0:T(8,128)(2,1)} %get-tuple-element.118.rest_0_), custom_call_target="tpu_custom_call" | custom-call | flops 4294967296 | bytes 13631488 | tf_op jit(solution)/shard_map/pallas_call | solution.py:252
  368.4 8.8 %add_convert_fusion.6 = bf16[512,1024]{1,0:T(8,128)(2,1)} fusion(f32[512,1024]{1,0:T(8,128)} %copy-done.12, bf16[512,3072]{1,0:T(8,128)(2,1)} %multiply_convert_fusion.2.left_ref, bf16[3072,1024]{1,0:T(8,128)(2,1)} %constant_dynamic-update-slice_fusion), kind=kOutput, calls=%fused_computation.30 | convolution fusion | flops 3222274048 | bytes 12582912 | tf_op jit(solution)/shard_map/dot_general | solution.py:690
  390.1 36.4 %collective-permute-done.54 = bf16[1,512,1024]{2,1,0:T(8,128)(2,1)S(1)} collective-permute-done((bf16[1,512,1024]{2,1,0:T(8,128)(2,1)S(1)}, bf16[1,512,1024]{2,1,0:T(8,128)(2,1)S(1)}, u32[]{:S(2)}, u32[]{:S(2)}) %collective-permute-start.54) | collective-permute-done | bytes 1048608 | tf_op jit(solution)/shard_map/ppermute | solution.py:61
  431.3 8.8 %fusion.10 = (f32[1024]{0:T(1024)S(1)}, f32[512]{0:T(512)S(1)}, f32[512,1024]{1,0:T(8,128)S(1)}) fusion(bf16[512,1024]{1,0:T(8,128)(2,1)S(1)} %copy-done.19, f32[512]{0:T(512)S(1)} %copy-done.61, f32[1024]{0:T(1024)S(1)} %bitcast.104, bf16[512,4096]{1,0:T(8,128)(2,1)} %get-tuple-element.118.rest_0_, bf16[1024,4096]{1,0:T(8,128)(2,1)} %constant_dynamic-update-slice_fusion.36), kind=kOutput, calls=%fused_computation.22 | convolution fusion | flops 4298635776 | bytes 15740928 | tf_op jit(solution)/shard_map/dot_general | solution.py:49
  448.9 16.7 %collective-permute-done.69 = bf16[1,768,128]{2,1,0:T(8,128)(2,1)S(1)} collective-permute-done((bf16[1,768,128]{2,1,0:T(8,128)(2,1)S(1)}, bf16[1,768,128]{2,1,0:T(8,128)(2,1)S(1)}, u32[]{:S(2)}, u32[]{:S(2)}) %collective-permute-start.69) | collective-permute-done | bytes 196640 | tf_op jit(solution)/shard_map/ppermute | solution.py:61
  478.6 9.0 %collective-permute-done.63 = bf16[1,512,128]{2,1,0:T(8,128)(2,1)S(1)} collective-permute-done((bf16[1,512,128]{2,1,0:T(8,128)(2,1)S(1)}, bf16[1,512,128]{2,1,0:T(8,128)(2,1)S(1)}, u32[]{:S(2)}, u32[]{:S(2)}) %collective-permute-start.63) | collective-permute-done | bytes 131104 | tf_op jit(solution)/shard_map/ppermute | solution.py:61
  497.1 5.5 collective-permute-done.67
  504.8 14.8 %collective-permute-done.59 = bf16[1,256,1024]{2,1,0:T(8,128)(2,1)S(1)} collective-permute-done((bf16[1,256,1024]{2,1,0:T(8,128)(2,1)S(1)}, bf16[1,256,1024]{2,1,0:T(8,128)(2,1)S(1)}, u32[]{:S(2)}, u32[]{:S(2)}) %collective-permute-start.59) | collective-permute-done | bytes 524320 | tf_op jit(solution)/shard_map/ppermute | solution.py:61
  520.9 9.9 %collective-permute-start.60 = (bf16[1,256,512]{2,1,0:T(8,128)(2,1)S(1)}, bf16[1,256,512]{2,1,0:T(8,128)(2,1)S(1)}, u32[]{:S(2)}, u32[]{:S(2)}) collective-permute-start(bf16[1,256,512]{2,1,0:T(8,128)(2,1)S(1)} %pad_maximum_fusion.15), channel_id=1, source_target_pairs={{0,16},{4,20},{8,24},{12,28},{16,0},{20,4},{24,8},{28,12},{1,17},{... | collective-permute-start | bytes 786440 | tf_op jit(solution)/shard_map/ppermute | solution.py:61
  535.7 7.3 %collective-permute-done.60 = bf16[1,256,512]{2,1,0:T(8,128)(2,1)S(1)} collective-permute-done((bf16[1,256,512]{2,1,0:T(8,128)(2,1)S(1)}, bf16[1,256,512]{2,1,0:T(8,128)(2,1)S(1)}, u32[]{:S(2)}, u32[]{:S(2)}) %collective-permute-start.60) | collective-permute-done | bytes 262176 | tf_op jit(solution)/shard_map/ppermute | solution.py:61
  548.7 24.4 %collective-permute-done.70 = bf16[1,256,512]{2,1,0:T(8,128)(2,1)S(1)} collective-permute-done((bf16[1,256,512]{2,1,0:T(8,128)(2,1)S(1)}, bf16[1,256,512]{2,1,0:T(8,128)(2,1)S(1)}, u32[]{:S(2)}, u32[]{:S(2)}) %collective-permute-start.70) | collective-permute-done | bytes 262176 | tf_op jit(solution)/shard_map/ppermute | solution.py:61
  583.9 49.7 %shard_map.317 = f32[8,1152]{1,0:T(8,128)} custom-call(f32[8,1152]{1,0:T(8,128)} %select_maximum_fusion.in_ref), custom_call_target="tpu_custom_call" | custom-call | tf_op jit(solution)/shard_map/pallas_call | solution.py:166
  649.5 9.0 %shard_map.321 = (f32[768,1024]{1,0:T(8,128)}, f32[2,768,1024]{2,1,0:T(8,128)}) custom-call(s32[1]{0:T(128)} %bitcast.8.where, f32[1,1]{1,0:T(1,128)} %bitcast.19.factor_ref, f32[768,1024]{1,0:T(8,128)S(1)} %copy-done.1, f32[2,768,1024]{2,1,0:T(8,128)} %moment_ref.7, bf16[4,768,128]{2,1,0:T(8,128)(2,1)S(1)} %pad_maximum_fusion.6.rest_0_, ...), custom_call_target="tpu_custom_call" | custom-call | flops 15728640 | bytes 20447232 | tf_op jit(solution)/shard_map/pallas_call | solution.py:403
  658.6 18.4 %shard_map.320 = (f32[256,6144]{1,0:T(8,128)}, f32[2,256,6144]{2,1,0:T(8,128)}) custom-call(s32[1]{0:T(128)} %bitcast.8.where, f32[1,1]{1,0:T(1,128)} %bitcast.19.factor_ref, f32[256,6144]{1,0:T(8,128)} %master_ref.6, f32[2,256,6144]{2,1,0:T(8,128)} %moment_ref.6, bf16[4,256,768]{2,1,0:T(8,128)(2,1)} %pad_maximum_fusion.1.rest_0_, ...), custom_call_target="tpu_custom_call" | custom-call | flops 31457280 | bytes 40894464 | tf_op jit(solution)/shard_map/pallas_call | solution.py:403
  677.0 10.5 %shard_map.318 = (f32[256,4096]{1,0:T(8,128)}, f32[2,256,4096]{2,1,0:T(8,128)}) custom-call(s32[1]{0:T(128)} %bitcast.8.where, f32[1,1]{1,0:T(1,128)} %bitcast.19.factor_ref, f32[256,4096]{1,0:T(8,128)} %master_ref.4, f32[2,256,4096]{2,1,0:T(8,128)} %moment_ref.4, bf16[4,256,512]{2,1,0:T(8,128)(2,1)S(1)} %pad_maximum_fusion.2.rest_0_, ...), custom_call_target="tpu_custom_call" | custom-call | flops 20971520 | bytes 27262976 | tf_op jit(solution)/shard_map/pallas_call | solution.py:403
  (474 shorter events, 259.5 us)
Async XLA Ops:
  12.1 90.7 %collective-permute-start.7 = (bf16[256,4096]{1,0:T(8,128)(2,1)}, bf16[256,4096]{1,0:T(8,128)(2,1)}, u32[]{:S(2)}, u32[]{:S(2)}) collective-permute-start(bf16[256,4096]{1,0:T(8,128)(2,1)} %get-tuple-element.169), channel_id=1, source_target_pairs={{0,1},{1,0},{2,3},{3,2},{4,5},{5,4},{6,7},{7,6},{8,9},{9,8},{10,11... | collective-permute-start | bytes 6291464 | tf_op jit(solution)/shard_map/ppermute | solution.py:61
  34.4 28.9 %collective-permute-start.3 = (bf16[64,4096]{1,0:T(8,128)(2,1)S(1)}, bf16[64,4096]{1,0:T(8,128)(2,1)S(1)}, u32[]{:S(2)}, u32[]{:S(2)}) collective-permute-start(bf16[64,4096]{1,0:T(8,128)(2,1)S(1)} %collective-permute-done.2), channel_id=1, source_target_pairs={{0,4},{4,0},{8,12},{12,8},{16,20},{20,16},{24,28},{28,24},{1,5},{5... | collective-permute-start | bytes 1572872 | tf_op jit(solution)/shard_map/ppermute | solution.py:61
  58.9 34.4 %collective-permute-start.18 = (bf16[512,1024]{1,0:T(8,128)(2,1)S(1)}, bf16[512,1024]{1,0:T(8,128)(2,1)S(1)}, u32[]{:S(2)}, u32[]{:S(2)}) collective-permute-start(bf16[512,1024]{1,0:T(8,128)(2,1)S(1)} %get-tuple-element.167), channel_id=1, source_target_pairs={{0,1},{1,0},{2,3},{3,2},{4,5},{5,4},{6,7},{7,6},{8,9},{9,8},{10,11... | collective-permute-start | bytes 3145736 | tf_op jit(solution)/shard_map/ppermute | solution.py:61
  70.6 35.5 %collective-permute-start.8 = (bf16[64,4096]{1,0:T(8,128)(2,1)S(1)}, bf16[64,4096]{1,0:T(8,128)(2,1)S(1)}, u32[]{:S(2)}, u32[]{:S(2)}) collective-permute-start(bf16[64,4096]{1,0:T(8,128)(2,1)S(1)} %collective-permute-done.2), channel_id=1, source_target_pairs={{0,1},{1,0},{2,3},{3,2},{4,5},{5,4},{6,7},{7,6},{8,9},{9,8},{10,11... | collective-permute-start | bytes 1572872 | tf_op jit(solution)/shard_map/ppermute | solution.py:61
  94.9 92.8 %collective-permute-start.29 = (bf16[256,6144]{1,0:T(8,128)(2,1)}, bf16[256,6144]{1,0:T(8,128)(2,1)}, u32[]{:S(2)}, u32[]{:S(2)}) collective-permute-start(bf16[256,6144]{1,0:T(8,128)(2,1)} %get-tuple-element.165), channel_id=1, source_target_pairs={{0,1},{1,0},{2,3},{3,2},{4,5},{5,4},{6,7},{7,6},{8,9},{9,8},{10,11... | collective-permute-start | bytes 9437192 | tf_op jit(solution)/shard_map/ppermute | solution.py:61
  107.3 45.6 %collective-permute-start.26 = (bf16[64,6144]{1,0:T(8,128)(2,1)}, bf16[64,6144]{1,0:T(8,128)(2,1)}, u32[]{:S(2)}, u32[]{:S(2)}) collective-permute-start(bf16[64,6144]{1,0:T(8,128)(2,1)} %collective-permute-done.24), channel_id=1, source_target_pairs={{0,8},{4,12},{8,0},{12,4},{16,24},{20,28},{24,16},{28,20},{1,9},{5... | collective-permute-start | bytes 2359304 | tf_op jit(solution)/shard_map/ppermute | solution.py:61
  108.6 46.6 %collective-permute-start.25 = (bf16[64,6144]{1,0:T(8,128)(2,1)}, bf16[64,6144]{1,0:T(8,128)(2,1)}, u32[]{:S(2)}, u32[]{:S(2)}) collective-permute-start(bf16[64,6144]{1,0:T(8,128)(2,1)} %collective-permute-done.24), channel_id=1, source_target_pairs={{0,4},{4,0},{8,12},{12,8},{16,20},{20,16},{24,28},{28,24},{1,5},{5... | collective-permute-start | bytes 2359304 | tf_op jit(solution)/shard_map/ppermute | solution.py:61
  125.5 58.2 %collective-permute-start.40 = (bf16[768,1024]{1,0:T(8,128)(2,1)}, bf16[768,1024]{1,0:T(8,128)(2,1)}, u32[]{:S(2)}, u32[]{:S(2)}) collective-permute-start(bf16[768,1024]{1,0:T(8,128)(2,1)} %get-tuple-element.163), channel_id=1, source_target_pairs={{0,1},{1,0},{2,3},{3,2},{4,5},{5,4},{6,7},{7,6},{8,9},{9,8},{10,11... | collective-permute-start | bytes 4718600 | tf_op jit(solution)/shard_map/ppermute | solution.py:61
  126.8 33.4 %collective-permute-start.35 = (bf16[192,1024]{1,0:T(8,128)(2,1)S(1)}, bf16[192,1024]{1,0:T(8,128)(2,1)S(1)}, u32[]{:S(2)}, u32[]{:S(2)}) collective-permute-start(bf16[192,1024]{1,0:T(8,128)(2,1)S(1)} %constant_dynamic-slice_fusion.2), channel_id=1, source_target_pairs={{0,2},{1,3},{2,0},{3,1},{4,6},{5,7},{6,4},{7,5},{8,10},{9,11},{10,... | collective-permute-start | bytes 1179656 | tf_op jit(solution)/shard_map/ppermute | solution.py:61
  191.3 29.5 %collective-permute-start.44 = (bf16[96,1024]{1,0:T(8,128)(2,1)S(1)}, bf16[96,1024]{1,0:T(8,128)(2,1)}, u32[]{:S(2)}, u32[]{:S(2)}) collective-permute-start(bf16[96,1024]{1,0:T(8,128)(2,1)S(1)} %collective-permute-done.38), channel_id=1, source_target_pairs={{0,1},{1,0},{2,3},{3,2},{4,5},{5,4},{6,7},{7,6},{8,9},{9,8},{10,11... | collective-permute-start | bytes 589832 | tf_op jit(solution)/shard_map/ppermute | solution.py:61
  191.5 30.9 %collective-permute-start.45 = (bf16[96,1024]{1,0:T(8,128)(2,1)}, bf16[96,1024]{1,0:T(8,128)(2,1)}, u32[]{:S(2)}, u32[]{:S(2)}) collective-permute-start(bf16[96,1024]{1,0:T(8,128)(2,1)} %collective-permute-done.39), channel_id=1, source_target_pairs={{0,1},{1,0},{2,3},{3,2},{4,5},{5,4},{6,7},{7,6},{8,9},{9,8},{10,11... | collective-permute-start | bytes 589832 | tf_op jit(solution)/shard_map/ppermute | solution.py:61
  259.8 39.0 %collective-permute-start.48 = (bf16[1,768,1024]{2,1,0:T(8,128)(2,1)}, bf16[1,768,1024]{2,1,0:T(8,128)(2,1)}, u32[]{:S(2)}, u32[]{:S(2)}) collective-permute-start(bf16[1,768,1024]{2,1,0:T(8,128)(2,1)} %add_convert_fusion.2), channel_id=1, source_target_pairs={{0,2},{1,3},{2,0},{3,1},{4,6},{5,7},{6,4},{7,5},{8,10},{9,11},{10,... | collective-permute-start | bytes 4718600 | tf_op jit(solution)/shard_map/ppermute | solution.py:61
  297.1 54.0 %collective-permute-start.50 = (bf16[1,128,6144]{2,1,0:T(8,128)(2,1)}, bf16[1,128,6144]{2,1,0:T(8,128)(2,1)}, u32[]{:S(2)}, u32[]{:S(2)}) collective-permute-start(bf16[1,128,6144]{2,1,0:T(8,128)(2,1)} %add_convert_fusion.1), channel_id=1, source_target_pairs={{0,2},{1,3},{2,0},{3,1},{4,6},{5,7},{6,4},{7,5},{8,10},{9,11},{10,... | collective-permute-start | bytes 4718600 | tf_op jit(solution)/shard_map/ppermute | solution.py:61
  297.2 53.8 %collective-permute-start.51 = (bf16[2,128,3072]{2,1,0:T(8,128)(2,1)}, bf16[2,128,3072]{2,1,0:T(8,128)(2,1)}, u32[]{:S(2)}, u32[]{:S(2)}) collective-permute-start(bf16[2,128,3072]{2,1,0:T(8,128)(2,1)} %add_convert_fusion), channel_id=1, source_target_pairs={{0,4},{4,0},{8,12},{12,8},{16,20},{20,16},{24,28},{28,24},{1,5},{5... | collective-permute-start | bytes 4718600 | tf_op jit(solution)/shard_map/ppermute | solution.py:61
  309.8 41.2 %collective-permute-start.52 = (bf16[1,768,512]{2,1,0:T(8,128)(2,1)}, bf16[1,768,512]{2,1,0:T(8,128)(2,1)}, u32[]{:S(2)}, u32[]{:S(2)}) collective-permute-start(bf16[1,768,512]{2,1,0:T(8,128)(2,1)} %add_convert_fusion.9), channel_id=1, source_target_pairs={{0,4},{4,0},{8,12},{12,8},{16,20},{20,16},{24,28},{28,24},{1,5},{5... | collective-permute-start | bytes 2359304 | tf_op jit(solution)/shard_map/ppermute | solution.py:61
  378.6 64.1 %collective-permute-start.68 = (bf16[1,768,256]{2,1,0:T(8,128)(2,1)}, bf16[1,768,256]{2,1,0:T(8,128)(2,1)}, u32[]{:S(2)}, u32[]{:S(2)}) collective-permute-start(bf16[1,768,256]{2,1,0:T(8,128)(2,1)} %add_convert_fusion.15), channel_id=1, source_target_pairs={{0,8},{4,12},{8,0},{12,4},{16,24},{20,28},{24,16},{28,20},{1,9},{5... | collective-permute-start | bytes 1179656 | tf_op jit(solution)/shard_map/ppermute | solution.py:61
  384.3 45.4 %collective-permute-start.65 = (bf16[1,128,3072]{2,1,0:T(8,128)(2,1)S(1)}, bf16[1,128,3072]{2,1,0:T(8,128)(2,1)S(1)}, u32[]{:S(2)}, u32[]{:S(2)}) collective-permute-start(bf16[1,128,3072]{2,1,0:T(8,128)(2,1)S(1)} %copy-done.56), channel_id=1, source_target_pairs={{0,2},{1,3},{2,0},{3,1},{4,6},{5,7},{6,4},{7,5},{8,10},{9,11},{10,... | collective-permute-start | bytes 2359304 | tf_op jit(solution)/shard_map/ppermute | solution.py:61
  386.0 45.3 %collective-permute-start.64 = (bf16[1,128,3072]{2,1,0:T(8,128)(2,1)S(1)}, bf16[1,128,3072]{2,1,0:T(8,128)(2,1)}, u32[]{:S(2)}, u32[]{:S(2)}) collective-permute-start(bf16[1,128,3072]{2,1,0:T(8,128)(2,1)S(1)} %copy-done.55), channel_id=1, source_target_pairs={{0,4},{4,0},{8,12},{12,8},{16,20},{20,16},{24,28},{28,24},{1,5},{5... | collective-permute-start | bytes 2359304 | tf_op jit(solution)/shard_map/ppermute | solution.py:61
  386.5 39.9 %collective-permute-start.54 = (bf16[1,512,1024]{2,1,0:T(8,128)(2,1)S(1)}, bf16[1,512,1024]{2,1,0:T(8,128)(2,1)S(1)}, u32[]{:S(2)}, u32[]{:S(2)}) collective-permute-start(bf16[1,512,1024]{2,1,0:T(8,128)(2,1)S(1)} %copy-done.47), channel_id=1, source_target_pairs={{0,2},{1,3},{2,0},{3,1},{4,6},{5,7},{6,4},{7,5},{8,10},{9,11},{10,... | collective-permute-start | bytes 3145736 | tf_op jit(solution)/shard_map/ppermute | solution.py:61
  428.0 47.0 %collective-permute-start.55 = (bf16[1,128,4096]{2,1,0:T(8,128)(2,1)S(1)}, bf16[1,128,4096]{2,1,0:T(8,128)(2,1)}, u32[]{:S(2)}, u32[]{:S(2)}) collective-permute-start(bf16[1,128,4096]{2,1,0:T(8,128)(2,1)S(1)} %add_convert_fusion.4), channel_id=1, source_target_pairs={{0,2},{1,3},{2,0},{3,1},{4,6},{5,7},{6,4},{7,5},{8,10},{9,11},{10,... | collective-permute-start | bytes 3145736 | tf_op jit(solution)/shard_map/ppermute | solution.py:61
  429.7 45.4 %collective-permute-start.57 = (bf16[2,128,2048]{2,1,0:T(8,128)(2,1)S(1)}, bf16[2,128,2048]{2,1,0:T(8,128)(2,1)}, u32[]{:S(2)}, u32[]{:S(2)}) collective-permute-start(bf16[2,128,2048]{2,1,0:T(8,128)(2,1)S(1)} %add_convert_fusion.3), channel_id=1, source_target_pairs={{0,4},{4,0},{8,12},{12,8},{16,20},{20,16},{24,28},{28,24},{1,5},{5... | collective-permute-start | bytes 3145736 | tf_op jit(solution)/shard_map/ppermute | solution.py:61
  442.8 30.7 %collective-permute-start.66 = (bf16[1,256,1536]{2,1,0:T(8,128)(2,1)S(1)}, bf16[1,256,1536]{2,1,0:T(8,128)(2,1)S(1)}, u32[]{:S(2)}, u32[]{:S(2)}) collective-permute-start(bf16[1,256,1536]{2,1,0:T(8,128)(2,1)S(1)} %pad_maximum_fusion.3), channel_id=1, source_target_pairs={{0,8},{4,12},{8,0},{12,4},{16,24},{20,28},{24,16},{28,20},{1,9},{5... | collective-permute-start | bytes 2359304 | tf_op jit(solution)/shard_map/ppermute | solution.py:61
  489.2 41.6 %collective-permute-start.73 = (bf16[1,512,128]{2,1,0:T(8,128)(2,1)S(1)}, bf16[1,512,128]{2,1,0:T(8,128)(2,1)S(1)}, u32[]{:S(2)}, u32[]{:S(2)}) collective-permute-start(bf16[1,512,128]{2,1,0:T(8,128)(2,1)S(1)} %convert_bitcast_fusion.3), channel_id=1, source_target_pairs={{0,16},{4,20},{8,24},{12,28},{16,0},{20,4},{24,8},{28,12},{1,17},{... | collective-permute-start | bytes 393224 | tf_op jit(solution)/shard_map/ppermute | solution.py:61
  489.4 44.0 %collective-permute-start.79 = (bf16[1,768,128]{2,1,0:T(8,128)(2,1)S(1)}, bf16[1,768,128]{2,1,0:T(8,128)(2,1)S(1)}, u32[]{:S(2)}, u32[]{:S(2)}) collective-permute-start(bf16[1,768,128]{2,1,0:T(8,128)(2,1)S(1)} %convert_bitcast_fusion.2), channel_id=1, source_target_pairs={{0,16},{4,20},{8,24},{12,28},{16,0},{20,4},{24,8},{28,12},{1,17},{... | collective-permute-start | bytes 589832 | tf_op jit(solution)/shard_map/ppermute | solution.py:61
  504.7 28.8 %collective-permute-start.76 = (bf16[1,256,768]{2,1,0:T(8,128)(2,1)S(1)}, bf16[1,256,768]{2,1,0:T(8,128)(2,1)S(1)}, u32[]{:S(2)}, u32[]{:S(2)}) collective-permute-start(bf16[1,256,768]{2,1,0:T(8,128)(2,1)S(1)} %convert_bitcast_fusion), channel_id=1, source_target_pairs={{0,16},{4,20},{8,24},{12,28},{16,0},{20,4},{24,8},{28,12},{1,17},{... | collective-permute-start | bytes 1179656 | tf_op jit(solution)/shard_map/ppermute | solution.py:61
  533.4 43.8 %collective-permute-start.80 = (bf16[2,768,128]{2,1,0:T(8,128)(2,1)S(1)}, bf16[2,768,128]{2,1,0:T(8,128)(2,1)S(1)}, u32[]{:S(2)}, u32[]{:S(2)}) collective-permute-start(bf16[2,768,128]{2,1,0:T(8,128)(2,1)S(1)} %pad_maximum_fusion.12), channel_id=1, source_target_pairs={{0,8},{4,12},{8,0},{12,4},{16,24},{20,28},{24,16},{28,20},{1,9},{5... | collective-permute-start | bytes 1179656 | tf_op jit(solution)/shard_map/ppermute | solution.py:61
  533.6 45.1 %collective-permute-start.77 = (bf16[2,256,768]{2,1,0:T(8,128)(2,1)S(1)}, bf16[2,256,768]{2,1,0:T(8,128)(2,1)S(1)}, u32[]{:S(2)}, u32[]{:S(2)}) collective-permute-start(bf16[2,256,768]{2,1,0:T(8,128)(2,1)S(1)} %pad_maximum_fusion.5), channel_id=1, source_target_pairs={{0,8},{4,12},{8,0},{12,4},{16,24},{20,28},{24,16},{28,20},{1,9},{5... | collective-permute-start | bytes 2359304 | tf_op jit(solution)/shard_map/ppermute | solution.py:61
  547.4 91.7 %collective-permute-start.75 = (bf16[4,512,128]{2,1,0:T(8,128)(2,1)S(1)}, bf16[4,512,128]{2,1,0:T(8,128)(2,1)}, u32[]{:S(2)}, u32[]{:S(2)}) collective-permute-start(bf16[4,512,128]{2,1,0:T(8,128)(2,1)S(1)} %pad_maximum_fusion.10.rest_0_), channel_id=1, source_target_pairs={{0,4},{4,0},{8,12},{12,8},{16,20},{20,16},{24,28},{28,24},{1,5},{5... | collective-permute-start | bytes 1572872 | tf_op jit(solution)/shard_map/ppermute | solution.py:61
  574.0 70.5 %collective-permute-start.71 = (bf16[2,256,512]{2,1,0:T(8,128)(2,1)}, bf16[2,256,512]{2,1,0:T(8,128)(2,1)}, u32[]{:S(2)}, u32[]{:S(2)}) collective-permute-start(bf16[2,256,512]{2,1,0:T(8,128)(2,1)} %pad_maximum_fusion.9), channel_id=1, source_target_pairs={{0,8},{4,12},{8,0},{12,4},{16,24},{20,28},{24,16},{28,20},{1,9},{5... | collective-permute-start | bytes 1572872 | tf_op jit(solution)/shard_map/ppermute | solution.py:61
  577.3 72.2 %collective-permute-start.81 = (bf16[4,768,128]{2,1,0:T(8,128)(2,1)S(1)}, bf16[4,768,128]{2,1,0:T(8,128)(2,1)}, u32[]{:S(2)}, u32[]{:S(2)}) collective-permute-start(bf16[4,768,128]{2,1,0:T(8,128)(2,1)S(1)} %pad_maximum_fusion.6.rest_0_), channel_id=1, source_target_pairs={{0,4},{4,0},{8,12},{12,8},{16,20},{20,16},{24,28},{28,24},{1,5},{5... | collective-permute-start | bytes 2359304 | tf_op jit(solution)/shard_map/ppermute | solution.py:61
  580.0 78.6 %collective-permute-start.78 = (bf16[4,256,768]{2,1,0:T(8,128)(2,1)}, bf16[4,256,768]{2,1,0:T(8,128)(2,1)}, u32[]{:S(2)}, u32[]{:S(2)}) collective-permute-start(bf16[4,256,768]{2,1,0:T(8,128)(2,1)} %pad_maximum_fusion.1.rest_0_), channel_id=1, source_target_pairs={{0,4},{4,0},{8,12},{12,8},{16,20},{20,16},{24,28},{28,24},{1,5},{5... | collective-permute-start | bytes 4718600 | tf_op jit(solution)/shard_map/ppermute | solution.py:61
  645.7 31.3 %collective-permute-start.72 = (bf16[4,256,512]{2,1,0:T(8,128)(2,1)S(1)}, bf16[4,256,512]{2,1,0:T(8,128)(2,1)S(1)}, u32[]{:S(2)}, u32[]{:S(2)}) collective-permute-start(bf16[4,256,512]{2,1,0:T(8,128)(2,1)S(1)} %pad_maximum_fusion.2.rest_0_), channel_id=1, source_target_pairs={{0,4},{4,0},{8,12},{12,8},{16,20},{20,16},{24,28},{28,24},{1,5},{5... | collective-permute-start | bytes 3145736 | tf_op jit(solution)/shard_map/ppermute | solution.py:61
  (124 other events, 1949.2 us)

commit v4 on v3

--- a/solution.py
+++ b/solution.py
@@ -1,3 +1,4 @@
+import functools
 import math
 
 import jax
@@ -69,6 +70,14 @@
     return lax.optimization_barrier((value, others))[0]
 
 
+def blank(shape, kind):
+    return pl.pallas_call(
+        lambda out_ref: None,
+        out_shape=jax.ShapeDtypeStruct(shape, kind),
+        out_specs=pl.BlockSpec(memory_space=pl.ANY),
+    )()
+
+
 def gather_rows(shard, previous):
     owners = lax.axis_size("group")
     copies = lax.axis_size("dp")
@@ -79,13 +88,12 @@
     shard = shard.astype(jnp.bfloat16)
     rows, columns = shard.shape
     pieces = [(shard, 0, 0)]
-    order = shard
+    order = by_one = by_two = shard
     if owners == 4 and copies % 4 == 0 and rows % 128 == 0:
         quarter, half = rows // 4, rows // 8
         place = (here & 1) * 2 + ((here >> 1) & 1)
-        order = swap(
-            lax.dynamic_slice_in_dim(shard, place * quarter, quarter, 0), "group", 2
-        )
+        near = lax.dynamic_slice_in_dim(shard, place * quarter, quarter, 0)
+        order = swap(near, "group", 2)
         by_one = swap(order, "dp", 1)
         by_two = swap(order, "dp", 2)
         last = (place ^ 3) * quarter
@@ -100,11 +108,11 @@
         for mask in bit_masks(owners)[1:]:
             pieces += [(swap(v, "group", mask), dg ^ mask, off) for v, dg, off in pieces]
     pieces += [(swap(v, "group", 1), dg ^ 1, off) for v, dg, off in pieces]
-    full = jnp.zeros((rows * owners, columns), shard.dtype)
+    full = blank((rows * owners, columns), shard.dtype)
     for value, delta, offset in pieces:
         start = (mine ^ delta) * rows + offset
         full = lax.dynamic_update_slice(full, value, (start, 0))
-    return full, order
+    return full, order, (by_one, by_two)
 
 
 def gather_small(shard):
@@ -283,67 +291,83 @@
         self.blocks = blocks
         group = [("group", m) for m in bit_masks(lax.axis_size("group"))]
         other = [("dp", m) for m in bit_masks(lax.axis_size("dp"))]
-        held = [blocks[-1]]
+        self.arrays = [blocks[-1]]
         if group:
-            held.append(swap(blocks[0], "group", 1))
+            self.arrays.append(swap(blocks[0], "group", 1))
         rest = group[1:]
         self.orders = [rest + other]
         if split:
             self.orders.append(other[:1] + rest + other[1:])
         count = len(self.orders)
-        size = blocks[-1].shape[1] // count
-        self.parts = [[v[:, i * size : (i + 1) * size] for v in held] for i in range(count)]
+        deep, tall, width = blocks[-1].shape
+        size = tall // count
+        self.parts = [
+            [(k, [(0, deep), (i * size, (i + 1) * size), (0, width)]) for k in range(len(self.arrays))]
+            for i in range(count)
+        ]
         self.common = len(rest) + 1
         self.length = len(rest) + len(other)
         self.step = 0
 
     def hold(self, *others):
-        self.parts = [[after(v, *others) for v in part] for part in self.parts]
+        self.arrays = list(lax.optimization_barrier((self.arrays, others))[0])
+
+    def read(self, part):
+        total = 0.0
+        for k, ranges in part:
+            at = tuple(slice(*r) for r in ranges)
+            total = total + self.arrays[k][at].astype(jnp.float32)
+        return total
+
+    def exchange(self, away, axis, mask):
+        self.arrays.append(swap(away, axis, mask))
+        return len(self.arrays) - 1
 
     def advance(self):
-        sent = []
         if self.step == self.length:
-            return sent
-        exchange = []
+            return []
+        outgoing = []
         for i, order in enumerate(self.orders):
             axis, mask = order[self.step]
             dim = 0 if axis == "group" else 2
-            size = self.parts[i][0].shape[dim] // 2
-            away = sum(
-                lax.slice_in_dim(v, size, 2 * size, axis=dim).astype(jnp.float32)
-                for v in self.parts[i]
-            ).astype(jnp.bfloat16)
-            self.parts[i] = [lax.slice_in_dim(v, 0, size, axis=dim) for v in self.parts[i]]
-            exchange.append((away, axis, mask))
+            far, near = [], []
+            for k, ranges in self.parts[i]:
+                start, stop = ranges[dim]
+                middle = (start + stop) // 2
+                near.append((k, ranges[:dim] + [(start, middle)] + ranges[dim + 1 :]))
+                far.append((k, ranges[:dim] + [(middle, stop)] + ranges[dim + 1 :]))
+            self.parts[i] = near
+            outgoing.append((self.read(far).astype(jnp.bfloat16), axis, mask))
+        deep, tall, width = outgoing[0][0].shape
         if self.step >= self.common:
-            rows = exchange[0][0].shape[1]
-            away = jnp.concatenate([v for v, _, _ in exchange], axis=1)
-            got = swap(away, *exchange[0][1:])
+            away = jnp.concatenate([v for v, _, _ in outgoing], axis=1)
+            sent = [away]
+            k = self.exchange(away, *outgoing[0][1:])
             for i, part in enumerate(self.parts):
-                part.append(got[:, i * rows : (i + 1) * rows])
-            sent.append(away)
+                part.append((k, [(0, deep), (i * tall, (i + 1) * tall), (0, width)]))
         else:
-            for i, (away, axis, mask) in enumerate(exchange):
-                self.parts[i].append(swap(away, axis, mask))
-                sent.append(away)
+            sent = [v for v, _, _ in outgoing]
+            for i, (away, axis, mask) in enumerate(outgoing):
+                k = self.exchange(away, axis, mask)
+                deep, tall, width = away.shape
+                self.parts[i].append((k, [(0, deep), (0, tall), (0, width)]))
         self.step += 1
         return sent
 
     def finish(self):
         while self.step < self.length:
             self.advance()
-        return jnp.concatenate(
-            [sum(v[0].astype(jnp.float32) for v in part) for part in self.parts], axis=0
-        )
-
-
-def gather_grad(own):
+        return jnp.concatenate([self.read(part)[0] for part in self.parts], axis=0)
+
+
+def gather_grad(own, last):
     held = own.astype(jnp.bfloat16)[None]
     deltas = [0]
     groups = [(held, deltas)]
     masks = list(reversed(bit_masks(lax.axis_size("dp"))))
     for i, mask in enumerate(masks):
-        got = swap(held, "dp", mask)
+        away = held if last is None or i + 1 < len(masks) else after(held, last)
+        got = swap(away, "dp", mask)
         got_deltas = [d ^ mask for d in deltas]
         if i + 1 < len(masks):
             held = jnp.concatenate([held, got], axis=0)
@@ -507,15 +531,23 @@
 
 def attend_back_body(
     query_ref, key_ref, value_ref, cos_ref, sin_ref, row_ref, col_ref, gain_ref, grad_ref,
-    out_ref, gain_out_ref,
+    *rest,
+    first,
 ):
-    head = pl.program_id(1)
+    out_ref, gain_out_ref = rest[-2:]
+    head = pl.program_id(1) + first
     cosine, sine = cos_ref[...], sin_ref[...]
     inv_head = 1.0 / math.sqrt(HD)
 
-    @pl.when((pl.program_id(0) == 0) & (head == 0))
+    @pl.when((pl.program_id(0) == 0) & (head == first))
     def _():
         gain_out_ref[...] = jnp.zeros_like(gain_out_ref)
+
+    if len(rest) == 3:
+
+        @pl.when(head == first)
+        def _():
+            out_ref[...] = rest[0][...]
 
     key_low, key_normed, key_root = head_forward(key_ref[...], gain_ref[1:2, :], cosine, sine)
     value_low = value_ref[...].astype(jnp.bfloat16)
@@ -583,16 +615,16 @@
     gain_out_ref[1:2, :] += gain_key
 
 
-def attention_call(body, projected, tables, segments, gains, grad_out):
+def attention_call(body, projected, tables, segments, gains, grad_out, first, count, base):
     token_rows = projected.shape[0]
     seq_count = token_rows // SEQ_LEN
     groups = HQ // HK
     wide = groups * HD
     full = lambda s, h: (s, 0)
     in_specs = [
-        pl.BlockSpec((SEQ_LEN, wide), lambda s, h: (s, h)),
-        pl.BlockSpec((SEQ_LEN, HD), lambda s, h: (s, HQ + h)),
-        pl.BlockSpec((SEQ_LEN, HD), lambda s, h: (s, HQ + HK + h)),
+        pl.BlockSpec((SEQ_LEN, wide), lambda s, h: (s, first + h)),
+        pl.BlockSpec((SEQ_LEN, HD), lambda s, h: (s, HQ + first + h)),
+        pl.BlockSpec((SEQ_LEN, HD), lambda s, h: (s, HQ + HK + first + h)),
         pl.BlockSpec((SEQ_LEN, HD), full),
         pl.BlockSpec((SEQ_LEN, HD), full),
         pl.BlockSpec((1, SEQ_LEN), lambda s, h: (0, s)),
@@ -608,14 +640,20 @@
         segments[:, None],
         gains,
     ]
-    pairs = token_rows * SEQ_LEN * HQ
+    pairs = token_rows * SEQ_LEN * groups * count
+    aliases = {}
     if grad_out is None:
-        out_specs = pl.BlockSpec((SEQ_LEN, wide), lambda s, h: (s, h))
+        out_specs = pl.BlockSpec((SEQ_LEN, wide), lambda s, h: (s, first + h))
         out_shape = jax.ShapeDtypeStruct((token_rows, HQ * HD), jnp.bfloat16)
     else:
         columns = projected.shape[1]
-        in_specs.append(pl.BlockSpec((SEQ_LEN, wide), lambda s, h: (s, h)))
+        in_specs.append(pl.BlockSpec((SEQ_LEN, wide), lambda s, h: (s, first + h)))
         operands.append(grad_out)
+        body = functools.partial(body, first=first)
+        if base is not None:
+            aliases = {len(operands): 0}
+            in_specs.append(pl.BlockSpec((SEQ_LEN, columns), full))
+            operands.append(base)
         out_specs = [
             pl.BlockSpec((SEQ_LEN, columns), full),
             pl.BlockSpec((2, HD), lambda s, h: (0, 0)),
@@ -626,10 +664,11 @@
         ]
     return pl.pallas_call(
         body,
-        grid=(seq_count, HK),
+        grid=(seq_count, count),
         in_specs=in_specs,
         out_specs=out_specs,
         out_shape=out_shape,
+        input_output_aliases=aliases,
         compiler_params=pltpu.CompilerParams(vmem_limit_bytes=48 * 1024 * 1024),
         cost_estimate=pl.CostEstimate(
             flops=(4 if grad_out is None else 10) * pairs * HD * 2,
@@ -637,6 +676,46 @@
             transcendentals=pairs,
         ),
     )(*operands)
+
+
+def gate_up_back(cotangent, full_down, gate_up):
+    tokens, columns = cotangent.shape
+    block = 512
+    steps = FF // block
+
+    def body(cot_ref, down_ref, gate_ref, up_ref, out_ref):
+        at = pl.program_id(0) * block
+        grad = lax.dot_general(
+            cot_ref[...],
+            down_ref[...],
+            (((1,), (1,)), ((), ())),
+            preferred_element_type=jnp.float32,
+        )
+        gate = gate_ref[...]
+        part = jax.nn.sigmoid(gate)
+        grad_gate = grad * up_ref[...] * part * (1.0 + gate * (1.0 - part))
+        grad_up = grad * gate * part
+        out_ref[:, pl.ds(pl.multiple_of(at, block), block)] = grad_gate.astype(jnp.bfloat16)
+        out_ref[:, pl.ds(pl.multiple_of(at + FF, block), block)] = grad_up.astype(jnp.bfloat16)
+
+    return pl.pallas_call(
+        body,
+        grid=(steps,),
+        in_specs=[
+            pl.BlockSpec((tokens, columns), lambda j: (0, 0)),
+            pl.BlockSpec((block, columns), lambda j: (j, 0)),
+            pl.BlockSpec((tokens, block), lambda j: (0, j)),
+            pl.BlockSpec((tokens, block), lambda j: (0, steps + j)),
+        ],
+        out_specs=pl.BlockSpec((tokens, 2 * FF), lambda j: (0, 0)),
+        out_shape=jax.ShapeDtypeStruct((tokens, 2 * FF), jnp.bfloat16),
+        compiler_params=pltpu.CompilerParams(vmem_limit_bytes=48 * 1024 * 1024),
+        cost_estimate=pl.CostEstimate(
+            flops=2 * tokens * FF * columns,
+            bytes_accessed=2 * FF * columns + 12 * tokens * FF,
+            transcendentals=tokens * FF,
+        ),
+    )(cotangent, full_down, gate_up, gate_up)
 
 
 def on_device(
@@ -663,9 +742,9 @@
     gains_all = gather_small(gains_low).reshape(2, owners, -1)
     full_norm = gains_all[:, :, :width].reshape(2, -1)
     full_head = gains_all[:, :, width:].reshape(2, -1)
-    full_qkv, order = gather_rows(qkv_weight, None)
-    full_out, order = gather_rows(out_weight, order)
-    full_gate_up, order = gather_rows(gate_up_weight, order)
+    full_qkv, _, order = gather_rows(qkv_weight, None)
+    full_out, order, _ = gather_rows(out_weight, order)
+    full_gate_up, order, _ = gather_rows(gate_up_weight, order)
     gain_one = full_norm[0].astype(jnp.float32)
     gain_two = full_norm[1].astype(jnp.float32)
     head_gain = full_head.astype(jnp.float32)
@@ -674,9 +753,9 @@
     normed_one = inputs * root_one
     hidden_one = (normed_one * gain_one).astype(jnp.bfloat16)
     projected = jnp.dot(hidden_one, full_qkv, preferred_element_type=jnp.float32)
-    full_down, _ = gather_rows(down_weight, (order, projected))
+    full_down, _, _ = gather_rows(down_weight, (order, projected))
     tables = rotary_tables(positions, HD)
-    mixed_low = attention_call(attend_body, projected, tables, segment_ids, head_gain, None)
+    mixed_low = attention_call(attend_body, projected, tables, segment_ids, head_gain, None, 0, HK, None)
     attended = jnp.dot(mixed_low, full_out, preferred_element_type=jnp.float32)
     residual = inputs + attended
     root_two = lax.rsqrt(jnp.mean(residual * residual, axis=-1, keepdims=True) + EPS_NORM)
@@ -690,43 +769,58 @@
     branch = jnp.dot(activated, full_down, preferred_element_type=jnp.float32)
     output = (residual + branch).astype(jnp.bfloat16)
     upstream = cotangent.astype(jnp.float32)
-    down_sum = GradSum(activated, cotangent, False)
-    grad_act = contract_cols(after(cotangent, *down_sum.blocks), full_down)
-    grad_gate = grad_act * upward * sigmoid_gate * (1.0 + gate_part * (1.0 - sigmoid_gate))
-    grad_up = grad_act * gate_part * sigmoid_gate
-    grad_gate_up = jnp.concatenate([grad_gate, grad_up], axis=-1).astype(jnp.bfloat16)
+    down_sum = GradSum(activated, cotangent, True)
+    grad_gate_up = gate_up_back(after(cotangent, *down_sum.blocks), full_down, gate_up)
     gate_up_sum = GradSum(hidden_two, after(grad_gate_up, *down_sum.advance()), True)
     grad_hidden_two = contract_cols(after(grad_gate_up, *gate_up_sum.blocks), full_gate_up)
     grad_gain_two = jnp.sum(grad_hidden_two * normed_two, axis=0)
     grad_residual = upstream + norm_back(grad_hidden_two, normed_two, root_two, gain_two)
     residual_low = grad_residual.astype(jnp.bfloat16)
-    out_sum = GradSum(mixed_low, after(residual_low, *gate_up_sum.advance()), False)
-    grad_mixed = contract_cols(after(residual_low, *out_sum.blocks), full_out).astype(
-        jnp.bfloat16
-    )
+    down_sum.hold(residual_low)
+    sent = down_sum.advance() + gate_up_sum.advance()
+    out_sum = GradSum(mixed_low, after(residual_low, *sent), False)
     down_sum.hold(out_sum.blocks)
-    grad_mixed = after(grad_mixed, *down_sum.advance(), *out_sum.advance())
+    grad_mixed = contract_cols(
+        after(residual_low, *out_sum.blocks, *down_sum.advance()), full_out
+    ).astype(jnp.bfloat16)
+    grad_mixed = after(grad_mixed, *out_sum.advance())
+    half = HK // 2
+    grad_half, gain_half = attention_call(
+        attend_back_body, projected, tables, segment_ids, head_gain, grad_mixed, 0, half, None
+    )
+    gate_up_sum.hold(grad_half)
+    down_sum.hold(grad_half)
+    sent = gate_up_sum.advance() + down_sum.advance()
     grad_projected, grad_gain_head = attention_call(
-        attend_back_body, projected, tables, segment_ids, head_gain, grad_mixed
-    )
+        attend_back_body,
+        projected,
+        tables,
+        segment_ids,
+        head_gain,
+        grad_mixed,
+        half,
+        HK - half,
+        after(grad_half, *sent),
+    )
+    grad_gain_head = grad_gain_head + gain_half
     gate_up_sum.hold(grad_projected)
-    down_sum.hold(grad_projected)
-    sent = gate_up_sum.advance() + down_sum.advance()
+    out_sum.hold(grad_projected)
+    sent = gate_up_sum.advance() + out_sum.advance()
     qkv_sum = GradSum(hidden_one, after(grad_projected, *sent), True)
+    gate_up_sum.hold(qkv_sum.blocks)
     sent = qkv_sum.advance()
+    gate_up_sum.hold(sent)
     out_sum.hold(sent)
-    gate_up_sum.hold(sent)
-    sent = sent + out_sum.advance()
+    down_sum.hold(sent)
+    sent = sent + gate_up_sum.advance() + out_sum.advance()
     grad_hidden_one = contract_cols(after(grad_projected, *qkv_sum.blocks, *sent), full_qkv)
     grad_gain_one = jnp.sum(grad_hidden_one * normed_one, axis=0)
     grad_inputs = grad_residual + norm_back(grad_hidden_one, normed_one, root_one, gain_one)
     tokens_grad = grad_inputs.astype(jnp.bfloat16)
-    down_sum.hold(sent)
     small = jnp.concatenate(
         [jnp.stack([grad_gain_one, grad_gain_two]), grad_gain_head],
         axis=1,
     )
-    sent = qkv_sum.advance()
     owned = tuple(v.finish() for v in (qkv_sum, out_sum, gate_up_sum, down_sum))
     local = sum(jnp.sum(v * v) for v in owned)
     summed = sum_all(
@@ -740,7 +834,13 @@
     squares = summed[2, 0] + jnp.sum(small * small)
     clip_limit = math.sqrt(PARAMS)
     factor = clip_limit / jnp.maximum(jnp.sqrt(squares), clip_limit)
-    gathered = [gather_grad(after(v, *sent)) for v in owned]
+    qkv_own, out_own, gate_up_own, down_own = owned
+    gathered = [
+        gather_grad(after(qkv_own, summed), None),
+        gather_grad(out_own, None),
+        gather_grad(gate_up_own, summed),
+        gather_grad(down_own, None),
+    ]
     masters = (qkv_weight, out_weight, gate_up_weight, down_weight)
     moments = (qkv_moments, out_moments, gate_up_moments, down_moments)
     later = after(factor, gathered[0][0][0])

time: 693 us -> 643 us (0.928)
  local copies, waits for them, and re-layouts: 88.9 us -> 52.5 us
  matrix products: 73.4 us -> 53.5 us
  starting transfers between devices: 81.3 us -> 64.5 us
  waiting for transfers between devices: 170 us -> 186 us
  other arithmetic: 85.6 us -> 100 us
  Pallas kernels: 182 us -> 170 us
    pallas_call x1, Pallas kernels: 49.7 us -> 19.8 us  [sum_all(): pl.pallas_call(body, out_shape=jax.ShapeDtypeStruct(shape, jnp.float32),...]
    slice x21 -> x0, local copies, waits for them, and re-layouts: 18.4 us -> none  [advance(): lax.slice_in_dim(v, 0, size, axis=dim)]
    pallas_call x2 -> x8, Pallas kernels: 50 us -> 67.5 us  [the longest x3 54.6 us: attention_call(): pl.pallas_call(body, grid=(seq_count, count), in_specs=in_specs, out_spec...]
    ppermute x82 -> x84, starting transfers between devices: 81.3 us -> 64.5 us  [swap(): return lax.ppermute(value, axis, [(i, i ^ mask) for i in range(count)])]
    ppermute x82 -> x84, waiting for transfers between devices: 170 us -> 186 us  [swap(): return lax.ppermute(value, axis, [(i, i ^ mask) for i in range(count)])]
    broadcast_in_dim x4 -> x0, local copies, waits for them, and re-layouts: 14.1 us -> none  [gather_rows(): full = jnp.zeros((rows * owners, columns), shard.dtype)]
    dot_general x4 -> x3, matrix products: 39.7 us -> 25.8 us  [contract_cols(): lax.dot_general(left_side, right_side, (((1,), (1,)), ((), ())), preferre...]
    dynamic_update_slice x44, local copies, waits for them, and re-layouts: 41.8 us -> 32.8 us  [gather_rows(): full = lax.dynamic_update_slice(full, value, (start, 0))]
  transfers between devices with their start and end apart: 82 -> 84, of which waited for: 21 -> 33; matrix products, arithmetic and copies ran while one was open for 34% -> 27% of each run, Pallas kernels for 22% -> 19%
where the time goes in v4:
time: 643 us; the launch traced here: 633 us
  waiting for transfers between devices  186 us (29%)
  Pallas kernels  170 us (26%)
  other arithmetic  100 us (16%)
  starting transfers between devices  64.5 us (10%)
  matrix products  53.5 us (8%)
  local copies, waits for them, and re-layouts  52.5 us (8%)
  between operations  6.61 us (1%)
    ppermute x84, waiting for transfers between devices, swap(): return lax.ppermute(value, axis, [(i, i ^ mask) for i in range(count)])  186 us
    ppermute x84, starting transfers between devices, swap(): return lax.ppermute(value, axis, [(i, i ^ mask) for i in range(count)])  64.5 us
    pallas_call x3, Pallas kernels, attention_call(): pl.pallas_call(body, grid=(seq_count, count), in_specs=in_specs, out_spec...  54.6 us
    pallas_call x4, Pallas kernels, adam_blocks(): pl.pallas_call(body, out_shape=[jax.ShapeDtypeStruct(master.shape, jnp.fl...  43.5 us
    pallas_call x4, Pallas kernels, grad_blocks(): pl.pallas_call(body, out_shape=[jax.ShapeDtypeStruct((len(row_set), row_b...  38.8 us
    convert_element_type x19, other arithmetic, advance(): outgoing.append((self.read(far).astype(jnp.bfloat16), axis, mask))  36.1 us
    dynamic_update_slice x44, local copies, waits for them, and re-layouts, gather_rows(): full = lax.dynamic_update_slice(full, value, (start, 0))  32.8 us
    dot_general x3, matrix products, contract_cols(): lax.dot_general(left_side, right_side, (((1,), (1,)), ((), ())), preferre...  25.8 us
  transfers between devices with their start and end apart: 84, of which 33 were waited for; matrix products, arithmetic and copies ran while one was open for 27% of the time, Pallas kernels for 19%

profile of v4, /device:TPU:0, one launch (start us, length us, event | category | flops | bytes accessed | tf_op | source)
XLA Modules:
  0.0 633.0 jit_solution(11554566156963862938)
XLA Ops:
  18.3 7.2 %collective-permute-done.2 = bf16[64,4096]{1,0:T(8,128)(2,1)} collective-permute-done((bf16[64,4096]{1,0:T(8,128)(2,1)S(1)}, bf16[64,4096]{1,0:T(8,128)(2,1)}, u32[]{:S(2)}, u32[]{:S(2)}) %collective-permute-start.2) | collective-permute-done | bytes 524320 | tf_op jit(solution)/shard_map/ppermute | solution.py:62
  30.6 8.6 %collective-permute-done.4 = bf16[64,4096]{1,0:T(8,128)(2,1)S(1)} collective-permute-done((bf16[64,4096]{1,0:T(8,128)(2,1)}, bf16[64,4096]{1,0:T(8,128)(2,1)S(1)}, u32[]{:S(2)}, u32[]{:S(2)}) %collective-permute-start.4) | collective-permute-done | bytes 524320 | tf_op jit(solution)/shard_map/ppermute | solution.py:62
  53.9 5.3 constant_dynamic-update-slice_fusion.23
  81.2 6.8 %fusion.32.query_ref.key_ref.value_ref = f32[512,4096]{1,0:T(8,128)} fusion(bf16[512,1024]{1,0:T(8,128)(2,1)S(1)} %copy-done.12, bf16[1024,4096]{1,0:T(8,128)(2,1)S(1)} %constant_dynamic-update-slice_fusion.36), kind=kOutput, calls=%fused_computation.185 | convolution fusion | flops 4294967296 | bytes 17825792 | tf_op jit(solution)/shard_map/dot_general | solution.py:755
  88.0 18.8 %shard_map.312.left_ref = bf16[512,2048]{1,0:T(8,128)(2,1)S(1)} custom-call(f32[512,4096]{1,0:T(8,128)} %fusion.32.query_ref.key_ref.value_ref, f32[512,4096]{1,0:T(8,128)} %fusion.32.query_ref.key_ref.value_ref, f32[512,4096]{1,0:T(8,128)} %fusion.32.query_ref.key_ref.value_ref, f32[512,128]{1,0:T(8,128)S(1)} %get-tuple-element.269.cos_ref, ...), custom_call_target="tpu_custom_call" | custom-call | flops 4294967296 | bytes 12582912 | tf_op jit(solution)/shard_map/pallas_call | solution.py:665
  116.3 15.6 %collective-permute-done.26 = bf16[64,6144]{1,0:T(8,128)(2,1)S(1)} collective-permute-done((bf16[64,6144]{1,0:T(8,128)(2,1)}, bf16[64,6144]{1,0:T(8,128)(2,1)S(1)}, u32[]{:S(2)}, u32[]{:S(2)}) %collective-permute-start.26) | collective-permute-done | bytes 786464 | tf_op jit(solution)/shard_map/ppermute | solution.py:62
  135.9 6.5 %collective-permute-done.27 = bf16[32,6144]{1,0:T(8,128)(2,1)S(1)} collective-permute-done((bf16[32,6144]{1,0:T(8,128)(2,1)S(1)}, bf16[32,6144]{1,0:T(8,128)(2,1)S(1)}, u32[]{:S(2)}, u32[]{:S(2)}) %collective-permute-start.27) | collective-permute-done | bytes 393248 | tf_op jit(solution)/shard_map/ppermute | solution.py:62
  151.3 9.3 %fusion.33.gate_ref.up_ref = f32[512,6144]{1,0:T(8,128)S(1)} fusion(bf16[512,1024]{1,0:T(8,128)(2,1)S(1)} %multiply_convert_fusion.left_ref, bf16[1024,6144]{1,0:T(8,128)(2,1)} %constant_dynamic-update-slice_fusion.12), kind=kOutput, calls=%fused_computation.186 | convolution fusion | flops 6442450944 | bytes 26214400 | tf_op jit(solution)/shard_map/dot_general | solution.py:764
  168.3 8.6 %shard_map.316 = (bf16[2,768,1024]{2,1,0:T(8,128)(2,1)}, bf16[2,768,1024]{2,1,0:T(8,128)(2,1)}) custom-call(s32[2]{0:T(128)S(1)} %pad_add_fusion.where, bf16[512,3072]{1,0:T(8,128)(2,1)} %fusion.left_ref, bf16[512,1024]{1,0:T(8,128)(2,1)S(1)} %copy-done.1, bf16[512,1024]{1,0:T(8,128)(2,1)S(1)} %copy-done.1), custom_call_target="tpu_custom_call" | custom-call | flops 3221225472 | bytes 10485760 | tf_op jit(solution)/shard_map/pallas_call | solution.py:260
  182.5 11.1 %collective-permute-done.35 = bf16[192,1024]{1,0:T(8,128)(2,1)} collective-permute-done((bf16[192,1024]{1,0:T(8,128)(2,1)S(1)}, bf16[192,1024]{1,0:T(8,128)(2,1)}, u32[]{:S(2)}, u32[]{:S(2)}) %collective-permute-start.35) | collective-permute-done | bytes 393248 | tf_op jit(solution)/shard_map/ppermute | solution.py:62
  197.4 7.2 %collective-permute-done.37 = bf16[192,1024]{1,0:T(8,128)(2,1)} collective-permute-done((bf16[192,1024]{1,0:T(8,128)(2,1)}, bf16[192,1024]{1,0:T(8,128)(2,1)}, u32[]{:S(2)}, u32[]{:S(2)}) %collective-permute-start.37) | collective-permute-done | bytes 393248 | tf_op jit(solution)/shard_map/ppermute | solution.py:62
  220.9 12.9 %shard_map.317.rest_0_ = bf16[512,6144]{1,0:T(8,128)(2,1)} custom-call(bf16[512,1024]{1,0:T(8,128)(2,1)S(1)} %copy-done.2, bf16[3072,1024]{1,0:T(8,128)(2,1)} %constant_dynamic-update-slice_fusion.down_ref, f32[512,6144]{1,0:T(8,128)} %copy-done.17, f32[512,6144]{1,0:T(8,128)} %copy-done.17), custom_call_target="tpu_custom_call" | custom-call | flops 3221225472 | bytes 25165824 | tf_op jit(solution)/shard_map/pallas_call | solution.py:701
  238.6 12.9 %shard_map.318 = (bf16[2,256,6144]{2,1,0:T(8,128)(2,1)}, bf16[2,256,6144]{2,1,0:T(8,128)(2,1)}) custom-call(s32[2]{0:T(128)S(1)} %pad_add_fusion.where, bf16[512,1024]{1,0:T(8,128)(2,1)S(1)} %copy-done.15, bf16[512,6144]{1,0:T(8,128)(2,1)} %shard_map.317.rest_0_), custom_call_target="tpu_custom_call" | custom-call | flops 6442450944 | bytes 19922944 | tf_op jit(solution)/shard_map/pallas_call | solution.py:260
  253.5 14.0 %multiply_reduce_fusion = (f32[1024]{0:T(1024)S(1)}, f32[512]{0:T(512)S(1)}, f32[512,1024]{1,0:T(8,128)}) fusion(f32[512,1024]{1,0:T(8,128)} %copy-done.18, f32[512]{0:T(512)S(1)} %add_rsqrt_fusion, f32[1024]{0:T(1024)S(1)} %bitcast.92, bf16[512,6144]{1,0:T(8,128)(2,1)} %shard_map.317.rest_0_, bf16[1024,6144]{1,0:T(8,128)(2,1)} %constant_dynamic-update-slice_fusion.12), kind=kOutput, calls=%fused_computation.20 | convolution fusion | flops 6445595136 | bytes 23080960 | tf_op jit(solution)/shard_map/dot_general | solution.py:50
  279.8 6.8 %shard_map.319 = (bf16[2,512,1024]{2,1,0:T(8,128)(2,1)S(1)}, bf16[2,512,1024]{2,1,0:T(8,128)(2,1)S(1)}) custom-call(s32[2]{0:T(128)S(1)} %pad_add_fusion.where, bf16[512,2048]{1,0:T(8,128)(2,1)} %copy-done.11, bf16[512,1024]{1,0:T(8,128)(2,1)S(1)} %fusion.30.rest_0_.rest_1_, bf16[512,1024]{1,0:T(8,128)(2,1)S(1)} %fusion.30.rest_0_.rest_1_), custom_call_target="tpu_custom_call" | custom-call | flops 2147483648 | bytes 7340032 | tf_op jit(solution)/shard_map/pallas_call | solution.py:260
  290.9 7.9 %collective-permute-done.51 = bf16[1,384,512]{2,1,0:T(8,128)(2,1)S(1)} collective-permute-done((bf16[1,384,512]{2,1,0:T(8,128)(2,1)S(1)}, bf16[1,384,512]{2,1,0:T(8,128)(2,1)S(1)}, u32[]{:S(2)}, u32[]{:S(2)}) %collective-permute-start.51) | collective-permute-done | bytes 393248 | tf_op jit(solution)/shard_map/ppermute | solution.py:62
  308.0 17.2 %shard_map.320 = (bf16[512,4096]{1,0:T(8,128)(2,1)}, f32[2,128]{1,0:T(2,128)S(1)}) custom-call(f32[512,4096]{1,0:T(8,128)} %fusion.32.query_ref.key_ref.value_ref, f32[512,4096]{1,0:T(8,128)} %fusion.32.query_ref.key_ref.value_ref, f32[512,4096]{1,0:T(8,128)} %fusion.32.query_ref.key_ref.value_ref, f32[512,128]{1,0:T(8,128)S(1)} %get-tuple-element.269.cos_ref, ...), custom_call_target="tpu_custom_call" | custom-call | flops 5368709120 | bytes 12582912 | tf_op jit(solution)/shard_map/pallas_call | solution.py:665
  325.2 7.4 %collective-permute-done.53 = bf16[1,128,6144]{2,1,0:T(8,128)(2,1)} collective-permute-done((bf16[1,128,6144]{2,1,0:T(8,128)(2,1)}, bf16[1,128,6144]{2,1,0:T(8,128)(2,1)}, u32[]{:S(2)}, u32[]{:S(2)}) %collective-permute-start.53) | collective-permute-done | bytes 1572896 | tf_op jit(solution)/shard_map/ppermute | solution.py:62
  340.5 18.6 %shard_map.321 = (bf16[512,4096]{1,0:T(8,128)(2,1)}, f32[2,128]{1,0:T(2,128)S(1)}) custom-call(f32[512,4096]{1,0:T(8,128)} %fusion.32.query_ref.key_ref.value_ref, f32[512,4096]{1,0:T(8,128)} %fusion.32.query_ref.key_ref.value_ref, f32[512,4096]{1,0:T(8,128)} %fusion.32.query_ref.key_ref.value_ref, ...), custom_call_target="tpu_custom_call", output_to_operand_aliasing={{0}: (9, {})} | custom-call | flops 5368709120 | bytes 12582912 | tf_op jit(solution)/shard_map/pallas_call | solution.py:665
  359.1 12.2 %collective-permute-done.57 = bf16[1,128,3072]{2,1,0:T(8,128)(2,1)S(1)} collective-permute-done((bf16[1,128,3072]{2,1,0:T(8,128)(2,1)S(1)}, bf16[1,128,3072]{2,1,0:T(8,128)(2,1)S(1)}, u32[]{:S(2)}, u32[]{:S(2)}) %collective-permute-start.57) | collective-permute-done | bytes 786464 | tf_op jit(solution)/shard_map/ppermute | solution.py:62
  378.0 10.4 %shard_map.322 = (bf16[2,256,4096]{2,1,0:T(8,128)(2,1)}, bf16[2,256,4096]{2,1,0:T(8,128)(2,1)}) custom-call(s32[2]{0:T(128)S(1)} %pad_add_fusion.where, bf16[512,1024]{1,0:T(8,128)(2,1)S(1)} %copy-done.13, bf16[512,4096]{1,0:T(8,128)(2,1)} %get-tuple-element.180.rest_0_), custom_call_target="tpu_custom_call" | custom-call | flops 4294967296 | bytes 13631488 | tf_op jit(solution)/shard_map/pallas_call | solution.py:260
  389.5 9.2 %add_convert_fusion.5 = bf16[512,1024]{1,0:T(8,128)(2,1)} fusion(f32[512,1024]{1,0:T(8,128)} %copy-done.18, bf16[512,3072]{1,0:T(8,128)(2,1)} %fusion.left_ref, bf16[3072,1024]{1,0:T(8,128)(2,1)} %constant_dynamic-update-slice_fusion.down_ref), kind=kOutput, calls=%fused_computation.26 | convolution fusion | flops 3222274048 | bytes 12582912 | tf_op jit(solution)/shard_map/dot_general | solution.py:769
  402.4 10.4 %collective-permute-done.60 = bf16[1,256,1536]{2,1,0:T(8,128)(2,1)S(1)} collective-permute-done((bf16[1,256,1536]{2,1,0:T(8,128)(2,1)}, bf16[1,256,1536]{2,1,0:T(8,128)(2,1)S(1)}, u32[]{:S(2)}, u32[]{:S(2)}) %collective-permute-start.60) | collective-permute-done | bytes 786464 | tf_op jit(solution)/shard_map/ppermute | solution.py:62
  429.9 9.4 %fusion.11 = (f32[1024]{0:T(1024)S(1)}, f32[512]{0:T(512)S(1)}, f32[512,1024]{1,0:T(8,128)}) fusion(bf16[512,1024]{1,0:T(8,128)(2,1)S(1)} %copy-done.22, f32[512]{0:T(512)S(1)} %copy-done.63, f32[1024]{0:T(1024)S(1)} %bitcast.96, bf16[512,4096]{1,0:T(8,128)(2,1)S(1)} %copy-done.27, bf16[1024,4096]{1,0:T(8,128)(2,1)} %copy-done.25), kind=kOutput, calls=%fused_computation.18 | convolution fusion | flops 4298635776 | bytes 15740928 | tf_op jit(solution)/shard_map/dot_general | solution.py:50
  470.2 16.0 %collective-permute-done.66 = bf16[1,256,1024]{2,1,0:T(8,128)(2,1)S(1)} collective-permute-done((bf16[1,256,1024]{2,1,0:T(8,128)(2,1)S(1)}, bf16[1,256,1024]{2,1,0:T(8,128)(2,1)S(1)}, u32[]{:S(2)}, u32[]{:S(2)}) %collective-permute-start.66) | collective-permute-done | bytes 524320 | tf_op jit(solution)/shard_map/ppermute | solution.py:62
  493.9 5.6 collective-permute-done.67
  505.4 19.8 %shard_map.323 = f32[8,1152]{1,0:T(8,128)} custom-call(f32[8,1152]{1,0:T(8,128)} %select_maximum_fusion.in_ref), custom_call_target="tpu_custom_call" | custom-call | tf_op jit(solution)/shard_map/pallas_call | solution.py:174
  550.0 5.3 shard_map.325
  560.8 33.5 %collective-permute-done.83.rest_1_ = bf16[4,768,128]{2,1,0:T(8,128)(2,1)} collective-permute-done((bf16[4,768,128]{2,1,0:T(8,128)(2,1)}, bf16[4,768,128]{2,1,0:T(8,128)(2,1)}, u32[]{:S(2)}, u32[]{:S(2)}) %collective-permute-start.83) | collective-permute-done | bytes 786464 | tf_op jit(solution)/shard_map/ppermute | solution.py:62
  594.3 9.3 %shard_map.327 = (f32[768,1024]{1,0:T(8,128)}, f32[2,768,1024]{2,1,0:T(8,128)}) custom-call(s32[1]{0:T(128)} %bitcast.8.where, f32[1,1]{1,0:T(1,128)} %bitcast.20.factor_ref, f32[768,1024]{1,0:T(8,128)S(1)} %copy-done, f32[2,768,1024]{2,1,0:T(8,128)} %moment_ref.7, bf16[4,768,128]{2,1,0:T(8,128)(2,1)} %pad_maximum_fusion.5.rest_0_, ...), custom_call_target="tpu_custom_call" | custom-call | flops 15728640 | bytes 20447232 | tf_op jit(solution)/shard_map/pallas_call | solution.py:427
  603.6 18.4 %shard_map.326 = (f32[256,6144]{1,0:T(8,128)}, f32[2,256,6144]{2,1,0:T(8,128)}) custom-call(s32[1]{0:T(128)} %bitcast.8.where, f32[1,1]{1,0:T(1,128)} %bitcast.20.factor_ref, f32[256,6144]{1,0:T(8,128)} %master_ref.6, f32[2,256,6144]{2,1,0:T(8,128)} %moment_ref.6, bf16[4,256,768]{2,1,0:T(8,128)(2,1)} %pad_maximum_fusion.rest_0_, ...), custom_call_target="tpu_custom_call" | custom-call | flops 31457280 | bytes 40894464 | tf_op jit(solution)/shard_map/pallas_call | solution.py:427
  622.0 10.5 %shard_map.324 = (f32[256,4096]{1,0:T(8,128)}, f32[2,256,4096]{2,1,0:T(8,128)}) custom-call(s32[1]{0:T(128)} %bitcast.8.where, f32[1,1]{1,0:T(1,128)} %bitcast.20.factor_ref, f32[256,4096]{1,0:T(8,128)} %master_ref.4, f32[2,256,4096]{2,1,0:T(8,128)} %moment_ref.4, bf16[4,256,512]{2,1,0:T(8,128)(2,1)S(1)} %pad_maximum_fusion.1.rest_0_, ...), custom_call_target="tpu_custom_call" | custom-call | flops 20971520 | bytes 27262976 | tf_op jit(solution)/shard_map/pallas_call | solution.py:427
  (459 shorter events, 253.6 us)
Async XLA Ops:
  9.9 63.7 %collective-permute-start.7 = (bf16[256,4096]{1,0:T(8,128)(2,1)}, bf16[256,4096]{1,0:T(8,128)(2,1)}, u32[]{:S(2)}, u32[]{:S(2)}) collective-permute-start(bf16[256,4096]{1,0:T(8,128)(2,1)} %get-tuple-element.225), channel_id=1, source_target_pairs={{0,1},{1,0},{2,3},{3,2},{4,5},{5,4},{6,7},{7,6},{8,9},{9,8},{10,11... | collective-permute-start | bytes 6291464 | tf_op jit(solution)/shard_map/ppermute | solution.py:62
  28.7 47.3 %collective-permute-start.8 = (bf16[64,4096]{1,0:T(8,128)(2,1)}, bf16[64,4096]{1,0:T(8,128)(2,1)S(1)}, u32[]{:S(2)}, u32[]{:S(2)}) collective-permute-start(bf16[64,4096]{1,0:T(8,128)(2,1)} %collective-permute-done.2), channel_id=1, source_target_pairs={{0,1},{1,0},{2,3},{3,2},{4,5},{5,4},{6,7},{7,6},{8,9},{9,8},{10,11... | collective-permute-start | bytes 1572872 | tf_op jit(solution)/shard_map/ppermute | solution.py:62
  42.4 64.4 %collective-permute-start.18 = (bf16[512,1024]{1,0:T(8,128)(2,1)}, bf16[512,1024]{1,0:T(8,128)(2,1)S(1)}, u32[]{:S(2)}, u32[]{:S(2)}) collective-permute-start(bf16[512,1024]{1,0:T(8,128)(2,1)} %get-tuple-element.223), channel_id=1, source_target_pairs={{0,1},{1,0},{2,3},{3,2},{4,5},{5,4},{6,7},{7,6},{8,9},{9,8},{10,11... | collective-permute-start | bytes 3145736 | tf_op jit(solution)/shard_map/ppermute | solution.py:62
  73.6 70.9 %collective-permute-start.29 = (bf16[256,6144]{1,0:T(8,128)(2,1)S(1)}, bf16[256,6144]{1,0:T(8,128)(2,1)S(1)}, u32[]{:S(2)}, u32[]{:S(2)}) collective-permute-start(bf16[256,6144]{1,0:T(8,128)(2,1)S(1)} %get-tuple-element.221), channel_id=1, source_target_pairs={{0,1},{1,0},{2,3},{3,2},{4,5},{5,4},{6,7},{7,6},{8,9},{9,8},{10,11... | collective-permute-start | bytes 9437192 | tf_op jit(solution)/shard_map/ppermute | solution.py:62
  76.0 35.6 %collective-permute-start.24 = (bf16[64,6144]{1,0:T(8,128)(2,1)}, bf16[64,6144]{1,0:T(8,128)(2,1)}, u32[]{:S(2)}, u32[]{:S(2)}) collective-permute-start(bf16[64,6144]{1,0:T(8,128)(2,1)} %constant_dynamic-slice_fusion.3), channel_id=1, source_target_pairs={{0,2},{1,3},{2,0},{3,1},{4,6},{5,7},{6,4},{7,5},{8,10},{9,11},{10,... | collective-permute-start | bytes 2359304 | tf_op jit(solution)/shard_map/ppermute | solution.py:62
  80.5 26.8 %collective-permute-start.19 = (bf16[128,1024]{1,0:T(8,128)(2,1)}, bf16[128,1024]{1,0:T(8,128)(2,1)S(1)}, u32[]{:S(2)}, u32[]{:S(2)}) collective-permute-start(bf16[128,1024]{1,0:T(8,128)(2,1)} %collective-permute-done.13), channel_id=1, source_target_pairs={{0,1},{1,0},{2,3},{3,2},{4,5},{5,4},{6,7},{7,6},{8,9},{9,8},{10,11... | collective-permute-start | bytes 786440 | tf_op jit(solution)/shard_map/ppermute | solution.py:62
  80.9 26.7 %collective-permute-start.20 = (bf16[128,1024]{1,0:T(8,128)(2,1)S(1)}, bf16[128,1024]{1,0:T(8,128)(2,1)S(1)}, u32[]{:S(2)}, u32[]{:S(2)}) collective-permute-start(bf16[128,1024]{1,0:T(8,128)(2,1)S(1)} %collective-permute-done.14), channel_id=1, source_target_pairs={{0,1},{1,0},{2,3},{3,2},{4,5},{5,4},{6,7},{7,6},{8,9},{9,8},{10,11... | collective-permute-start | bytes 786440 | tf_op jit(solution)/shard_map/ppermute | solution.py:62
  111.6 35.3 %collective-permute-start.30 = (bf16[64,6144]{1,0:T(8,128)(2,1)}, bf16[64,6144]{1,0:T(8,128)(2,1)S(1)}, u32[]{:S(2)}, u32[]{:S(2)}) collective-permute-start(bf16[64,6144]{1,0:T(8,128)(2,1)} %collective-permute-done.24), channel_id=1, source_target_pairs={{0,1},{1,0},{2,3},{3,2},{4,5},{5,4},{6,7},{7,6},{8,9},{9,8},{10,11... | collective-permute-start | bytes 2359304 | tf_op jit(solution)/shard_map/ppermute | solution.py:62
  176.9 57.0 %collective-permute-start.46 = (bf16[2,768,1024]{2,1,0:T(8,128)(2,1)}, bf16[2,768,1024]{2,1,0:T(8,128)(2,1)}, u32[]{:S(2)}, u32[]{:S(2)}) collective-permute-start(bf16[2,768,1024]{2,1,0:T(8,128)(2,1)} %get-tuple-element.114), channel_id=1, source_target_pairs={{0,1},{1,0},{2,3},{3,2},{4,5},{5,4},{6,7},{7,6},{8,9},{9,8},{10,11... | collective-permute-start | bytes 9437192 | tf_op jit(solution)/shard_map/ppermute | solution.py:62
  180.9 33.2 %collective-permute-start.40 = (bf16[768,1024]{1,0:T(8,128)(2,1)}, bf16[768,1024]{1,0:T(8,128)(2,1)}, u32[]{:S(2)}, u32[]{:S(2)}) collective-permute-start(bf16[768,1024]{1,0:T(8,128)(2,1)} %get-tuple-element.219), channel_id=1, source_target_pairs={{0,1},{1,0},{2,3},{3,2},{4,5},{5,4},{6,7},{7,6},{8,9},{9,8},{10,11... | collective-permute-start | bytes 4718600 | tf_op jit(solution)/shard_map/ppermute | solution.py:62
  251.5 22.4 %collective-permute-start.49 = (bf16[2,256,6144]{2,1,0:T(8,128)(2,1)}, bf16[2,256,6144]{2,1,0:T(8,128)(2,1)}, u32[]{:S(2)}, u32[]{:S(2)}) collective-permute-start(bf16[2,256,6144]{2,1,0:T(8,128)(2,1)} %get-tuple-element.118), channel_id=1, source_target_pairs={{0,1},{1,0},{2,3},{3,2},{4,5},{5,4},{6,7},{7,6},{8,9},{9,8},{10,11... | collective-permute-start | bytes 18874376 | tf_op jit(solution)/shard_map/ppermute | solution.py:62
  289.4 43.2 %collective-permute-start.53 = (bf16[1,128,6144]{2,1,0:T(8,128)(2,1)}, bf16[1,128,6144]{2,1,0:T(8,128)(2,1)}, u32[]{:S(2)}, u32[]{:S(2)}) collective-permute-start(bf16[1,128,6144]{2,1,0:T(8,128)(2,1)} %add_convert_fusion.1), channel_id=1, source_target_pairs={{0,2},{1,3},{2,0},{3,1},{4,6},{5,7},{6,4},{7,5},{8,10},{9,11},{10,... | collective-permute-start | bytes 4718600 | tf_op jit(solution)/shard_map/ppermute | solution.py:62
  290.0 43.5 %collective-permute-start.54 = (bf16[2,128,3072]{2,1,0:T(8,128)(2,1)}, bf16[2,128,3072]{2,1,0:T(8,128)(2,1)}, u32[]{:S(2)}, u32[]{:S(2)}) collective-permute-start(bf16[2,128,3072]{2,1,0:T(8,128)(2,1)} %add_convert_fusion), channel_id=1, source_target_pairs={{0,4},{4,0},{8,12},{12,8},{16,20},{20,16},{24,28},{28,24},{1,5},{5... | collective-permute-start | bytes 4718600 | tf_op jit(solution)/shard_map/ppermute | solution.py:62
  307.6 67.3 %collective-permute-start.58 = (bf16[1,512,1024]{2,1,0:T(8,128)(2,1)S(1)}, bf16[1,512,1024]{2,1,0:T(8,128)(2,1)S(1)}, u32[]{:S(2)}, u32[]{:S(2)}) collective-permute-start(bf16[1,512,1024]{2,1,0:T(8,128)(2,1)S(1)} %add_convert_fusion.4), channel_id=1, source_target_pairs={{0,2},{1,3},{2,0},{3,1},{4,6},{5,7},{6,4},{7,5},{8,10},{9,11},{10,... | collective-permute-start | bytes 3145736 | tf_op jit(solution)/shard_map/ppermute | solution.py:62
  336.6 34.7 %collective-permute-start.57 = (bf16[1,128,3072]{2,1,0:T(8,128)(2,1)S(1)}, bf16[1,128,3072]{2,1,0:T(8,128)(2,1)S(1)}, u32[]{:S(2)}, u32[]{:S(2)}) collective-permute-start(bf16[1,128,3072]{2,1,0:T(8,128)(2,1)S(1)} %get-tuple-element.234), channel_id=1, source_target_pairs={{0,2},{1,3},{2,0},{3,1},{4,6},{5,7},{6,4},{7,5},{8,10},{9,11},{10,... | collective-permute-start | bytes 2359304 | tf_op jit(solution)/shard_map/ppermute | solution.py:62
  337.4 33.9 %collective-permute-start.56 = (bf16[1,128,3072]{2,1,0:T(8,128)(2,1)S(1)}, bf16[1,128,3072]{2,1,0:T(8,128)(2,1)S(1)}, u32[]{:S(2)}, u32[]{:S(2)}) collective-permute-start(bf16[1,128,3072]{2,1,0:T(8,128)(2,1)S(1)} %get-tuple-element.235), channel_id=1, source_target_pairs={{0,4},{4,0},{8,12},{12,8},{16,20},{20,16},{24,28},{28,24},{1,5},{5... | collective-permute-start | bytes 2359304 | tf_op jit(solution)/shard_map/ppermute | solution.py:62
  388.4 24.5 %collective-permute-start.59 = (bf16[2,256,4096]{2,1,0:T(8,128)(2,1)}, bf16[2,256,4096]{2,1,0:T(8,128)(2,1)}, u32[]{:S(2)}, u32[]{:S(2)}) collective-permute-start(bf16[2,256,4096]{2,1,0:T(8,128)(2,1)} %get-tuple-element.160), channel_id=1, source_target_pairs={{0,1},{1,0},{2,3},{3,2},{4,5},{5,4},{6,7},{7,6},{8,9},{9,8},{10,11... | collective-permute-start | bytes 12582920 | tf_op jit(solution)/shard_map/ppermute | solution.py:62
  388.5 24.3 %collective-permute-start.60 = (bf16[1,256,1536]{2,1,0:T(8,128)(2,1)}, bf16[1,256,1536]{2,1,0:T(8,128)(2,1)S(1)}, u32[]{:S(2)}, u32[]{:S(2)}) collective-permute-start(bf16[1,256,1536]{2,1,0:T(8,128)(2,1)} %pad_maximum_fusion.2), channel_id=1, source_target_pairs={{0,8},{4,12},{8,0},{12,4},{16,24},{20,28},{24,16},{28,20},{1,9},{5... | collective-permute-start | bytes 2359304 | tf_op jit(solution)/shard_map/ppermute | solution.py:62
  398.7 28.2 %collective-permute-start.71 = (bf16[1,768,128]{2,1,0:T(8,128)(2,1)S(1)}, bf16[1,768,128]{2,1,0:T(8,128)(2,1)S(1)}, u32[]{:S(2)}, u32[]{:S(2)}) collective-permute-start(bf16[1,768,128]{2,1,0:T(8,128)(2,1)S(1)} %copy-done.56), channel_id=1, source_target_pairs={{0,16},{4,20},{8,24},{12,28},{16,0},{20,4},{24,8},{28,12},{1,17},{... | collective-permute-start | bytes 589832 | tf_op jit(solution)/shard_map/ppermute | solution.py:62
  418.2 22.5 %collective-permute-start.68 = (bf16[1,512,256]{2,1,0:T(8,128)(2,1)}, bf16[1,512,256]{2,1,0:T(8,128)(2,1)S(1)}, u32[]{:S(2)}, u32[]{:S(2)}) collective-permute-start(bf16[1,512,256]{2,1,0:T(8,128)(2,1)} %add_convert_fusion.19), channel_id=1, source_target_pairs={{0,8},{4,12},{8,0},{12,4},{16,24},{20,28},{24,16},{28,20},{1,9},{5... | collective-permute-start | bytes 786440 | tf_op jit(solution)/shard_map/ppermute | solution.py:62
  420.6 38.1 %collective-permute-start.70 = (bf16[1,256,768]{2,1,0:T(8,128)(2,1)}, bf16[1,256,768]{2,1,0:T(8,128)(2,1)S(1)}, u32[]{:S(2)}, u32[]{:S(2)}) collective-permute-start(bf16[1,256,768]{2,1,0:T(8,128)(2,1)} %pad_maximum_fusion.11), channel_id=1, source_target_pairs={{0,16},{4,20},{8,24},{12,28},{16,0},{20,4},{24,8},{28,12},{1,17},{... | collective-permute-start | bytes 1179656 | tf_op jit(solution)/shard_map/ppermute | solution.py:62
  424.1 24.0 %collective-permute-start.62 = (bf16[1,128,4096]{2,1,0:T(8,128)(2,1)S(1)}, bf16[1,128,4096]{2,1,0:T(8,128)(2,1)S(1)}, u32[]{:S(2)}, u32[]{:S(2)}) collective-permute-start(bf16[1,128,4096]{2,1,0:T(8,128)(2,1)S(1)} %add_convert_fusion.3), channel_id=1, source_target_pairs={{0,2},{1,3},{2,0},{3,1},{4,6},{5,7},{6,4},{7,5},{8,10},{9,11},{10,... | collective-permute-start | bytes 3145736 | tf_op jit(solution)/shard_map/ppermute | solution.py:62
  425.7 23.8 %collective-permute-start.64 = (bf16[2,128,2048]{2,1,0:T(8,128)(2,1)S(1)}, bf16[2,128,2048]{2,1,0:T(8,128)(2,1)S(1)}, u32[]{:S(2)}, u32[]{:S(2)}) collective-permute-start(bf16[2,128,2048]{2,1,0:T(8,128)(2,1)S(1)} %add_convert_fusion.2), channel_id=1, source_target_pairs={{0,4},{4,0},{8,12},{12,8},{16,20},{20,16},{24,28},{28,24},{1,5},{5... | collective-permute-start | bytes 3145736 | tf_op jit(solution)/shard_map/ppermute | solution.py:62
  429.9 24.1 %collective-permute-start.81 = (bf16[1,768,128]{2,1,0:T(8,128)(2,1)}, bf16[1,768,128]{2,1,0:T(8,128)(2,1)S(1)}, u32[]{:S(2)}, u32[]{:S(2)}) collective-permute-start(bf16[1,768,128]{2,1,0:T(8,128)(2,1)} %pad_maximum_fusion.20), channel_id=1, source_target_pairs={{0,16},{4,20},{8,24},{12,28},{16,0},{20,4},{24,8},{28,12},{1,17},{... | collective-permute-start | bytes 589832 | tf_op jit(solution)/shard_map/ppermute | solution.py:62
  454.7 88.8 %collective-permute-start.82 = (bf16[2,768,128]{2,1,0:T(8,128)(2,1)}, bf16[2,768,128]{2,1,0:T(8,128)(2,1)}, u32[]{:S(2)}, u32[]{:S(2)}) collective-permute-start(bf16[2,768,128]{2,1,0:T(8,128)(2,1)} %pad_maximum_fusion.14), channel_id=1, source_target_pairs={{0,8},{4,12},{8,0},{12,4},{16,24},{20,28},{24,16},{28,20},{1,9},{5... | collective-permute-start | bytes 1179656 | tf_op jit(solution)/shard_map/ppermute | solution.py:62
  456.5 33.1 %collective-permute-start.75 = (bf16[1,512,128]{2,1,0:T(8,128)(2,1)S(1)}, bf16[1,512,128]{2,1,0:T(8,128)(2,1)S(1)}, u32[]{:S(2)}, u32[]{:S(2)}) collective-permute-start(bf16[1,512,128]{2,1,0:T(8,128)(2,1)S(1)} %fusion.24), channel_id=1, source_target_pairs={{0,16},{4,20},{8,24},{12,28},{16,0},{20,4},{24,8},{28,12},{1,17},{... | collective-permute-start | bytes 393224 | tf_op jit(solution)/shard_map/ppermute | solution.py:62
  467.1 25.8 %collective-permute-start.78 = (bf16[1,256,768]{2,1,0:T(8,128)(2,1)S(1)}, bf16[1,256,768]{2,1,0:T(8,128)(2,1)S(1)}, u32[]{:S(2)}, u32[]{:S(2)}) collective-permute-start(bf16[1,256,768]{2,1,0:T(8,128)(2,1)S(1)} %pad_maximum_fusion.13), channel_id=1, source_target_pairs={{0,16},{4,20},{8,24},{12,28},{16,0},{20,4},{24,8},{28,12},{1,17},{... | collective-permute-start | bytes 1179656 | tf_op jit(solution)/shard_map/ppermute | solution.py:62
  490.4 36.2 %collective-permute-start.76 = (bf16[2,512,128]{2,1,0:T(8,128)(2,1)}, bf16[2,512,128]{2,1,0:T(8,128)(2,1)}, u32[]{:S(2)}, u32[]{:S(2)}) collective-permute-start(bf16[2,512,128]{2,1,0:T(8,128)(2,1)} %pad_maximum_fusion.18), channel_id=1, source_target_pairs={{0,8},{4,12},{8,0},{12,4},{16,24},{20,28},{24,16},{28,20},{1,9},{5... | collective-permute-start | bytes 786440 | tf_op jit(solution)/shard_map/ppermute | solution.py:62
  493.8 35.6 %collective-permute-start.79 = (bf16[2,256,768]{2,1,0:T(8,128)(2,1)}, bf16[2,256,768]{2,1,0:T(8,128)(2,1)}, u32[]{:S(2)}, u32[]{:S(2)}) collective-permute-start(bf16[2,256,768]{2,1,0:T(8,128)(2,1)} %pad_maximum_fusion.4), channel_id=1, source_target_pairs={{0,8},{4,12},{8,0},{12,4},{16,24},{20,28},{24,16},{28,20},{1,9},{5... | collective-permute-start | bytes 2359304 | tf_op jit(solution)/shard_map/ppermute | solution.py:62
  532.0 71.6 %collective-permute-start.80 = (bf16[4,256,768]{2,1,0:T(8,128)(2,1)}, bf16[4,256,768]{2,1,0:T(8,128)(2,1)}, u32[]{:S(2)}, u32[]{:S(2)}) collective-permute-start(bf16[4,256,768]{2,1,0:T(8,128)(2,1)} %pad_maximum_fusion.rest_0_), channel_id=1, source_target_pairs={{0,4},{4,0},{8,12},{12,8},{16,20},{20,16},{24,28},{28,24},{1,5},{5... | collective-permute-start | bytes 4718600 | tf_op jit(solution)/shard_map/ppermute | solution.py:62
  545.5 48.8 %collective-permute-start.83 = (bf16[4,768,128]{2,1,0:T(8,128)(2,1)}, bf16[4,768,128]{2,1,0:T(8,128)(2,1)}, u32[]{:S(2)}, u32[]{:S(2)}) collective-permute-start(bf16[4,768,128]{2,1,0:T(8,128)(2,1)} %pad_maximum_fusion.5.rest_0_), channel_id=1, source_target_pairs={{0,4},{4,0},{8,12},{12,8},{16,20},{20,16},{24,28},{28,24},{1,5},{5... | collective-permute-start | bytes 2359304 | tf_op jit(solution)/shard_map/ppermute | solution.py:62
  556.6 65.4 %collective-permute-start.74 = (bf16[4,256,512]{2,1,0:T(8,128)(2,1)S(1)}, bf16[4,256,512]{2,1,0:T(8,128)(2,1)S(1)}, u32[]{:S(2)}, u32[]{:S(2)}) collective-permute-start(bf16[4,256,512]{2,1,0:T(8,128)(2,1)S(1)} %pad_maximum_fusion.1.rest_0_), channel_id=1, source_target_pairs={{0,4},{4,0},{8,12},{12,8},{16,20},{20,16},{24,28},{28,24},{1,5},{5... | collective-permute-start | bytes 3145736 | tf_op jit(solution)/shard_map/ppermute | solution.py:62
  (125 other events, 1704.9 us)

commit v5 on v4

--- a/solution.py
+++ b/solution.py
@@ -70,49 +70,95 @@
     return lax.optimization_barrier((value, others))[0]
 
 
-def blank(shape, kind):
+def place_rows(pieces, rows, owners):
+    columns = pieces[0][0].shape[1]
+    kind = pieces[0][0].dtype
+    sizes = [v.shape[0] for v, _, _ in pieces]
+
+    def body(*refs):
+        count = len(pieces)
+        ins, out_ref, held = refs[:count], refs[count], refs[count + 1]
+        into, away = refs[count + 2 :]
+        mine = lax.axis_index("group")
+        here = lax.axis_index("dp")
+        arriving, leaving, at = [], [], 0
+        for k, (_, delta, offset) in enumerate(pieces):
+            slot = held.at[pl.ds(at, sizes[k])]
+            start = pl.multiple_of((mine ^ delta) * rows + offset(here), 16)
+            arriving.append(pltpu.make_async_copy(ins[k], slot, into.at[k]))
+            leaving.append(
+                pltpu.make_async_copy(slot, out_ref.at[pl.ds(start, sizes[k])], away.at[k])
+            )
+            at += sizes[k]
+        for copy in arriving:
+            copy.start()
+        for first, second in zip(arriving, leaving):
+            first.wait()
+            second.start()
+        for copy in leaving:
+            copy.wait()
+
     return pl.pallas_call(
-        lambda out_ref: None,
-        out_shape=jax.ShapeDtypeStruct(shape, kind),
+        body,
+        out_shape=jax.ShapeDtypeStruct((rows * owners, columns), kind),
+        in_specs=[pl.BlockSpec(memory_space=pl.ANY)] * len(pieces),
         out_specs=pl.BlockSpec(memory_space=pl.ANY),
-    )()
-
-
-def gather_rows(shard, previous):
+        scratch_shapes=[
+            pltpu.VMEM((rows * owners, columns), kind),
+            pltpu.SemaphoreType.DMA((len(pieces),)),
+            pltpu.SemaphoreType.DMA((len(pieces),)),
+        ],
+        compiler_params=pltpu.CompilerParams(vmem_limit_bytes=32 * 1024 * 1024),
+        cost_estimate=pl.CostEstimate(
+            flops=0, bytes_accessed=4 * rows * owners * columns, transcendentals=0
+        ),
+    )(*[v for v, _, _ in pieces])
+
+
+def gather_rows(shard, early, late, middle, hold):
     owners = lax.axis_size("group")
     copies = lax.axis_size("dp")
-    mine = lax.axis_index("group")
     here = lax.axis_index("dp")
-    if previous is not None:
-        shard = after(shard, previous)
+    if early is not None:
+        shard = after(shard, early)
     shard = shard.astype(jnp.bfloat16)
-    rows, columns = shard.shape
-    pieces = [(shard, 0, 0)]
-    order = by_one = by_two = shard
+    rows, _ = shard.shape
+
+    def none(_):
+        return 0
+
+    pieces = [(shard, 0, none)]
+    near = order = by_one = by_two = shard
     if owners == 4 and copies % 4 == 0 and rows % 128 == 0:
         quarter, half = rows // 4, rows // 8
-        place = (here & 1) * 2 + ((here >> 1) & 1)
-        near = lax.dynamic_slice_in_dim(shard, place * quarter, quarter, 0)
+
+        def place(here):
+            return (here & 1) * 2 + ((here >> 1) & 1)
+
+        def quarter_at(mask, more=0):
+            return lambda here: (place(here) ^ mask) * quarter + more
+
+        near = lax.dynamic_slice_in_dim(shard, place(here) * quarter, quarter, 0)
+        if late is not None:
+            near = after(near, late)
         order = swap(near, "group", 2)
-        by_one = swap(order, "dp", 1)
-        by_two = swap(order, "dp", 2)
-        last = (place ^ 3) * quarter
+        passed = order if middle is None else after(order, middle)
+        by_one = swap(passed, "dp", 1)
+        by_two = swap(passed, "dp", 2)
         pieces += [
-            (order, 2, place * quarter),
-            (by_one, 2, (place ^ 2) * quarter),
-            (by_two, 2, (place ^ 1) * quarter),
-            (swap(by_two[:half], "dp", 1), 2, last),
-            (swap(by_one[half:], "dp", 2), 2, last + half),
+            (order, 2, quarter_at(0)),
+            (by_one, 2, quarter_at(2)),
+            (by_two, 2, quarter_at(1)),
+            (swap(by_two[:half], "dp", 1), 2, quarter_at(3)),
+            (swap(by_one[half:], "dp", 2), 2, quarter_at(3, half)),
         ]
     else:
         for mask in bit_masks(owners)[1:]:
-            pieces += [(swap(v, "group", mask), dg ^ mask, off) for v, dg, off in pieces]
-    pieces += [(swap(v, "group", 1), dg ^ 1, off) for v, dg, off in pieces]
-    full = blank((rows * owners, columns), shard.dtype)
-    for value, delta, offset in pieces:
-        start = (mine ^ delta) * rows + offset
-        full = lax.dynamic_update_slice(full, value, (start, 0))
-    return full, order, (by_one, by_two)
+            pieces += [(swap(v, "group", mask), dg ^ mask, at) for v, dg, at in pieces]
+    pieces += [(swap(v, "group", 1), dg ^ 1, at) for v, dg, at in pieces]
+    if hold is not None:
+        pieces[0] = (after(shard, hold), 0, none)
+    return place_rows(pieces, rows, owners), near, order, (by_one, by_two)
 
 
 def gather_small(shard):
@@ -493,7 +539,14 @@
 SPAN = 256
 
 
-def span_weights(query_low, key_low, seg_row_ref, seg_col_ref, start):
+def fill_bias(bias_ref, row_ref, col_ref):
+    key_at = lax.broadcasted_iota(jnp.int32, (SEQ_LEN, SEQ_LEN), 0)
+    query_at = lax.broadcasted_iota(jnp.int32, (SEQ_LEN, SEQ_LEN), 1)
+    allowed = (key_at <= query_at) & (col_ref[...] == row_ref[...])
+    bias_ref[...] = jnp.where(allowed, 0.0, MASKED)
+
+
+def span_weights(query_low, key_low, bias_ref, start):
     stop = start + SPAN
     scores = lax.dot_general(
         key_low[:stop],
@@ -501,17 +554,18 @@
         (((1,), (1,)), ((), ())),
         preferred_element_type=jnp.float32,
     ) * (1.0 / math.sqrt(HD))
-    key_at = lax.broadcasted_iota(jnp.int32, (stop, SPAN), 0)
-    query_at = lax.broadcasted_iota(jnp.int32, (stop, SPAN), 1) + start
-    allowed = (key_at <= query_at) & (seg_col_ref[:stop, :] == seg_row_ref[:, start:stop])
-    scores = jnp.where(allowed, scores, MASKED)
+    scores = scores + bias_ref[:stop, start:stop]
     raised = jnp.exp(scores - jnp.max(scores, axis=0, keepdims=True))
     return raised * (1.0 / jnp.sum(raised, axis=0, keepdims=True))
 
 
 def attend_body(
-    query_ref, key_ref, value_ref, cos_ref, sin_ref, row_ref, col_ref, gain_ref, out_ref
+    query_ref, key_ref, value_ref, cos_ref, sin_ref, row_ref, col_ref, gain_ref, out_ref, bias_ref
 ):
+    @pl.when(pl.program_id(1) == 0)
+    def _():
+        fill_bias(bias_ref, row_ref, col_ref)
+
     cosine, sine = cos_ref[...], sin_ref[...]
     key_low, _, _ = head_forward(key_ref[...], gain_ref[1:2, :], cosine, sine)
     value_turned = value_ref[...].astype(jnp.bfloat16).T
@@ -520,7 +574,7 @@
         query_low, _, _ = head_forward(query_ref[:, at], gain_ref[0:1, :], cosine, sine)
         for start in range(0, SEQ_LEN, SPAN):
             stop = start + SPAN
-            weights = span_weights(query_low, key_low, row_ref, col_ref, start)
+            weights = span_weights(query_low, key_low, bias_ref, start)
             mixed = jnp.dot(
                 value_turned[:, :stop],
                 weights.astype(jnp.bfloat16),
@@ -534,8 +588,13 @@
     *rest,
     first,
 ):
-    out_ref, gain_out_ref = rest[-2:]
+    out_ref, gain_out_ref, bias_ref = rest[-3:]
     head = pl.program_id(1) + first
+
+    @pl.when(head == first)
+    def _():
+        fill_bias(bias_ref, row_ref, col_ref)
+
     cosine, sine = cos_ref[...], sin_ref[...]
     inv_head = 1.0 / math.sqrt(HD)
 
@@ -543,7 +602,7 @@
     def _():
         gain_out_ref[...] = jnp.zeros_like(gain_out_ref)
 
-    if len(rest) == 3:
+    if len(rest) == 4:
 
         @pl.when(head == first)
         def _():
@@ -561,7 +620,7 @@
         grad_query = []
         for start in range(0, SEQ_LEN, SPAN):
             stop = start + SPAN
-            weights = span_weights(query_low, key_low, row_ref, col_ref, start)
+            weights = span_weights(query_low, key_low, bias_ref, start)
             grad_out = grad_ref[start:stop, at]
             grad_weights = lax.dot_general(
                 value_low[:stop],
@@ -669,6 +728,7 @@
         out_specs=out_specs,
         out_shape=out_shape,
         input_output_aliases=aliases,
+        scratch_shapes=[pltpu.VMEM((SEQ_LEN, SEQ_LEN), jnp.float32)],
         compiler_params=pltpu.CompilerParams(vmem_limit_bytes=48 * 1024 * 1024),
         cost_estimate=pl.CostEstimate(
             flops=(4 if grad_out is None else 10) * pairs * HD * 2,
@@ -742,9 +802,7 @@
     gains_all = gather_small(gains_low).reshape(2, owners, -1)
     full_norm = gains_all[:, :, :width].reshape(2, -1)
     full_head = gains_all[:, :, width:].reshape(2, -1)
-    full_qkv, _, order = gather_rows(qkv_weight, None)
-    full_out, order, _ = gather_rows(out_weight, order)
-    full_gate_up, order, _ = gather_rows(gate_up_weight, order)
+    full_qkv, first, _, late = gather_rows(qkv_weight, None, None, None, None)
     gain_one = full_norm[0].astype(jnp.float32)
     gain_two = full_norm[1].astype(jnp.float32)
     head_gain = full_head.astype(jnp.float32)
@@ -753,7 +811,9 @@
     normed_one = inputs * root_one
     hidden_one = (normed_one * gain_one).astype(jnp.bfloat16)
     projected = jnp.dot(hidden_one, full_qkv, preferred_element_type=jnp.float32)
-    full_down, _, _ = gather_rows(down_weight, (order, projected))
+    full_out, _, late, _ = gather_rows(out_weight, first, late, None, projected)
+    full_gate_up, _, late, _ = gather_rows(gate_up_weight, first, late, projected, None)
+    full_down, _, _, _ = gather_rows(down_weight, first, late, None, None)
     tables = rotary_tables(positions, HD)
     mixed_low = attention_call(attend_body, projected, tables, segment_ids, head_gain, None, 0, HK, None)
     attended = jnp.dot(mixed_low, full_out, preferred_element_type=jnp.float32)
@@ -778,7 +838,7 @@
     residual_low = grad_residual.astype(jnp.bfloat16)
     down_sum.hold(residual_low)
     sent = down_sum.advance() + gate_up_sum.advance()
-    out_sum = GradSum(mixed_low, after(residual_low, *sent), False)
+    out_sum = GradSum(mixed_low, after(residual_low, *sent), True)
     down_sum.hold(out_sum.blocks)
     grad_mixed = contract_cols(
         after(residual_low, *out_sum.blocks, *down_sum.advance()), full_out
@@ -822,24 +882,24 @@
         axis=1,
     )
     owned = tuple(v.finish() for v in (qkv_sum, out_sum, gate_up_sum, down_sum))
+    qkv_own, out_own, gate_up_own, down_own = owned
+    down_gathered = gather_grad(down_own, None)
     local = sum(jnp.sum(v * v) for v in owned)
-    summed = sum_all(
-        jnp.concatenate(
-            [small, jnp.full((6, small.shape[1]), local, jnp.float32)], axis=0
-        )
-    )
+    partial = jnp.concatenate(
+        [small, jnp.full((6, small.shape[1]), local, jnp.float32)], axis=0
+    )
+    summed = sum_all(after(partial, down_gathered[0][0]))
     small = summed[:2]
     norm_total = small[:, :-HD]
     head_total = small[:, -HD:]
     squares = summed[2, 0] + jnp.sum(small * small)
     clip_limit = math.sqrt(PARAMS)
     factor = clip_limit / jnp.maximum(jnp.sqrt(squares), clip_limit)
-    qkv_own, out_own, gate_up_own, down_own = owned
     gathered = [
         gather_grad(after(qkv_own, summed), None),
         gather_grad(out_own, None),
         gather_grad(gate_up_own, summed),
-        gather_grad(down_own, None),
+        down_gathered,
     ]
     masters = (qkv_weight, out_weight, gate_up_weight, down_weight)
     moments = (qkv_moments, out_moments, gate_up_moments, down_moments)
@@ -847,7 +907,7 @@
     renewed = [
         adam_blocks(master, moment, blocks, scale, LEARN_RATE, WEIGHT_DECAY)
         for master, moment, blocks, scale in zip(
-            masters, moments, gathered, (later, factor, later, later)
+            masters, moments, gathered, (later, later, later, factor)
         )
     ]
     mine = lax.axis_index("group")

time: 643 us -> 624 us (0.970)
  local copies, waits for them, and re-layouts: 52.5 us -> 25.6 us
  waiting for transfers between devices: 186 us -> 162 us
  Pallas kernels: 170 us -> 183 us
  starting transfers between devices: 64.5 us -> 72.7 us
  matrix products: 53.5 us -> 60.2 us
    dynamic_update_slice x44 -> x0, local copies, waits for them, and re-layouts: 32.8 us -> none  [gather_rows(): full = lax.dynamic_update_slice(full, value, (start, 0))]
    ppermute x84 -> x86, waiting for transfers between devices: 186 us -> 162 us  [swap(): return lax.ppermute(value, axis, [(i, i ^ mask) for i in range(count)])]
    pallas_call x4, Pallas kernels: 0.01 us -> 18.3 us  [place_rows(): pl.pallas_call(body, out_shape=jax.ShapeDtypeStruct((rows * owners, colum...]
    dynamic_update_slice x4 -> x0, other arithmetic: 13.9 us -> none  [gather_rows(): full = lax.dynamic_update_slice(full, value, (start, 0))]
    convert_element_type x1 -> x4, other arithmetic: 1.08 us -> 9.67 us  [gather_rows(): shard = shard.astype(jnp.bfloat16)]
    ppermute x84 -> x86, starting transfers between devices: 64.5 us -> 72.7 us  [swap(): return lax.ppermute(value, axis, [(i, i ^ mask) for i in range(count)])]
    convert_element_type x19 -> x20, other arithmetic: 36.1 us -> 36.1 us  [advance(): outgoing.append((self.read(far).astype(jnp.bfloat16), axis, mask))]
  transfers between devices with their start and end apart: 84 -> 86, of which waited for: 33 -> 29; matrix products, arithmetic and copies ran while one was open for 27% -> 22% of each run, Pallas kernels for 19% -> 21%
where the time goes in v5:
time: 624 us; the launch traced here: 611 us
  Pallas kernels  183 us (29%)
  waiting for transfers between devices  162 us (26%)
  other arithmetic  101 us (16%)
  starting transfers between devices  72.7 us (12%)
  matrix products  60.2 us (10%)
  local copies, waits for them, and re-layouts  25.6 us (4%)
  between operations  6.41 us (1%)
    ppermute x86, waiting for transfers between devices, swap(): return lax.ppermute(value, axis, [(i, i ^ mask) for i in range(count)])  162 us
    ppermute x86, starting transfers between devices, swap(): return lax.ppermute(value, axis, [(i, i ^ mask) for i in range(count)])  72.7 us
    pallas_call x3, Pallas kernels, attention_call(): pl.pallas_call(body, grid=(seq_count, count), in_specs=in_specs, out_spec...  54.6 us
    pallas_call x4, Pallas kernels, adam_blocks(): pl.pallas_call(body, out_shape=[jax.ShapeDtypeStruct(master.shape, jnp.fl...  43.2 us
    pallas_call x4, Pallas kernels, grad_blocks(): pl.pallas_call(body, out_shape=[jax.ShapeDtypeStruct((len(row_set), row_b...  38.6 us
    convert_element_type x20, other arithmetic, advance(): outgoing.append((self.read(far).astype(jnp.bfloat16), axis, mask))  36.1 us
    dot_general x3, matrix products, contract_cols(): lax.dot_general(left_side, right_side, (((1,), (1,)), ((), ())), preferre...  27.7 us
    pallas_call x4, Pallas kernels, place_rows(): pl.pallas_call(body, out_shape=jax.ShapeDtypeStruct((rows * owners, colum...  18.3 us
  transfers between devices with their start and end apart: 86, of which 29 were waited for; matrix products, arithmetic and copies ran while one was open for 22% of the time, Pallas kernels for 21%

profile of v5, /device:TPU:0, one launch (start us, length us, event | category | flops | bytes accessed | tf_op | source)
XLA Modules:
  0.0 611.5 jit_solution(14262865671189806793)
XLA Ops:
  12.1 9.2 %collective-permute-done.2.refs_1_ = bf16[64,4096]{1,0:T(8,128)(2,1)} collective-permute-done((bf16[64,4096]{1,0:T(8,128)(2,1)S(1)}, bf16[64,4096]{1,0:T(8,128)(2,1)}, u32[]{:S(2)}, u32[]{:S(2)}) %collective-permute-start.2) | collective-permute-done | bytes 524320 | tf_op jit(solution)/shard_map/ppermute | solution.py:62
  26.7 9.9 %collective-permute-done.4.refs_3_ = bf16[64,4096]{1,0:T(8,128)(2,1)} collective-permute-done((bf16[64,4096]{1,0:T(8,128)(2,1)}, bf16[64,4096]{1,0:T(8,128)(2,1)}, u32[]{:S(2)}, u32[]{:S(2)}) %collective-permute-start.4) | collective-permute-done | bytes 524320 | tf_op jit(solution)/shard_map/ppermute | solution.py:62
  73.1 6.7 %fusion.33.query_ref.key_ref.value_ref = f32[512,4096]{1,0:T(8,128)} fusion(bf16[512,1024]{1,0:T(8,128)(2,1)S(1)} %fusion.5.left_ref, bf16[1024,4096]{1,0:T(8,128)(2,1)S(1)} %shard_map.311), kind=kOutput, calls=%fused_computation.148 | convolution fusion | flops 4294967296 | bytes 17825792 | tf_op jit(solution)/shard_map/dot_general | solution.py:813
  97.4 18.2 %shard_map.312.left_ref = bf16[512,2048]{1,0:T(8,128)(2,1)S(1)} custom-call(f32[512,4096]{1,0:T(8,128)} %fusion.33.query_ref.key_ref.value_ref, f32[512,4096]{1,0:T(8,128)} %fusion.33.query_ref.key_ref.value_ref, f32[512,4096]{1,0:T(8,128)} %fusion.33.query_ref.key_ref.value_ref, f32[512,128]{1,0:T(8,128)S(1)} %get-tuple-element.289.cos_ref, ...), custom_call_target="tpu_custom_call" | custom-call | flops 4294967296 | bytes 12582912 | tf_op jit(solution)/shard_map/pallas_call | solution.py:724
  131.4 7.7 %shard_map.314 = bf16[1024,6144]{1,0:T(8,128)(2,1)} custom-call(bf16[256,6144]{1,0:T(8,128)(2,1)S(1)} %convert_element_type.690.refs_0_, bf16[64,6144]{1,0:T(8,128)(2,1)} %collective-permute-done.24.refs_1_, bf16[64,6144]{1,0:T(8,128)(2,1)} %collective-permute-done.25.refs_2_, bf16[64,6144]{1,0:T(8,128)(2,1)} %collective-permute-done.26.refs_3_, ...), custom_call_target="tpu_custom_call" | custom-call | bytes 25165824 | tf_op jit(solution)/shard_map/pallas_call | solution.py:101
  139.1 14.4 %fusion.34.gate_ref.up_ref = f32[512,6144]{1,0:T(8,128)} fusion(bf16[512,1024]{1,0:T(8,128)(2,1)S(1)} %multiply_convert_fusion.left_ref, bf16[1024,6144]{1,0:T(8,128)(2,1)} %shard_map.314), kind=kOutput, calls=%fused_computation.149 | convolution fusion | flops 6442450944 | bytes 26214400 | tf_op jit(solution)/shard_map/dot_general | solution.py:824
  153.4 6.8 %fusion.left_ref = bf16[512,3072]{1,0:T(8,128)(2,1)} fusion(f32[512,6144]{1,0:T(8,128)} %fusion.34.gate_ref.up_ref), kind=kLoop, calls=%fused_computation.1 | loop fusion | flops 9437184 | bytes 15728640 | tf_op jit(solution)/shard_map/convert_element_type | solution.py:828
  160.2 8.8 %shard_map.316 = (bf16[2,768,1024]{2,1,0:T(8,128)(2,1)}, bf16[2,768,1024]{2,1,0:T(8,128)(2,1)}) custom-call(s32[2]{0:T(128)S(1)} %pad_add_fusion.where, bf16[512,3072]{1,0:T(8,128)(2,1)} %fusion.left_ref, bf16[512,1024]{1,0:T(8,128)(2,1)S(1)} %copy-done.2, bf16[512,1024]{1,0:T(8,128)(2,1)S(1)} %copy-done.2), custom_call_target="tpu_custom_call" | custom-call | flops 3221225472 | bytes 10485760 | tf_op jit(solution)/shard_map/pallas_call | solution.py:306
  172.9 10.3 %collective-permute-done.35.refs_1_ = bf16[192,1024]{1,0:T(8,128)(2,1)S(1)} collective-permute-done((bf16[192,1024]{1,0:T(8,128)(2,1)S(1)}, bf16[192,1024]{1,0:T(8,128)(2,1)S(1)}, u32[]{:S(2)}, u32[]{:S(2)}) %collective-permute-start.35) | collective-permute-done | bytes 393248 | tf_op jit(solution)/shard_map/ppermute | solution.py:62
  185.2 8.2 %collective-permute-done.37.refs_3_ = bf16[192,1024]{1,0:T(8,128)(2,1)S(1)} collective-permute-done((bf16[192,1024]{1,0:T(8,128)(2,1)S(1)}, bf16[192,1024]{1,0:T(8,128)(2,1)S(1)}, u32[]{:S(2)}, u32[]{:S(2)}) %collective-permute-start.37) | collective-permute-done | bytes 393248 | tf_op jit(solution)/shard_map/ppermute | solution.py:62
  211.5 12.9 %shard_map.317.rest_0_ = bf16[512,6144]{1,0:T(8,128)(2,1)} custom-call(bf16[512,1024]{1,0:T(8,128)(2,1)S(1)} %copy-done.3, bf16[3072,1024]{1,0:T(8,128)(2,1)} %copy-done, f32[512,6144]{1,0:T(8,128)} %fusion.34.gate_ref.up_ref, f32[512,6144]{1,0:T(8,128)} %fusion.34.gate_ref.up_ref), custom_call_target="tpu_custom_call" | custom-call | flops 3221225472 | bytes 25165824 | tf_op jit(solution)/shard_map/pallas_call | solution.py:761
  229.1 12.6 %shard_map.318 = (bf16[2,256,6144]{2,1,0:T(8,128)(2,1)}, bf16[2,256,6144]{2,1,0:T(8,128)(2,1)}) custom-call(s32[2]{0:T(128)S(1)} %pad_add_fusion.where, bf16[512,1024]{1,0:T(8,128)(2,1)S(1)} %copy-done.21, bf16[512,6144]{1,0:T(8,128)(2,1)} %shard_map.317.rest_0_), custom_call_target="tpu_custom_call" | custom-call | flops 6442450944 | bytes 19922944 | tf_op jit(solution)/shard_map/pallas_call | solution.py:306
  243.6 15.2 %multiply_reduce_fusion = (f32[1024]{0:T(1024)}, f32[512]{0:T(512)S(1)}, f32[512,1024]{1,0:T(8,128)}) fusion(f32[512,1024]{1,0:T(8,128)} %copy-done.35, f32[512]{0:T(512)S(1)} %add_rsqrt_fusion, f32[1024]{0:T(1024)S(1)} %bitcast.93, bf16[512,6144]{1,0:T(8,128)(2,1)} %shard_map.317.rest_0_, bf16[1024,6144]{1,0:T(8,128)(2,1)} %shard_map.314), kind=kOutput, calls=%fused_computation.20 | convolution fusion | flops 6445595136 | bytes 23080960 | tf_op jit(solution)/shard_map/dot_general | solution.py:50
  270.4 6.8 %shard_map.319 = (bf16[2,512,1024]{2,1,0:T(8,128)(2,1)S(1)}, bf16[2,512,1024]{2,1,0:T(8,128)(2,1)S(1)}) custom-call(s32[2]{0:T(128)S(1)} %pad_add_fusion.where, bf16[512,2048]{1,0:T(8,128)(2,1)} %copy-done.16, bf16[512,1024]{1,0:T(8,128)(2,1)S(1)} %fusion.32.rest_0_.rest_1_, bf16[512,1024]{1,0:T(8,128)(2,1)S(1)} %fusion.32.rest_0_.rest_1_), custom_call_target="tpu_custom_call" | custom-call | flops 2147483648 | bytes 7340032 | tf_op jit(solution)/shard_map/pallas_call | solution.py:306
  281.4 7.9 %collective-permute-done.50 = bf16[1,384,512]{2,1,0:T(8,128)(2,1)S(1)} collective-permute-done((bf16[1,384,512]{2,1,0:T(8,128)(2,1)S(1)}, bf16[1,384,512]{2,1,0:T(8,128)(2,1)S(1)}, u32[]{:S(2)}, u32[]{:S(2)}) %collective-permute-start.50) | collective-permute-done | bytes 393248 | tf_op jit(solution)/shard_map/ppermute | solution.py:62
  298.9 17.5 %shard_map.320 = (bf16[512,4096]{1,0:T(8,128)(2,1)}, f32[2,128]{1,0:T(2,128)S(1)}) custom-call(f32[512,4096]{1,0:T(8,128)} %fusion.33.query_ref.key_ref.value_ref, f32[512,4096]{1,0:T(8,128)} %fusion.33.query_ref.key_ref.value_ref, f32[512,4096]{1,0:T(8,128)} %fusion.33.query_ref.key_ref.value_ref, f32[512,128]{1,0:T(8,128)S(1)} %get-tuple-element.289.cos_ref, ...), custom_call_target="tpu_custom_call" | custom-call | flops 5368709120 | bytes 12582912 | tf_op jit(solution)/shard_map/pallas_call | solution.py:724
  316.4 7.8 %collective-permute-done.53 = bf16[1,128,6144]{2,1,0:T(8,128)(2,1)S(1)} collective-permute-done((bf16[1,128,6144]{2,1,0:T(8,128)(2,1)}, bf16[1,128,6144]{2,1,0:T(8,128)(2,1)S(1)}, u32[]{:S(2)}, u32[]{:S(2)}) %collective-permute-start.53) | collective-permute-done | bytes 1572896 | tf_op jit(solution)/shard_map/ppermute | solution.py:62
  332.1 18.9 %shard_map.321 = (bf16[512,4096]{1,0:T(8,128)(2,1)}, f32[2,128]{1,0:T(2,128)S(1)}) custom-call(f32[512,4096]{1,0:T(8,128)} %fusion.33.query_ref.key_ref.value_ref, f32[512,4096]{1,0:T(8,128)} %fusion.33.query_ref.key_ref.value_ref, f32[512,4096]{1,0:T(8,128)} %fusion.33.query_ref.key_ref.value_ref, ...), custom_call_target="tpu_custom_call", output_to_operand_aliasing={{0}: (9, {})} | custom-call | flops 5368709120 | bytes 12582912 | tf_op jit(solution)/shard_map/pallas_call | solution.py:724
  356.9 10.4 %shard_map.322 = (bf16[2,256,4096]{2,1,0:T(8,128)(2,1)}, bf16[2,256,4096]{2,1,0:T(8,128)(2,1)}) custom-call(s32[2]{0:T(128)S(1)} %pad_add_fusion.where, bf16[512,1024]{1,0:T(8,128)(2,1)S(1)} %copy-done.19, bf16[512,4096]{1,0:T(8,128)(2,1)} %get-tuple-element.197.rest_0_), custom_call_target="tpu_custom_call" | custom-call | flops 4294967296 | bytes 13631488 | tf_op jit(solution)/shard_map/pallas_call | solution.py:306
  368.0 9.0 %add_convert_fusion.4 = bf16[512,1024]{1,0:T(8,128)(2,1)} fusion(f32[512,1024]{1,0:T(8,128)} %copy-done.35, bf16[512,3072]{1,0:T(8,128)(2,1)} %fusion.left_ref, bf16[3072,1024]{1,0:T(8,128)(2,1)} %copy-done), kind=kOutput, calls=%fused_computation.25 | convolution fusion | flops 3222274048 | bytes 12582912 | tf_op jit(solution)/shard_map/dot_general | solution.py:829
  382.4 9.4 %collective-permute-done.61 = bf16[1,256,1536]{2,1,0:T(8,128)(2,1)S(1)} collective-permute-done((bf16[1,256,1536]{2,1,0:T(8,128)(2,1)}, bf16[1,256,1536]{2,1,0:T(8,128)(2,1)S(1)}, u32[]{:S(2)}, u32[]{:S(2)}) %collective-permute-start.61) | collective-permute-done | bytes 786464 | tf_op jit(solution)/shard_map/ppermute | solution.py:62
  403.8 10.2 %fusion.11 = (f32[1024]{0:T(1024)}, f32[512]{0:T(512)S(1)}, f32[512,1024]{1,0:T(8,128)}) fusion(bf16[512,1024]{1,0:T(8,128)(2,1)S(1)} %copy-done.39, f32[512]{0:T(512)S(1)} %copy-done.76, f32[1024]{0:T(1024)S(1)} %bitcast.97, bf16[512,4096]{1,0:T(8,128)(2,1)S(1)} %copy-done.42, bf16[1024,4096]{1,0:T(8,128)(2,1)} %copy-done.5), kind=kOutput, calls=%fused_computation.18 | convolution fusion | flops 4298635776 | bytes 15740928 | tf_op jit(solution)/shard_map/dot_general | solution.py:50
  422.8 10.2 %collective-permute-done.74 = bf16[1,768,128]{2,1,0:T(8,128)(2,1)S(1)} collective-permute-done((bf16[1,768,128]{2,1,0:T(8,128)(2,1)S(1)}, bf16[1,768,128]{2,1,0:T(8,128)(2,1)S(1)}, u32[]{:S(2)}, u32[]{:S(2)}) %collective-permute-start.74) | collective-permute-done | bytes 196640 | tf_op jit(solution)/shard_map/ppermute | solution.py:62
  443.4 5.8 collective-permute-done.65
  459.2 11.7 %collective-permute-done.68 = bf16[1,256,1024]{2,1,0:T(8,128)(2,1)S(1)} collective-permute-done((bf16[1,256,1024]{2,1,0:T(8,128)(2,1)S(1)}, bf16[1,256,1024]{2,1,0:T(8,128)(2,1)S(1)}, u32[]{:S(2)}, u32[]{:S(2)}) %collective-permute-start.68) | collective-permute-done | bytes 524320 | tf_op jit(solution)/shard_map/ppermute | solution.py:62
  477.9 6.0 collective-permute-done.69
  490.8 15.1 %shard_map.323 = f32[8,1152]{1,0:T(8,128)} custom-call(f32[8,1152]{1,0:T(8,128)} %select_maximum_fusion.in_ref), custom_call_target="tpu_custom_call" | custom-call | tf_op jit(solution)/shard_map/pallas_call | solution.py:220
  515.7 6.0 collective-permute-done.76
  533.5 9.1 %shard_map.327 = (f32[768,1024]{1,0:T(8,128)}, f32[2,768,1024]{2,1,0:T(8,128)}) custom-call(s32[1]{0:T(128)} %bitcast.8.where, f32[1,1]{1,0:T(1,128)} %bitcast.22.factor_ref, f32[768,1024]{1,0:T(8,128)S(1)} %copy-done.1, f32[2,768,1024]{2,1,0:T(8,128)} %moment_ref.7, bf16[4,768,128]{2,1,0:T(8,128)(2,1)S(1)} %copy-done.15, ...), custom_call_target="tpu_custom_call" | custom-call | flops 15728640 | bytes 20447232 | tf_op jit(solution)/shard_map/pallas_call | solution.py:473
  547.6 29.3 %collective-permute-done.81.rest_1_ = bf16[4,512,128]{2,1,0:T(8,128)(2,1)} collective-permute-done((bf16[4,512,128]{2,1,0:T(8,128)(2,1)}, bf16[4,512,128]{2,1,0:T(8,128)(2,1)}, u32[]{:S(2)}, u32[]{:S(2)}) %collective-permute-start.81) | collective-permute-done | bytes 524320 | tf_op jit(solution)/shard_map/ppermute | solution.py:62
  582.2 18.4 %shard_map.326 = (f32[256,6144]{1,0:T(8,128)}, f32[2,256,6144]{2,1,0:T(8,128)}) custom-call(s32[1]{0:T(128)} %bitcast.8.where, f32[1,1]{1,0:T(1,128)} %bitcast.21.factor_ref, f32[256,6144]{1,0:T(8,128)} %master_ref.6, f32[2,256,6144]{2,1,0:T(8,128)} %moment_ref.6, bf16[4,256,768]{2,1,0:T(8,128)(2,1)} %pad_maximum_fusion.rest_0_, ...), custom_call_target="tpu_custom_call" | custom-call | flops 31457280 | bytes 40894464 | tf_op jit(solution)/shard_map/pallas_call | solution.py:473
  600.5 10.5 %shard_map.324 = (f32[256,4096]{1,0:T(8,128)}, f32[2,256,4096]{2,1,0:T(8,128)}) custom-call(s32[1]{0:T(128)} %bitcast.8.where, f32[1,1]{1,0:T(1,128)} %bitcast.21.factor_ref, f32[256,4096]{1,0:T(8,128)} %master_ref.4, f32[2,256,4096]{2,1,0:T(8,128)} %moment_ref.4, bf16[4,256,512]{2,1,0:T(8,128)(2,1)S(1)} %pad_maximum_fusion.1.rest_0_, ...), custom_call_target="tpu_custom_call" | custom-call | flops 20971520 | bytes 27262976 | tf_op jit(solution)/shard_map/pallas_call | solution.py:473
  (458 shorter events, 244.4 us)
Async XLA Ops:
  4.5 62.9 %collective-permute-start.7 = (bf16[256,4096]{1,0:T(8,128)(2,1)}, bf16[256,4096]{1,0:T(8,128)(2,1)}, u32[]{:S(2)}, u32[]{:S(2)}) collective-permute-start(bf16[256,4096]{1,0:T(8,128)(2,1)} %convert_element_type.682.refs_0_), channel_id=1, source_target_pairs={{0,1},{1,0},{2,3},{3,2},{4,5},{5,4},{6,7},{7,6},{8,9},{9,8},{10,11... | collective-permute-start | bytes 6291464 | tf_op jit(solution)/shard_map/ppermute | solution.py:62
  8.6 31.2 %collective-permute-start = (bf16[1,2,288]{2,1,0:T(2,128)(2,1)S(1)}, bf16[1,2,288]{2,1,0:T(2,128)(2,1)S(1)}, u32[]{:S(2)}, u32[]{:S(2)}) collective-permute-start(bf16[1,2,288]{2,1,0:T(2,128)(2,1)S(1)} %pad_maximum_fusion.29), channel_id=1, source_target_pairs={{0,2},{1,3},{2,0},{3,1},{4,6},{5,7},{6,4},{7,5},{8,10},{9,11},{10,... | collective-permute-start | bytes 3464 | tf_op jit(solution)/shard_map/ppermute | solution.py:62
  50.5 21.0 %collective-permute-start.18 = (bf16[512,1024]{1,0:T(8,128)(2,1)}, bf16[512,1024]{1,0:T(8,128)(2,1)}, u32[]{:S(2)}, u32[]{:S(2)}) collective-permute-start(bf16[512,1024]{1,0:T(8,128)(2,1)} %convert_element_type.686.refs_0_), channel_id=1, source_target_pairs={{0,1},{1,0},{2,3},{3,2},{4,5},{5,4},{6,7},{7,6},{8,9},{9,8},{10,11... | collective-permute-start | bytes 3145736 | tf_op jit(solution)/shard_map/ppermute | solution.py:62
  51.9 20.7 %collective-permute-start.24 = (bf16[64,6144]{1,0:T(8,128)(2,1)}, bf16[64,6144]{1,0:T(8,128)(2,1)}, u32[]{:S(2)}, u32[]{:S(2)}) collective-permute-start(bf16[64,6144]{1,0:T(8,128)(2,1)} %constant_dynamic-slice_fusion.3), channel_id=1, source_target_pairs={{0,2},{1,3},{2,0},{3,1},{4,6},{5,7},{6,4},{7,5},{8,10},{9,11},{10,... | collective-permute-start | bytes 2359304 | tf_op jit(solution)/shard_map/ppermute | solution.py:62
  66.8 63.1 %collective-permute-start.29 = (bf16[256,6144]{1,0:T(8,128)(2,1)S(1)}, bf16[256,6144]{1,0:T(8,128)(2,1)}, u32[]{:S(2)}, u32[]{:S(2)}) collective-permute-start(bf16[256,6144]{1,0:T(8,128)(2,1)S(1)} %convert_element_type.690.refs_0_), channel_id=1, source_target_pairs={{0,1},{1,0},{2,3},{3,2},{4,5},{5,4},{6,7},{7,6},{8,9},{9,8},{10,11... | collective-permute-start | bytes 9437192 | tf_op jit(solution)/shard_map/ppermute | solution.py:62
  80.0 37.6 %collective-permute-start.25 = (bf16[64,6144]{1,0:T(8,128)(2,1)}, bf16[64,6144]{1,0:T(8,128)(2,1)}, u32[]{:S(2)}, u32[]{:S(2)}) collective-permute-start(bf16[64,6144]{1,0:T(8,128)(2,1)} %collective-permute-done.24.refs_1_), channel_id=1, source_target_pairs={{0,4},{4,0},{8,12},{12,8},{16,20},{20,16},{24,28},{28,24},{1,5},{5... | collective-permute-start | bytes 2359304 | tf_op jit(solution)/shard_map/ppermute | solution.py:62
  81.8 33.9 %collective-permute-start.26 = (bf16[64,6144]{1,0:T(8,128)(2,1)}, bf16[64,6144]{1,0:T(8,128)(2,1)}, u32[]{:S(2)}, u32[]{:S(2)}) collective-permute-start(bf16[64,6144]{1,0:T(8,128)(2,1)} %collective-permute-done.24.refs_1_), channel_id=1, source_target_pairs={{0,8},{4,12},{8,0},{12,4},{16,24},{20,28},{24,16},{28,20},{1,9},{5... | collective-permute-start | bytes 2359304 | tf_op jit(solution)/shard_map/ppermute | solution.py:62
  84.0 35.6 %collective-permute-start.30 = (bf16[64,6144]{1,0:T(8,128)(2,1)}, bf16[64,6144]{1,0:T(8,128)(2,1)}, u32[]{:S(2)}, u32[]{:S(2)}) collective-permute-start(bf16[64,6144]{1,0:T(8,128)(2,1)} %collective-permute-done.24.refs_1_), channel_id=1, source_target_pairs={{0,1},{1,0},{2,3},{3,2},{4,5},{5,4},{6,7},{7,6},{8,9},{9,8},{10,11... | collective-permute-start | bytes 2359304 | tf_op jit(solution)/shard_map/ppermute | solution.py:62
  169.0 55.4 %collective-permute-start.46 = (bf16[2,768,1024]{2,1,0:T(8,128)(2,1)}, bf16[2,768,1024]{2,1,0:T(8,128)(2,1)}, u32[]{:S(2)}, u32[]{:S(2)}) collective-permute-start(bf16[2,768,1024]{2,1,0:T(8,128)(2,1)} %get-tuple-element.128), channel_id=1, source_target_pairs={{0,1},{1,0},{2,3},{3,2},{4,5},{5,4},{6,7},{7,6},{8,9},{9,8},{10,11... | collective-permute-start | bytes 9437192 | tf_op jit(solution)/shard_map/ppermute | solution.py:62
  170.6 24.6 %collective-permute-start.40 = (bf16[768,1024]{1,0:T(8,128)(2,1)}, bf16[768,1024]{1,0:T(8,128)(2,1)}, u32[]{:S(2)}, u32[]{:S(2)}) collective-permute-start(bf16[768,1024]{1,0:T(8,128)(2,1)} %convert_element_type.692.refs_0_), channel_id=1, source_target_pairs={{0,1},{1,0},{2,3},{3,2},{4,5},{5,4},{6,7},{7,6},{8,9},{9,8},{10,11... | collective-permute-start | bytes 4718600 | tf_op jit(solution)/shard_map/ppermute | solution.py:62
  241.7 22.6 %collective-permute-start.49 = (bf16[2,256,6144]{2,1,0:T(8,128)(2,1)}, bf16[2,256,6144]{2,1,0:T(8,128)(2,1)}, u32[]{:S(2)}, u32[]{:S(2)}) collective-permute-start(bf16[2,256,6144]{2,1,0:T(8,128)(2,1)} %get-tuple-element.132), channel_id=1, source_target_pairs={{0,1},{1,0},{2,3},{3,2},{4,5},{5,4},{6,7},{7,6},{8,9},{9,8},{10,11... | collective-permute-start | bytes 18874376 | tf_op jit(solution)/shard_map/ppermute | solution.py:62
  279.2 44.9 %collective-permute-start.53 = (bf16[1,128,6144]{2,1,0:T(8,128)(2,1)}, bf16[1,128,6144]{2,1,0:T(8,128)(2,1)S(1)}, u32[]{:S(2)}, u32[]{:S(2)}) collective-permute-start(bf16[1,128,6144]{2,1,0:T(8,128)(2,1)} %add_convert_fusion.1), channel_id=1, source_target_pairs={{0,2},{1,3},{2,0},{3,1},{4,6},{5,7},{6,4},{7,5},{8,10},{9,11},{10,... | collective-permute-start | bytes 4718600 | tf_op jit(solution)/shard_map/ppermute | solution.py:62
  280.5 43.7 %collective-permute-start.54 = (bf16[2,128,3072]{2,1,0:T(8,128)(2,1)}, bf16[2,128,3072]{2,1,0:T(8,128)(2,1)}, u32[]{:S(2)}, u32[]{:S(2)}) collective-permute-start(bf16[2,128,3072]{2,1,0:T(8,128)(2,1)} %add_convert_fusion), channel_id=1, source_target_pairs={{0,4},{4,0},{8,12},{12,8},{16,20},{20,16},{24,28},{28,24},{1,5},{5... | collective-permute-start | bytes 4718600 | tf_op jit(solution)/shard_map/ppermute | solution.py:62
  292.9 31.3 %collective-permute-start.55 = (bf16[1,768,256]{2,1,0:T(8,128)(2,1)}, bf16[1,768,256]{2,1,0:T(8,128)(2,1)}, u32[]{:S(2)}, u32[]{:S(2)}) collective-permute-start(bf16[1,768,256]{2,1,0:T(8,128)(2,1)} %pad_maximum_fusion.10), channel_id=1, source_target_pairs={{0,8},{4,12},{8,0},{12,4},{16,24},{20,28},{24,16},{28,20},{1,9},{5... | collective-permute-start | bytes 1179656 | tf_op jit(solution)/shard_map/ppermute | solution.py:62
  296.7 54.3 %collective-permute-start.58 = (bf16[1,256,1024]{2,1,0:T(8,128)(2,1)S(1)}, bf16[1,256,1024]{2,1,0:T(8,128)(2,1)S(1)}, u32[]{:S(2)}, u32[]{:S(2)}) collective-permute-start(bf16[1,256,1024]{2,1,0:T(8,128)(2,1)S(1)} %add_convert_fusion.12), channel_id=1, source_target_pairs={{0,2},{1,3},{2,0},{3,1},{4,6},{5,7},{6,4},{7,5},{8,10},{9,11},{10,... | collective-permute-start | bytes 1572872 | tf_op jit(solution)/shard_map/ppermute | solution.py:62
  297.8 53.2 %collective-permute-start.59 = (bf16[2,256,512]{2,1,0:T(8,128)(2,1)S(1)}, bf16[2,256,512]{2,1,0:T(8,128)(2,1)S(1)}, u32[]{:S(2)}, u32[]{:S(2)}) collective-permute-start(bf16[2,256,512]{2,1,0:T(8,128)(2,1)S(1)} %add_convert_fusion.11), channel_id=1, source_target_pairs={{0,4},{4,0},{8,12},{12,8},{16,20},{20,16},{24,28},{28,24},{1,5},{5... | collective-permute-start | bytes 1572872 | tf_op jit(solution)/shard_map/ppermute | solution.py:62
  327.6 25.8 %collective-permute-start.56 = (bf16[1,128,3072]{2,1,0:T(8,128)(2,1)S(1)}, bf16[1,128,3072]{2,1,0:T(8,128)(2,1)S(1)}, u32[]{:S(2)}, u32[]{:S(2)}) collective-permute-start(bf16[1,128,3072]{2,1,0:T(8,128)(2,1)S(1)} %get-tuple-element.245), channel_id=1, source_target_pairs={{0,4},{4,0},{8,12},{12,8},{16,20},{20,16},{24,28},{28,24},{1,5},{5... | collective-permute-start | bytes 2359304 | tf_op jit(solution)/shard_map/ppermute | solution.py:62
  328.6 24.8 %collective-permute-start.57 = (bf16[1,128,3072]{2,1,0:T(8,128)(2,1)S(1)}, bf16[1,128,3072]{2,1,0:T(8,128)(2,1)S(1)}, u32[]{:S(2)}, u32[]{:S(2)}) collective-permute-start(bf16[1,128,3072]{2,1,0:T(8,128)(2,1)S(1)} %get-tuple-element.244), channel_id=1, source_target_pairs={{0,2},{1,3},{2,0},{3,1},{4,6},{5,7},{6,4},{7,5},{8,10},{9,11},{10,... | collective-permute-start | bytes 2359304 | tf_op jit(solution)/shard_map/ppermute | solution.py:62
  367.3 24.5 %collective-permute-start.60 = (bf16[2,256,4096]{2,1,0:T(8,128)(2,1)}, bf16[2,256,4096]{2,1,0:T(8,128)(2,1)}, u32[]{:S(2)}, u32[]{:S(2)}) collective-permute-start(bf16[2,256,4096]{2,1,0:T(8,128)(2,1)} %get-tuple-element.175), channel_id=1, source_target_pairs={{0,1},{1,0},{2,3},{3,2},{4,5},{5,4},{6,7},{7,6},{8,9},{9,8},{10,11... | collective-permute-start | bytes 12582920 | tf_op jit(solution)/shard_map/ppermute | solution.py:62
  367.4 24.3 %collective-permute-start.61 = (bf16[1,256,1536]{2,1,0:T(8,128)(2,1)}, bf16[1,256,1536]{2,1,0:T(8,128)(2,1)S(1)}, u32[]{:S(2)}, u32[]{:S(2)}) collective-permute-start(bf16[1,256,1536]{2,1,0:T(8,128)(2,1)} %pad_maximum_fusion.2), channel_id=1, source_target_pairs={{0,8},{4,12},{8,0},{12,4},{16,24},{20,28},{24,16},{28,20},{1,9},{5... | collective-permute-start | bytes 2359304 | tf_op jit(solution)/shard_map/ppermute | solution.py:62
  377.0 37.1 %collective-permute-start.73 = (bf16[1,768,128]{2,1,0:T(8,128)(2,1)}, bf16[1,768,128]{2,1,0:T(8,128)(2,1)}, u32[]{:S(2)}, u32[]{:S(2)}) collective-permute-start(bf16[1,768,128]{2,1,0:T(8,128)(2,1)} %pad_maximum_fusion.21), channel_id=1, source_target_pairs={{0,16},{4,20},{8,24},{12,28},{16,0},{20,4},{24,8},{28,12},{1,17},{... | collective-permute-start | bytes 589832 | tf_op jit(solution)/shard_map/ppermute | solution.py:62
  393.3 42.1 %collective-permute-start.64 = (bf16[1,128,4096]{2,1,0:T(8,128)(2,1)S(1)}, bf16[1,128,4096]{2,1,0:T(8,128)(2,1)S(1)}, u32[]{:S(2)}, u32[]{:S(2)}) collective-permute-start(bf16[1,128,4096]{2,1,0:T(8,128)(2,1)S(1)} %add_convert_fusion.3), channel_id=1, source_target_pairs={{0,2},{1,3},{2,0},{3,1},{4,6},{5,7},{6,4},{7,5},{8,10},{9,11},{10,... | collective-permute-start | bytes 3145736 | tf_op jit(solution)/shard_map/ppermute | solution.py:62
  395.8 39.6 %collective-permute-start.66 = (bf16[2,128,2048]{2,1,0:T(8,128)(2,1)S(1)}, bf16[2,128,2048]{2,1,0:T(8,128)(2,1)S(1)}, u32[]{:S(2)}, u32[]{:S(2)}) collective-permute-start(bf16[2,128,2048]{2,1,0:T(8,128)(2,1)S(1)} %add_convert_fusion.2), channel_id=1, source_target_pairs={{0,4},{4,0},{8,12},{12,8},{16,20},{20,16},{24,28},{28,24},{1,5},{5... | collective-permute-start | bytes 3145736 | tf_op jit(solution)/shard_map/ppermute | solution.py:62
  400.1 42.1 %collective-permute-start.72 = (bf16[1,256,768]{2,1,0:T(8,128)(2,1)S(1)}, bf16[1,256,768]{2,1,0:T(8,128)(2,1)S(1)}, u32[]{:S(2)}, u32[]{:S(2)}) collective-permute-start(bf16[1,256,768]{2,1,0:T(8,128)(2,1)S(1)} %pad_maximum_fusion.11), channel_id=1, source_target_pairs={{0,16},{4,20},{8,24},{12,28},{16,0},{20,4},{24,8},{28,12},{1,17},{... | collective-permute-start | bytes 1179656 | tf_op jit(solution)/shard_map/ppermute | solution.py:62
  433.0 40.5 %collective-permute-start.75 = (bf16[2,768,128]{2,1,0:T(8,128)(2,1)S(1)}, bf16[2,768,128]{2,1,0:T(8,128)(2,1)S(1)}, u32[]{:S(2)}, u32[]{:S(2)}) collective-permute-start(bf16[2,768,128]{2,1,0:T(8,128)(2,1)S(1)} %pad_maximum_fusion.13), channel_id=1, source_target_pairs={{0,8},{4,12},{8,0},{12,4},{16,24},{20,28},{24,16},{28,20},{1,9},{5... | collective-permute-start | bytes 1179656 | tf_op jit(solution)/shard_map/ppermute | solution.py:62
  440.5 68.4 %collective-permute-start.79 = (bf16[1,512,128]{2,1,0:T(8,128)(2,1)}, bf16[1,512,128]{2,1,0:T(8,128)(2,1)}, u32[]{:S(2)}, u32[]{:S(2)}) collective-permute-start(bf16[1,512,128]{2,1,0:T(8,128)(2,1)} %pad_maximum_fusion.24), channel_id=1, source_target_pairs={{0,16},{4,20},{8,24},{12,28},{16,0},{20,4},{24,8},{28,12},{1,17},{... | collective-permute-start | bytes 393224 | tf_op jit(solution)/shard_map/ppermute | solution.py:62
  452.9 21.6 %collective-permute-start.82 = (bf16[1,256,768]{2,1,0:T(8,128)(2,1)S(1)}, bf16[1,256,768]{2,1,0:T(8,128)(2,1)S(1)}, u32[]{:S(2)}, u32[]{:S(2)}) collective-permute-start(bf16[1,256,768]{2,1,0:T(8,128)(2,1)S(1)} %pad_maximum_fusion.14), channel_id=1, source_target_pairs={{0,16},{4,20},{8,24},{12,28},{16,0},{20,4},{24,8},{28,12},{1,17},{... | collective-permute-start | bytes 1179656 | tf_op jit(solution)/shard_map/ppermute | solution.py:62
  475.5 36.9 %collective-permute-start.83 = (bf16[2,256,768]{2,1,0:T(8,128)(2,1)}, bf16[2,256,768]{2,1,0:T(8,128)(2,1)}, u32[]{:S(2)}, u32[]{:S(2)}) collective-permute-start(bf16[2,256,768]{2,1,0:T(8,128)(2,1)} %pad_maximum_fusion.5), channel_id=1, source_target_pairs={{0,8},{4,12},{8,0},{12,4},{16,24},{20,28},{24,16},{28,20},{1,9},{5... | collective-permute-start | bytes 2359304 | tf_op jit(solution)/shard_map/ppermute | solution.py:62
  511.2 21.2 %collective-permute-start.85 = (bf16[4,768,128]{2,1,0:T(8,128)(2,1)}, bf16[4,768,128]{2,1,0:T(8,128)(2,1)}, u32[]{:S(2)}, u32[]{:S(2)}) collective-permute-start(bf16[4,768,128]{2,1,0:T(8,128)(2,1)} %pad_maximum_fusion.4.rest_0_), channel_id=1, source_target_pairs={{0,4},{4,0},{8,12},{12,8},{16,20},{20,16},{24,28},{28,24},{1,5},{5... | collective-permute-start | bytes 2359304 | tf_op jit(solution)/shard_map/ppermute | solution.py:62
  514.8 67.3 %collective-permute-start.84 = (bf16[4,256,768]{2,1,0:T(8,128)(2,1)}, bf16[4,256,768]{2,1,0:T(8,128)(2,1)}, u32[]{:S(2)}, u32[]{:S(2)}) collective-permute-start(bf16[4,256,768]{2,1,0:T(8,128)(2,1)} %pad_maximum_fusion.rest_0_), channel_id=1, source_target_pairs={{0,4},{4,0},{8,12},{12,8},{16,20},{20,16},{24,28},{28,24},{1,5},{5... | collective-permute-start | bytes 4718600 | tf_op jit(solution)/shard_map/ppermute | solution.py:62
  528.9 48.0 %collective-permute-start.81 = (bf16[4,512,128]{2,1,0:T(8,128)(2,1)}, bf16[4,512,128]{2,1,0:T(8,128)(2,1)}, u32[]{:S(2)}, u32[]{:S(2)}) collective-permute-start(bf16[4,512,128]{2,1,0:T(8,128)(2,1)} %pad_maximum_fusion.9.rest_0_), channel_id=1, source_target_pairs={{0,4},{4,0},{8,12},{12,8},{16,20},{20,16},{24,28},{28,24},{1,5},{5... | collective-permute-start | bytes 1572872 | tf_op jit(solution)/shard_map/ppermute | solution.py:62
  544.0 56.5 %collective-permute-start.78 = (bf16[4,256,512]{2,1,0:T(8,128)(2,1)S(1)}, bf16[4,256,512]{2,1,0:T(8,128)(2,1)S(1)}, u32[]{:S(2)}, u32[]{:S(2)}) collective-permute-start(bf16[4,256,512]{2,1,0:T(8,128)(2,1)S(1)} %pad_maximum_fusion.1.rest_0_), channel_id=1, source_target_pairs={{0,4},{4,0},{8,12},{12,8},{16,20},{20,16},{24,28},{28,24},{1,5},{5... | collective-permute-start | bytes 3145736 | tf_op jit(solution)/shard_map/ppermute | solution.py:62
  (144 other events, 1617.1 us)

commit v6 on v5

--- a/solution.py
+++ b/solution.py
@@ -15,6 +15,8 @@
 FF = 3072
 SEQ_LEN = 512
 PARAMS = 15730944
+GROUP = "group"
+DP = "dp"
 
 
 EPS_NORM = 1e-06
@@ -79,8 +81,8 @@
         count = len(pieces)
         ins, out_ref, held = refs[:count], refs[count], refs[count + 1]
         into, away = refs[count + 2 :]
-        mine = lax.axis_index("group")
-        here = lax.axis_index("dp")
+        mine = lax.axis_index(GROUP)
+        here = lax.axis_index(DP)
         arriving, leaving, at = [], [], 0
         for k, (_, delta, offset) in enumerate(pieces):
             slot = held.at[pl.ds(at, sizes[k])]
@@ -116,9 +118,9 @@
 
 
 def gather_rows(shard, early, late, middle, hold):
-    owners = lax.axis_size("group")
-    copies = lax.axis_size("dp")
-    here = lax.axis_index("dp")
+    owners = lax.axis_size(GROUP)
+    copies = lax.axis_size(DP)
+    here = lax.axis_index(DP)
     if early is not None:
         shard = after(shard, early)
     shard = shard.astype(jnp.bfloat16)
@@ -141,34 +143,36 @@
         near = lax.dynamic_slice_in_dim(shard, place(here) * quarter, quarter, 0)
         if late is not None:
             near = after(near, late)
-        order = swap(near, "group", 2)
+        order = swap(near, GROUP, 2)
         passed = order if middle is None else after(order, middle)
-        by_one = swap(passed, "dp", 1)
-        by_two = swap(passed, "dp", 2)
+        by_one = swap(passed, DP, 1)
+        by_two = swap(passed, DP, 2)
+        last_one = swap(by_two[:half], DP, 1)
+        last_two = swap(by_one[half:], DP, 2)
         pieces += [
             (order, 2, quarter_at(0)),
             (by_one, 2, quarter_at(2)),
             (by_two, 2, quarter_at(1)),
-            (swap(by_two[:half], "dp", 1), 2, quarter_at(3)),
-            (swap(by_one[half:], "dp", 2), 2, quarter_at(3, half)),
+            (last_one, 2, quarter_at(3)),
+            (last_two, 2, quarter_at(3, half)),
         ]
     else:
         for mask in bit_masks(owners)[1:]:
-            pieces += [(swap(v, "group", mask), dg ^ mask, at) for v, dg, at in pieces]
-    pieces += [(swap(v, "group", 1), dg ^ 1, at) for v, dg, at in pieces]
+            pieces += [(swap(v, GROUP, mask), dg ^ mask, at) for v, dg, at in pieces]
+    pieces += [(swap(v, GROUP, 1), dg ^ 1, at) for v, dg, at in pieces]
     if hold is not None:
         pieces[0] = (after(shard, hold), 0, none)
     return place_rows(pieces, rows, owners), near, order, (by_one, by_two)
 
 
 def gather_small(shard):
-    owners = lax.axis_size("group")
-    mine = lax.axis_index("group")
+    owners = lax.axis_size(GROUP)
+    mine = lax.axis_index(GROUP)
     width = shard.shape[1]
     held = shard[None]
     deltas = [0]
     for mask in reversed(bit_masks(owners)):
-        held = jnp.concatenate([held, swap(held, "group", mask)], axis=0)
+        held = jnp.concatenate([held, swap(held, GROUP, mask)], axis=0)
         deltas += [d ^ mask for d in deltas]
     full = jnp.zeros((shard.shape[0], width * owners), shard.dtype)
     for k, delta in enumerate(deltas):
@@ -177,13 +181,13 @@
 
 
 def sum_all(value):
-    owners = lax.axis_size("group")
-    copies = lax.axis_size("dp")
+    owners = lax.axis_size(GROUP)
+    copies = lax.axis_size(DP)
     mesh_type = pl.DeviceIdType.MESH
 
     def body(in_ref, out_ref, near, near_sum, far, near_send, near_recv, far_send, far_recv):
-        mine = lax.axis_index("group")
-        here = lax.axis_index("dp")
+        mine = lax.axis_index(GROUP)
+        here = lax.axis_index(DP)
         near_peers = [(here, mine ^ k) for k in range(1, owners)]
         far_peers = [(here ^ k, mine) for k in range(1, copies)]
         barrier = pltpu.get_barrier_semaphore()
@@ -246,16 +250,16 @@
 def grad_blocks(left, right):
     tokens, rows = left.shape
     columns = right.shape[1]
-    owners = lax.axis_size("group")
-    copies = lax.axis_size("dp")
+    owners = lax.axis_size(GROUP)
+    copies = lax.axis_size(DP)
     column_masks = bit_masks(copies)
     later = bit_masks(owners)[1:]
     staying = [spread_bits(p, later) for p in range(1 << len(later))]
     row_sets = [[dg + 1 for dg in staying], staying] if owners > 1 else [[0]]
     row_block = rows // owners
     column_block = columns // copies
-    mine = lax.axis_index("group")
-    here = lax.axis_index("dp")
+    mine = lax.axis_index(GROUP)
+    here = lax.axis_index(DP)
     if column_block % 128 or row_block % 16:
         ordered = jnp.concatenate(
             [
@@ -335,11 +339,11 @@
     def __init__(self, left, right, split):
         blocks = grad_blocks(left, right)
         self.blocks = blocks
-        group = [("group", m) for m in bit_masks(lax.axis_size("group"))]
-        other = [("dp", m) for m in bit_masks(lax.axis_size("dp"))]
+        group = [(GROUP, m) for m in bit_masks(lax.axis_size(GROUP))]
+        other = [(DP, m) for m in bit_masks(lax.axis_size(DP))]
         self.arrays = [blocks[-1]]
         if group:
-            self.arrays.append(swap(blocks[0], "group", 1))
+            self.arrays.append(swap(blocks[0], GROUP, 1))
         rest = group[1:]
         self.orders = [rest + other]
         if split:
@@ -375,7 +379,7 @@
         outgoing = []
         for i, order in enumerate(self.orders):
             axis, mask = order[self.step]
-            dim = 0 if axis == "group" else 2
+            dim = 0 if axis == GROUP else 2
             far, near = [], []
             for k, ranges in self.parts[i]:
                 start, stop = ranges[dim]
@@ -406,14 +410,18 @@
         return jnp.concatenate([self.read(part)[0] for part in self.parts], axis=0)
 
 
-def gather_grad(own, last):
+def gather_grad(own, second, last):
     held = own.astype(jnp.bfloat16)[None]
     deltas = [0]
     groups = [(held, deltas)]
-    masks = list(reversed(bit_masks(lax.axis_size("dp"))))
+    masks = list(reversed(bit_masks(lax.axis_size(DP))))
     for i, mask in enumerate(masks):
-        away = held if last is None or i + 1 < len(masks) else after(held, last)
-        got = swap(away, "dp", mask)
+        away = held
+        if i == 1 and second is not None:
+            away = after(away, second)
+        if i + 1 == len(masks) and last is not None:
+            away = after(away, last)
+        got = swap(away, DP, mask)
         got_deltas = [d ^ mask for d in deltas]
         if i + 1 < len(masks):
             held = jnp.concatenate([held, got], axis=0)
@@ -437,8 +445,8 @@
 
 def adam_blocks(master, moment, blocks, factor, step_rate, decay_rate):
     rows, columns = master.shape
-    copies = lax.axis_size("dp")
-    here = lax.axis_index("dp")
+    copies = lax.axis_size(DP)
+    here = lax.axis_index(DP)
     width = columns // copies
     if width % 128:
         full = jnp.zeros(master.shape, jnp.float32)
@@ -738,7 +746,110 @@
     )(*operands)
 
 
-def gate_up_back(cotangent, full_down, gate_up):
+def gate_up_forward(hidden, full_gate_up):
+    tokens, depth = hidden.shape
+    block = 512
+    steps = FF // block
+
+    def body(hidden_ref, left_ref, right_ref, gate_ref, up_ref, out_ref):
+        gate = jnp.dot(hidden_ref[...], left_ref[...], preferred_element_type=jnp.float32)
+        upward = jnp.dot(hidden_ref[...], right_ref[...], preferred_element_type=jnp.float32)
+        gate_ref[...] = gate
+        up_ref[...] = upward
+        out_ref[...] = (gate * jax.nn.sigmoid(gate) * upward).astype(jnp.bfloat16)
+
+    wide = pl.BlockSpec((tokens, block), lambda j: (0, j))
+    return pl.pallas_call(
+        body,
+        grid=(steps,),
+        in_specs=[
+            pl.BlockSpec((tokens, depth), lambda j: (0, 0)),
+            pl.BlockSpec((depth, block), lambda j: (0, j)),
+            pl.BlockSpec((depth, block), lambda j: (0, steps + j)),
+        ],
+        out_specs=[wide, wide, wide],
+        out_shape=[
+            jax.ShapeDtypeStruct((tokens, FF), jnp.float32),
+            jax.ShapeDtypeStruct((tokens, FF), jnp.float32),
+            jax.ShapeDtypeStruct((tokens, FF), jnp.bfloat16),
+        ],
+        compiler_params=pltpu.CompilerParams(vmem_limit_bytes=48 * 1024 * 1024),
+        cost_estimate=pl.CostEstimate(
+            flops=4 * tokens * FF * depth,
+            bytes_accessed=4 * FF * depth + 10 * tokens * FF,
+            transcendentals=tokens * FF,
+        ),
+    )(hidden, full_gate_up, full_gate_up)
+
+
+def project_back(grad_low, weight, value, upstream, gain, whole):
+    tokens, width = grad_low.shape
+    depth = weight.shape[0]
+    block = 1024
+    steps = width // block
+
+    def body(grad_ref, weight_ref, value_ref, up_ref, gain_ref, *rest):
+        total_ref = rest[-1]
+        step = pl.program_id(0)
+        more = lax.dot_general(
+            grad_ref[...],
+            weight_ref[...],
+            (((1,), (1,)), ((), ())),
+            preferred_element_type=jnp.float32,
+        )
+
+        @pl.when(step == 0)
+        def _():
+            total_ref[...] = more
+
+        @pl.when(step > 0)
+        def _():
+            total_ref[...] += more
+
+        @pl.when(step == steps - 1)
+        def _():
+            raw = value_ref[...].astype(jnp.float32)
+            root = lax.rsqrt(jnp.mean(raw * raw, axis=-1, keepdims=True) + EPS_NORM)
+            normed = raw * root
+            grad = total_ref[...]
+            rest[1][...] = jnp.sum(grad * normed, axis=0, keepdims=True)
+            full = up_ref[...].astype(jnp.float32) + norm_back(grad, normed, root, gain_ref[...])
+            rest[0][...] = full.astype(jnp.bfloat16)
+            if whole:
+                rest[2][...] = full
+
+    fixed = lambda j: (0, 0)
+    square = pl.BlockSpec((tokens, depth), fixed)
+    row = pl.BlockSpec((1, depth), fixed)
+    shapes = [
+        jax.ShapeDtypeStruct((tokens, depth), jnp.bfloat16),
+        jax.ShapeDtypeStruct((1, depth), jnp.float32),
+    ]
+    if whole:
+        shapes.append(jax.ShapeDtypeStruct((tokens, depth), jnp.float32))
+    return pl.pallas_call(
+        body,
+        grid=(steps,),
+        in_specs=[
+            pl.BlockSpec((tokens, block), lambda j: (0, j)),
+            pl.BlockSpec((depth, block), lambda j: (0, j)),
+            square,
+            square,
+            row,
+        ],
+        out_specs=[square, row] + [square] * whole,
+        out_shape=shapes,
+        scratch_shapes=[pltpu.VMEM((tokens, depth), jnp.float32)],
+        compiler_params=pltpu.CompilerParams(vmem_limit_bytes=48 * 1024 * 1024),
+        cost_estimate=pl.CostEstimate(
+            flops=2 * tokens * width * depth,
+            bytes_accessed=2 * width * (depth + tokens) + 14 * tokens * depth,
+            transcendentals=tokens,
+        ),
+    )(grad_low, weight, value, upstream, gain)
+
+
+def gate_up_back(cotangent, full_down, gate_part, upward):
     tokens, columns = cotangent.shape
     block = 512
     steps = FF // block
@@ -765,7 +876,7 @@
             pl.BlockSpec((tokens, columns), lambda j: (0, 0)),
             pl.BlockSpec((block, columns), lambda j: (j, 0)),
             pl.BlockSpec((tokens, block), lambda j: (0, j)),
-            pl.BlockSpec((tokens, block), lambda j: (0, steps + j)),
+            pl.BlockSpec((tokens, block), lambda j: (0, j)),
         ],
         out_specs=pl.BlockSpec((tokens, 2 * FF), lambda j: (0, 0)),
         out_shape=jax.ShapeDtypeStruct((tokens, 2 * FF), jnp.bfloat16),
@@ -775,7 +886,7 @@
             bytes_accessed=2 * FF * columns + 12 * tokens * FF,
             transcendentals=tokens * FF,
         ),
-    )(cotangent, full_down, gate_up, gate_up)
+    )(cotangent, full_down, gate_part, upward)
 
 
 def on_device(
@@ -798,11 +909,11 @@
 ):
     width = norm_gains.shape[1]
     gains_low = jnp.concatenate([norm_gains, head_gains], axis=1).astype(jnp.bfloat16)
-    owners = lax.axis_size("group")
+    owners = lax.axis_size(GROUP)
     gains_all = gather_small(gains_low).reshape(2, owners, -1)
     full_norm = gains_all[:, :, :width].reshape(2, -1)
     full_head = gains_all[:, :, width:].reshape(2, -1)
-    full_qkv, first, _, late = gather_rows(qkv_weight, None, None, None, None)
+    full_qkv, first, late, _ = gather_rows(qkv_weight, None, None, None, None)
     gain_one = full_norm[0].astype(jnp.float32)
     gain_two = full_norm[1].astype(jnp.float32)
     head_gain = full_head.astype(jnp.float32)
@@ -811,9 +922,11 @@
     normed_one = inputs * root_one
     hidden_one = (normed_one * gain_one).astype(jnp.bfloat16)
     projected = jnp.dot(hidden_one, full_qkv, preferred_element_type=jnp.float32)
-    full_out, _, late, _ = gather_rows(out_weight, first, late, None, projected)
-    full_gate_up, _, late, _ = gather_rows(gate_up_weight, first, late, projected, None)
-    full_down, _, _, _ = gather_rows(down_weight, first, late, None, None)
+    full_out, _, down_late, _ = gather_rows(out_weight, first, late, projected, projected)
+    full_gate_up, _, more_late, _ = gather_rows(gate_up_weight, first, late, projected, None)
+    full_down, _, _, _ = gather_rows(
+        down_weight, first, (down_late, more_late, projected), None, None
+    )
     tables = rotary_tables(positions, HD)
     mixed_low = attention_call(attend_body, projected, tables, segment_ids, head_gain, None, 0, HK, None)
     attended = jnp.dot(mixed_low, full_out, preferred_element_type=jnp.float32)
@@ -821,21 +934,20 @@
     root_two = lax.rsqrt(jnp.mean(residual * residual, axis=-1, keepdims=True) + EPS_NORM)
     normed_two = residual * root_two
     hidden_two = (normed_two * gain_two).astype(jnp.bfloat16)
-    gate_up = jnp.dot(hidden_two, full_gate_up, preferred_element_type=jnp.float32)
-    gate_part = gate_up[:, :FF]
-    upward = gate_up[:, FF:]
-    sigmoid_gate = jax.nn.sigmoid(gate_part)
-    activated = (gate_part * sigmoid_gate * upward).astype(jnp.bfloat16)
-    branch = jnp.dot(activated, full_down, preferred_element_type=jnp.float32)
-    output = (residual + branch).astype(jnp.bfloat16)
-    upstream = cotangent.astype(jnp.float32)
+    gate_part, upward, activated = gate_up_forward(hidden_two, full_gate_up)
     down_sum = GradSum(activated, cotangent, True)
-    grad_gate_up = gate_up_back(after(cotangent, *down_sum.blocks), full_down, gate_up)
+    grad_gate_up = gate_up_back(
+        after(cotangent, *down_sum.blocks), full_down, gate_part, upward
+    )
     gate_up_sum = GradSum(hidden_two, after(grad_gate_up, *down_sum.advance()), True)
-    grad_hidden_two = contract_cols(after(grad_gate_up, *gate_up_sum.blocks), full_gate_up)
-    grad_gain_two = jnp.sum(grad_hidden_two * normed_two, axis=0)
-    grad_residual = upstream + norm_back(grad_hidden_two, normed_two, root_two, gain_two)
-    residual_low = grad_residual.astype(jnp.bfloat16)
+    residual_low, grad_gain_two, grad_residual = project_back(
+        after(grad_gate_up, *gate_up_sum.blocks),
+        full_gate_up,
+        residual,
+        cotangent,
+        gain_two[None],
+        True,
+    )
     down_sum.hold(residual_low)
     sent = down_sum.advance() + gate_up_sum.advance()
     out_sum = GradSum(mixed_low, after(residual_low, *sent), True)
@@ -873,17 +985,26 @@
     out_sum.hold(sent)
     down_sum.hold(sent)
     sent = sent + gate_up_sum.advance() + out_sum.advance()
-    grad_hidden_one = contract_cols(after(grad_projected, *qkv_sum.blocks, *sent), full_qkv)
-    grad_gain_one = jnp.sum(grad_hidden_one * normed_one, axis=0)
-    grad_inputs = grad_residual + norm_back(grad_hidden_one, normed_one, root_one, gain_one)
-    tokens_grad = grad_inputs.astype(jnp.bfloat16)
+    branch = jnp.dot(after(activated, *sent), full_down, preferred_element_type=jnp.float32)
+    output = (residual + branch).astype(jnp.bfloat16)
+    tokens_grad, grad_gain_one = project_back(
+        after(grad_projected, *qkv_sum.blocks, *sent),
+        full_qkv,
+        tokens,
+        grad_residual,
+        gain_one[None],
+        False,
+    )
     small = jnp.concatenate(
-        [jnp.stack([grad_gain_one, grad_gain_two]), grad_gain_head],
+        [jnp.concatenate([grad_gain_one, grad_gain_two]), grad_gain_head],
         axis=1,
     )
-    owned = tuple(v.finish() for v in (qkv_sum, out_sum, gate_up_sum, down_sum))
-    qkv_own, out_own, gate_up_own, down_own = owned
-    down_gathered = gather_grad(down_own, None)
+    sent_next = qkv_sum.advance()
+    sent_last = qkv_sum.advance()
+    qkv_own, out_own, gate_up_own, down_own = owned = tuple(
+        v.finish() for v in (qkv_sum, out_sum, gate_up_sum, down_sum)
+    )
+    down_gathered = gather_grad(after(down_own, *sent_next), None, None)
     local = sum(jnp.sum(v * v) for v in owned)
     partial = jnp.concatenate(
         [small, jnp.full((6, small.shape[1]), local, jnp.float32)], axis=0
@@ -895,22 +1016,29 @@
     squares = summed[2, 0] + jnp.sum(small * small)
     clip_limit = math.sqrt(PARAMS)
     factor = clip_limit / jnp.maximum(jnp.sqrt(squares), clip_limit)
+    renewed_down = adam_blocks(
+        down_weight, down_moments, down_gathered, factor, LEARN_RATE, WEIGHT_DECAY
+    )
     gathered = [
-        gather_grad(after(qkv_own, summed), None),
-        gather_grad(out_own, None),
-        gather_grad(gate_up_own, summed),
-        down_gathered,
+        gather_grad(after(qkv_own, summed), renewed_down[0], None),
+        gather_grad(after(out_own, *sent_last), None, None),
+        gather_grad(after(gate_up_own, *sent_last), None, summed),
     ]
-    masters = (qkv_weight, out_weight, gate_up_weight, down_weight)
-    moments = (qkv_moments, out_moments, gate_up_moments, down_moments)
     later = after(factor, gathered[0][0][0])
-    renewed = [
-        adam_blocks(master, moment, blocks, scale, LEARN_RATE, WEIGHT_DECAY)
-        for master, moment, blocks, scale in zip(
-            masters, moments, gathered, (later, later, later, factor)
-        )
-    ]
-    mine = lax.axis_index("group")
+    renewed_gate_up = adam_blocks(
+        gate_up_weight, gate_up_moments, gathered[2], later, LEARN_RATE, WEIGHT_DECAY
+    )
+    later = after(factor, renewed_gate_up[0])
+    renewed_out = adam_blocks(
+        out_weight, out_moments, gathered[1], later, LEARN_RATE, WEIGHT_DECAY
+    )
+    later = after(factor, renewed_out[0])
+    renewed_qkv = adam_blocks(
+        qkv_weight, qkv_moments, gathered[0], later, LEARN_RATE, WEIGHT_DECAY
+    )
+    renewed = [renewed_qkv, renewed_out, renewed_gate_up]
+    renewed.append(renewed_down)
+    mine = lax.axis_index(GROUP)
     norm_grad = lax.dynamic_slice_in_dim(
         norm_total, mine * norm_gains.shape[1], norm_gains.shape[1], 1
     )
@@ -932,48 +1060,48 @@
 
 def solution(mesh):
     placed = (
-        P(("dp", "group"), None),
-        P(("dp", "group")),
-        P(("dp", "group")),
-        P(("dp", "group"), None),
-        P("group", None),
-        P("group", None),
-        P("group", None),
-        P("group", None),
-        P(None, "group"),
-        P(None, "group"),
-        P(None, "group", None),
-        P(None, "group", None),
-        P(None, "group", None),
-        P(None, "group", None),
-        P(None, None, "group"),
-        P(None, None, "group"),
+        P((DP, GROUP), None),
+        P((DP, GROUP)),
+        P((DP, GROUP)),
+        P((DP, GROUP), None),
+        P(GROUP, None),
+        P(GROUP, None),
+        P(GROUP, None),
+        P(GROUP, None),
+        P(None, GROUP),
+        P(None, GROUP),
+        P(None, GROUP, None),
+        P(None, GROUP, None),
+        P(None, GROUP, None),
+        P(None, GROUP, None),
+        P(None, None, GROUP),
+        P(None, None, GROUP),
     )
     return jax.shard_map(
         on_device,
         mesh=mesh,
         in_specs=placed,
         out_specs=(
-            P(("dp", "group"), None),
-            P(("dp", "group"), None),
-            P("group", "dp"),
-            P("group", "dp"),
-            P("group", "dp"),
-            P("group", "dp"),
-            P(None, "group"),
-            P(None, "group"),
-            P("group", None),
-            P("group", None),
-            P("group", None),
-            P("group", None),
-            P(None, "group"),
-            P(None, "group"),
-            P(None, "group", None),
-            P(None, "group", None),
-            P(None, "group", None),
-            P(None, "group", None),
-            P(None, None, "group"),
-            P(None, None, "group"),
+            P((DP, GROUP), None),
+            P((DP, GROUP), None),
+            P(GROUP, DP),
+            P(GROUP, DP),
+            P(GROUP, DP),
+            P(GROUP, DP),
+            P(None, GROUP),
+            P(None, GROUP),
+            P(GROUP, None),
+            P(GROUP, None),
+            P(GROUP, None),
+            P(GROUP, None),
+            P(None, GROUP),
+            P(None, GROUP),
+            P(None, GROUP, None),
+            P(None, GROUP, None),
+            P(None, GROUP, None),
+            P(None, GROUP, None),
+            P(None, None, GROUP),
+            P(None, None, GROUP),
         ),
         check_vma=False,
     )

time: 624 us -> 616 us (0.987)
  matrix products: 60.2 us -> 17.2 us
  Pallas kernels: 183 us -> 222 us
  waiting for transfers between devices: 162 us -> 178 us
  other arithmetic: 101 us -> 86.9 us
    pallas_call x0 -> x3, Pallas kernels: none -> 37.4 us  [the longest x2 24.2 us: project_back(): pl.pallas_call(body, grid=(steps,), in_specs=[pl.BlockSpec((tokens, block...]
    dot_general x3 -> x1, matrix products: 27.7 us -> 2.37 us  [contract_cols(): lax.dot_general(left_side, right_side, (((1,), (1,)), ((), ())), preferre...]
    dot_general x2 -> x1, matrix products: 23.3 us -> 5.66 us  [on_device(): jnp.dot(after(activated, *sent), full_down, preferred_element_type=jnp.fl...]
    ppermute x86, waiting for transfers between devices: 162 us -> 178 us  [swap(): return lax.ppermute(value, axis, [(i, i ^ mask) for i in range(count)])]
    convert_element_type x3 -> x0, other arithmetic: 13.6 us -> none  [the longest x1 6.79 us: on_device(): activated = (gate_part * sigmoid_gate * upward).astype(jnp.bfloat16)]
    another operation x8 -> x2, other arithmetic: 6.91 us -> 0.01 us
  transfers between devices with their start and end apart: 86 -> 86, of which waited for: 29 -> 32; matrix products, arithmetic and copies ran while one was open for 22% -> 18% of each run, Pallas kernels for 21% -> 25%
where the time goes in v6:
time: 616 us; the launch traced here: 604 us
  Pallas kernels  222 us (36%)
  waiting for transfers between devices  178 us (29%)
  other arithmetic  86.9 us (14%)
  starting transfers between devices  67.5 us (11%)
  local copies, waits for them, and re-layouts  26.6 us (4%)
  matrix products  17.2 us (3%)
  between operations  6.25 us (1%)
    ppermute x86, waiting for transfers between devices, swap(): return lax.ppermute(value, axis, [(i, i ^ mask) for i in range(count)])  178 us
    ppermute x86, starting transfers between devices, swap(): return lax.ppermute(value, axis, [(i, i ^ mask) for i in range(count)])  67.5 us
    pallas_call x3, Pallas kernels, attention_call(): pl.pallas_call(body, grid=(seq_count, count), in_specs=in_specs, out_spec...  54 us
    pallas_call x4, Pallas kernels, adam_blocks(): pl.pallas_call(body, out_shape=[jax.ShapeDtypeStruct(master.shape, jnp.fl...  44.4 us
    pallas_call x4, Pallas kernels, grad_blocks(): pl.pallas_call(body, out_shape=[jax.ShapeDtypeStruct((len(row_set), row_b...  38.6 us
    convert_element_type x20, other arithmetic, advance(): outgoing.append((self.read(far).astype(jnp.bfloat16), axis, mask))  38.5 us
    pallas_call x2, Pallas kernels, project_back(): pl.pallas_call(body, grid=(steps,), in_specs=[pl.BlockSpec((tokens, block...  24.2 us
    pallas_call x4, Pallas kernels, place_rows(): pl.pallas_call(body, out_shape=jax.ShapeDtypeStruct((rows * owners, colum...  18.9 us
  transfers between devices with their start and end apart: 86, of which 32 were waited for; matrix products, arithmetic and copies ran while one was open for 18% of the time, Pallas kernels for 25%

profile of v6, /device:TPU:0, one launch (start us, length us, event | category | flops | bytes accessed | tf_op | source)
XLA Modules:
  0.0 604.4 jit_solution(16603501672296744439)
XLA Ops:
  17.7 7.8 %collective-permute-done.2.refs_1_ = bf16[64,4096]{1,0:T(8,128)(2,1)} collective-permute-done((bf16[64,4096]{1,0:T(8,128)(2,1)}, bf16[64,4096]{1,0:T(8,128)(2,1)}, u32[]{:S(2)}, u32[]{:S(2)}) %collective-permute-start.2) | collective-permute-done | bytes 524320 | tf_op jit(solution)/shard_map/ppermute | solution.py:64
  31.4 9.1 %collective-permute-done.4.refs_3_ = bf16[64,4096]{1,0:T(8,128)(2,1)} collective-permute-done((bf16[64,4096]{1,0:T(8,128)(2,1)}, bf16[64,4096]{1,0:T(8,128)(2,1)}, u32[]{:S(2)}, u32[]{:S(2)}) %collective-permute-start.4) | collective-permute-done | bytes 524320 | tf_op jit(solution)/shard_map/ppermute | solution.py:64
  58.9 6.7 %fusion.10.query_ref.key_ref.value_ref = f32[512,4096]{1,0:T(8,128)} fusion(bf16[512,1024]{1,0:T(8,128)(2,1)S(1)} %fusion.2.left_ref, bf16[1024,4096]{1,0:T(8,128)(2,1)S(1)} %shard_map.311.weight_ref), kind=kOutput, calls=%fused_computation.121 | convolution fusion | flops 4294967296 | bytes 17825792 | tf_op jit(solution)/shard_map/dot_general | solution.py:924
  94.0 17.5 %shard_map.312.left_ref = bf16[512,2048]{1,0:T(8,128)(2,1)S(1)} custom-call(f32[512,4096]{1,0:T(8,128)} %fusion.10.query_ref.key_ref.value_ref, f32[512,4096]{1,0:T(8,128)} %fusion.10.query_ref.key_ref.value_ref, f32[512,4096]{1,0:T(8,128)} %fusion.10.query_ref.key_ref.value_ref, f32[512,128]{1,0:T(8,128)S(1)} %get-tuple-element.311.cos_ref, ...), custom_call_target="tpu_custom_call" | custom-call | flops 4294967296 | bytes 12582912 | tf_op jit(solution)/shard_map/pallas_call | solution.py:732
  121.1 6.0 collective-permute-done.27.refs_4_
  130.1 7.7 %shard_map.314.left_ref.right_ref.weight_ref = bf16[1024,6144]{1,0:T(8,128)(2,1)} custom-call(bf16[256,6144]{1,0:T(8,128)(2,1)S(1)} %convert_element_type.681.refs_0_, bf16[64,6144]{1,0:T(8,128)(2,1)} %collective-permute-done.24.refs_1_, bf16[64,6144]{1,0:T(8,128)(2,1)} %collective-permute-done.25.refs_2_, bf16[64,6144]{1,0:T(8,128)(2,1)} %collective-permute-done.26.refs_3_, ...), custom_call_target="tpu_custom_call" | custom-call | bytes 25165824 | tf_op jit(solution)/shard_map/pallas_call | solution.py:103
  137.9 13.2 %shard_map.315 = (f32[512,3072]{1,0:T(8,128)}, f32[512,3072]{1,0:T(8,128)}, bf16[512,3072]{1,0:T(8,128)(2,1)S(1)}) custom-call(bf16[512,1024]{1,0:T(8,128)(2,1)S(1)} %multiply_convert_fusion.hidden_ref.left_ref, bf16[1024,6144]{1,0:T(8,128)(2,1)} %shard_map.314.left_ref.right_ref.weight_ref, bf16[1024,6144]{1,0:T(8,128)(2,1)} %shard_map.314.left_ref.right_ref.weight_ref), custom_call_target="tpu_custom_call" | custom-call | flops 6442450944 | bytes 28311552 | tf_op jit(solution)/shard_map/pallas_call | solution.py:762
  152.7 8.8 %shard_map.316 = (bf16[2,768,1024]{2,1,0:T(8,128)(2,1)}, bf16[2,768,1024]{2,1,0:T(8,128)(2,1)}) custom-call(s32[2]{0:T(128)S(1)} %pad_add_fusion.where, bf16[512,3072]{1,0:T(8,128)(2,1)} %copy-done.35, bf16[512,1024]{1,0:T(8,128)(2,1)S(1)} %copy-done.18, bf16[512,1024]{1,0:T(8,128)(2,1)S(1)} %copy-done.18), custom_call_target="tpu_custom_call" | custom-call | flops 3221225472 | bytes 10485760 | tf_op jit(solution)/shard_map/pallas_call | solution.py:310
  165.1 10.6 %collective-permute-done.35.refs_1_ = bf16[192,1024]{1,0:T(8,128)(2,1)S(1)} collective-permute-done((bf16[192,1024]{1,0:T(8,128)(2,1)S(1)}, bf16[192,1024]{1,0:T(8,128)(2,1)S(1)}, u32[]{:S(2)}, u32[]{:S(2)}) %collective-permute-start.35) | collective-permute-done | bytes 393248 | tf_op jit(solution)/shard_map/ppermute | solution.py:64
  177.7 8.3 %collective-permute-done.37.refs_3_ = bf16[192,1024]{1,0:T(8,128)(2,1)S(1)} collective-permute-done((bf16[192,1024]{1,0:T(8,128)(2,1)S(1)}, bf16[192,1024]{1,0:T(8,128)(2,1)S(1)}, u32[]{:S(2)}, u32[]{:S(2)}) %collective-permute-start.37) | collective-permute-done | bytes 393248 | tf_op jit(solution)/shard_map/ppermute | solution.py:64
  204.0 12.8 %shard_map.318.rest_0_.grad_ref = bf16[512,6144]{1,0:T(8,128)(2,1)} custom-call(bf16[512,1024]{1,0:T(8,128)(2,1)S(1)} %copy-done.19, bf16[3072,1024]{1,0:T(8,128)(2,1)} %copy-done, f32[512,3072]{1,0:T(8,128)} %get-tuple-element.149.gate_ref, f32[512,3072]{1,0:T(8,128)} %get-tuple-element.150.up_ref), custom_call_target="tpu_custom_call" | custom-call | flops 3221225472 | bytes 25165824 | tf_op jit(solution)/shard_map/pallas_call | solution.py:872
  220.6 12.5 %shard_map.319 = (bf16[2,256,6144]{2,1,0:T(8,128)(2,1)}, bf16[2,256,6144]{2,1,0:T(8,128)(2,1)}) custom-call(s32[2]{0:T(128)S(1)} %pad_add_fusion.where, bf16[512,1024]{1,0:T(8,128)(2,1)S(1)} %copy-done.12, bf16[512,6144]{1,0:T(8,128)(2,1)} %shard_map.318.rest_0_.grad_ref), custom_call_target="tpu_custom_call" | custom-call | flops 6442450944 | bytes 19922944 | tf_op jit(solution)/shard_map/pallas_call | solution.py:310
  234.4 13.8 %shard_map.320 = (bf16[512,1024]{1,0:T(8,128)(2,1)S(1)}, f32[1,1024]{1,0:T(1,128)S(1)}, f32[512,1024]{1,0:T(8,128)S(1)}) custom-call(bf16[512,6144]{1,0:T(8,128)(2,1)} %shard_map.318.rest_0_.grad_ref, bf16[1024,6144]{1,0:T(8,128)(2,1)} %shard_map.314.left_ref.right_ref.weight_ref, f32[512,1024]{1,0:T(8,128)} %copy-done.42, bf16[512,1024]{1,0:T(8,128)(2,1)S(1)} %copy-done.19, ...), custom_call_target="tpu_custom_call" | custom-call | flops 6442450944 | bytes 26214400 | tf_op jit(solution)/shard_map/pallas_call | solution.py:830
  262.5 7.1 %shard_map.321 = (bf16[2,512,1024]{2,1,0:T(8,128)(2,1)S(1)}, bf16[2,512,1024]{2,1,0:T(8,128)(2,1)S(1)}) custom-call(s32[2]{0:T(128)S(1)} %pad_add_fusion.where, bf16[512,2048]{1,0:T(8,128)(2,1)} %copy-done.17, bf16[512,1024]{1,0:T(8,128)(2,1)S(1)} %get-tuple-element.169.rest_0_.rest_1_, bf16[512,1024]{1,0:T(8,128)(2,1)S(1)} %get-tuple-element.169.rest_0_.rest_1_), custom_call_target="tpu_custom_call" | custom-call | flops 2147483648 | bytes 7340032 | tf_op jit(solution)/shard_map/pallas_call | solution.py:310
  273.8 8.1 %collective-permute-done.50 = bf16[1,384,512]{2,1,0:T(8,128)(2,1)S(1)} collective-permute-done((bf16[1,384,512]{2,1,0:T(8,128)(2,1)}, bf16[1,384,512]{2,1,0:T(8,128)(2,1)S(1)}, u32[]{:S(2)}, u32[]{:S(2)}) %collective-permute-start.50) | collective-permute-done | bytes 393248 | tf_op jit(solution)/shard_map/ppermute | solution.py:64
  291.1 17.3 %shard_map.322 = (bf16[512,4096]{1,0:T(8,128)(2,1)}, f32[2,128]{1,0:T(2,128)S(1)}) custom-call(f32[512,4096]{1,0:T(8,128)} %fusion.10.query_ref.key_ref.value_ref, f32[512,4096]{1,0:T(8,128)} %fusion.10.query_ref.key_ref.value_ref, f32[512,4096]{1,0:T(8,128)} %fusion.10.query_ref.key_ref.value_ref, f32[512,128]{1,0:T(8,128)S(1)} %get-tuple-element.311.cos_ref, ...), custom_call_target="tpu_custom_call" | custom-call | flops 5368709120 | bytes 12582912 | tf_op jit(solution)/shard_map/pallas_call | solution.py:732
  308.4 7.8 %collective-permute-done.53 = bf16[1,128,6144]{2,1,0:T(8,128)(2,1)S(1)} collective-permute-done((bf16[1,128,6144]{2,1,0:T(8,128)(2,1)}, bf16[1,128,6144]{2,1,0:T(8,128)(2,1)S(1)}, u32[]{:S(2)}, u32[]{:S(2)}) %collective-permute-start.53) | collective-permute-done | bytes 1572896 | tf_op jit(solution)/shard_map/ppermute | solution.py:64
  324.6 19.2 %shard_map.323 = (bf16[512,4096]{1,0:T(8,128)(2,1)}, f32[2,128]{1,0:T(2,128)S(1)}) custom-call(f32[512,4096]{1,0:T(8,128)} %fusion.10.query_ref.key_ref.value_ref, f32[512,4096]{1,0:T(8,128)} %fusion.10.query_ref.key_ref.value_ref, f32[512,4096]{1,0:T(8,128)} %fusion.10.query_ref.key_ref.value_ref, ...), custom_call_target="tpu_custom_call", output_to_operand_aliasing={{0}: (9, {})} | custom-call | flops 5368709120 | bytes 12582912 | tf_op jit(solution)/shard_map/pallas_call | solution.py:732
  350.0 10.3 %shard_map.324 = (bf16[2,256,4096]{2,1,0:T(8,128)(2,1)S(1)}, bf16[2,256,4096]{2,1,0:T(8,128)(2,1)}) custom-call(s32[2]{0:T(128)S(1)} %pad_add_fusion.where, bf16[512,1024]{1,0:T(8,128)(2,1)S(1)} %copy-done.21, bf16[512,4096]{1,0:T(8,128)(2,1)} %get-tuple-element.219.rest_0_.grad_ref), custom_call_target="tpu_custom_call" | custom-call | flops 4294967296 | bytes 13631488 | tf_op jit(solution)/shard_map/pallas_call | solution.py:310
  365.7 19.1 %collective-permute-done.61 = bf16[1,256,1536]{2,1,0:T(8,128)(2,1)S(1)} collective-permute-done((bf16[1,256,1536]{2,1,0:T(8,128)(2,1)}, bf16[1,256,1536]{2,1,0:T(8,128)(2,1)S(1)}, u32[]{:S(2)}, u32[]{:S(2)}) %collective-permute-start.61) | collective-permute-done | bytes 786464 | tf_op jit(solution)/shard_map/ppermute | solution.py:64
  399.9 10.4 %shard_map.325 = (bf16[512,1024]{1,0:T(8,128)(2,1)}, f32[1,1024]{1,0:T(1,128)S(1)}) custom-call(bf16[512,4096]{1,0:T(8,128)(2,1)} %get-tuple-element.219.rest_0_.grad_ref, bf16[1024,4096]{1,0:T(8,128)(2,1)} %copy-done.2, bf16[512,1024]{1,0:T(8,128)(2,1)S(1)} %copy-done.14, f32[512,1024]{1,0:T(8,128)S(1)} %copy-done.38, f32[1,1024]{1,0:T(1,128)S(1)} %bitcast.100), custom_call_target="tpu_custom_call" | custom-call | flops 4294967296 | bytes 19922944 | tf_op jit(solution)/shard_map/pallas_call | solution.py:830
  414.0 6.1 %collective-permute-done.72 = bf16[1,256,768]{2,1,0:T(8,128)(2,1)S(1)} collective-permute-done((bf16[1,256,768]{2,1,0:T(8,128)(2,1)}, bf16[1,256,768]{2,1,0:T(8,128)(2,1)S(1)}, u32[]{:S(2)}, u32[]{:S(2)}) %collective-permute-start.72) | collective-permute-done | bytes 393248 | tf_op jit(solution)/shard_map/ppermute | solution.py:64
  441.7 20.4 %collective-permute-done.68 = bf16[1,256,1024]{2,1,0:T(8,128)(2,1)S(1)} collective-permute-done((bf16[1,256,1024]{2,1,0:T(8,128)(2,1)S(1)}, bf16[1,256,1024]{2,1,0:T(8,128)(2,1)S(1)}, u32[]{:S(2)}, u32[]{:S(2)}) %collective-permute-start.68) | collective-permute-done | bytes 524320 | tf_op jit(solution)/shard_map/ppermute | solution.py:64
  471.5 8.3 %collective-permute-done.69 = bf16[1,256,512]{2,1,0:T(8,128)(2,1)S(1)} collective-permute-done((bf16[1,256,512]{2,1,0:T(8,128)(2,1)S(1)}, bf16[1,256,512]{2,1,0:T(8,128)(2,1)S(1)}, u32[]{:S(2)}, u32[]{:S(2)}) %collective-permute-start.69) | collective-permute-done | bytes 262176 | tf_op jit(solution)/shard_map/ppermute | solution.py:64
  485.7 15.8 %shard_map.326 = f32[8,1152]{1,0:T(8,128)} custom-call(f32[8,1152]{1,0:T(8,128)} %select_maximum_fusion.in_ref), custom_call_target="tpu_custom_call" | custom-call | tf_op jit(solution)/shard_map/pallas_call | solution.py:224
  510.1 10.3 %shard_map.327 = (f32[768,1024]{1,0:T(8,128)}, f32[2,768,1024]{2,1,0:T(8,128)}) custom-call(s32[1]{0:T(128)} %bitcast.8.where, f32[1,1]{1,0:T(1,128)} %bitcast.20.factor_ref, f32[768,1024]{1,0:T(8,128)S(1)} %copy-done.1, f32[2,768,1024]{2,1,0:T(8,128)} %moment_ref.4, bf16[4,768,128]{2,1,0:T(8,128)(2,1)} %pad_maximum_fusion.4.rest_0_, ...), custom_call_target="tpu_custom_call" | custom-call | flops 15728640 | bytes 20447232 | tf_op jit(solution)/shard_map/pallas_call | solution.py:481
  526.2 5.7 add_convert_fusion.2
  540.2 21.9 %collective-permute-done.81.rest_1_ = bf16[4,256,768]{2,1,0:T(8,128)(2,1)S(1)} collective-permute-done((bf16[4,256,768]{2,1,0:T(8,128)(2,1)S(1)}, bf16[4,256,768]{2,1,0:T(8,128)(2,1)S(1)}, u32[]{:S(2)}, u32[]{:S(2)}) %collective-permute-start.81) | collective-permute-done | bytes 1572896 | tf_op jit(solution)/shard_map/ppermute | solution.py:64
  562.1 18.4 %shard_map.328 = (f32[256,6144]{1,0:T(8,128)}, f32[2,256,6144]{2,1,0:T(8,128)}) custom-call(s32[1]{0:T(128)} %bitcast.8.where, f32[1,1]{1,0:T(1,128)} %bitcast.21.factor_ref, f32[256,6144]{1,0:T(8,128)} %master_ref.5, f32[2,256,6144]{2,1,0:T(8,128)} %moment_ref.5, bf16[4,256,768]{2,1,0:T(8,128)(2,1)S(1)} %pad_maximum_fusion.rest_0_, ...), custom_call_target="tpu_custom_call" | custom-call | flops 31457280 | bytes 40894464 | tf_op jit(solution)/shard_map/pallas_call | solution.py:481
  580.5 5.2 shard_map.329
  585.7 7.8 %collective-permute-done.85.rest_1_ = bf16[4,256,512]{2,1,0:T(8,128)(2,1)S(1)} collective-permute-done((bf16[4,256,512]{2,1,0:T(8,128)(2,1)S(1)}, bf16[4,256,512]{2,1,0:T(8,128)(2,1)S(1)}, u32[]{:S(2)}, u32[]{:S(2)}) %collective-permute-start.85) | collective-permute-done | bytes 1048608 | tf_op jit(solution)/shard_map/ppermute | solution.py:64
  593.5 10.5 %shard_map.330 = (f32[256,4096]{1,0:T(8,128)}, f32[2,256,4096]{2,1,0:T(8,128)}) custom-call(s32[1]{0:T(128)} %bitcast.8.where, f32[1,1]{1,0:T(1,128)} %bitcast.25.factor_ref, f32[256,4096]{1,0:T(8,128)} %master_ref.7, f32[2,256,4096]{2,1,0:T(8,128)} %moment_ref.7, bf16[4,256,512]{2,1,0:T(8,128)(2,1)S(1)} %pad_maximum_fusion.1.rest_0_, ...), custom_call_target="tpu_custom_call" | custom-call | flops 20971520 | bytes 27262976 | tf_op jit(solution)/shard_map/pallas_call | solution.py:481
  (438 shorter events, 233.6 us)
Async XLA Ops:
  2.0 28.3 %collective-permute-start = (bf16[1,2,288]{2,1,0:T(2,128)(2,1)S(1)}, bf16[1,2,288]{2,1,0:T(2,128)(2,1)S(1)}, u32[]{:S(2)}, u32[]{:S(2)}) collective-permute-start(bf16[1,2,288]{2,1,0:T(2,128)(2,1)S(1)} %pad_maximum_fusion.26), channel_id=1, source_target_pairs={{0,2},{1,3},{2,0},{3,1},{4,6},{5,7},{6,4},{7,5},{8,10},{9,11},{10,... | collective-permute-start | bytes 3464 | tf_op jit(solution)/shard_map/ppermute | solution.py:64
  9.0 46.4 %collective-permute-start.7 = (bf16[256,4096]{1,0:T(8,128)(2,1)}, bf16[256,4096]{1,0:T(8,128)(2,1)}, u32[]{:S(2)}, u32[]{:S(2)}) collective-permute-start(bf16[256,4096]{1,0:T(8,128)(2,1)} %convert_element_type.673.refs_0_), channel_id=1, source_target_pairs={{0,1},{1,0},{2,3},{3,2},{4,5},{5,4},{6,7},{7,6},{8,9},{9,8},{10,11... | collective-permute-start | bytes 6291464 | tf_op jit(solution)/shard_map/ppermute | solution.py:64
  53.3 75.4 %collective-permute-start.29 = (bf16[256,6144]{1,0:T(8,128)(2,1)S(1)}, bf16[256,6144]{1,0:T(8,128)(2,1)}, u32[]{:S(2)}, u32[]{:S(2)}) collective-permute-start(bf16[256,6144]{1,0:T(8,128)(2,1)S(1)} %convert_element_type.681.refs_0_), channel_id=1, source_target_pairs={{0,1},{1,0},{2,3},{3,2},{4,5},{5,4},{6,7},{7,6},{8,9},{9,8},{10,11... | collective-permute-start | bytes 9437192 | tf_op jit(solution)/shard_map/ppermute | solution.py:64
  54.2 25.2 %collective-permute-start.24 = (bf16[64,6144]{1,0:T(8,128)(2,1)S(1)}, bf16[64,6144]{1,0:T(8,128)(2,1)}, u32[]{:S(2)}, u32[]{:S(2)}) collective-permute-start(bf16[64,6144]{1,0:T(8,128)(2,1)S(1)} %copy-done.52), channel_id=1, source_target_pairs={{0,2},{1,3},{2,0},{3,1},{4,6},{5,7},{6,4},{7,5},{8,10},{9,11},{10,... | collective-permute-start | bytes 2359304 | tf_op jit(solution)/shard_map/ppermute | solution.py:64
  83.0 35.1 %collective-permute-start.30 = (bf16[64,6144]{1,0:T(8,128)(2,1)}, bf16[64,6144]{1,0:T(8,128)(2,1)}, u32[]{:S(2)}, u32[]{:S(2)}) collective-permute-start(bf16[64,6144]{1,0:T(8,128)(2,1)} %collective-permute-done.24.refs_1_), channel_id=1, source_target_pairs={{0,1},{1,0},{2,3},{3,2},{4,5},{5,4},{6,7},{7,6},{8,9},{9,8},{10,11... | collective-permute-start | bytes 2359304 | tf_op jit(solution)/shard_map/ppermute | solution.py:64
  83.3 33.3 %collective-permute-start.25 = (bf16[64,6144]{1,0:T(8,128)(2,1)}, bf16[64,6144]{1,0:T(8,128)(2,1)}, u32[]{:S(2)}, u32[]{:S(2)}) collective-permute-start(bf16[64,6144]{1,0:T(8,128)(2,1)} %collective-permute-done.24.refs_1_), channel_id=1, source_target_pairs={{0,4},{4,0},{8,12},{12,8},{16,20},{20,16},{24,28},{28,24},{1,5},{5... | collective-permute-start | bytes 2359304 | tf_op jit(solution)/shard_map/ppermute | solution.py:64
  85.5 29.2 %collective-permute-start.26 = (bf16[64,6144]{1,0:T(8,128)(2,1)}, bf16[64,6144]{1,0:T(8,128)(2,1)}, u32[]{:S(2)}, u32[]{:S(2)}) collective-permute-start(bf16[64,6144]{1,0:T(8,128)(2,1)} %collective-permute-done.24.refs_1_), channel_id=1, source_target_pairs={{0,8},{4,12},{8,0},{12,4},{16,24},{20,28},{24,16},{28,20},{1,9},{5... | collective-permute-start | bytes 2359304 | tf_op jit(solution)/shard_map/ppermute | solution.py:64
  161.5 55.3 %collective-permute-start.46 = (bf16[2,768,1024]{2,1,0:T(8,128)(2,1)}, bf16[2,768,1024]{2,1,0:T(8,128)(2,1)}, u32[]{:S(2)}, u32[]{:S(2)}) collective-permute-start(bf16[2,768,1024]{2,1,0:T(8,128)(2,1)} %get-tuple-element.144), channel_id=1, source_target_pairs={{0,1},{1,0},{2,3},{3,2},{4,5},{5,4},{6,7},{7,6},{8,9},{9,8},{10,11... | collective-permute-start | bytes 9437192 | tf_op jit(solution)/shard_map/ppermute | solution.py:64
  163.1 24.6 %collective-permute-start.40 = (bf16[768,1024]{1,0:T(8,128)(2,1)}, bf16[768,1024]{1,0:T(8,128)(2,1)}, u32[]{:S(2)}, u32[]{:S(2)}) collective-permute-start(bf16[768,1024]{1,0:T(8,128)(2,1)} %convert_element_type.682.refs_0_), channel_id=1, source_target_pairs={{0,1},{1,0},{2,3},{3,2},{4,5},{5,4},{6,7},{7,6},{8,9},{9,8},{10,11... | collective-permute-start | bytes 4718600 | tf_op jit(solution)/shard_map/ppermute | solution.py:64
  271.5 44.7 %collective-permute-start.53 = (bf16[1,128,6144]{2,1,0:T(8,128)(2,1)}, bf16[1,128,6144]{2,1,0:T(8,128)(2,1)S(1)}, u32[]{:S(2)}, u32[]{:S(2)}) collective-permute-start(bf16[1,128,6144]{2,1,0:T(8,128)(2,1)} %add_convert_fusion.1), channel_id=1, source_target_pairs={{0,2},{1,3},{2,0},{3,1},{4,6},{5,7},{6,4},{7,5},{8,10},{9,11},{10,... | collective-permute-start | bytes 4718600 | tf_op jit(solution)/shard_map/ppermute | solution.py:64
  272.3 43.9 %collective-permute-start.54 = (bf16[2,128,3072]{2,1,0:T(8,128)(2,1)}, bf16[2,128,3072]{2,1,0:T(8,128)(2,1)}, u32[]{:S(2)}, u32[]{:S(2)}) collective-permute-start(bf16[2,128,3072]{2,1,0:T(8,128)(2,1)} %add_convert_fusion), channel_id=1, source_target_pairs={{0,4},{4,0},{8,12},{12,8},{16,20},{20,16},{24,28},{28,24},{1,5},{5... | collective-permute-start | bytes 4718600 | tf_op jit(solution)/shard_map/ppermute | solution.py:64
  285.0 31.3 %collective-permute-start.55 = (bf16[1,768,256]{2,1,0:T(8,128)(2,1)}, bf16[1,768,256]{2,1,0:T(8,128)(2,1)}, u32[]{:S(2)}, u32[]{:S(2)}) collective-permute-start(bf16[1,768,256]{2,1,0:T(8,128)(2,1)} %pad_maximum_fusion.10), channel_id=1, source_target_pairs={{0,8},{4,12},{8,0},{12,4},{16,24},{20,28},{24,16},{28,20},{1,9},{5... | collective-permute-start | bytes 1179656 | tf_op jit(solution)/shard_map/ppermute | solution.py:64
  288.9 54.9 %collective-permute-start.58 = (bf16[1,256,1024]{2,1,0:T(8,128)(2,1)S(1)}, bf16[1,256,1024]{2,1,0:T(8,128)(2,1)S(1)}, u32[]{:S(2)}, u32[]{:S(2)}) collective-permute-start(bf16[1,256,1024]{2,1,0:T(8,128)(2,1)S(1)} %add_convert_fusion.12), channel_id=1, source_target_pairs={{0,2},{1,3},{2,0},{3,1},{4,6},{5,7},{6,4},{7,5},{8,10},{9,11},{10,... | collective-permute-start | bytes 1572872 | tf_op jit(solution)/shard_map/ppermute | solution.py:64
  290.4 53.4 %collective-permute-start.59 = (bf16[2,256,512]{2,1,0:T(8,128)(2,1)S(1)}, bf16[2,256,512]{2,1,0:T(8,128)(2,1)}, u32[]{:S(2)}, u32[]{:S(2)}) collective-permute-start(bf16[2,256,512]{2,1,0:T(8,128)(2,1)S(1)} %add_convert_fusion.11), channel_id=1, source_target_pairs={{0,4},{4,0},{8,12},{12,8},{16,20},{20,16},{24,28},{28,24},{1,5},{5... | collective-permute-start | bytes 1572872 | tf_op jit(solution)/shard_map/ppermute | solution.py:64
  319.6 26.8 %collective-permute-start.56 = (bf16[1,128,3072]{2,1,0:T(8,128)(2,1)S(1)}, bf16[1,128,3072]{2,1,0:T(8,128)(2,1)S(1)}, u32[]{:S(2)}, u32[]{:S(2)}) collective-permute-start(bf16[1,128,3072]{2,1,0:T(8,128)(2,1)S(1)} %get-tuple-element.271), channel_id=1, source_target_pairs={{0,4},{4,0},{8,12},{12,8},{16,20},{20,16},{24,28},{28,24},{1,5},{5... | collective-permute-start | bytes 2359304 | tf_op jit(solution)/shard_map/ppermute | solution.py:64
  321.2 25.3 %collective-permute-start.57 = (bf16[1,128,3072]{2,1,0:T(8,128)(2,1)S(1)}, bf16[1,128,3072]{2,1,0:T(8,128)(2,1)S(1)}, u32[]{:S(2)}, u32[]{:S(2)}) collective-permute-start(bf16[1,128,3072]{2,1,0:T(8,128)(2,1)S(1)} %get-tuple-element.270), channel_id=1, source_target_pairs={{0,2},{1,3},{2,0},{3,1},{4,6},{5,7},{6,4},{7,5},{8,10},{9,11},{10,... | collective-permute-start | bytes 2359304 | tf_op jit(solution)/shard_map/ppermute | solution.py:64
  360.3 24.4 %collective-permute-start.60 = (bf16[2,256,4096]{2,1,0:T(8,128)(2,1)S(1)}, bf16[2,256,4096]{2,1,0:T(8,128)(2,1)S(1)}, u32[]{:S(2)}, u32[]{:S(2)}) collective-permute-start(bf16[2,256,4096]{2,1,0:T(8,128)(2,1)S(1)} %get-tuple-element.197), channel_id=1, source_target_pairs={{0,1},{1,0},{2,3},{3,2},{4,5},{5,4},{6,7},{7,6},{8,9},{9,8},{10,11... | collective-permute-start | bytes 12582920 | tf_op jit(solution)/shard_map/ppermute | solution.py:64
  360.8 49.6 %collective-permute-start.73 = (bf16[1,768,128]{2,1,0:T(8,128)(2,1)}, bf16[1,768,128]{2,1,0:T(8,128)(2,1)}, u32[]{:S(2)}, u32[]{:S(2)}) collective-permute-start(bf16[1,768,128]{2,1,0:T(8,128)(2,1)} %pad_maximum_fusion.20), channel_id=1, source_target_pairs={{0,16},{4,20},{8,24},{12,28},{16,0},{20,4},{24,8},{28,12},{1,17},{... | collective-permute-start | bytes 589832 | tf_op jit(solution)/shard_map/ppermute | solution.py:64
  363.5 27.9 %collective-permute-start.62 = (bf16[1,256,512]{2,1,0:T(8,128)(2,1)S(1)}, bf16[1,256,512]{2,1,0:T(8,128)(2,1)S(1)}, u32[]{:S(2)}, u32[]{:S(2)}) collective-permute-start(bf16[1,256,512]{2,1,0:T(8,128)(2,1)S(1)} %copy-done.65), channel_id=1, source_target_pairs={{0,4},{4,0},{8,12},{12,8},{16,20},{20,16},{24,28},{28,24},{1,5},{5... | collective-permute-start | bytes 786440 | tf_op jit(solution)/shard_map/ppermute | solution.py:64
  364.9 26.5 %collective-permute-start.63 = (bf16[1,256,512]{2,1,0:T(8,128)(2,1)S(1)}, bf16[1,256,512]{2,1,0:T(8,128)(2,1)S(1)}, u32[]{:S(2)}, u32[]{:S(2)}) collective-permute-start(bf16[1,256,512]{2,1,0:T(8,128)(2,1)S(1)} %get-tuple-element.294), channel_id=1, source_target_pairs={{0,2},{1,3},{2,0},{3,1},{4,6},{5,7},{6,4},{7,5},{8,10},{9,11},{10,... | collective-permute-start | bytes 786440 | tf_op jit(solution)/shard_map/ppermute | solution.py:64
  387.4 34.5 %collective-permute-start.64 = (bf16[1,128,4096]{2,1,0:T(8,128)(2,1)}, bf16[1,128,4096]{2,1,0:T(8,128)(2,1)}, u32[]{:S(2)}, u32[]{:S(2)}) collective-permute-start(bf16[1,128,4096]{2,1,0:T(8,128)(2,1)} %add_convert_fusion.4), channel_id=1, source_target_pairs={{0,2},{1,3},{2,0},{3,1},{4,6},{5,7},{6,4},{7,5},{8,10},{9,11},{10,... | collective-permute-start | bytes 3145736 | tf_op jit(solution)/shard_map/ppermute | solution.py:64
  390.8 31.1 %collective-permute-start.66 = (bf16[2,128,2048]{2,1,0:T(8,128)(2,1)}, bf16[2,128,2048]{2,1,0:T(8,128)(2,1)}, u32[]{:S(2)}, u32[]{:S(2)}) collective-permute-start(bf16[2,128,2048]{2,1,0:T(8,128)(2,1)} %add_convert_fusion.3), channel_id=1, source_target_pairs={{0,4},{4,0},{8,12},{12,8},{16,20},{20,16},{24,28},{28,24},{1,5},{5... | collective-permute-start | bytes 3145736 | tf_op jit(solution)/shard_map/ppermute | solution.py:64
  435.2 26.8 %collective-permute-start.68 = (bf16[1,256,1024]{2,1,0:T(8,128)(2,1)S(1)}, bf16[1,256,1024]{2,1,0:T(8,128)(2,1)S(1)}, u32[]{:S(2)}, u32[]{:S(2)}) collective-permute-start(bf16[1,256,1024]{2,1,0:T(8,128)(2,1)S(1)} %pad_maximum_fusion.6), channel_id=1, source_target_pairs={{0,8},{4,12},{8,0},{12,4},{16,24},{20,28},{24,16},{28,20},{1,9},{5... | collective-permute-start | bytes 1572872 | tf_op jit(solution)/shard_map/ppermute | solution.py:64
  437.3 29.0 %collective-permute-start.75 = (bf16[2,768,128]{2,1,0:T(8,128)(2,1)S(1)}, bf16[2,768,128]{2,1,0:T(8,128)(2,1)S(1)}, u32[]{:S(2)}, u32[]{:S(2)}) collective-permute-start(bf16[2,768,128]{2,1,0:T(8,128)(2,1)S(1)} %pad_maximum_fusion.13), channel_id=1, source_target_pairs={{0,8},{4,12},{8,0},{12,4},{16,24},{20,28},{24,16},{28,20},{1,9},{5... | collective-permute-start | bytes 1179656 | tf_op jit(solution)/shard_map/ppermute | solution.py:64
  437.5 31.3 %collective-permute-start.79 = (bf16[1,256,768]{2,1,0:T(8,128)(2,1)S(1)}, bf16[1,256,768]{2,1,0:T(8,128)(2,1)S(1)}, u32[]{:S(2)}, u32[]{:S(2)}) collective-permute-start(bf16[1,256,768]{2,1,0:T(8,128)(2,1)S(1)} %convert_bitcast_fusion), channel_id=1, source_target_pairs={{0,16},{4,20},{8,24},{12,28},{16,0},{20,4},{24,8},{28,12},{1,17},{... | collective-permute-start | bytes 1179656 | tf_op jit(solution)/shard_map/ppermute | solution.py:64
  441.7 62.4 %collective-permute-start.82 = (bf16[1,512,128]{2,1,0:T(8,128)(2,1)}, bf16[1,512,128]{2,1,0:T(8,128)(2,1)}, u32[]{:S(2)}, u32[]{:S(2)}) collective-permute-start(bf16[1,512,128]{2,1,0:T(8,128)(2,1)} %convert_bitcast_fusion.3), channel_id=1, source_target_pairs={{0,16},{4,20},{8,24},{12,28},{16,0},{20,4},{24,8},{28,12},{1,17},{... | collective-permute-start | bytes 393224 | tf_op jit(solution)/shard_map/ppermute | solution.py:64
  467.2 42.8 %collective-permute-start.77 = (bf16[4,768,128]{2,1,0:T(8,128)(2,1)}, bf16[4,768,128]{2,1,0:T(8,128)(2,1)}, u32[]{:S(2)}, u32[]{:S(2)}) collective-permute-start(bf16[4,768,128]{2,1,0:T(8,128)(2,1)} %pad_maximum_fusion.4.rest_0_), channel_id=1, source_target_pairs={{0,4},{4,0},{8,12},{12,8},{16,20},{20,16},{24,28},{28,24},{1,5},{5... | collective-permute-start | bytes 2359304 | tf_op jit(solution)/shard_map/ppermute | solution.py:64
  469.8 53.6 %collective-permute-start.80 = (bf16[2,256,768]{2,1,0:T(8,128)(2,1)}, bf16[2,256,768]{2,1,0:T(8,128)(2,1)}, u32[]{:S(2)}, u32[]{:S(2)}) collective-permute-start(bf16[2,256,768]{2,1,0:T(8,128)(2,1)} %pad_maximum_fusion.5), channel_id=1, source_target_pairs={{0,8},{4,12},{8,0},{12,4},{16,24},{20,28},{24,16},{28,20},{1,9},{5... | collective-permute-start | bytes 2359304 | tf_op jit(solution)/shard_map/ppermute | solution.py:64
  505.7 26.1 %collective-permute-start.83 = (bf16[2,512,128]{2,1,0:T(8,128)(2,1)}, bf16[2,512,128]{2,1,0:T(8,128)(2,1)}, u32[]{:S(2)}, u32[]{:S(2)}) collective-permute-start(bf16[2,512,128]{2,1,0:T(8,128)(2,1)} %pad_maximum_fusion.19), channel_id=1, source_target_pairs={{0,8},{4,12},{8,0},{12,4},{16,24},{20,28},{24,16},{28,20},{1,9},{5... | collective-permute-start | bytes 786440 | tf_op jit(solution)/shard_map/ppermute | solution.py:64
  524.8 37.3 %collective-permute-start.81 = (bf16[4,256,768]{2,1,0:T(8,128)(2,1)S(1)}, bf16[4,256,768]{2,1,0:T(8,128)(2,1)S(1)}, u32[]{:S(2)}, u32[]{:S(2)}) collective-permute-start(bf16[4,256,768]{2,1,0:T(8,128)(2,1)S(1)} %pad_maximum_fusion.rest_0_), channel_id=1, source_target_pairs={{0,4},{4,0},{8,12},{12,8},{16,20},{20,16},{24,28},{28,24},{1,5},{5... | collective-permute-start | bytes 4718600 | tf_op jit(solution)/shard_map/ppermute | solution.py:64
  533.0 47.5 %collective-permute-start.84 = (bf16[4,512,128]{2,1,0:T(8,128)(2,1)S(1)}, bf16[4,512,128]{2,1,0:T(8,128)(2,1)S(1)}, u32[]{:S(2)}, u32[]{:S(2)}) collective-permute-start(bf16[4,512,128]{2,1,0:T(8,128)(2,1)S(1)} %pad_maximum_fusion.9.rest_0_), channel_id=1, source_target_pairs={{0,4},{4,0},{8,12},{12,8},{16,20},{20,16},{24,28},{28,24},{1,5},{5... | collective-permute-start | bytes 1572872 | tf_op jit(solution)/shard_map/ppermute | solution.py:64
  536.3 57.1 %collective-permute-start.85 = (bf16[4,256,512]{2,1,0:T(8,128)(2,1)S(1)}, bf16[4,256,512]{2,1,0:T(8,128)(2,1)S(1)}, u32[]{:S(2)}, u32[]{:S(2)}) collective-permute-start(bf16[4,256,512]{2,1,0:T(8,128)(2,1)S(1)} %pad_maximum_fusion.1.rest_0_), channel_id=1, source_target_pairs={{0,4},{4,0},{8,12},{12,8},{16,20},{20,16},{24,28},{28,24},{1,5},{5... | collective-permute-start | bytes 3145736 | tf_op jit(solution)/shard_map/ppermute | solution.py:64
  (136 other events, 1458.9 us)

commit v7 on v6

--- a/solution.py
+++ b/solution.py
@@ -117,7 +117,7 @@
     )(*[v for v, _, _ in pieces])
 
 
-def gather_rows(shard, early, late, middle, hold):
+def gather_rows(shard, early, late, middle, third, hold):
     owners = lax.axis_size(GROUP)
     copies = lax.axis_size(DP)
     here = lax.axis_index(DP)
@@ -147,8 +147,13 @@
         passed = order if middle is None else after(order, middle)
         by_one = swap(passed, DP, 1)
         by_two = swap(passed, DP, 2)
-        last_one = swap(by_two[:half], DP, 1)
-        last_two = swap(by_one[half:], DP, 2)
+        go_one, go_two = by_one, by_two
+        if third is not None:
+            go_one, go_two = after((by_one, by_two), third)
+        last_one = swap(go_two[:half], DP, 1)
+        last_two = swap(go_one[half:], DP, 2)
+        if hold is not None:
+            last_one, last_two = after((last_one, last_two), hold)
         pieces += [
             (order, 2, quarter_at(0)),
             (by_one, 2, quarter_at(2)),
@@ -913,7 +918,7 @@
     gains_all = gather_small(gains_low).reshape(2, owners, -1)
     full_norm = gains_all[:, :, :width].reshape(2, -1)
     full_head = gains_all[:, :, width:].reshape(2, -1)
-    full_qkv, first, late, _ = gather_rows(qkv_weight, None, None, None, None)
+    full_qkv, first, late, _ = gather_rows(qkv_weight, None, None, None, None, None)
     gain_one = full_norm[0].astype(jnp.float32)
     gain_two = full_norm[1].astype(jnp.float32)
     head_gain = full_head.astype(jnp.float32)
@@ -922,13 +927,13 @@
     normed_one = inputs * root_one
     hidden_one = (normed_one * gain_one).astype(jnp.bfloat16)
     projected = jnp.dot(hidden_one, full_qkv, preferred_element_type=jnp.float32)
-    full_out, _, down_late, _ = gather_rows(out_weight, first, late, projected, projected)
-    full_gate_up, _, more_late, _ = gather_rows(gate_up_weight, first, late, projected, None)
-    full_down, _, _, _ = gather_rows(
-        down_weight, first, (down_late, more_late, projected), None, None
-    )
     tables = rotary_tables(positions, HD)
     mixed_low = attention_call(attend_body, projected, tables, segment_ids, head_gain, None, 0, HK, None)
+    full_out, _, down_late, _ = gather_rows(out_weight, first, late, None, projected, mixed_low)
+    full_gate_up, _, more_late, _ = gather_rows(gate_up_weight, first, late, projected, None, None)
+    full_down, _, _, _ = gather_rows(
+        down_weight, first, (down_late, more_late, projected), None, None, None
+    )
     attended = jnp.dot(mixed_low, full_out, preferred_element_type=jnp.float32)
     residual = inputs + attended
     root_two = lax.rsqrt(jnp.mean(residual * residual, axis=-1, keepdims=True) + EPS_NORM)
@@ -1000,6 +1005,7 @@
         axis=1,
     )
     sent_next = qkv_sum.advance()
+    qkv_sum.advance()
     sent_last = qkv_sum.advance()
     qkv_own, out_own, gate_up_own, down_own = owned = tuple(
         v.finish() for v in (qkv_sum, out_sum, gate_up_sum, down_sum)
@@ -1022,7 +1028,7 @@
     gathered = [
         gather_grad(after(qkv_own, summed), renewed_down[0], None),
         gather_grad(after(out_own, *sent_last), None, None),
-        gather_grad(after(gate_up_own, *sent_last), None, summed),
+        gather_grad(after(gate_up_own, *sent_last), summed, None),
     ]
     later = after(factor, gathered[0][0][0])
     renewed_gate_up = adam_blocks(

time: 616 us -> 645 us (1.047)
  waiting for transfers between devices: 178 us -> 198 us
  starting transfers between devices: 67.5 us -> 76.4 us
    ppermute x86, waiting for transfers between devices: 178 us -> 198 us  [swap(): return lax.ppermute(value, axis, [(i, i ^ mask) for i in range(count)])]
    ppermute x86, starting transfers between devices: 67.5 us -> 76.4 us  [swap(): return lax.ppermute(value, axis, [(i, i ^ mask) for i in range(count)])]
  transfers between devices with their start and end apart: 86 -> 86, of which waited for: 32 -> 35; matrix products, arithmetic and copies ran while one was open for 18% -> 17% of each run, Pallas kernels for 25% -> 24%
where the time goes in v7:
time: 645 us; the launch traced here: 633 us
  Pallas kernels  221 us (34%)
  waiting for transfers between devices  198 us (31%)
  other arithmetic  88.9 us (14%)
  starting transfers between devices  76.4 us (12%)
  local copies, waits for them, and re-layouts  25.4 us (4%)
  matrix products  17.2 us (3%)
    ppermute x86, waiting for transfers between devices, swap(): return lax.ppermute(value, axis, [(i, i ^ mask) for i in range(count)])  198 us
    ppermute x86, starting transfers between devices, swap(): return lax.ppermute(value, axis, [(i, i ^ mask) for i in range(count)])  76.4 us
    pallas_call x3, Pallas kernels, attention_call(): pl.pallas_call(body, grid=(seq_count, count), in_specs=in_specs, out_spec...  53.9 us
    pallas_call x4, Pallas kernels, adam_blocks(): pl.pallas_call(body, out_shape=[jax.ShapeDtypeStruct(master.shape, jnp.fl...  44.3 us
    convert_element_type x20, other arithmetic, advance(): outgoing.append((self.read(far).astype(jnp.bfloat16), axis, mask))  39.6 us
    pallas_call x4, Pallas kernels, grad_blocks(): pl.pallas_call(body, out_shape=[jax.ShapeDtypeStruct((len(row_set), row_b...  38.7 us
    pallas_call x2, Pallas kernels, project_back(): pl.pallas_call(body, grid=(steps,), in_specs=[pl.BlockSpec((tokens, block...  24.4 us
    pallas_call x4, Pallas kernels, place_rows(): pl.pallas_call(body, out_shape=jax.ShapeDtypeStruct((rows * owners, colum...  18.4 us
  transfers between devices with their start and end apart: 86, of which 35 were waited for; matrix products, arithmetic and copies ran while one was open for 17% of the time, Pallas kernels for 24%

profile of v7, /device:TPU:0, one launch (start us, length us, event | category | flops | bytes accessed | tf_op | source)
XLA Modules:
  0.0 632.8 jit_solution(4200353291015974332)
XLA Ops:
  14.7 9.8 %collective-permute-done.2.refs_1_ = bf16[64,4096]{1,0:T(8,128)(2,1)} collective-permute-done((bf16[64,4096]{1,0:T(8,128)(2,1)S(1)}, bf16[64,4096]{1,0:T(8,128)(2,1)}, u32[]{:S(2)}, u32[]{:S(2)}) %collective-permute-start.2) | collective-permute-done | bytes 524320 | tf_op jit(solution)/shard_map/ppermute | solution.py:64
  31.0 8.5 %collective-permute-done.4.refs_3_ = bf16[64,4096]{1,0:T(8,128)(2,1)} collective-permute-done((bf16[64,4096]{1,0:T(8,128)(2,1)}, bf16[64,4096]{1,0:T(8,128)(2,1)}, u32[]{:S(2)}, u32[]{:S(2)}) %collective-permute-start.4) | collective-permute-done | bytes 524320 | tf_op jit(solution)/shard_map/ppermute | solution.py:64
  63.1 6.7 %fusion.10.query_ref.key_ref.value_ref = f32[512,4096]{1,0:T(8,128)} fusion(bf16[512,1024]{1,0:T(8,128)(2,1)S(1)} %fusion.2.left_ref, bf16[1024,4096]{1,0:T(8,128)(2,1)S(1)} %shard_map.311.weight_ref), kind=kOutput, calls=%fused_computation.121 | convolution fusion | flops 4294967296 | bytes 17825792 | tf_op jit(solution)/shard_map/dot_general | solution.py:929
  86.5 20.6 %collective-permute-done.17.refs_5_ = bf16[64,1024]{1,0:T(8,128)(2,1)} collective-permute-done((bf16[64,1024]{1,0:T(8,128)(2,1)}, bf16[64,1024]{1,0:T(8,128)(2,1)}, u32[]{:S(2)}, u32[]{:S(2)}) %collective-permute-start.17) | collective-permute-done | bytes 131104 | tf_op jit(solution)/shard_map/ppermute | solution.py:64
  109.1 17.4 %shard_map.312.left_ref = bf16[512,2048]{1,0:T(8,128)(2,1)S(1)} custom-call(f32[512,4096]{1,0:T(8,128)} %fusion.10.query_ref.key_ref.value_ref, f32[512,4096]{1,0:T(8,128)} %fusion.10.query_ref.key_ref.value_ref, f32[512,4096]{1,0:T(8,128)} %fusion.10.query_ref.key_ref.value_ref, f32[512,128]{1,0:T(8,128)S(1)} %get-tuple-element.317.cos_ref, ...), custom_call_target="tpu_custom_call" | custom-call | flops 4294967296 | bytes 12582912 | tf_op jit(solution)/shard_map/pallas_call | solution.py:737
  148.9 7.7 %shard_map.314.left_ref.right_ref.weight_ref = bf16[1024,6144]{1,0:T(8,128)(2,1)} custom-call(bf16[256,6144]{1,0:T(8,128)(2,1)S(1)} %convert_element_type.681.refs_0_, bf16[64,6144]{1,0:T(8,128)(2,1)} %collective-permute-done.24.refs_1_, bf16[64,6144]{1,0:T(8,128)(2,1)} %collective-permute-done.25.refs_2_, bf16[64,6144]{1,0:T(8,128)(2,1)} %collective-permute-done.26.refs_3_, ...), custom_call_target="tpu_custom_call" | custom-call | bytes 25165824 | tf_op jit(solution)/shard_map/pallas_call | solution.py:103
  156.6 13.2 %shard_map.315 = (f32[512,3072]{1,0:T(8,128)}, f32[512,3072]{1,0:T(8,128)}, bf16[512,3072]{1,0:T(8,128)(2,1)S(1)}) custom-call(bf16[512,1024]{1,0:T(8,128)(2,1)S(1)} %multiply_convert_fusion.hidden_ref.left_ref, bf16[1024,6144]{1,0:T(8,128)(2,1)} %shard_map.314.left_ref.right_ref.weight_ref, bf16[1024,6144]{1,0:T(8,128)(2,1)} %shard_map.314.left_ref.right_ref.weight_ref), custom_call_target="tpu_custom_call" | custom-call | flops 6442450944 | bytes 28311552 | tf_op jit(solution)/shard_map/pallas_call | solution.py:767
  171.4 8.9 %shard_map.316 = (bf16[2,768,1024]{2,1,0:T(8,128)(2,1)}, bf16[2,768,1024]{2,1,0:T(8,128)(2,1)}) custom-call(s32[2]{0:T(128)S(1)} %pad_add_fusion.where, bf16[512,3072]{1,0:T(8,128)(2,1)} %copy-done.24, bf16[512,1024]{1,0:T(8,128)(2,1)S(1)} %copy-done.17, bf16[512,1024]{1,0:T(8,128)(2,1)S(1)} %copy-done.17), custom_call_target="tpu_custom_call" | custom-call | flops 3221225472 | bytes 10485760 | tf_op jit(solution)/shard_map/pallas_call | solution.py:315
  183.9 10.6 %collective-permute-done.35.refs_1_ = bf16[192,1024]{1,0:T(8,128)(2,1)S(1)} collective-permute-done((bf16[192,1024]{1,0:T(8,128)(2,1)S(1)}, bf16[192,1024]{1,0:T(8,128)(2,1)S(1)}, u32[]{:S(2)}, u32[]{:S(2)}) %collective-permute-start.35) | collective-permute-done | bytes 393248 | tf_op jit(solution)/shard_map/ppermute | solution.py:64
  196.6 8.2 %collective-permute-done.37.refs_3_ = bf16[192,1024]{1,0:T(8,128)(2,1)S(1)} collective-permute-done((bf16[192,1024]{1,0:T(8,128)(2,1)S(1)}, bf16[192,1024]{1,0:T(8,128)(2,1)S(1)}, u32[]{:S(2)}, u32[]{:S(2)}) %collective-permute-start.37) | collective-permute-done | bytes 393248 | tf_op jit(solution)/shard_map/ppermute | solution.py:64
  222.6 12.9 %shard_map.318.rest_0_.grad_ref = bf16[512,6144]{1,0:T(8,128)(2,1)} custom-call(bf16[512,1024]{1,0:T(8,128)(2,1)S(1)} %copy-done.18, bf16[3072,1024]{1,0:T(8,128)(2,1)} %copy-done, f32[512,3072]{1,0:T(8,128)} %get-tuple-element.155.gate_ref, f32[512,3072]{1,0:T(8,128)} %get-tuple-element.156.up_ref), custom_call_target="tpu_custom_call" | custom-call | flops 3221225472 | bytes 25165824 | tf_op jit(solution)/shard_map/pallas_call | solution.py:877
  239.4 12.5 %shard_map.319 = (bf16[2,256,6144]{2,1,0:T(8,128)(2,1)}, bf16[2,256,6144]{2,1,0:T(8,128)(2,1)}) custom-call(s32[2]{0:T(128)S(1)} %pad_add_fusion.where, bf16[512,1024]{1,0:T(8,128)(2,1)S(1)} %copy-done.10, bf16[512,6144]{1,0:T(8,128)(2,1)} %shard_map.318.rest_0_.grad_ref), custom_call_target="tpu_custom_call" | custom-call | flops 6442450944 | bytes 19922944 | tf_op jit(solution)/shard_map/pallas_call | solution.py:315
  253.2 13.8 %shard_map.320 = (bf16[512,1024]{1,0:T(8,128)(2,1)S(1)}, f32[1,1024]{1,0:T(1,128)S(1)}, f32[512,1024]{1,0:T(8,128)S(1)}) custom-call(bf16[512,6144]{1,0:T(8,128)(2,1)} %shard_map.318.rest_0_.grad_ref, bf16[1024,6144]{1,0:T(8,128)(2,1)} %shard_map.314.left_ref.right_ref.weight_ref, f32[512,1024]{1,0:T(8,128)} %copy-done.32, bf16[512,1024]{1,0:T(8,128)(2,1)S(1)} %copy-done.18, ...), custom_call_target="tpu_custom_call" | custom-call | flops 6442450944 | bytes 26214400 | tf_op jit(solution)/shard_map/pallas_call | solution.py:835
  281.3 7.1 %shard_map.321 = (bf16[2,512,1024]{2,1,0:T(8,128)(2,1)S(1)}, bf16[2,512,1024]{2,1,0:T(8,128)(2,1)S(1)}) custom-call(s32[2]{0:T(128)S(1)} %pad_add_fusion.where, bf16[512,2048]{1,0:T(8,128)(2,1)} %copy-done.16, bf16[512,1024]{1,0:T(8,128)(2,1)S(1)} %get-tuple-element.175.rest_0_.rest_1_, bf16[512,1024]{1,0:T(8,128)(2,1)S(1)} %get-tuple-element.175.rest_0_.rest_1_), custom_call_target="tpu_custom_call" | custom-call | flops 2147483648 | bytes 7340032 | tf_op jit(solution)/shard_map/pallas_call | solution.py:315
  292.6 8.1 %collective-permute-done.50 = bf16[1,384,512]{2,1,0:T(8,128)(2,1)S(1)} collective-permute-done((bf16[1,384,512]{2,1,0:T(8,128)(2,1)}, bf16[1,384,512]{2,1,0:T(8,128)(2,1)S(1)}, u32[]{:S(2)}, u32[]{:S(2)}) %collective-permute-start.50) | collective-permute-done | bytes 393248 | tf_op jit(solution)/shard_map/ppermute | solution.py:64
  310.1 17.3 %shard_map.322 = (bf16[512,4096]{1,0:T(8,128)(2,1)}, f32[2,128]{1,0:T(2,128)S(1)}) custom-call(f32[512,4096]{1,0:T(8,128)} %fusion.10.query_ref.key_ref.value_ref, f32[512,4096]{1,0:T(8,128)} %fusion.10.query_ref.key_ref.value_ref, f32[512,4096]{1,0:T(8,128)} %fusion.10.query_ref.key_ref.value_ref, f32[512,128]{1,0:T(8,128)S(1)} %get-tuple-element.317.cos_ref, ...), custom_call_target="tpu_custom_call" | custom-call | flops 5368709120 | bytes 12582912 | tf_op jit(solution)/shard_map/pallas_call | solution.py:737
  327.4 7.7 %collective-permute-done.53 = bf16[1,128,6144]{2,1,0:T(8,128)(2,1)S(1)} collective-permute-done((bf16[1,128,6144]{2,1,0:T(8,128)(2,1)}, bf16[1,128,6144]{2,1,0:T(8,128)(2,1)S(1)}, u32[]{:S(2)}, u32[]{:S(2)}) %collective-permute-start.53) | collective-permute-done | bytes 1572896 | tf_op jit(solution)/shard_map/ppermute | solution.py:64
  343.3 19.2 %shard_map.323 = (bf16[512,4096]{1,0:T(8,128)(2,1)}, f32[2,128]{1,0:T(2,128)S(1)}) custom-call(f32[512,4096]{1,0:T(8,128)} %fusion.10.query_ref.key_ref.value_ref, f32[512,4096]{1,0:T(8,128)} %fusion.10.query_ref.key_ref.value_ref, f32[512,4096]{1,0:T(8,128)} %fusion.10.query_ref.key_ref.value_ref, ...), custom_call_target="tpu_custom_call", output_to_operand_aliasing={{0}: (9, {})} | custom-call | flops 5368709120 | bytes 12582912 | tf_op jit(solution)/shard_map/pallas_call | solution.py:737
  368.8 10.3 %shard_map.324 = (bf16[2,256,4096]{2,1,0:T(8,128)(2,1)S(1)}, bf16[2,256,4096]{2,1,0:T(8,128)(2,1)}) custom-call(s32[2]{0:T(128)S(1)} %pad_add_fusion.where, bf16[512,1024]{1,0:T(8,128)(2,1)S(1)} %copy-done.20, bf16[512,4096]{1,0:T(8,128)(2,1)} %get-tuple-element.225.rest_0_.grad_ref), custom_call_target="tpu_custom_call" | custom-call | flops 4294967296 | bytes 13631488 | tf_op jit(solution)/shard_map/pallas_call | solution.py:315
  384.8 18.7 %collective-permute-done.61 = bf16[1,256,1536]{2,1,0:T(8,128)(2,1)S(1)} collective-permute-done((bf16[1,256,1536]{2,1,0:T(8,128)(2,1)}, bf16[1,256,1536]{2,1,0:T(8,128)(2,1)S(1)}, u32[]{:S(2)}, u32[]{:S(2)}) %collective-permute-start.61) | collective-permute-done | bytes 786464 | tf_op jit(solution)/shard_map/ppermute | solution.py:64
  420.2 10.6 %shard_map.325 = (bf16[512,1024]{1,0:T(8,128)(2,1)}, f32[1,1024]{1,0:T(1,128)S(1)}) custom-call(bf16[512,4096]{1,0:T(8,128)(2,1)} %get-tuple-element.225.rest_0_.grad_ref, bf16[1024,4096]{1,0:T(8,128)(2,1)} %copy-done.2, bf16[512,1024]{1,0:T(8,128)(2,1)S(1)} %copy-done.13, f32[512,1024]{1,0:T(8,128)S(1)} %copy-done.27, f32[1,1024]{1,0:T(1,128)S(1)} %bitcast.100), custom_call_target="tpu_custom_call" | custom-call | flops 4294967296 | bytes 19922944 | tf_op jit(solution)/shard_map/pallas_call | solution.py:835
  443.3 6.0 collective-permute-done.65
  456.6 7.9 %collective-permute-done.74 = bf16[1,768,128]{2,1,0:T(8,128)(2,1)S(1)} collective-permute-done((bf16[1,768,128]{2,1,0:T(8,128)(2,1)S(1)}, bf16[1,768,128]{2,1,0:T(8,128)(2,1)S(1)}, u32[]{:S(2)}, u32[]{:S(2)}) %collective-permute-start.74) | collective-permute-done | bytes 196640 | tf_op jit(solution)/shard_map/ppermute | solution.py:64
  464.6 6.7 %collective-permute-start.75 = (bf16[2,768,128]{2,1,0:T(8,128)(2,1)S(1)}, bf16[2,768,128]{2,1,0:T(8,128)(2,1)S(1)}, u32[]{:S(2)}, u32[]{:S(2)}) collective-permute-start(bf16[2,768,128]{2,1,0:T(8,128)(2,1)S(1)} %pad_maximum_fusion.13), channel_id=1, source_target_pairs={{0,8},{4,12},{8,0},{12,4},{16,24},{20,28},{24,16},{28,20},{1,9},{5... | collective-permute-start | bytes 1179656 | tf_op jit(solution)/shard_map/ppermute | solution.py:64
  474.0 6.1 collective-permute-done.75
  483.3 12.5 %collective-permute-done.69 = bf16[1,256,512]{2,1,0:T(8,128)(2,1)S(1)} collective-permute-done((bf16[1,256,512]{2,1,0:T(8,128)(2,1)S(1)}, bf16[1,256,512]{2,1,0:T(8,128)(2,1)S(1)}, u32[]{:S(2)}, u32[]{:S(2)}) %collective-permute-start.69) | collective-permute-done | bytes 262176 | tf_op jit(solution)/shard_map/ppermute | solution.py:64
  501.8 15.4 %shard_map.326 = f32[8,1152]{1,0:T(8,128)} custom-call(f32[8,1152]{1,0:T(8,128)} %select_maximum_fusion.in_ref), custom_call_target="tpu_custom_call" | custom-call | tf_op jit(solution)/shard_map/pallas_call | solution.py:229
  530.7 10.2 %shard_map.327 = (f32[768,1024]{1,0:T(8,128)}, f32[2,768,1024]{2,1,0:T(8,128)}) custom-call(s32[1]{0:T(128)} %bitcast.8.where, f32[1,1]{1,0:T(1,128)} %bitcast.20.factor_ref, f32[768,1024]{1,0:T(8,128)S(1)} %copy-done.1, f32[2,768,1024]{2,1,0:T(8,128)} %moment_ref.4, bf16[4,768,128]{2,1,0:T(8,128)(2,1)} %pad_maximum_fusion.4.rest_0_, ...), custom_call_target="tpu_custom_call" | custom-call | flops 15728640 | bytes 20447232 | tf_op jit(solution)/shard_map/pallas_call | solution.py:486
  566.9 19.6 %collective-permute-done.81.rest_1_ = bf16[4,256,768]{2,1,0:T(8,128)(2,1)S(1)} collective-permute-done((bf16[4,256,768]{2,1,0:T(8,128)(2,1)S(1)}, bf16[4,256,768]{2,1,0:T(8,128)(2,1)S(1)}, u32[]{:S(2)}, u32[]{:S(2)}) %collective-permute-start.81) | collective-permute-done | bytes 1572896 | tf_op jit(solution)/shard_map/ppermute | solution.py:64
  586.5 18.4 %shard_map.328 = (f32[256,6144]{1,0:T(8,128)}, f32[2,256,6144]{2,1,0:T(8,128)}) custom-call(s32[1]{0:T(128)} %bitcast.8.where, f32[1,1]{1,0:T(1,128)} %bitcast.21.factor_ref, f32[256,6144]{1,0:T(8,128)} %master_ref.5, f32[2,256,6144]{2,1,0:T(8,128)} %moment_ref.5, bf16[4,256,768]{2,1,0:T(8,128)(2,1)S(1)} %pad_maximum_fusion.rest_0_, ...), custom_call_target="tpu_custom_call" | custom-call | flops 31457280 | bytes 40894464 | tf_op jit(solution)/shard_map/pallas_call | solution.py:486
  604.9 11.7 %collective-permute-done.84.rest_1_ = bf16[4,512,128]{2,1,0:T(8,128)(2,1)S(1)} collective-permute-done((bf16[4,512,128]{2,1,0:T(8,128)(2,1)S(1)}, bf16[4,512,128]{2,1,0:T(8,128)(2,1)S(1)}, u32[]{:S(2)}, u32[]{:S(2)}) %collective-permute-start.84) | collective-permute-done | bytes 524320 | tf_op jit(solution)/shard_map/ppermute | solution.py:64
  621.8 10.5 %shard_map.330 = (f32[256,4096]{1,0:T(8,128)}, f32[2,256,4096]{2,1,0:T(8,128)}) custom-call(s32[1]{0:T(128)} %bitcast.8.where, f32[1,1]{1,0:T(1,128)} %bitcast.25.factor_ref, f32[256,4096]{1,0:T(8,128)} %master_ref.7, f32[2,256,4096]{2,1,0:T(8,128)} %moment_ref.7, bf16[4,256,512]{2,1,0:T(8,128)(2,1)S(1)} %pad_maximum_fusion.1.rest_0_, ...), custom_call_target="tpu_custom_call" | custom-call | flops 20971520 | bytes 27262976 | tf_op jit(solution)/shard_map/pallas_call | solution.py:486
  (418 shorter events, 252.1 us)
Async XLA Ops:
  2.0 28.3 %collective-permute-start = (bf16[1,2,288]{2,1,0:T(2,128)(2,1)S(1)}, bf16[1,2,288]{2,1,0:T(2,128)(2,1)S(1)}, u32[]{:S(2)}, u32[]{:S(2)}) collective-permute-start(bf16[1,2,288]{2,1,0:T(2,128)(2,1)S(1)} %pad_maximum_fusion.26), channel_id=1, source_target_pairs={{0,2},{1,3},{2,0},{3,1},{4,6},{5,7},{6,4},{7,5},{8,10},{9,11},{10,... | collective-permute-start | bytes 3464 | tf_op jit(solution)/shard_map/ppermute | solution.py:64
  8.9 49.2 %collective-permute-start.7 = (bf16[256,4096]{1,0:T(8,128)(2,1)}, bf16[256,4096]{1,0:T(8,128)(2,1)}, u32[]{:S(2)}, u32[]{:S(2)}) collective-permute-start(bf16[256,4096]{1,0:T(8,128)(2,1)} %convert_element_type.673.refs_0_), channel_id=1, source_target_pairs={{0,1},{1,0},{2,3},{3,2},{4,5},{5,4},{6,7},{7,6},{8,9},{9,8},{10,11... | collective-permute-start | bytes 6291464 | tf_op jit(solution)/shard_map/ppermute | solution.py:64
  55.3 28.5 %collective-permute-start.18 = (bf16[512,1024]{1,0:T(8,128)(2,1)}, bf16[512,1024]{1,0:T(8,128)(2,1)}, u32[]{:S(2)}, u32[]{:S(2)}) collective-permute-start(bf16[512,1024]{1,0:T(8,128)(2,1)} %convert_element_type.677.refs_0_), channel_id=1, source_target_pairs={{0,1},{1,0},{2,3},{3,2},{4,5},{5,4},{6,7},{7,6},{8,9},{9,8},{10,11... | collective-permute-start | bytes 3145736 | tf_op jit(solution)/shard_map/ppermute | solution.py:64
  55.9 91.6 %collective-permute-start.29 = (bf16[256,6144]{1,0:T(8,128)(2,1)S(1)}, bf16[256,6144]{1,0:T(8,128)(2,1)}, u32[]{:S(2)}, u32[]{:S(2)}) collective-permute-start(bf16[256,6144]{1,0:T(8,128)(2,1)S(1)} %convert_element_type.681.refs_0_), channel_id=1, source_target_pairs={{0,1},{1,0},{2,3},{3,2},{4,5},{5,4},{6,7},{7,6},{8,9},{9,8},{10,11... | collective-permute-start | bytes 9437192 | tf_op jit(solution)/shard_map/ppermute | solution.py:64
  83.8 53.9 %collective-permute-start.30 = (bf16[64,6144]{1,0:T(8,128)(2,1)}, bf16[64,6144]{1,0:T(8,128)(2,1)}, u32[]{:S(2)}, u32[]{:S(2)}) collective-permute-start(bf16[64,6144]{1,0:T(8,128)(2,1)} %collective-permute-done.24.refs_1_), channel_id=1, source_target_pairs={{0,1},{1,0},{2,3},{3,2},{4,5},{5,4},{6,7},{7,6},{8,9},{9,8},{10,11... | collective-permute-start | bytes 2359304 | tf_op jit(solution)/shard_map/ppermute | solution.py:64
  83.8 51.2 %collective-permute-start.25 = (bf16[64,6144]{1,0:T(8,128)(2,1)}, bf16[64,6144]{1,0:T(8,128)(2,1)}, u32[]{:S(2)}, u32[]{:S(2)}) collective-permute-start(bf16[64,6144]{1,0:T(8,128)(2,1)} %collective-permute-done.24.refs_1_), channel_id=1, source_target_pairs={{0,4},{4,0},{8,12},{12,8},{16,20},{20,16},{24,28},{28,24},{1,5},{5... | collective-permute-start | bytes 2359304 | tf_op jit(solution)/shard_map/ppermute | solution.py:64
  84.4 47.7 %collective-permute-start.26 = (bf16[64,6144]{1,0:T(8,128)(2,1)}, bf16[64,6144]{1,0:T(8,128)(2,1)}, u32[]{:S(2)}, u32[]{:S(2)}) collective-permute-start(bf16[64,6144]{1,0:T(8,128)(2,1)} %collective-permute-done.24.refs_1_), channel_id=1, source_target_pairs={{0,8},{4,12},{8,0},{12,4},{16,24},{20,28},{24,16},{28,20},{1,9},{5... | collective-permute-start | bytes 2359304 | tf_op jit(solution)/shard_map/ppermute | solution.py:64
  180.3 55.2 %collective-permute-start.46 = (bf16[2,768,1024]{2,1,0:T(8,128)(2,1)}, bf16[2,768,1024]{2,1,0:T(8,128)(2,1)}, u32[]{:S(2)}, u32[]{:S(2)}) collective-permute-start(bf16[2,768,1024]{2,1,0:T(8,128)(2,1)} %get-tuple-element.150), channel_id=1, source_target_pairs={{0,1},{1,0},{2,3},{3,2},{4,5},{5,4},{6,7},{7,6},{8,9},{9,8},{10,11... | collective-permute-start | bytes 9437192 | tf_op jit(solution)/shard_map/ppermute | solution.py:64
  181.9 24.5 %collective-permute-start.40 = (bf16[768,1024]{1,0:T(8,128)(2,1)}, bf16[768,1024]{1,0:T(8,128)(2,1)}, u32[]{:S(2)}, u32[]{:S(2)}) collective-permute-start(bf16[768,1024]{1,0:T(8,128)(2,1)} %convert_element_type.682.refs_0_), channel_id=1, source_target_pairs={{0,1},{1,0},{2,3},{3,2},{4,5},{5,4},{6,7},{7,6},{8,9},{9,8},{10,11... | collective-permute-start | bytes 4718600 | tf_op jit(solution)/shard_map/ppermute | solution.py:64
  251.9 23.3 %collective-permute-start.49 = (bf16[2,256,6144]{2,1,0:T(8,128)(2,1)}, bf16[2,256,6144]{2,1,0:T(8,128)(2,1)}, u32[]{:S(2)}, u32[]{:S(2)}) collective-permute-start(bf16[2,256,6144]{2,1,0:T(8,128)(2,1)} %get-tuple-element.158), channel_id=1, source_target_pairs={{0,1},{1,0},{2,3},{3,2},{4,5},{5,4},{6,7},{7,6},{8,9},{9,8},{10,11... | collective-permute-start | bytes 18874376 | tf_op jit(solution)/shard_map/ppermute | solution.py:64
  290.4 44.7 %collective-permute-start.53 = (bf16[1,128,6144]{2,1,0:T(8,128)(2,1)}, bf16[1,128,6144]{2,1,0:T(8,128)(2,1)S(1)}, u32[]{:S(2)}, u32[]{:S(2)}) collective-permute-start(bf16[1,128,6144]{2,1,0:T(8,128)(2,1)} %add_convert_fusion.1), channel_id=1, source_target_pairs={{0,2},{1,3},{2,0},{3,1},{4,6},{5,7},{6,4},{7,5},{8,10},{9,11},{10,... | collective-permute-start | bytes 4718600 | tf_op jit(solution)/shard_map/ppermute | solution.py:64
  291.2 43.9 %collective-permute-start.54 = (bf16[2,128,3072]{2,1,0:T(8,128)(2,1)}, bf16[2,128,3072]{2,1,0:T(8,128)(2,1)}, u32[]{:S(2)}, u32[]{:S(2)}) collective-permute-start(bf16[2,128,3072]{2,1,0:T(8,128)(2,1)} %add_convert_fusion), channel_id=1, source_target_pairs={{0,4},{4,0},{8,12},{12,8},{16,20},{20,16},{24,28},{28,24},{1,5},{5... | collective-permute-start | bytes 4718600 | tf_op jit(solution)/shard_map/ppermute | solution.py:64
  303.8 31.3 %collective-permute-start.55 = (bf16[1,768,256]{2,1,0:T(8,128)(2,1)}, bf16[1,768,256]{2,1,0:T(8,128)(2,1)}, u32[]{:S(2)}, u32[]{:S(2)}) collective-permute-start(bf16[1,768,256]{2,1,0:T(8,128)(2,1)} %pad_maximum_fusion.10), channel_id=1, source_target_pairs={{0,8},{4,12},{8,0},{12,4},{16,24},{20,28},{24,16},{28,20},{1,9},{5... | collective-permute-start | bytes 1179656 | tf_op jit(solution)/shard_map/ppermute | solution.py:64
  308.0 54.6 %collective-permute-start.58 = (bf16[1,256,1024]{2,1,0:T(8,128)(2,1)S(1)}, bf16[1,256,1024]{2,1,0:T(8,128)(2,1)S(1)}, u32[]{:S(2)}, u32[]{:S(2)}) collective-permute-start(bf16[1,256,1024]{2,1,0:T(8,128)(2,1)S(1)} %add_convert_fusion.12), channel_id=1, source_target_pairs={{0,2},{1,3},{2,0},{3,1},{4,6},{5,7},{6,4},{7,5},{8,10},{9,11},{10,... | collective-permute-start | bytes 1572872 | tf_op jit(solution)/shard_map/ppermute | solution.py:64
  309.5 53.1 %collective-permute-start.59 = (bf16[2,256,512]{2,1,0:T(8,128)(2,1)S(1)}, bf16[2,256,512]{2,1,0:T(8,128)(2,1)}, u32[]{:S(2)}, u32[]{:S(2)}) collective-permute-start(bf16[2,256,512]{2,1,0:T(8,128)(2,1)S(1)} %add_convert_fusion.11), channel_id=1, source_target_pairs={{0,4},{4,0},{8,12},{12,8},{16,20},{20,16},{24,28},{28,24},{1,5},{5... | collective-permute-start | bytes 1572872 | tf_op jit(solution)/shard_map/ppermute | solution.py:64
  338.5 26.8 %collective-permute-start.56 = (bf16[1,128,3072]{2,1,0:T(8,128)(2,1)S(1)}, bf16[1,128,3072]{2,1,0:T(8,128)(2,1)S(1)}, u32[]{:S(2)}, u32[]{:S(2)}) collective-permute-start(bf16[1,128,3072]{2,1,0:T(8,128)(2,1)S(1)} %get-tuple-element.277), channel_id=1, source_target_pairs={{0,4},{4,0},{8,12},{12,8},{16,20},{20,16},{24,28},{28,24},{1,5},{5... | collective-permute-start | bytes 2359304 | tf_op jit(solution)/shard_map/ppermute | solution.py:64
  340.0 25.3 %collective-permute-start.57 = (bf16[1,128,3072]{2,1,0:T(8,128)(2,1)S(1)}, bf16[1,128,3072]{2,1,0:T(8,128)(2,1)S(1)}, u32[]{:S(2)}, u32[]{:S(2)}) collective-permute-start(bf16[1,128,3072]{2,1,0:T(8,128)(2,1)S(1)} %get-tuple-element.276), channel_id=1, source_target_pairs={{0,2},{1,3},{2,0},{3,1},{4,6},{5,7},{6,4},{7,5},{8,10},{9,11},{10,... | collective-permute-start | bytes 2359304 | tf_op jit(solution)/shard_map/ppermute | solution.py:64
  379.1 24.4 %collective-permute-start.60 = (bf16[2,256,4096]{2,1,0:T(8,128)(2,1)S(1)}, bf16[2,256,4096]{2,1,0:T(8,128)(2,1)S(1)}, u32[]{:S(2)}, u32[]{:S(2)}) collective-permute-start(bf16[2,256,4096]{2,1,0:T(8,128)(2,1)S(1)} %get-tuple-element.203), channel_id=1, source_target_pairs={{0,1},{1,0},{2,3},{3,2},{4,5},{5,4},{6,7},{7,6},{8,9},{9,8},{10,11... | collective-permute-start | bytes 12582920 | tf_op jit(solution)/shard_map/ppermute | solution.py:64
  379.1 24.4 %collective-permute-start.61 = (bf16[1,256,1536]{2,1,0:T(8,128)(2,1)}, bf16[1,256,1536]{2,1,0:T(8,128)(2,1)S(1)}, u32[]{:S(2)}, u32[]{:S(2)}) collective-permute-start(bf16[1,256,1536]{2,1,0:T(8,128)(2,1)} %pad_maximum_fusion.2), channel_id=1, source_target_pairs={{0,8},{4,12},{8,0},{12,4},{16,24},{20,28},{24,16},{28,20},{1,9},{5... | collective-permute-start | bytes 2359304 | tf_op jit(solution)/shard_map/ppermute | solution.py:64
  379.8 39.7 %collective-permute-start.73 = (bf16[1,768,128]{2,1,0:T(8,128)(2,1)}, bf16[1,768,128]{2,1,0:T(8,128)(2,1)S(1)}, u32[]{:S(2)}, u32[]{:S(2)}) collective-permute-start(bf16[1,768,128]{2,1,0:T(8,128)(2,1)} %pad_maximum_fusion.20), channel_id=1, source_target_pairs={{0,16},{4,20},{8,24},{12,28},{16,0},{20,4},{24,8},{28,12},{1,17},{... | collective-permute-start | bytes 589832 | tf_op jit(solution)/shard_map/ppermute | solution.py:64
  382.5 28.2 %collective-permute-start.62 = (bf16[1,256,512]{2,1,0:T(8,128)(2,1)S(1)}, bf16[1,256,512]{2,1,0:T(8,128)(2,1)S(1)}, u32[]{:S(2)}, u32[]{:S(2)}) collective-permute-start(bf16[1,256,512]{2,1,0:T(8,128)(2,1)S(1)} %copy-done.51), channel_id=1, source_target_pairs={{0,4},{4,0},{8,12},{12,8},{16,20},{20,16},{24,28},{28,24},{1,5},{5... | collective-permute-start | bytes 786440 | tf_op jit(solution)/shard_map/ppermute | solution.py:64
  384.0 26.7 %collective-permute-start.63 = (bf16[1,256,512]{2,1,0:T(8,128)(2,1)S(1)}, bf16[1,256,512]{2,1,0:T(8,128)(2,1)S(1)}, u32[]{:S(2)}, u32[]{:S(2)}) collective-permute-start(bf16[1,256,512]{2,1,0:T(8,128)(2,1)S(1)} %get-tuple-element.300), channel_id=1, source_target_pairs={{0,2},{1,3},{2,0},{3,1},{4,6},{5,7},{6,4},{7,5},{8,10},{9,11},{10,... | collective-permute-start | bytes 786440 | tf_op jit(solution)/shard_map/ppermute | solution.py:64
  406.7 27.5 %collective-permute-start.64 = (bf16[1,128,4096]{2,1,0:T(8,128)(2,1)}, bf16[1,128,4096]{2,1,0:T(8,128)(2,1)}, u32[]{:S(2)}, u32[]{:S(2)}) collective-permute-start(bf16[1,128,4096]{2,1,0:T(8,128)(2,1)} %add_convert_fusion.4), channel_id=1, source_target_pairs={{0,2},{1,3},{2,0},{3,1},{4,6},{5,7},{6,4},{7,5},{8,10},{9,11},{10,... | collective-permute-start | bytes 3145736 | tf_op jit(solution)/shard_map/ppermute | solution.py:64
  410.1 24.7 %collective-permute-start.66 = (bf16[2,128,2048]{2,1,0:T(8,128)(2,1)}, bf16[2,128,2048]{2,1,0:T(8,128)(2,1)}, u32[]{:S(2)}, u32[]{:S(2)}) collective-permute-start(bf16[2,128,2048]{2,1,0:T(8,128)(2,1)} %add_convert_fusion.3), channel_id=1, source_target_pairs={{0,4},{4,0},{8,12},{12,8},{16,20},{20,16},{24,28},{28,24},{1,5},{5... | collective-permute-start | bytes 3145736 | tf_op jit(solution)/shard_map/ppermute | solution.py:64
  415.6 25.1 %collective-permute-start.72 = (bf16[1,256,768]{2,1,0:T(8,128)(2,1)}, bf16[1,256,768]{2,1,0:T(8,128)(2,1)S(1)}, u32[]{:S(2)}, u32[]{:S(2)}) collective-permute-start(bf16[1,256,768]{2,1,0:T(8,128)(2,1)} %pad_maximum_fusion.11), channel_id=1, source_target_pairs={{0,16},{4,20},{8,24},{12,28},{16,0},{20,4},{24,8},{28,12},{1,17},{... | collective-permute-start | bytes 1179656 | tf_op jit(solution)/shard_map/ppermute | solution.py:64
  481.1 49.6 %collective-permute-start.77 = (bf16[4,768,128]{2,1,0:T(8,128)(2,1)}, bf16[4,768,128]{2,1,0:T(8,128)(2,1)}, u32[]{:S(2)}, u32[]{:S(2)}) collective-permute-start(bf16[4,768,128]{2,1,0:T(8,128)(2,1)} %pad_maximum_fusion.4.rest_0_), channel_id=1, source_target_pairs={{0,4},{4,0},{8,12},{12,8},{16,20},{20,16},{24,28},{28,24},{1,5},{5... | collective-permute-start | bytes 2359304 | tf_op jit(solution)/shard_map/ppermute | solution.py:64
  481.9 35.4 %collective-permute-start.79 = (bf16[1,256,768]{2,1,0:T(8,128)(2,1)S(1)}, bf16[1,256,768]{2,1,0:T(8,128)(2,1)}, u32[]{:S(2)}, u32[]{:S(2)}) collective-permute-start(bf16[1,256,768]{2,1,0:T(8,128)(2,1)S(1)} %convert_bitcast_fusion), channel_id=1, source_target_pairs={{0,16},{4,20},{8,24},{12,28},{16,0},{20,4},{24,8},{28,12},{1,17},{... | collective-permute-start | bytes 1179656 | tf_op jit(solution)/shard_map/ppermute | solution.py:64
  519.2 28.6 %collective-permute-start.80 = (bf16[2,256,768]{2,1,0:T(8,128)(2,1)}, bf16[2,256,768]{2,1,0:T(8,128)(2,1)}, u32[]{:S(2)}, u32[]{:S(2)}) collective-permute-start(bf16[2,256,768]{2,1,0:T(8,128)(2,1)} %pad_maximum_fusion.5), channel_id=1, source_target_pairs={{0,8},{4,12},{8,0},{12,4},{16,24},{20,28},{24,16},{28,20},{1,9},{5... | collective-permute-start | bytes 2359304 | tf_op jit(solution)/shard_map/ppermute | solution.py:64
  524.1 31.4 %collective-permute-start.82 = (bf16[1,512,128]{2,1,0:T(8,128)(2,1)}, bf16[1,512,128]{2,1,0:T(8,128)(2,1)}, u32[]{:S(2)}, u32[]{:S(2)}) collective-permute-start(bf16[1,512,128]{2,1,0:T(8,128)(2,1)} %convert_bitcast_fusion.3), channel_id=1, source_target_pairs={{0,16},{4,20},{8,24},{12,28},{16,0},{20,4},{24,8},{28,12},{1,17},{... | collective-permute-start | bytes 393224 | tf_op jit(solution)/shard_map/ppermute | solution.py:64
  549.2 37.3 %collective-permute-start.81 = (bf16[4,256,768]{2,1,0:T(8,128)(2,1)S(1)}, bf16[4,256,768]{2,1,0:T(8,128)(2,1)S(1)}, u32[]{:S(2)}, u32[]{:S(2)}) collective-permute-start(bf16[4,256,768]{2,1,0:T(8,128)(2,1)S(1)} %pad_maximum_fusion.rest_0_), channel_id=1, source_target_pairs={{0,4},{4,0},{8,12},{12,8},{16,20},{20,16},{24,28},{28,24},{1,5},{5... | collective-permute-start | bytes 4718600 | tf_op jit(solution)/shard_map/ppermute | solution.py:64
  560.5 61.3 %collective-permute-start.85 = (bf16[4,256,512]{2,1,0:T(8,128)(2,1)S(1)}, bf16[4,256,512]{2,1,0:T(8,128)(2,1)S(1)}, u32[]{:S(2)}, u32[]{:S(2)}) collective-permute-start(bf16[4,256,512]{2,1,0:T(8,128)(2,1)S(1)} %pad_maximum_fusion.1.rest_0_), channel_id=1, source_target_pairs={{0,4},{4,0},{8,12},{12,8},{16,20},{20,16},{24,28},{28,24},{1,5},{5... | collective-permute-start | bytes 3145736 | tf_op jit(solution)/shard_map/ppermute | solution.py:64
  564.5 52.2 %collective-permute-start.84 = (bf16[4,512,128]{2,1,0:T(8,128)(2,1)S(1)}, bf16[4,512,128]{2,1,0:T(8,128)(2,1)S(1)}, u32[]{:S(2)}, u32[]{:S(2)}) collective-permute-start(bf16[4,512,128]{2,1,0:T(8,128)(2,1)S(1)} %pad_maximum_fusion.9.rest_0_), channel_id=1, source_target_pairs={{0,4},{4,0},{8,12},{12,8},{16,20},{20,16},{24,28},{28,24},{1,5},{5... | collective-permute-start | bytes 1572872 | tf_op jit(solution)/shard_map/ppermute | solution.py:64
  (126 other events, 1438.5 us)

commit v8 on v7

--- a/solution.py
+++ b/solution.py
@@ -167,7 +167,8 @@
     pieces += [(swap(v, GROUP, 1), dg ^ 1, at) for v, dg, at in pieces]
     if hold is not None:
         pieces[0] = (after(shard, hold), 0, none)
-    return place_rows(pieces, rows, owners), near, order, (by_one, by_two)
+    full = place_rows(pieces, rows, owners)
+    return full, near, order, (by_one, by_two)
 
 
 def gather_small(shard):
@@ -931,15 +932,15 @@
     mixed_low = attention_call(attend_body, projected, tables, segment_ids, head_gain, None, 0, HK, None)
     full_out, _, down_late, _ = gather_rows(out_weight, first, late, None, projected, mixed_low)
     full_gate_up, _, more_late, _ = gather_rows(gate_up_weight, first, late, projected, None, None)
-    full_down, _, _, _ = gather_rows(
-        down_weight, first, (down_late, more_late, projected), None, None, None
-    )
     attended = jnp.dot(mixed_low, full_out, preferred_element_type=jnp.float32)
     residual = inputs + attended
     root_two = lax.rsqrt(jnp.mean(residual * residual, axis=-1, keepdims=True) + EPS_NORM)
     normed_two = residual * root_two
     hidden_two = (normed_two * gain_two).astype(jnp.bfloat16)
     gate_part, upward, activated = gate_up_forward(hidden_two, full_gate_up)
+    full_down, _, _, _ = gather_rows(
+        down_weight, first, (down_late, more_late, projected), None, full_gate_up, activated
+    )
     down_sum = GradSum(activated, cotangent, True)
     grad_gate_up = gate_up_back(
         after(cotangent, *down_sum.blocks), full_down, gate_part, upward
@@ -1005,8 +1006,6 @@
         axis=1,
     )
     sent_next = qkv_sum.advance()
-    qkv_sum.advance()
-    sent_last = qkv_sum.advance()
     qkv_own, out_own, gate_up_own, down_own = owned = tuple(
         v.finish() for v in (qkv_sum, out_sum, gate_up_sum, down_sum)
     )
@@ -1027,8 +1026,8 @@
     )
     gathered = [
         gather_grad(after(qkv_own, summed), renewed_down[0], None),
-        gather_grad(after(out_own, *sent_last), None, None),
-        gather_grad(after(gate_up_own, *sent_last), summed, None),
+        gather_grad(after(out_own, *sent_next), None, None),
+        gather_grad(after(gate_up_own, *sent_next), None, summed),
     ]
     later = after(factor, gathered[0][0][0])
     renewed_gate_up = adam_blocks(

time: 645 us -> 616 us (0.955)
  waiting for transfers between devices: 198 us -> 180 us
  other arithmetic: 88.9 us -> 76.7 us
    ppermute x86, waiting for transfers between devices: 198 us -> 180 us  [swap(): return lax.ppermute(value, axis, [(i, i ^ mask) for i in range(count)])]
  transfers between devices with their start and end apart: 86 -> 86, of which waited for: 35 -> 34; matrix products, arithmetic and copies ran while one was open for 17% -> 16% of each run, Pallas kernels for 24% -> 25%
where the time goes in v8:
time: 616 us; the launch traced here: 604 us
  Pallas kernels  222 us (36%)
  waiting for transfers between devices  180 us (29%)
  other arithmetic  76.7 us (12%)
  starting transfers between devices  75.7 us (12%)
  local copies, waits for them, and re-layouts  26.3 us (4%)
  matrix products  17.8 us (3%)
  between operations  6.2 us (1%)
    ppermute x86, waiting for transfers between devices, swap(): return lax.ppermute(value, axis, [(i, i ^ mask) for i in range(count)])  180 us
    ppermute x86, starting transfers between devices, swap(): return lax.ppermute(value, axis, [(i, i ^ mask) for i in range(count)])  75.7 us
    pallas_call x3, Pallas kernels, attention_call(): pl.pallas_call(body, grid=(seq_count, count), in_specs=in_specs, out_spec...  53.6 us
    pallas_call x4, Pallas kernels, adam_blocks(): pl.pallas_call(body, out_shape=[jax.ShapeDtypeStruct(master.shape, jnp.fl...  44 us
    pallas_call x4, Pallas kernels, grad_blocks(): pl.pallas_call(body, out_shape=[jax.ShapeDtypeStruct((len(row_set), row_b...  38.6 us
    convert_element_type x20, other arithmetic, advance(): outgoing.append((self.read(far).astype(jnp.bfloat16), axis, mask))  36.4 us
    pallas_call x2, Pallas kernels, project_back(): pl.pallas_call(body, grid=(steps,), in_specs=[pl.BlockSpec((tokens, block...  24.1 us
    pallas_call x4, Pallas kernels, place_rows(): pl.pallas_call(body, out_shape=jax.ShapeDtypeStruct((rows * owners, colum...  18.6 us
  transfers between devices with their start and end apart: 86, of which 34 were waited for; matrix products, arithmetic and copies ran while one was open for 16% of the time, Pallas kernels for 25%

profile of v8, /device:TPU:0, one launch (start us, length us, event | category | flops | bytes accessed | tf_op | source)
XLA Modules:
  0.0 604.4 jit_solution(2513181274730843542)
XLA Ops:
  14.7 9.8 %collective-permute-done.2.refs_1_ = bf16[64,4096]{1,0:T(8,128)(2,1)} collective-permute-done((bf16[64,4096]{1,0:T(8,128)(2,1)S(1)}, bf16[64,4096]{1,0:T(8,128)(2,1)}, u32[]{:S(2)}, u32[]{:S(2)}) %collective-permute-start.2) | collective-permute-done | bytes 524320 | tf_op jit(solution)/shard_map/ppermute | solution.py:64
  31.0 8.5 %collective-permute-done.4.refs_3_ = bf16[64,4096]{1,0:T(8,128)(2,1)} collective-permute-done((bf16[64,4096]{1,0:T(8,128)(2,1)}, bf16[64,4096]{1,0:T(8,128)(2,1)}, u32[]{:S(2)}, u32[]{:S(2)}) %collective-permute-start.4) | collective-permute-done | bytes 524320 | tf_op jit(solution)/shard_map/ppermute | solution.py:64
  63.1 6.7 %fusion.10.query_ref.key_ref.value_ref = f32[512,4096]{1,0:T(8,128)} fusion(bf16[512,1024]{1,0:T(8,128)(2,1)S(1)} %fusion.2.left_ref, bf16[1024,4096]{1,0:T(8,128)(2,1)S(1)} %shard_map.311.weight_ref), kind=kOutput, calls=%fused_computation.121 | convolution fusion | flops 4294967296 | bytes 17825792 | tf_op jit(solution)/shard_map/dot_general | solution.py:930
  87.8 19.3 %collective-permute-done.17.refs_5_ = bf16[64,1024]{1,0:T(8,128)(2,1)} collective-permute-done((bf16[64,1024]{1,0:T(8,128)(2,1)}, bf16[64,1024]{1,0:T(8,128)(2,1)}, u32[]{:S(2)}, u32[]{:S(2)}) %collective-permute-start.17) | collective-permute-done | bytes 131104 | tf_op jit(solution)/shard_map/ppermute | solution.py:64
  109.1 17.2 %shard_map.312.left_ref = bf16[512,2048]{1,0:T(8,128)(2,1)S(1)} custom-call(f32[512,4096]{1,0:T(8,128)} %fusion.10.query_ref.key_ref.value_ref, f32[512,4096]{1,0:T(8,128)} %fusion.10.query_ref.key_ref.value_ref, f32[512,4096]{1,0:T(8,128)} %fusion.10.query_ref.key_ref.value_ref, f32[512,128]{1,0:T(8,128)S(1)} %get-tuple-element.327.cos_ref, ...), custom_call_target="tpu_custom_call" | custom-call | flops 4294967296 | bytes 12582912 | tf_op jit(solution)/shard_map/pallas_call | solution.py:738
  148.9 7.7 %shard_map.314.left_ref.right_ref.weight_ref = bf16[1024,6144]{1,0:T(8,128)(2,1)} custom-call(bf16[256,6144]{1,0:T(8,128)(2,1)S(1)} %convert_element_type.681.refs_0_, bf16[64,6144]{1,0:T(8,128)(2,1)} %collective-permute-done.24.refs_1_, bf16[64,6144]{1,0:T(8,128)(2,1)} %collective-permute-done.25.refs_2_, bf16[64,6144]{1,0:T(8,128)(2,1)} %collective-permute-done.26.refs_3_, ...), custom_call_target="tpu_custom_call" | custom-call | bytes 25165824 | tf_op jit(solution)/shard_map/pallas_call | solution.py:103
  156.6 13.2 %shard_map.315 = (f32[512,3072]{1,0:T(8,128)}, f32[512,3072]{1,0:T(8,128)}, bf16[512,3072]{1,0:T(8,128)(2,1)S(1)}) custom-call(bf16[512,1024]{1,0:T(8,128)(2,1)S(1)} %multiply_convert_fusion.hidden_ref.left_ref, bf16[1024,6144]{1,0:T(8,128)(2,1)} %shard_map.314.left_ref.right_ref.weight_ref, bf16[1024,6144]{1,0:T(8,128)(2,1)} %shard_map.314.left_ref.right_ref.weight_ref), custom_call_target="tpu_custom_call" | custom-call | flops 6442450944 | bytes 28311552 | tf_op jit(solution)/shard_map/pallas_call | solution.py:768
  171.4 8.9 %shard_map.316 = (bf16[2,768,1024]{2,1,0:T(8,128)(2,1)}, bf16[2,768,1024]{2,1,0:T(8,128)(2,1)}) custom-call(s32[2]{0:T(128)S(1)} %pad_add_fusion.where, bf16[512,3072]{1,0:T(8,128)(2,1)} %copy-done.24, bf16[512,1024]{1,0:T(8,128)(2,1)S(1)} %copy-done.19, bf16[512,1024]{1,0:T(8,128)(2,1)S(1)} %copy-done.19), custom_call_target="tpu_custom_call" | custom-call | flops 3221225472 | bytes 10485760 | tf_op jit(solution)/shard_map/pallas_call | solution.py:316
  181.7 10.6 %collective-permute-done.35.refs_1_ = bf16[192,1024]{1,0:T(8,128)(2,1)S(1)} collective-permute-done((bf16[192,1024]{1,0:T(8,128)(2,1)S(1)}, bf16[192,1024]{1,0:T(8,128)(2,1)S(1)}, u32[]{:S(2)}, u32[]{:S(2)}) %collective-permute-start.35) | collective-permute-done | bytes 393248 | tf_op jit(solution)/shard_map/ppermute | solution.py:64
  194.4 8.2 %collective-permute-done.36.refs_2_ = bf16[192,1024]{1,0:T(8,128)(2,1)S(1)} collective-permute-done((bf16[192,1024]{1,0:T(8,128)(2,1)S(1)}, bf16[192,1024]{1,0:T(8,128)(2,1)S(1)}, u32[]{:S(2)}, u32[]{:S(2)}) %collective-permute-start.36) | collective-permute-done | bytes 393248 | tf_op jit(solution)/shard_map/ppermute | solution.py:64
  220.1 12.9 %shard_map.318.rest_0_.grad_ref = bf16[512,6144]{1,0:T(8,128)(2,1)} custom-call(bf16[512,1024]{1,0:T(8,128)(2,1)S(1)} %copy-done.20, bf16[3072,1024]{1,0:T(8,128)(2,1)} %copy-done, f32[512,3072]{1,0:T(8,128)} %get-tuple-element.165.gate_ref, f32[512,3072]{1,0:T(8,128)} %get-tuple-element.166.up_ref), custom_call_target="tpu_custom_call" | custom-call | flops 3221225472 | bytes 25165824 | tf_op jit(solution)/shard_map/pallas_call | solution.py:878
  237.8 12.5 %shard_map.319 = (bf16[2,256,6144]{2,1,0:T(8,128)(2,1)}, bf16[2,256,6144]{2,1,0:T(8,128)(2,1)}) custom-call(s32[2]{0:T(128)S(1)} %pad_add_fusion.where, bf16[512,1024]{1,0:T(8,128)(2,1)S(1)} %copy-done.12, bf16[512,6144]{1,0:T(8,128)(2,1)} %shard_map.318.rest_0_.grad_ref), custom_call_target="tpu_custom_call" | custom-call | flops 6442450944 | bytes 19922944 | tf_op jit(solution)/shard_map/pallas_call | solution.py:316
  251.4 13.8 %shard_map.320 = (bf16[512,1024]{1,0:T(8,128)(2,1)S(1)}, f32[1,1024]{1,0:T(1,128)S(1)}, f32[512,1024]{1,0:T(8,128)S(1)}) custom-call(bf16[512,6144]{1,0:T(8,128)(2,1)} %shard_map.318.rest_0_.grad_ref, bf16[1024,6144]{1,0:T(8,128)(2,1)} %shard_map.314.left_ref.right_ref.weight_ref, f32[512,1024]{1,0:T(8,128)} %copy-done.30, bf16[512,1024]{1,0:T(8,128)(2,1)S(1)} %copy-done.20, ...), custom_call_target="tpu_custom_call" | custom-call | flops 6442450944 | bytes 26214400 | tf_op jit(solution)/shard_map/pallas_call | solution.py:836
  279.4 7.1 %shard_map.321 = (bf16[2,512,1024]{2,1,0:T(8,128)(2,1)S(1)}, bf16[2,512,1024]{2,1,0:T(8,128)(2,1)S(1)}) custom-call(s32[2]{0:T(128)S(1)} %pad_add_fusion.where, bf16[512,2048]{1,0:T(8,128)(2,1)} %copy-done.18, bf16[512,1024]{1,0:T(8,128)(2,1)S(1)} %get-tuple-element.185.rest_0_.rest_1_, bf16[512,1024]{1,0:T(8,128)(2,1)S(1)} %get-tuple-element.185.rest_0_.rest_1_), custom_call_target="tpu_custom_call" | custom-call | flops 2147483648 | bytes 7340032 | tf_op jit(solution)/shard_map/pallas_call | solution.py:316
  290.7 7.9 %collective-permute-done.50 = bf16[1,384,512]{2,1,0:T(8,128)(2,1)S(1)} collective-permute-done((bf16[1,384,512]{2,1,0:T(8,128)(2,1)S(1)}, bf16[1,384,512]{2,1,0:T(8,128)(2,1)S(1)}, u32[]{:S(2)}, u32[]{:S(2)}) %collective-permute-start.50) | collective-permute-done | bytes 393248 | tf_op jit(solution)/shard_map/ppermute | solution.py:64
  309.1 17.3 %shard_map.322 = (bf16[512,4096]{1,0:T(8,128)(2,1)}, f32[2,128]{1,0:T(2,128)S(1)}) custom-call(f32[512,4096]{1,0:T(8,128)} %fusion.10.query_ref.key_ref.value_ref, f32[512,4096]{1,0:T(8,128)} %fusion.10.query_ref.key_ref.value_ref, f32[512,4096]{1,0:T(8,128)} %fusion.10.query_ref.key_ref.value_ref, f32[512,128]{1,0:T(8,128)S(1)} %get-tuple-element.327.cos_ref, ...), custom_call_target="tpu_custom_call" | custom-call | flops 5368709120 | bytes 12582912 | tf_op jit(solution)/shard_map/pallas_call | solution.py:738
  326.4 6.4 %collective-permute-done.53 = bf16[1,128,6144]{2,1,0:T(8,128)(2,1)S(1)} collective-permute-done((bf16[1,128,6144]{2,1,0:T(8,128)(2,1)}, bf16[1,128,6144]{2,1,0:T(8,128)(2,1)S(1)}, u32[]{:S(2)}, u32[]{:S(2)}) %collective-permute-start.53) | collective-permute-done | bytes 1572896 | tf_op jit(solution)/shard_map/ppermute | solution.py:64
  341.5 19.1 %shard_map.323 = (bf16[512,4096]{1,0:T(8,128)(2,1)}, f32[2,128]{1,0:T(2,128)S(1)}) custom-call(f32[512,4096]{1,0:T(8,128)} %fusion.10.query_ref.key_ref.value_ref, f32[512,4096]{1,0:T(8,128)} %fusion.10.query_ref.key_ref.value_ref, f32[512,4096]{1,0:T(8,128)} %fusion.10.query_ref.key_ref.value_ref, ...), custom_call_target="tpu_custom_call", output_to_operand_aliasing={{0}: (9, {})} | custom-call | flops 5368709120 | bytes 12582912 | tf_op jit(solution)/shard_map/pallas_call | solution.py:738
  365.1 10.2 %shard_map.324 = (bf16[2,256,4096]{2,1,0:T(8,128)(2,1)}, bf16[2,256,4096]{2,1,0:T(8,128)(2,1)}) custom-call(s32[2]{0:T(128)S(1)} %pad_add_fusion.where, bf16[512,1024]{1,0:T(8,128)(2,1)S(1)} %copy-done.22, bf16[512,4096]{1,0:T(8,128)(2,1)} %get-tuple-element.235.rest_0_.grad_ref), custom_call_target="tpu_custom_call" | custom-call | flops 4294967296 | bytes 13631488 | tf_op jit(solution)/shard_map/pallas_call | solution.py:316
  380.8 18.8 %collective-permute-done.61 = bf16[1,256,1536]{2,1,0:T(8,128)(2,1)S(1)} collective-permute-done((bf16[1,256,1536]{2,1,0:T(8,128)(2,1)}, bf16[1,256,1536]{2,1,0:T(8,128)(2,1)S(1)}, u32[]{:S(2)}, u32[]{:S(2)}) %collective-permute-start.61) | collective-permute-done | bytes 786464 | tf_op jit(solution)/shard_map/ppermute | solution.py:64
  412.3 10.3 %shard_map.325 = (bf16[512,1024]{1,0:T(8,128)(2,1)}, f32[1,1024]{1,0:T(1,128)S(1)}) custom-call(bf16[512,4096]{1,0:T(8,128)(2,1)} %get-tuple-element.235.rest_0_.grad_ref, bf16[1024,4096]{1,0:T(8,128)(2,1)} %copy-done.3, bf16[512,1024]{1,0:T(8,128)(2,1)S(1)} %copy-done.15, f32[512,1024]{1,0:T(8,128)S(1)} %copy-done.26, f32[1,1024]{1,0:T(1,128)S(1)} %bitcast.100), custom_call_target="tpu_custom_call" | custom-call | flops 4294967296 | bytes 19922944 | tf_op jit(solution)/shard_map/pallas_call | solution.py:836
  426.2 6.4 %collective-permute-done.72 = bf16[1,256,768]{2,1,0:T(8,128)(2,1)S(1)} collective-permute-done((bf16[1,256,768]{2,1,0:T(8,128)(2,1)S(1)}, bf16[1,256,768]{2,1,0:T(8,128)(2,1)S(1)}, u32[]{:S(2)}, u32[]{:S(2)}) %collective-permute-start.72) | collective-permute-done | bytes 393248 | tf_op jit(solution)/shard_map/ppermute | solution.py:64
  452.9 10.9 %collective-permute-done.82 = bf16[1,512,128]{2,1,0:T(8,128)(2,1)S(1)} collective-permute-done((bf16[1,512,128]{2,1,0:T(8,128)(2,1)S(1)}, bf16[1,512,128]{2,1,0:T(8,128)(2,1)S(1)}, u32[]{:S(2)}, u32[]{:S(2)}) %collective-permute-start.82) | collective-permute-done | bytes 131104 | tf_op jit(solution)/shard_map/ppermute | solution.py:64
  477.4 14.9 %collective-permute-done.75 = bf16[2,768,128]{2,1,0:T(8,128)(2,1)S(1)} collective-permute-done((bf16[2,768,128]{2,1,0:T(8,128)(2,1)S(1)}, bf16[2,768,128]{2,1,0:T(8,128)(2,1)S(1)}, u32[]{:S(2)}, u32[]{:S(2)}) %collective-permute-start.75) | collective-permute-done | bytes 393248 | tf_op jit(solution)/shard_map/ppermute | solution.py:64
  499.0 16.5 %shard_map.326 = f32[8,1152]{1,0:T(8,128)} custom-call(f32[8,1152]{1,0:T(8,128)} %select_maximum_fusion.in_ref), custom_call_target="tpu_custom_call" | custom-call | tf_op jit(solution)/shard_map/pallas_call | solution.py:230
  526.4 9.9 %shard_map.327 = (f32[768,1024]{1,0:T(8,128)}, f32[2,768,1024]{2,1,0:T(8,128)}) custom-call(s32[1]{0:T(128)} %bitcast.8.where, f32[1,1]{1,0:T(1,128)} %bitcast.20.factor_ref, f32[768,1024]{1,0:T(8,128)S(1)} %copy-done.2, f32[2,768,1024]{2,1,0:T(8,128)} %moment_ref.4, bf16[4,768,128]{2,1,0:T(8,128)(2,1)S(1)} %pad_maximum_fusion.4.rest_0_, ...), custom_call_target="tpu_custom_call" | custom-call | flops 15728640 | bytes 20447232 | tf_op jit(solution)/shard_map/pallas_call | solution.py:487
  538.0 6.3 %add_convert_fusion.2 = bf16[512,1024]{1,0:T(8,128)(2,1)} fusion(f32[512,1024]{1,0:T(8,128)S(1)} %copy-done.31, bf16[512,3072]{1,0:T(8,128)(2,1)} %copy-done.24, bf16[3072,1024]{1,0:T(8,128)(2,1)S(1)} %bitcast.95), kind=kOutput, calls=%fused_computation.9 | convolution fusion | flops 3222274048 | bytes 12582912 | tf_op jit(solution)/shard_map/dot_general | solution.py:994
  555.3 6.4 %collective-permute-done.81.rest_1_ = bf16[4,256,768]{2,1,0:T(8,128)(2,1)S(1)} collective-permute-done((bf16[4,256,768]{2,1,0:T(8,128)(2,1)}, bf16[4,256,768]{2,1,0:T(8,128)(2,1)S(1)}, u32[]{:S(2)}, u32[]{:S(2)}) %collective-permute-start.81) | collective-permute-done | bytes 1572896 | tf_op jit(solution)/shard_map/ppermute | solution.py:64
  561.6 18.4 %shard_map.328 = (f32[256,6144]{1,0:T(8,128)}, f32[2,256,6144]{2,1,0:T(8,128)}) custom-call(s32[1]{0:T(128)} %bitcast.8.where, f32[1,1]{1,0:T(1,128)} %bitcast.21.factor_ref, f32[256,6144]{1,0:T(8,128)} %master_ref.5, f32[2,256,6144]{2,1,0:T(8,128)} %moment_ref.5, bf16[4,256,768]{2,1,0:T(8,128)(2,1)S(1)} %copy-done.6, ...), custom_call_target="tpu_custom_call" | custom-call | flops 31457280 | bytes 40894464 | tf_op jit(solution)/shard_map/pallas_call | solution.py:487
  580.1 5.2 shard_map.329
  585.3 8.2 %collective-permute-done.85.rest_1_ = bf16[4,256,512]{2,1,0:T(8,128)(2,1)S(1)} collective-permute-done((bf16[4,256,512]{2,1,0:T(8,128)(2,1)S(1)}, bf16[4,256,512]{2,1,0:T(8,128)(2,1)S(1)}, u32[]{:S(2)}, u32[]{:S(2)}) %collective-permute-start.85) | collective-permute-done | bytes 1048608 | tf_op jit(solution)/shard_map/ppermute | solution.py:64
  593.4 10.5 %shard_map.330 = (f32[256,4096]{1,0:T(8,128)}, f32[2,256,4096]{2,1,0:T(8,128)}) custom-call(s32[1]{0:T(128)} %bitcast.8.where, f32[1,1]{1,0:T(1,128)} %bitcast.25.factor_ref, f32[256,4096]{1,0:T(8,128)} %master_ref.7, f32[2,256,4096]{2,1,0:T(8,128)} %moment_ref.7, bf16[4,256,512]{2,1,0:T(8,128)(2,1)S(1)} %pad_maximum_fusion.1.rest_0_, ...), custom_call_target="tpu_custom_call" | custom-call | flops 20971520 | bytes 27262976 | tf_op jit(solution)/shard_map/pallas_call | solution.py:487
  (424 shorter events, 238.2 us)
Async XLA Ops:
  2.0 28.3 %collective-permute-start = (bf16[1,2,288]{2,1,0:T(2,128)(2,1)S(1)}, bf16[1,2,288]{2,1,0:T(2,128)(2,1)S(1)}, u32[]{:S(2)}, u32[]{:S(2)}) collective-permute-start(bf16[1,2,288]{2,1,0:T(2,128)(2,1)S(1)} %pad_maximum_fusion.26), channel_id=1, source_target_pairs={{0,2},{1,3},{2,0},{3,1},{4,6},{5,7},{6,4},{7,5},{8,10},{9,11},{10,... | collective-permute-start | bytes 3464 | tf_op jit(solution)/shard_map/ppermute | solution.py:64
  8.9 49.2 %collective-permute-start.7 = (bf16[256,4096]{1,0:T(8,128)(2,1)}, bf16[256,4096]{1,0:T(8,128)(2,1)}, u32[]{:S(2)}, u32[]{:S(2)}) collective-permute-start(bf16[256,4096]{1,0:T(8,128)(2,1)} %convert_element_type.673.refs_0_), channel_id=1, source_target_pairs={{0,1},{1,0},{2,3},{3,2},{4,5},{5,4},{6,7},{7,6},{8,9},{9,8},{10,11... | collective-permute-start | bytes 6291464 | tf_op jit(solution)/shard_map/ppermute | solution.py:64
  55.3 28.5 %collective-permute-start.18 = (bf16[512,1024]{1,0:T(8,128)(2,1)}, bf16[512,1024]{1,0:T(8,128)(2,1)}, u32[]{:S(2)}, u32[]{:S(2)}) collective-permute-start(bf16[512,1024]{1,0:T(8,128)(2,1)} %convert_element_type.677.refs_0_), channel_id=1, source_target_pairs={{0,1},{1,0},{2,3},{3,2},{4,5},{5,4},{6,7},{7,6},{8,9},{9,8},{10,11... | collective-permute-start | bytes 3145736 | tf_op jit(solution)/shard_map/ppermute | solution.py:64
  55.9 91.6 %collective-permute-start.29 = (bf16[256,6144]{1,0:T(8,128)(2,1)S(1)}, bf16[256,6144]{1,0:T(8,128)(2,1)}, u32[]{:S(2)}, u32[]{:S(2)}) collective-permute-start(bf16[256,6144]{1,0:T(8,128)(2,1)S(1)} %convert_element_type.681.refs_0_), channel_id=1, source_target_pairs={{0,1},{1,0},{2,3},{3,2},{4,5},{5,4},{6,7},{7,6},{8,9},{9,8},{10,11... | collective-permute-start | bytes 9437192 | tf_op jit(solution)/shard_map/ppermute | solution.py:64
  83.8 53.8 %collective-permute-start.30 = (bf16[64,6144]{1,0:T(8,128)(2,1)}, bf16[64,6144]{1,0:T(8,128)(2,1)}, u32[]{:S(2)}, u32[]{:S(2)}) collective-permute-start(bf16[64,6144]{1,0:T(8,128)(2,1)} %collective-permute-done.24.refs_1_), channel_id=1, source_target_pairs={{0,1},{1,0},{2,3},{3,2},{4,5},{5,4},{6,7},{7,6},{8,9},{9,8},{10,11... | collective-permute-start | bytes 2359304 | tf_op jit(solution)/shard_map/ppermute | solution.py:64
  83.8 51.1 %collective-permute-start.25 = (bf16[64,6144]{1,0:T(8,128)(2,1)}, bf16[64,6144]{1,0:T(8,128)(2,1)}, u32[]{:S(2)}, u32[]{:S(2)}) collective-permute-start(bf16[64,6144]{1,0:T(8,128)(2,1)} %collective-permute-done.24.refs_1_), channel_id=1, source_target_pairs={{0,4},{4,0},{8,12},{12,8},{16,20},{20,16},{24,28},{28,24},{1,5},{5... | collective-permute-start | bytes 2359304 | tf_op jit(solution)/shard_map/ppermute | solution.py:64
  84.4 47.6 %collective-permute-start.26 = (bf16[64,6144]{1,0:T(8,128)(2,1)}, bf16[64,6144]{1,0:T(8,128)(2,1)}, u32[]{:S(2)}, u32[]{:S(2)}) collective-permute-start(bf16[64,6144]{1,0:T(8,128)(2,1)} %collective-permute-done.24.refs_1_), channel_id=1, source_target_pairs={{0,8},{4,12},{8,0},{12,4},{16,24},{20,28},{24,16},{28,20},{1,9},{5... | collective-permute-start | bytes 2359304 | tf_op jit(solution)/shard_map/ppermute | solution.py:64
  180.3 52.7 %collective-permute-start.46 = (bf16[2,768,1024]{2,1,0:T(8,128)(2,1)}, bf16[2,768,1024]{2,1,0:T(8,128)(2,1)}, u32[]{:S(2)}, u32[]{:S(2)}) collective-permute-start(bf16[2,768,1024]{2,1,0:T(8,128)(2,1)} %get-tuple-element.155), channel_id=1, source_target_pairs={{0,1},{1,0},{2,3},{3,2},{4,5},{5,4},{6,7},{7,6},{8,9},{9,8},{10,11... | collective-permute-start | bytes 9437192 | tf_op jit(solution)/shard_map/ppermute | solution.py:64
  180.7 29.6 %collective-permute-start.40 = (bf16[768,1024]{1,0:T(8,128)(2,1)S(1)}, bf16[768,1024]{1,0:T(8,128)(2,1)S(1)}, u32[]{:S(2)}, u32[]{:S(2)}) collective-permute-start(bf16[768,1024]{1,0:T(8,128)(2,1)S(1)} %convert_element_type.682.refs_0_), channel_id=1, source_target_pairs={{0,1},{1,0},{2,3},{3,2},{4,5},{5,4},{6,7},{7,6},{8,9},{9,8},{10,11... | collective-permute-start | bytes 4718600 | tf_op jit(solution)/shard_map/ppermute | solution.py:64
  288.6 44.2 %collective-permute-start.53 = (bf16[1,128,6144]{2,1,0:T(8,128)(2,1)}, bf16[1,128,6144]{2,1,0:T(8,128)(2,1)S(1)}, u32[]{:S(2)}, u32[]{:S(2)}) collective-permute-start(bf16[1,128,6144]{2,1,0:T(8,128)(2,1)} %add_convert_fusion.1), channel_id=1, source_target_pairs={{0,2},{1,3},{2,0},{3,1},{4,6},{5,7},{6,4},{7,5},{8,10},{9,11},{10,... | collective-permute-start | bytes 4718600 | tf_op jit(solution)/shard_map/ppermute | solution.py:64
  289.2 43.7 %collective-permute-start.54 = (bf16[2,128,3072]{2,1,0:T(8,128)(2,1)}, bf16[2,128,3072]{2,1,0:T(8,128)(2,1)}, u32[]{:S(2)}, u32[]{:S(2)}) collective-permute-start(bf16[2,128,3072]{2,1,0:T(8,128)(2,1)} %add_convert_fusion), channel_id=1, source_target_pairs={{0,4},{4,0},{8,12},{12,8},{16,20},{20,16},{24,28},{28,24},{1,5},{5... | collective-permute-start | bytes 4718600 | tf_op jit(solution)/shard_map/ppermute | solution.py:64
  301.6 31.3 %collective-permute-start.55 = (bf16[1,768,256]{2,1,0:T(8,128)(2,1)}, bf16[1,768,256]{2,1,0:T(8,128)(2,1)}, u32[]{:S(2)}, u32[]{:S(2)}) collective-permute-start(bf16[1,768,256]{2,1,0:T(8,128)(2,1)} %pad_maximum_fusion.10), channel_id=1, source_target_pairs={{0,8},{4,12},{8,0},{12,4},{16,24},{20,28},{24,16},{28,20},{1,9},{5... | collective-permute-start | bytes 1179656 | tf_op jit(solution)/shard_map/ppermute | solution.py:64
  305.8 54.8 %collective-permute-start.58 = (bf16[1,256,1024]{2,1,0:T(8,128)(2,1)S(1)}, bf16[1,256,1024]{2,1,0:T(8,128)(2,1)S(1)}, u32[]{:S(2)}, u32[]{:S(2)}) collective-permute-start(bf16[1,256,1024]{2,1,0:T(8,128)(2,1)S(1)} %add_convert_fusion.12), channel_id=1, source_target_pairs={{0,2},{1,3},{2,0},{3,1},{4,6},{5,7},{6,4},{7,5},{8,10},{9,11},{10,... | collective-permute-start | bytes 1572872 | tf_op jit(solution)/shard_map/ppermute | solution.py:64
  307.5 53.1 %collective-permute-start.59 = (bf16[2,256,512]{2,1,0:T(8,128)(2,1)S(1)}, bf16[2,256,512]{2,1,0:T(8,128)(2,1)S(1)}, u32[]{:S(2)}, u32[]{:S(2)}) collective-permute-start(bf16[2,256,512]{2,1,0:T(8,128)(2,1)S(1)} %add_convert_fusion.11), channel_id=1, source_target_pairs={{0,4},{4,0},{8,12},{12,8},{16,20},{20,16},{24,28},{28,24},{1,5},{5... | collective-permute-start | bytes 1572872 | tf_op jit(solution)/shard_map/ppermute | solution.py:64
  336.3 25.3 %collective-permute-start.56 = (bf16[1,128,3072]{2,1,0:T(8,128)(2,1)S(1)}, bf16[1,128,3072]{2,1,0:T(8,128)(2,1)S(1)}, u32[]{:S(2)}, u32[]{:S(2)}) collective-permute-start(bf16[1,128,3072]{2,1,0:T(8,128)(2,1)S(1)} %get-tuple-element.287), channel_id=1, source_target_pairs={{0,4},{4,0},{8,12},{12,8},{16,20},{20,16},{24,28},{28,24},{1,5},{5... | collective-permute-start | bytes 2359304 | tf_op jit(solution)/shard_map/ppermute | solution.py:64
  337.9 23.8 %collective-permute-start.57 = (bf16[1,128,3072]{2,1,0:T(8,128)(2,1)S(1)}, bf16[1,128,3072]{2,1,0:T(8,128)(2,1)S(1)}, u32[]{:S(2)}, u32[]{:S(2)}) collective-permute-start(bf16[1,128,3072]{2,1,0:T(8,128)(2,1)S(1)} %get-tuple-element.286), channel_id=1, source_target_pairs={{0,2},{1,3},{2,0},{3,1},{4,6},{5,7},{6,4},{7,5},{8,10},{9,11},{10,... | collective-permute-start | bytes 2359304 | tf_op jit(solution)/shard_map/ppermute | solution.py:64
  375.3 24.4 %collective-permute-start.60 = (bf16[2,256,4096]{2,1,0:T(8,128)(2,1)}, bf16[2,256,4096]{2,1,0:T(8,128)(2,1)}, u32[]{:S(2)}, u32[]{:S(2)}) collective-permute-start(bf16[2,256,4096]{2,1,0:T(8,128)(2,1)} %get-tuple-element.213), channel_id=1, source_target_pairs={{0,1},{1,0},{2,3},{3,2},{4,5},{5,4},{6,7},{7,6},{8,9},{9,8},{10,11... | collective-permute-start | bytes 12582920 | tf_op jit(solution)/shard_map/ppermute | solution.py:64
  375.3 24.4 %collective-permute-start.61 = (bf16[1,256,1536]{2,1,0:T(8,128)(2,1)}, bf16[1,256,1536]{2,1,0:T(8,128)(2,1)S(1)}, u32[]{:S(2)}, u32[]{:S(2)}) collective-permute-start(bf16[1,256,1536]{2,1,0:T(8,128)(2,1)} %pad_maximum_fusion.2), channel_id=1, source_target_pairs={{0,8},{4,12},{8,0},{12,4},{16,24},{20,28},{24,16},{28,20},{1,9},{5... | collective-permute-start | bytes 2359304 | tf_op jit(solution)/shard_map/ppermute | solution.py:64
  376.9 45.8 %collective-permute-start.73 = (bf16[1,768,128]{2,1,0:T(8,128)(2,1)}, bf16[1,768,128]{2,1,0:T(8,128)(2,1)S(1)}, u32[]{:S(2)}, u32[]{:S(2)}) collective-permute-start(bf16[1,768,128]{2,1,0:T(8,128)(2,1)} %pad_maximum_fusion.20), channel_id=1, source_target_pairs={{0,16},{4,20},{8,24},{12,28},{16,0},{20,4},{24,8},{28,12},{1,17},{... | collective-permute-start | bytes 589832 | tf_op jit(solution)/shard_map/ppermute | solution.py:64
  379.5 25.7 %collective-permute-start.62 = (bf16[1,256,512]{2,1,0:T(8,128)(2,1)}, bf16[1,256,512]{2,1,0:T(8,128)(2,1)S(1)}, u32[]{:S(2)}, u32[]{:S(2)}) collective-permute-start(bf16[1,256,512]{2,1,0:T(8,128)(2,1)} %get-tuple-element.311), channel_id=1, source_target_pairs={{0,4},{4,0},{8,12},{12,8},{16,20},{20,16},{24,28},{28,24},{1,5},{5... | collective-permute-start | bytes 786440 | tf_op jit(solution)/shard_map/ppermute | solution.py:64
  380.0 25.2 %collective-permute-start.63 = (bf16[1,256,512]{2,1,0:T(8,128)(2,1)S(1)}, bf16[1,256,512]{2,1,0:T(8,128)(2,1)S(1)}, u32[]{:S(2)}, u32[]{:S(2)}) collective-permute-start(bf16[1,256,512]{2,1,0:T(8,128)(2,1)S(1)} %get-tuple-element.310), channel_id=1, source_target_pairs={{0,2},{1,3},{2,0},{3,1},{4,6},{5,7},{6,4},{7,5},{8,10},{9,11},{10,... | collective-permute-start | bytes 786440 | tf_op jit(solution)/shard_map/ppermute | solution.py:64
  401.8 32.4 %collective-permute-start.64 = (bf16[1,128,4096]{2,1,0:T(8,128)(2,1)S(1)}, bf16[1,128,4096]{2,1,0:T(8,128)(2,1)S(1)}, u32[]{:S(2)}, u32[]{:S(2)}) collective-permute-start(bf16[1,128,4096]{2,1,0:T(8,128)(2,1)S(1)} %add_convert_fusion.4), channel_id=1, source_target_pairs={{0,2},{1,3},{2,0},{3,1},{4,6},{5,7},{6,4},{7,5},{8,10},{9,11},{10,... | collective-permute-start | bytes 3145736 | tf_op jit(solution)/shard_map/ppermute | solution.py:64
  404.5 29.8 %collective-permute-start.66 = (bf16[2,128,2048]{2,1,0:T(8,128)(2,1)S(1)}, bf16[2,128,2048]{2,1,0:T(8,128)(2,1)S(1)}, u32[]{:S(2)}, u32[]{:S(2)}) collective-permute-start(bf16[2,128,2048]{2,1,0:T(8,128)(2,1)S(1)} %add_convert_fusion.3), channel_id=1, source_target_pairs={{0,4},{4,0},{8,12},{12,8},{16,20},{20,16},{24,28},{28,24},{1,5},{5... | collective-permute-start | bytes 3145736 | tf_op jit(solution)/shard_map/ppermute | solution.py:64
  408.3 24.3 %collective-permute-start.72 = (bf16[1,256,768]{2,1,0:T(8,128)(2,1)S(1)}, bf16[1,256,768]{2,1,0:T(8,128)(2,1)S(1)}, u32[]{:S(2)}, u32[]{:S(2)}) collective-permute-start(bf16[1,256,768]{2,1,0:T(8,128)(2,1)S(1)} %pad_maximum_fusion.11), channel_id=1, source_target_pairs={{0,16},{4,20},{8,24},{12,28},{16,0},{20,4},{24,8},{28,12},{1,17},{... | collective-permute-start | bytes 1179656 | tf_op jit(solution)/shard_map/ppermute | solution.py:64
  441.2 27.9 %collective-permute-start.74 = (bf16[1,768,128]{2,1,0:T(8,128)(2,1)S(1)}, bf16[1,768,128]{2,1,0:T(8,128)(2,1)S(1)}, u32[]{:S(2)}, u32[]{:S(2)}) collective-permute-start(bf16[1,768,128]{2,1,0:T(8,128)(2,1)S(1)} %convert_bitcast_fusion.2), channel_id=1, source_target_pairs={{0,16},{4,20},{8,24},{12,28},{16,0},{20,4},{24,8},{28,12},{1,17},{... | collective-permute-start | bytes 589832 | tf_op jit(solution)/shard_map/ppermute | solution.py:64
  448.0 26.4 %collective-permute-start.68 = (bf16[1,256,1024]{2,1,0:T(8,128)(2,1)S(1)}, bf16[1,256,1024]{2,1,0:T(8,128)(2,1)S(1)}, u32[]{:S(2)}, u32[]{:S(2)}) collective-permute-start(bf16[1,256,1024]{2,1,0:T(8,128)(2,1)S(1)} %pad_maximum_fusion.6), channel_id=1, source_target_pairs={{0,8},{4,12},{8,0},{12,4},{16,24},{20,28},{24,16},{28,20},{1,9},{5... | collective-permute-start | bytes 1572872 | tf_op jit(solution)/shard_map/ppermute | solution.py:64
  464.6 79.8 %collective-permute-start.83 = (bf16[2,512,128]{2,1,0:T(8,128)(2,1)}, bf16[2,512,128]{2,1,0:T(8,128)(2,1)}, u32[]{:S(2)}, u32[]{:S(2)}) collective-permute-start(bf16[2,512,128]{2,1,0:T(8,128)(2,1)} %pad_maximum_fusion.19), channel_id=1, source_target_pairs={{0,8},{4,12},{8,0},{12,4},{16,24},{20,28},{24,16},{28,20},{1,9},{5... | collective-permute-start | bytes 786440 | tf_op jit(solution)/shard_map/ppermute | solution.py:64
  475.8 41.7 %collective-permute-start.80 = (bf16[2,256,768]{2,1,0:T(8,128)(2,1)S(1)}, bf16[2,256,768]{2,1,0:T(8,128)(2,1)}, u32[]{:S(2)}, u32[]{:S(2)}) collective-permute-start(bf16[2,256,768]{2,1,0:T(8,128)(2,1)S(1)} %pad_maximum_fusion.5), channel_id=1, source_target_pairs={{0,8},{4,12},{8,0},{12,4},{16,24},{20,28},{24,16},{28,20},{1,9},{5... | collective-permute-start | bytes 2359304 | tf_op jit(solution)/shard_map/ppermute | solution.py:64
  492.4 32.1 %collective-permute-start.77 = (bf16[4,768,128]{2,1,0:T(8,128)(2,1)S(1)}, bf16[4,768,128]{2,1,0:T(8,128)(2,1)}, u32[]{:S(2)}, u32[]{:S(2)}) collective-permute-start(bf16[4,768,128]{2,1,0:T(8,128)(2,1)S(1)} %pad_maximum_fusion.4.rest_0_), channel_id=1, source_target_pairs={{0,4},{4,0},{8,12},{12,8},{16,20},{20,16},{24,28},{28,24},{1,5},{5... | collective-permute-start | bytes 2359304 | tf_op jit(solution)/shard_map/ppermute | solution.py:64
  524.1 37.5 %collective-permute-start.81 = (bf16[4,256,768]{2,1,0:T(8,128)(2,1)}, bf16[4,256,768]{2,1,0:T(8,128)(2,1)S(1)}, u32[]{:S(2)}, u32[]{:S(2)}) collective-permute-start(bf16[4,256,768]{2,1,0:T(8,128)(2,1)} %pad_maximum_fusion.rest_0_), channel_id=1, source_target_pairs={{0,4},{4,0},{8,12},{12,8},{16,20},{20,16},{24,28},{28,24},{1,5},{5... | collective-permute-start | bytes 4718600 | tf_op jit(solution)/shard_map/ppermute | solution.py:64
  545.5 34.6 %collective-permute-start.84 = (bf16[4,512,128]{2,1,0:T(8,128)(2,1)S(1)}, bf16[4,512,128]{2,1,0:T(8,128)(2,1)S(1)}, u32[]{:S(2)}, u32[]{:S(2)}) collective-permute-start(bf16[4,512,128]{2,1,0:T(8,128)(2,1)S(1)} %pad_maximum_fusion.9.rest_0_), channel_id=1, source_target_pairs={{0,4},{4,0},{8,12},{12,8},{16,20},{20,16},{24,28},{28,24},{1,5},{5... | collective-permute-start | bytes 1572872 | tf_op jit(solution)/shard_map/ppermute | solution.py:64
  551.1 42.3 %collective-permute-start.85 = (bf16[4,256,512]{2,1,0:T(8,128)(2,1)S(1)}, bf16[4,256,512]{2,1,0:T(8,128)(2,1)S(1)}, u32[]{:S(2)}, u32[]{:S(2)}) collective-permute-start(bf16[4,256,512]{2,1,0:T(8,128)(2,1)S(1)} %pad_maximum_fusion.1.rest_0_), channel_id=1, source_target_pairs={{0,4},{4,0},{8,12},{12,8},{16,20},{20,16},{24,28},{28,24},{1,5},{5... | collective-permute-start | bytes 3145736 | tf_op jit(solution)/shard_map/ppermute | solution.py:64
  (129 other events, 1482.9 us)
